TPU v7x, 128 devices: a whole 4x4x4 slice. The times are simulated.
128 devices in a mesh: face: 2 (over z_lo), gx: 8 (over y, core), gy: 8 (over x, z_hi).
Axes of the slice: x: 4, y: 4, z: 4 (z_hi: 2, z_lo: 2; z = z_hi * 2 + z_lo), core: 2. Of those that a mesh axis runs over, the one named last changes fastest.
Arguments:
- atmos_state: float32 [4, 32, 512, 1024], P(None, None, ('face', 'gy'), 'gx'), may hold values from -5 to 5
- atmos_kappa: float32 [512, 1024], P(('face', 'gy'), 'gx'), may hold values from 0.05 to 0.24
- ocean_tracers: float32 [2, 32, 512, 1024], P(None, None, ('face', 'gy'), 'gx'), may hold values from -5 to 5
- ocean_flow: float32 [2, 32, 512, 1024], P(None, None, ('face', 'gy'), 'gx'), may hold values from -0.3 to 0.3
- ocean_kappa: float32 [32, 512, 1024], P(None, ('face', 'gy'), 'gx'), may hold values from 0.02 to 0.08
- sea_mask: int32 [512, 1024], P(('face', 'gy'), 'gx'), may hold values 0 or 1
- xgrid_atmos_cell: int32 [48, 24, 1024], P(('face', 'gy'), 'gx'), may hold values from 0 to 4095
- xgrid_ocean_cell: int32 [48, 24, 1024], P(('face', 'gy'), 'gx'), may hold values from 0 to 4095
- xgrid_weights: float32 [2, 48, 24, 1024], P(None, ('face', 'gy'), 'gx'), may hold values from 0 to 0.6, as said below
Outputs:
- atmos_next: float32 [4, 32, 512, 1024], P(None, None, ('face', 'gy'), 'gx')
- ocean_next: float32 [2, 32, 512, 1024], P(None, None, ('face', 'gy'), 'gx')
- ocean_stress: float32 [2, 512, 1024], P(None, ('face', 'gy'), 'gx')
Inputs may be any that keep to these rules, and one draw needn't show every extreme that they name: `xgrid_weights`: both weights of a slot are zero exactly where the slot carries no intersection and positive elsewhere; within each aligned block of 1024 slots the live ones come first; the run of a block's own offset (a = b = 1) is full, and runs pointing below the first or above the last row of blocks are empty.
All inputs are finite; a program needn't handle non-finite values. No bound on the sum of `sea_mask` on one device may be relied on, other than what follows from the above.
Results may differ from a plain program's by a relative error of at most 0.00002.
Values sent between devices are 32-bit elements; how exact they have to be, the bound alone decides.
No kernel may reach another device: no remote copies, remote signals or barrier semaphores. Data moves between devices by JAX's collectives and lax.ppermute only.
A program may use at most 192 MiB of HBM per device.

v0:
```python
import jax
import jax.numpy as jnp
from jax import lax
from jax.sharding import PartitionSpec as P

ITERS = 24
ATM_SUB = 4


current_scale = 2.0
atmos_gain = 0.5
ocean_gain = 0.02


def partner_2(value, axis, distance):
    mask = 2**distance
    pairs = [(source, source ^ mask) for source in range(lax.axis_size(axis))]
    return lax.ppermute(value, axis, pairs)


def padded_2(block, sides, width):
    for axis, dim in sides:
        count = lax.axis_size(axis)
        forward = [(i, i + 1) for i in range(count - 1)]
        forward.append((count - 1, 0))
        backward = [(target, source) for source, target in forward]
        low = lax.ppermute(
            lax.slice_in_dim(block, block.shape[dim] - width, None, axis=dim), axis, forward
        )
        high = lax.ppermute(lax.slice_in_dim(block, 0, width, axis=dim), axis, backward)
        block = jnp.concatenate([low, block, high], axis=dim)
    return block


def bulk_fluxes(air_vals, sea_vals):
    temp_air, humid_air, wind_east, wind_north = (
        air_vals[0],
        air_vals[1],
        air_vals[2],
        air_vals[3],
    )
    sea_temp, current_east, current_north = (sea_vals[0], sea_vals[1], sea_vals[2])
    shear_east = wind_east - current_east
    shear_north = wind_north - current_north
    wind_speed = jnp.sqrt(shear_east * shear_east + shear_north * shear_north + 0.25)
    richardson = (temp_air - sea_temp) / (wind_speed * wind_speed)
    heat_coeff = 0.1 + 0.4 * jax.nn.sigmoid(-2.0 * richardson)
    drag_coeff = 0.2 + 0.1 * jnp.tanh(wind_speed)
    sensible = heat_coeff * wind_speed * (sea_temp - temp_air)
    latent = heat_coeff * wind_speed * (0.5 * jnp.exp(0.3 * sea_temp) - humid_air)
    return jnp.stack(
        [
            sensible,
            latent,
            drag_coeff * wind_speed * shear_east,
            drag_coeff * wind_speed * shear_north,
        ]
    )


def tendency(
    tracers,
    west_cells,
    east_cells,
    south_cells,
    north_cells,
    east_flow,
    north_flow,
    diffusion,
    forcing,
):
    change = -jnp.maximum(east_flow, 0.0) * (tracers - west_cells) + jnp.maximum(
        -east_flow, 0.0
    ) * (east_cells - tracers)
    change = (
        change
        - jnp.maximum(north_flow, 0.0) * (tracers - south_cells)
        + jnp.maximum(-north_flow, 0.0) * (north_cells - tracers)
    )
    change = change + diffusion * (
        west_cells + east_cells + south_cells + north_cells - 4.0 * tracers
    )
    return change.at[:, 0].add(forcing)


def mirrored(top_rows):
    for bit_index in range(lax.axis_size("gx").bit_length() - 1):
        top_rows = partner_2(top_rows, "gx", bit_index)
    return top_rows


def extend(field, depth, fold_signs, south_signs):
    rows = field.shape[2]
    padded = padded_2(field, ((("face", "gy"), 2), ("gx", 3)), depth)
    partner = mirrored(padded[:, :, rows : rows + depth, :])[:, :, ::-1, ::-1] * fold_signs
    bottom = padded[:, :, depth : 2 * depth, :][:, :, ::-1, :] * south_signs
    position = lax.axis_index(("face", "gy"))
    south_part = jnp.where(position == 0, bottom, padded[:, :, :depth])
    north_part = jnp.where(
        position == lax.axis_size(("face", "gy")) - 1, partner, padded[:, :, rows + depth :]
    )
    return jnp.concatenate([south_part, padded[:, :, depth : rows + depth], north_part], axis=2)


def local(
    atmos_state,
    atmos_kappa,
    ocean_tracers,
    ocean_flow,
    ocean_kappa,
    sea_mask,
    xgrid_atmos_cell,
    xgrid_ocean_cell,
    xgrid_weights,
):
    rows_atmos, cols_atmos = (atmos_state.shape[2], atmos_state.shape[3])
    rows_ocean, cols_ocean = (ocean_tracers.shape[2], ocean_tracers.shape[3])
    levels_ocean = ocean_tracers.shape[1]
    slot_count = xgrid_atmos_cell.shape[2]
    atmos_cells = rows_atmos * cols_atmos
    ocean_cells = rows_ocean * cols_ocean
    lowest = atmos_state[:, 0].reshape(4, atmos_cells)
    surface = jnp.stack(
        [ocean_tracers[0, 0], current_scale * ocean_flow[0, 0], current_scale * ocean_flow[1, 0]]
    ).reshape(3, ocean_cells)
    atmos_slots = xgrid_atmos_cell.reshape(-1)
    air_vals = jnp.take(lowest, atmos_slots, axis=1)
    ocean_lists = padded_2(xgrid_ocean_cell, ((("face", "gy"), 0), ("gx", 1)), 1)[0::2, 0::2]
    ocean_lists = ocean_lists.reshape(-1)
    packed = jnp.take(surface, ocean_lists, axis=1).reshape(3, 3, 3, slot_count)
    sea_vals = padded_2(packed, ((("face", "gy"), 1), ("gx", 2)), 1)[:, 0::2, 0::2].reshape(3, -1)
    fluxes = bulk_fluxes(air_vals, sea_vals)
    payload = (xgrid_weights[1].reshape(-1) * fluxes).reshape(4, 3, 3, slot_count)
    returned = padded_2(payload, ((("face", "gy"), 1), ("gx", 2)), 1)[:, 0::2, 0::2].reshape(4, -1)
    ocean_flux = jnp.zeros((4, ocean_cells), jnp.float32).at[:, ocean_lists].add(returned)
    atmos_flux = (
        jnp.zeros((4, atmos_cells), jnp.float32)
        .at[:, atmos_slots]
        .add(xgrid_weights[0].reshape(-1) * fluxes)
    )
    atmos_flux = atmos_flux.reshape(4, rows_atmos, cols_atmos)
    flux_gains = jnp.array([atmos_gain, atmos_gain, -atmos_gain, -atmos_gain], jnp.float32)
    atmos_now = atmos_state.at[:, 0].add(flux_gains[:, None, None] * atmos_flux)
    for _ in range(ATM_SUB):
        above_cells = jnp.concatenate([atmos_now[:, 1:], atmos_now[:, -1:]], axis=1)
        below_cells = jnp.concatenate([atmos_now[:, :1], atmos_now[:, :-1]], axis=1)
        atmos_now = atmos_now + atmos_kappa * (above_cells + below_cells - 2.0 * atmos_now)
    ocean_flux = ocean_flux.reshape(4, rows_ocean, cols_ocean)
    sea_weight = sea_mask.astype(jnp.float32)
    forcing_slab = jnp.zeros((levels_ocean, rows_ocean, cols_ocean), jnp.float32)
    forcing_slab = forcing_slab.at[0].set(-ocean_gain * (ocean_flux[0] + ocean_flux[1]))
    forcing_slab = forcing_slab.at[1].set(ocean_gain * ocean_flux[1])
    mask_levels = jnp.broadcast_to(sea_weight[None], (levels_ocean, rows_ocean, cols_ocean))
    statics = jnp.stack([ocean_flow[0], ocean_flow[1], ocean_kappa, mask_levels, forcing_slab])
    depth = 4
    tracer_signs = jnp.ones((2, 1, 1, 1), jnp.float32)
    fold_signs = jnp.array([-1.0, -1.0, 1.0, 1.0, 1.0], jnp.float32).reshape(5, 1, 1, 1)
    south_signs = jnp.array([1.0, -1.0, 1.0, 1.0, 1.0], jnp.float32).reshape(5, 1, 1, 1)
    widened = extend(statics, depth, fold_signs, south_signs)

    def advance(iteration, tracers):
        grown = extend(tracers, depth, tracer_signs, tracer_signs)
        for inner in range(depth):
            margin = inner + 1
            near = widened[
                :, :, margin : widened.shape[2] - margin, margin : widened.shape[3] - margin
            ]
            center = grown[:, :, 1:-1, 1:-1]
            near_forcing = jnp.stack([near[4, 0], near[4, 1]])
            change = tendency(
                center,
                grown[:, :, 1:-1, :-2],
                grown[:, :, 1:-1, 2:],
                grown[:, :, :-2, 1:-1],
                grown[:, :, 2:, 1:-1],
                near[0],
                near[1],
                near[2],
                near_forcing,
            )
            grown = center + near[3] * change
        return grown

    ocean_now = lax.fori_loop(0, ITERS // depth, advance, ocean_tracers)
    ocean_stress = sea_weight * ocean_flux[2:4]
    return (atmos_now, ocean_now, ocean_stress)


def solution(mesh):
    placed = (
        P(None, None, ("face", "gy"), "gx"),
        P(("face", "gy"), "gx"),
        P(None, None, ("face", "gy"), "gx"),
        P(None, None, ("face", "gy"), "gx"),
        P(None, ("face", "gy"), "gx"),
        P(("face", "gy"), "gx"),
        P(("face", "gy"), "gx", None),
        P(("face", "gy"), "gx", None),
        P(None, ("face", "gy"), "gx", None),
    )
    return jax.shard_map(
        local,
        mesh=mesh,
        in_specs=placed,
        out_specs=(
            P(None, None, ("face", "gy"), "gx"),
            P(None, None, ("face", "gy"), "gx"),
            P(None, ("face", "gy"), "gx"),
        ),
        check_vma=False,
    )
```

profile of v0, /device:TPU:4, one launch (start us, length us, event | category | flops | bytes accessed | tf_op | source)
XLA Modules:
  0.0 1028.7 jit_solution(9774720111843362574)
XLA Ops:
  2.3 3.9 collective-permute-start.7
  9.5 32.8 %gather_fusion = f32[9216,4]{1,0:T(8,128)} fusion(f32[4,4096]{0,1:T(8,128)} %bitcast.132, s32[9216]{0:T(1024)S(1)} %broadcast_clamp_fusion.1), kind=kCustom, calls=%fused_computation | custom fusion | bytes 331776 | tf_op jit(solution)/shard_map/jit(_take)/gather | solution.py:127
  55.3 32.8 %gather_fusion.1 = f32[9216,3]{1,0:T(8,128)} fusion(f32[3,4096]{0,1:T(8,128)} %copy.217, s32[9216]{0:T(1024)S(1)} %broadcast_clamp_fusion), kind=kCustom, calls=%fused_computation.1 | custom fusion | bytes 258048 | tf_op jit(solution)/shard_map/jit(_take)/gather | solution.py:130
  88.1 4.1 copy.218
  109.9 4.2 slice.749
  123.6 51.1 %scatter_custom_fusion = f32[4,4096]{0,1:T(8,128)} fusion(s32[9216]{0:T(1024)} %bitcast.143, f32[9216,4]{1,0:T(8,128)} %copy.219, f32[]{:T(128)} %constant.293.clone.1), kind=kCustom, calls=%fused_computation.84 | custom fusion | flops 36864 | bytes 66048 | tf_op jit(solution)/shard_map/scatter-add | solution.py:139
  198.1 50.2 %scatter_custom_fusion.1 = f32[4,4096]{0,1:T(8,128)S(1)} fusion(s32[9216]{0:T(1024)} %bitcast.141, f32[9216,4]{1,0:T(8,128)} %copy.221, f32[]{:T(128)} %constant.293.clone.1), kind=kCustom, calls=%fused_computation.82 | custom fusion | flops 36864 | bytes 66048 | tf_op jit(solution)/shard_map/scatter-add | solution.py:135
  259.8 9.8 copy.225
  269.6 5.6 copy.224
  275.2 5.6 copy.226
  290.6 12.4 %pad_maximum_fusion.5 = f32[5,32,40,136]{2,1,3,0:T(8,128)S(1)} fusion(f32[5,32,40,4]{2,1,3,0:T(8,128)S(1)} %collective-permute-done.22, f32[5,32,4,128]{2,1,3,0:T(8,128)} %copy.226, f32[5,32,32,128]{2,1,3,0:T(8,128)} %copy.225, f32[5,32,4,128]{2,1,3,0:T(8,128)} %copy.224, f32[5,32,40,4]{2,1,3,0:T(8,128)S(1)} %collective-permute-done.21), kind=kLoop, calls=%fused_computation.53 | loop fusion | flops 3481600 | bytes 6963200 | tf_op jit(solution)/shard_map/concatenate | solution.py:31
  303.0 10.8 %fusion.35 = (f32[5,32,4,136]{2,1,3,0:T(8,128)}, f32[5,32,4,136]{2,1,3,0:T(8,128)}) fusion(f32[5,32,40,136]{2,1,3,0:T(8,128)S(1)} %pad_maximum_fusion.5), kind=kLoop, calls=%fused_computation.153 | loop fusion | bytes 1392640 | tf_op jit(solution)/shard_map/slice | solution.py:96
  313.8 8.2 copy.227
  327.3 15.0 %collective-permute-done.24 = f32[5,32,4,136]{3,1,2,0:T(8,128)} collective-permute-done((f32[5,32,4,136]{3,1,2,0:T(8,128)S(1)}, f32[5,32,4,136]{3,1,2,0:T(8,128)}, u32[]{:S(2)}, u32[]{:S(2)}) %collective-permute-start.24) | collective-permute-done | bytes 348192 | tf_op jit(solution)/shard_map/ppermute | solution.py:18
  350.4 11.2 %slice.870 = f32[5,32,32,136]{2,1,3,0:T(8,128)} slice(f32[5,32,40,136]{2,1,3,0:T(8,128)} %copy-done.2), slice={[0:5], [0:32], [4:36], [0:136]} | slice | bytes 5570560 | tf_op jit(solution)/shard_map/slice | solution.py:102
  361.6 26.4 %rev.18 = f32[5,32,4,136]{2,1,3,0:T(8,128)} reverse(f32[5,32,4,136]{2,1,3,0:T(8,128)} %get-tuple-element.390), dimensions={2} | reverse | bytes 696320 | tf_op jit(solution)/shard_map/rev | solution.py:96
  388.0 11.5 %copy.243 = f32[5,32,32,136]{3,2,1,0:T(8,128)} copy(f32[5,32,32,136]{2,1,3,0:T(8,128)} %slice.870) | data formatting | bytes 5570560 | tf_op jit(solution)/shard_map/while | solution.py:184
  399.5 6.1 copy.228
  405.6 18.2 %rev.19 = f32[5,32,4,136]{2,1,3,0:T(8,128)} reverse(f32[5,32,4,136]{2,1,3,0:T(8,128)} %copy.228), dimensions={2,3} | reverse | bytes 696320 | tf_op jit(solution)/shard_map/rev | solution.py:95
  423.8 24.4 %slice_select_fusion.1 = (f32[5,32,4,136]{2,1,3,0:T(8,128)}, f32[5,32,4,136]{2,1,3,0:T(8,128)}) fusion(f32[5,32,40,136]{2,1,3,0:T(8,128)} %copy-done.2, f32[5,32,4,136]{2,1,3,0:T(8,128)} %rev.18, f32[5]{0:T(128)S(1)} %copy-done.61, pred[]{:T(512)S(6)} %eq.18, f32[5,32,4,136]{2,1,3,0:T(8,128)} %rev.19, f32[5]{0:T(128)S(1)} %copy-done.60, pred[]{:T(512)S(6)} %eq.19), kind=kLoop, calls=%fused_computation.52 | loop fusion | flops 348160 | bytes 2089002 | tf_op jit(solution)/shard_map/jit(_where)/select_n | solution.py:98
  448.2 10.4 %pad_maximum_fusion.6 = f32[5,32,40,136]{2,1,3,0:T(8,128)S(1)} fusion(f32[5,32,4,136]{2,1,3,0:T(8,128)} %get-tuple-element.389, f32[5,32,32,136]{2,1,3,0:T(8,128)S(1)} %bitcast.129, f32[5,32,4,136]{2,1,3,0:T(8,128)} %get-tuple-element.388), kind=kLoop, calls=%fused_computation.54 | loop fusion | flops 1740800 | bytes 6963200 | tf_op jit(solution)/shard_map/concatenate | solution.py:102
  463.0 11.8 %copy.233 = f32[5,32,40,136]{3,2,1,0:T(8,128)} copy(f32[5,32,40,136]{2,1,3,0:T(8,128)} %copy-done.22) | data formatting | bytes 6963200 | tf_op jit(solution)/shard_map/while | solution.py:184
  474.9 4.8 slice_negate_fusion
  479.7 5.5 slice_negate_fusion.2
  485.2 5.5 slice_negate_fusion.4
  492.8 3.8 copy.234
  510.7 516.8 %while.19 = (s32[]{:T(128)}, f32[2,32,32,128]{3,2,0,1:T(8,128)S(1)}, f32[5,32,40,136]{3,2,1,0:T(8,128)}, f32[1,32,38,134]{3,2,1,0:T(8,128)}, f32[1,32,38,134]{3,...) while((s32[]{:T(128)}, ...), condition=%wide.region_3.4_spmd, body=%wide.region_2.3_spmd.sunk | while | flops 29846140 | bytes 177864752 | solution.py:184
  514.5 6.4 slice_bitcast_fusion.19
  520.9 3.7 slice_bitcast_fusion.20
  524.7 3.9 slice_bitcast_fusion.21
  548.5 4.1 slice_bitcast_fusion.22
  555.7 5.9 collective-permute-done.5
  567.0 4.4 collective-permute-done.6
  600.1 6.4 slice_bitcast_fusion.19
  610.2 3.9 slice_bitcast_fusion.21
  634.1 4.1 slice_bitcast_fusion.22
  641.3 5.9 collective-permute-done.5
  652.5 4.4 collective-permute-done.6
  682.0 4.1 collective-permute-start
  686.2 6.4 slice_bitcast_fusion.19
  696.3 3.9 slice_bitcast_fusion.21
  720.2 4.1 slice_bitcast_fusion.22
  727.4 5.9 collective-permute-done.5
  738.6 4.4 collective-permute-done.6
  768.2 4.5 collective-permute-start
  772.7 6.4 slice_bitcast_fusion.19
  779.1 3.7 slice_bitcast_fusion.20
  782.8 3.9 slice_bitcast_fusion.21
  806.6 4.1 slice_bitcast_fusion.22
  813.9 5.9 collective-permute-done.5
  825.1 4.4 collective-permute-done.6
  854.6 4.5 collective-permute-start
  859.1 6.4 slice_bitcast_fusion.19
  869.3 3.9 slice_bitcast_fusion.21
  893.1 4.1 slice_bitcast_fusion.22
  900.3 5.9 collective-permute-done.5
  911.6 4.4 collective-permute-done.6
  941.1 4.5 collective-permute-start
  945.6 6.4 slice_bitcast_fusion.19
  952.0 3.7 slice_bitcast_fusion.20
  955.7 3.9 slice_bitcast_fusion.21
  979.6 4.1 slice_bitcast_fusion.22
  986.8 5.9 collective-permute-done.5
  998.0 4.4 collective-permute-done.6
  (798 shorter events, 461.7 us)
Async XLA Ops:
  2.3 44.0 %collective-permute-start.7 = (s32[1,3,1024]{2,1,0:T(4,128)S(1)}, s32[1,3,1024]{2,1,0:T(4,128)S(1)}, u32[]{:S(2)}, u32[]{:S(2)}) collective-permute-start(s32[1,3,1024]{2,1,0:T(4,128)S(1)} %get-tuple-element.434), channel_id=1, source_target_pairs={{0,1},{1,2},{2,3},{3,4},{4,5},{5,6},{6,7},{7,64},{64,65},{65,66},{... | collective-permute-start | bytes 36872 | tf_op jit(solution)/shard_map/ppermute | solution.py:27
  6.2 40.1 %collective-permute-start.8 = (s32[1,3,1024]{2,1,0:T(4,128)S(1)}, s32[1,3,1024]{2,1,0:T(4,128)S(1)}, u32[]{:S(2)}, u32[]{:S(2)}) collective-permute-start(s32[1,3,1024]{2,1,0:T(4,128)S(1)} %get-tuple-element.433), channel_id=1, source_target_pairs={{1,0},{2,1},{3,2},{4,3},{5,4},{6,5},{7,6},{64,7},{65,64},{66,65},{... | collective-permute-start | bytes 36872 | tf_op jit(solution)/shard_map/ppermute | solution.py:30
  46.4 3.9 collective-permute-start.10
  48.3 4.4 collective-permute-start.9
  55.3 32.8 %copy-start.55 = (s32[9216,1]{0,1:T(1,128)}, s32[9216,1]{0,1:T(1,128)S(1)}, u32[]{:S(2)}) copy-start(s32[9216,1]{0,1:T(1,128)S(1)} %compare_select_fusion) | copy-start | bytes 110596
  93.3 6.6 collective-permute-start.11
  96.4 5.6 collective-permute-start.12
  102.7 5.4 collective-permute-start.13
  102.7 5.4 collective-permute-start.14
  123.6 53.3 %copy-start.62 = (f32[4]{0:T(128)S(1)}, f32[4]{0:T(128)}, u32[]{:S(2)}) copy-start(f32[4]{0:T(128)} %constant.315.clone) | copy-start | bytes 52
  180.8 7.7 collective-permute-start.15
  183.0 6.0 collective-permute-start.16
  189.2 5.1 collective-permute-start.17
  189.2 5.1 collective-permute-start.18
  252.6 17.0 %collective-permute-start.19 = (f32[5,32,4,128]{3,1,2,0:T(8,128)S(1)}, f32[5,32,4,128]{3,1,2,0:T(8,128)S(1)}, u32[]{:S(2)}, u32[]{:S(2)}) collective-permute-start(f32[5,32,4,128]{3,1,2,0:T(8,128)S(1)} %copy.247), channel_id=1, source_target_pairs={{0,1},{1,2},{2,3},{3,4},{4,5},{5,6},{6,7},{7,64},{64,65},{65,66},{... | collective-permute-start | bytes 983048 | tf_op jit(solution)/shard_map/ppermute | solution.py:27
  255.7 19.6 %collective-permute-start.20 = (f32[5,32,4,128]{3,1,2,0:T(8,128)S(1)}, f32[5,32,4,128]{3,1,2,0:T(8,128)S(1)}, u32[]{:S(2)}, u32[]{:S(2)}) collective-permute-start(f32[5,32,4,128]{3,1,2,0:T(8,128)S(1)} %copy.248), channel_id=1, source_target_pairs={{1,0},{2,1},{3,2},{4,3},{5,4},{6,5},{7,6},{64,7},{65,64},{66,65},{... | collective-permute-start | bytes 983048 | tf_op jit(solution)/shard_map/ppermute | solution.py:30
  282.9 7.7 collective-permute-start.21
  282.9 7.7 collective-permute-start.22
  322.0 3.0 collective-permute-start.23
  325.1 17.2 %collective-permute-start.24 = (f32[5,32,4,136]{3,1,2,0:T(8,128)S(1)}, f32[5,32,4,136]{3,1,2,0:T(8,128)}, u32[]{:S(2)}, u32[]{:S(2)}) collective-permute-start(f32[5,32,4,136]{3,1,2,0:T(8,128)S(1)} %collective-permute-done.23), channel_id=1, source_target_pairs={{0,16},{8,24},{16,0},{24,8},{32,48},{40,56},{48,32},{56,40},{1,17}... | collective-permute-start | bytes 1044488 | tf_op jit(solution)/shard_map/ppermute | solution.py:18
  342.2 57.3 %collective-permute-start.25 = (f32[5,32,4,136]{3,1,2,0:T(8,128)}, f32[5,32,4,136]{3,1,2,0:T(8,128)S(1)}, u32[]{:S(2)}, u32[]{:S(2)}) collective-permute-start(f32[5,32,4,136]{3,1,2,0:T(8,128)} %collective-permute-done.24), channel_id=1, source_target_pairs={{0,32},{8,40},{16,48},{24,56},{32,0},{40,8},{48,16},{56,24},{1,33}... | collective-permute-start | bytes 1044488 | tf_op jit(solution)/shard_map/ppermute | solution.py:18
  405.6 42.6 %slice-start = ((s8[11141120]{0:T(1024)(128)(4,1)}), s8[2752512]{0:T(1024)(128)(4,1)S(1)}, s32[]{:S(2)}) async-start(s8[11141120]{0:T(1024)(128)(4,1)} %bitcast.128), calls=%async_computation | async-start | bytes 5505024
  510.9 24.4 %collective-permute-start = (f32[2,32,4,128]{3,2,0,1:T(4,128)S(1)}, f32[2,32,4,128]{3,2,0,1:T(4,128)S(1)}, u32[]{:S(2)}, u32[]{:S(2)}) collective-permute-start(f32[2,32,4,128]{3,2,0,1:T(4,128)S(1)} %get-tuple-element.564), channel_id=1, source_target_pairs={{1,0},{2,1},{3,2},{4,3},{5,4},{6,5},{7,6},{64,7},{65,64},{66,65},{... | collective-permute-start | bytes 393224 | tf_op jit(solution)/shard_map/while/body/eval_jaxpr/ppermute | solution.py:30
  513.3 22.0 %collective-permute-start.1 = (f32[2,32,4,128]{3,2,0,1:T(4,128)S(1)}, f32[2,32,4,128]{3,2,0,1:T(4,128)S(1)}, u32[]{:S(2)}, u32[]{:S(2)}) collective-permute-start(f32[2,32,4,128]{3,2,0,1:T(4,128)S(1)} %get-tuple-element.565), channel_id=1, source_target_pairs={{0,1},{1,2},{2,3},{3,4},{4,5},{5,6},{6,7},{7,64},{64,65},{65,66},{... | collective-permute-start | bytes 393224 | tf_op jit(solution)/shard_map/while/body/eval_jaxpr/ppermute | solution.py:27
  538.8 4.5 collective-permute-start.2
  539.4 5.6 collective-permute-start.3
  548.4 4.2 collective-permute-start.4
  552.6 9.1 collective-permute-start.5
  561.7 9.7 collective-permute-start.6
  596.5 24.4 %collective-permute-start = (f32[2,32,4,128]{3,2,0,1:T(4,128)S(1)}, f32[2,32,4,128]{3,2,0,1:T(4,128)S(1)}, u32[]{:S(2)}, u32[]{:S(2)}) collective-permute-start(f32[2,32,4,128]{3,2,0,1:T(4,128)S(1)} %get-tuple-element.564), channel_id=1, source_target_pairs={{1,0},{2,1},{3,2},{4,3},{5,4},{6,5},{7,6},{64,7},{65,64},{66,65},{... | collective-permute-start | bytes 393224 | tf_op jit(solution)/shard_map/while/body/eval_jaxpr/ppermute | solution.py:30
  599.7 21.1 %collective-permute-start.1 = (f32[2,32,4,128]{3,2,0,1:T(4,128)S(1)}, f32[2,32,4,128]{3,2,0,1:T(4,128)S(1)}, u32[]{:S(2)}, u32[]{:S(2)}) collective-permute-start(f32[2,32,4,128]{3,2,0,1:T(4,128)S(1)} %get-tuple-element.565), channel_id=1, source_target_pairs={{0,1},{1,2},{2,3},{3,4},{4,5},{5,6},{6,7},{7,64},{64,65},{65,66},{... | collective-permute-start | bytes 393224 | tf_op jit(solution)/shard_map/while/body/eval_jaxpr/ppermute | solution.py:27
  624.4 4.5 collective-permute-start.2
  624.9 5.6 collective-permute-start.3
  634.0 4.2 collective-permute-start.4
  638.1 9.1 collective-permute-start.5
  647.2 9.7 collective-permute-start.6
  682.0 24.9 %collective-permute-start = (f32[2,32,4,128]{3,2,0,1:T(4,128)S(1)}, f32[2,32,4,128]{3,2,0,1:T(4,128)S(1)}, u32[]{:S(2)}, u32[]{:S(2)}) collective-permute-start(f32[2,32,4,128]{3,2,0,1:T(4,128)S(1)} %get-tuple-element.564), channel_id=1, source_target_pairs={{1,0},{2,1},{3,2},{4,3},{5,4},{6,5},{7,6},{64,7},{65,64},{66,65},{... | collective-permute-start | bytes 393224 | tf_op jit(solution)/shard_map/while/body/eval_jaxpr/ppermute | solution.py:30
  686.2 20.8 %collective-permute-start.1 = (f32[2,32,4,128]{3,2,0,1:T(4,128)S(1)}, f32[2,32,4,128]{3,2,0,1:T(4,128)S(1)}, u32[]{:S(2)}, u32[]{:S(2)}) collective-permute-start(f32[2,32,4,128]{3,2,0,1:T(4,128)S(1)} %get-tuple-element.565), channel_id=1, source_target_pairs={{0,1},{1,2},{2,3},{3,4},{4,5},{5,6},{6,7},{7,64},{64,65},{65,66},{... | collective-permute-start | bytes 393224 | tf_op jit(solution)/shard_map/while/body/eval_jaxpr/ppermute | solution.py:27
  710.5 4.5 collective-permute-start.2
  711.0 5.6 collective-permute-start.3
  720.1 4.2 collective-permute-start.4
  724.3 9.1 collective-permute-start.5
  733.3 9.7 collective-permute-start.6
  768.2 25.3 %collective-permute-start = (f32[2,32,4,128]{3,2,0,1:T(4,128)S(1)}, f32[2,32,4,128]{3,2,0,1:T(4,128)S(1)}, u32[]{:S(2)}, u32[]{:S(2)}) collective-permute-start(f32[2,32,4,128]{3,2,0,1:T(4,128)S(1)} %get-tuple-element.564), channel_id=1, source_target_pairs={{1,0},{2,1},{3,2},{4,3},{5,4},{6,5},{7,6},{64,7},{65,64},{66,65},{... | collective-permute-start | bytes 393224 | tf_op jit(solution)/shard_map/while/body/eval_jaxpr/ppermute | solution.py:30
  772.7 20.8 %collective-permute-start.1 = (f32[2,32,4,128]{3,2,0,1:T(4,128)S(1)}, f32[2,32,4,128]{3,2,0,1:T(4,128)S(1)}, u32[]{:S(2)}, u32[]{:S(2)}) collective-permute-start(f32[2,32,4,128]{3,2,0,1:T(4,128)S(1)} %get-tuple-element.565), channel_id=1, source_target_pairs={{0,1},{1,2},{2,3},{3,4},{4,5},{5,6},{6,7},{7,64},{64,65},{65,66},{... | collective-permute-start | bytes 393224 | tf_op jit(solution)/shard_map/while/body/eval_jaxpr/ppermute | solution.py:27
  797.0 4.5 collective-permute-start.2
  797.5 5.6 collective-permute-start.3
  806.5 4.2 collective-permute-start.4
  810.7 9.1 collective-permute-start.5
  819.8 9.7 collective-permute-start.6
  854.6 25.3 %collective-permute-start = (f32[2,32,4,128]{3,2,0,1:T(4,128)S(1)}, f32[2,32,4,128]{3,2,0,1:T(4,128)S(1)}, u32[]{:S(2)}, u32[]{:S(2)}) collective-permute-start(f32[2,32,4,128]{3,2,0,1:T(4,128)S(1)} %get-tuple-element.564), channel_id=1, source_target_pairs={{1,0},{2,1},{3,2},{4,3},{5,4},{6,5},{7,6},{64,7},{65,64},{66,65},{... | collective-permute-start | bytes 393224 | tf_op jit(solution)/shard_map/while/body/eval_jaxpr/ppermute | solution.py:30
  859.1 20.8 %collective-permute-start.1 = (f32[2,32,4,128]{3,2,0,1:T(4,128)S(1)}, f32[2,32,4,128]{3,2,0,1:T(4,128)S(1)}, u32[]{:S(2)}, u32[]{:S(2)}) collective-permute-start(f32[2,32,4,128]{3,2,0,1:T(4,128)S(1)} %get-tuple-element.565), channel_id=1, source_target_pairs={{0,1},{1,2},{2,3},{3,4},{4,5},{5,6},{6,7},{7,64},{64,65},{65,66},{... | collective-permute-start | bytes 393224 | tf_op jit(solution)/shard_map/while/body/eval_jaxpr/ppermute | solution.py:27
  883.4 4.5 collective-permute-start.2
  884.0 5.6 collective-permute-start.3
  893.0 4.2 collective-permute-start.4
  897.2 9.1 collective-permute-start.5
  906.3 9.7 collective-permute-start.6
  941.1 25.3 %collective-permute-start = (f32[2,32,4,128]{3,2,0,1:T(4,128)S(1)}, f32[2,32,4,128]{3,2,0,1:T(4,128)S(1)}, u32[]{:S(2)}, u32[]{:S(2)}) collective-permute-start(f32[2,32,4,128]{3,2,0,1:T(4,128)S(1)} %get-tuple-element.564), channel_id=1, source_target_pairs={{1,0},{2,1},{3,2},{4,3},{5,4},{6,5},{7,6},{64,7},{65,64},{66,65},{... | collective-permute-start | bytes 393224 | tf_op jit(solution)/shard_map/while/body/eval_jaxpr/ppermute | solution.py:30
  945.6 20.8 %collective-permute-start.1 = (f32[2,32,4,128]{3,2,0,1:T(4,128)S(1)}, f32[2,32,4,128]{3,2,0,1:T(4,128)S(1)}, u32[]{:S(2)}, u32[]{:S(2)}) collective-permute-start(f32[2,32,4,128]{3,2,0,1:T(4,128)S(1)} %get-tuple-element.565), channel_id=1, source_target_pairs={{0,1},{1,2},{2,3},{3,4},{4,5},{5,6},{6,7},{7,64},{64,65},{65,66},{... | collective-permute-start | bytes 393224 | tf_op jit(solution)/shard_map/while/body/eval_jaxpr/ppermute | solution.py:27
  969.9 4.5 collective-permute-start.2
  970.4 5.6 collective-permute-start.3
  979.5 4.2 collective-permute-start.4
  983.6 9.1 collective-permute-start.5
  992.7 9.7 collective-permute-start.6
  (203 other events, 633.7 us)
where the time goes:
time: 1040 us; the launch traced here: 1030 us
  other arithmetic  497 us (48%)
  local copies, waits for them, and re-layouts  366 us (35%)
  waiting for transfers between devices  94.5 us (9%)
  starting transfers between devices  66.6 us (6%)
    mul x24, other arithmetic, advance(): grown = center + near[3] * change  108 us
    ppermute x21, waiting for transfers between devices, partner_2(): return lax.ppermute(value, axis, pairs)  76.8 us
    max x24, other arithmetic, tendency(): jnp.maximum(-north_flow, 0.0) * (north_cells - tracers)  73.7 us
    add x24, other arithmetic, tendency(): change + diffusion * (west_cells + east_cells + south_cells + north_cells...  63.2 us
    scatter-add x1, other arithmetic, local(): atmos_flux = jnp.zeros((4, atmos_cells), jnp.float32).at[:, atmos_slots]....  51.1 us
    scatter-add x1, other arithmetic, local(): jnp.zeros((4, ocean_cells), jnp.float32).at[:, ocean_lists].add(returned)  50.2 us
    while x342, local copies, waits for them, and re-layouts  49.4 us
    while x12, local copies, waits for them, and re-layouts, local(): ocean_now = lax.fori_loop(0, ITERS // depth, advance, ocean_tracers)  44 us
  transfers between devices with their start and end apart: 61, of which 25 were waited for; matrix products, arithmetic and copies ran while one was open for 34% of the time, Pallas kernels for 0%

commit v1 on v0

v1 whole, which is shorter than its diff:
```python
import functools

import jax
import jax.numpy as jnp
from jax import lax
from jax.experimental import pallas as pl
from jax.experimental.pallas import tpu as pltpu
from jax.sharding import PartitionSpec as P

ITERS = 24
ATM_SUB = 4

current_scale = 2.0
atmos_gain = 0.5
ocean_gain = 0.02

AXES = ("face", "gx", "gy")
F32 = jnp.float32
BF16 = jnp.bfloat16
LV = 32
RW = 32
CL = 128
HALO = 12
ROUNDS = ITERS // HALO
NI = RW // 2 + HALO
NC = CL + 2 * HALO
JB = NC // 8
OFF = 24 - HALO
WIDTH = 168
DEEP = ITERS
SR = RW + 2 * DEEP

VMEM = pl.BlockSpec(memory_space=pltpu.VMEM)
SMEM = pl.BlockSpec(memory_space=pltpu.SMEM)


def call(kernel, outs, args, scratch=(), flops=1_000_000, **kw):
    return pl.pallas_call(
        kernel,
        out_shape=outs,
        in_specs=[SMEM if a.dtype == jnp.int32 and a.ndim == 1 else VMEM for a in args],
        out_specs=jax.tree.map(lambda _: VMEM, outs),
        scratch_shapes=list(scratch),
        compiler_params=pltpu.CompilerParams(vmem_limit_bytes=56 * 2**20),
        cost_estimate=pl.CostEstimate(flops=flops, bytes_accessed=1_000_000, transcendentals=0),
        **kw,
    )(*args)


def shape(*dims):
    return jax.ShapeDtypeStruct(dims, F32)


def block_id(r, x):
    gx, gy = lax.axis_size("gx"), lax.axis_size("gy")
    return (r // gy) * gx * gy + x * gy + r % gy


def sizes():
    return lax.axis_size("face") * lax.axis_size("gy"), lax.axis_size("gx")


def to_north(value):
    nr, nx = sizes()
    pairs = [(block_id(r, x), block_id(r + 1, x)) for r in range(nr - 1) for x in range(nx)]
    return lax.ppermute(value, AXES, pairs)


def to_south(value):
    nr, nx = sizes()
    pairs = [(block_id(r, x), block_id(r - 1, x)) for r in range(1, nr) for x in range(nx)]
    return lax.ppermute(value, AXES, pairs)


def across_fold(value):
    nr, nx = sizes()
    pairs = [(block_id(nr - 1, x), block_id(nr - 1, nx - 1 - x)) for x in range(nx)]
    return lax.ppermute(value, AXES, pairs)


def to_east(value):
    nx = lax.axis_size("gx")
    return lax.ppermute(value, "gx", [(x, (x + 1) % nx) for x in range(nx)])


def to_west(value):
    nx = lax.axis_size("gx")
    return lax.ppermute(value, "gx", [(x, (x - 1) % nx) for x in range(nx)])


def reversed_lanes(value):
    index = CL - 1 - lax.broadcasted_iota(jnp.int32, value.shape, 1)
    return jnp.take_along_axis(value, index, axis=1, mode="promise_in_bounds")


def level_rows(ref, base, row):
    return ref[pl.ds(base + row, LV, stride=RW), :]


def edge_kernel(tracers, flow, kappa, mask, top, bottom):
    def body(k, carry):
        for out, row in ((bottom, k), (top, RW - 1 - k)):
            sea = mask[pl.ds(row, 1), :]
            out[k, 0:LV] = level_rows(tracers, 0, row)
            out[k, LV : 2 * LV] = level_rows(tracers, LV * RW, row)
            out[k, 2 * LV : 3 * LV] = sea * level_rows(flow, 0, row)
            out[k, 3 * LV : 4 * LV] = sea * level_rows(flow, LV * RW, row)
            out[k, 4 * LV : 5 * LV] = sea * level_rows(kappa, 0, row)
        return carry

    lax.fori_loop(0, HALO, body, 0)


def columns(low, high, sign=1.0):
    a, b = low
    c, d = high
    return jnp.concatenate([a, b, c, d] if sign > 0 else [a, b, -c, -d], axis=0).T


def build_kernel(
    tracers, flow, kappa, mask, own, south, north, fold, flags, xts, xu, xv, xk, mw, me
):
    first = flags[0] > 0
    last = flags[1] > 0

    def emit(p, pairs):
        for f, out in enumerate((xts, xu, xv, xk)):
            pair = []
            for n in range(2):
                low, high = pairs[n]
                if f == 0:
                    t = columns((low[0], low[1]), (high[0], high[1]))
                else:
                    part_low, part_high = low[f + 1], high[f + 1]
                    t = columns((part_low, part_low), (part_high, part_high), -1.0 if f == 2 else 1.0)
                out[2 * p + n] = t
                pair.append(t)
            rows = pl.ds(pl.multiple_of(p * 2 * HALO, 8), 2 * HALO)
            mw[f, rows, :] = jnp.concatenate([t[:HALO] for t in pair], axis=0)
            me[f, rows, :] = jnp.concatenate([t[CL - HALO :] for t in pair], axis=0)

    def halo(p, carry):
        pairs = []
        for n in range(2):
            k = HALO - 1 - (2 * p + n)
            low, high = [], []
            for f in range(5):
                part = slice(f * LV, (f + 1) * LV)
                mirror = own[k, part]
                turned = reversed_lanes(fold[k, part])
                if f == 3:
                    mirror = -mirror
                if f in (2, 3):
                    turned = -turned
                low.append(jnp.where(first, mirror, south[k, part]))
                high.append(jnp.where(last, turned, north[k, part]))
            pairs.append((low, high))
        emit(p, pairs)
        return carry

    lax.fori_loop(0, HALO // 2, halo, 0)

    def inner(p, carry):
        pairs = []
        for n in range(2):
            sides = []
            for row in (2 * p + n - HALO, RW - 1 - (2 * p + n - HALO)):
                sea = mask[pl.ds(row, 1), :]
                sides.append(
                    [
                        level_rows(tracers, 0, row),
                        level_rows(tracers, LV * RW, row),
                        sea * level_rows(flow, 0, row),
                        sea * level_rows(flow, LV * RW, row),
                        sea * level_rows(kappa, 0, row),
                    ]
                )
            pairs.append(tuple(sides))
        emit(p, pairs)
        return carry

    lax.fori_loop(HALO // 2, NI // 2, inner, 0)


def deep_kernel(final, *refs):
    if final:
        xts, xu, xv, xk, ww, we, ww2, we2, surface, out = refs[:10]
        scratch = refs[10:]
    else:
        xts, xu, xv, xk, ww, we, state, top, bottom = refs[:9]
        scratch = refs[9:]
    s0, s1, cw, ce, cd, cu = scratch
    mid = slice(24, 24 + CL)

    def coefficients(i, where, u, v, k):
        cw[i, where] = jnp.maximum(u, 0.0) + k
        ce[i, where] = jnp.maximum(-u, 0.0) + k
        cd[i, where] = jnp.maximum(v, 0.0) + k
        cu[i, where] = jnp.maximum(-v, 0.0) + k

    def fill(p, carry):
        rows = pl.ds(pl.multiple_of(p * 2 * HALO, 8), 2 * HALO)
        west = [ww[f, rows, :] for f in range(4)]
        east = [we[f, rows, :] for f in range(4)]
        if final:
            west[0] = ww2[rows, :]
            east[0] = we2[rows, :]
        for n in range(2):
            i = 2 * p + n
            part = slice(n * HALO, (n + 1) * HALO)
            s0[i, mid] = xts[i]
            coefficients(i, mid, xu[i], xv[i], xk[i])
            for side, where in (
                (west, slice(24 - HALO, 24)),
                (east, slice(24 + CL, 24 + CL + HALO)),
            ):
                s0[i, where] = side[0][part]
                coefficients(i, where, side[1][part], side[2][part], side[3][part])
        return carry

    lax.fori_loop(0, NI // 2, fill, 0)

    def at(ref, i, j):
        return ref[i, pl.ds(OFF + j, 8, stride=JB), :]

    def row(src, dst, i, inner):
        c = [at(src, i, j - 1) for j in range(JB + 2)]
        for j in range(JB):
            centre = c[j + 1]
            down = at(src, i - 1, j)
            up = at(src, i + 1, j) if inner else pltpu.roll(centre, CL // 2, 1)
            new = (
                centre
                + at(cw, i, j) * (c[j] - centre)
                + at(ce, i, j) * (c[j + 2] - centre)
                + at(cd, i, j) * (down - centre)
                + at(cu, i, j) * (up - centre)
            )
            dst[i, pl.ds(OFF + j, 8, stride=JB), :] = new

    def step(src, dst, s):
        def body(i, carry):
            row(src, dst, i, True)
            return carry

        lax.fori_loop(s, NI - 1, body, 0)
        row(src, dst, NI - 1, False)

    def two(n, carry):
        step(s0, s1, 2 * n + 1)
        step(s1, s0, 2 * n + 2)
        return carry

    lax.fori_loop(0, HALO // 2, two, 0)

    if final:

        def write(i, carry):
            t = s0[i + HALO, mid].T
            for h, r in ((0, i), (1, RW - 1 - i)):
                for tracer in range(2):
                    base = h * 2 * LV + tracer * LV
                    out[pl.ds(tracer * LV * RW + r, LV, stride=RW), :] = t[base : base + LV]
            return carry

        lax.fori_loop(0, RW // 2, write, 0)
        for tracer in range(2):
            out[pl.ds(tracer * LV * RW, RW), :] = surface[tracer]
    else:
        low = lax.broadcasted_iota(jnp.int32, (CL, CL), 1) < CL // 2
        for i in range(RW // 2):
            state[i] = s0[i + HALO, mid]
        half = HALO // 2
        for k in range(half):
            near, far = s0[HALO + k, mid], s0[HALO + k + half, mid]
            top[k] = jnp.where(low, pltpu.roll(near, CL // 2, 1), far)
            bottom[k] = jnp.where(low, near, pltpu.roll(far, CL // 2, 1))


def join_kernel(state, south, north, fold, flags, xts, mw, me):
    first = flags[0] > 0
    last = flags[1] > 0
    low = lax.broadcasted_iota(jnp.int32, (CL, CL), 1) < CL // 2
    half = HALO // 2
    flip = jnp.where(
        lax.broadcasted_iota(jnp.int32, (CL, CL), 0)
        + lax.broadcasted_iota(jnp.int32, (CL, CL), 1)
        == CL - 1,
        1.0,
        0.0,
    ).astype(F32)
    rows = {}
    for i in range(RW // 2):
        rows[HALO + i] = state[i]
    for k in range(half):
        s, n = south[k], north[k]
        f = jnp.dot(flip, fold[k], precision=lax.Precision.HIGHEST, preferred_element_type=F32)
        s_roll, n_roll, f_roll = (pltpu.roll(v, CL // 2, 1) for v in (s, n, f))
        for kk, sv, nv, fv in ((k, s, n_roll, f_roll), (k + half, s_roll, n, f)):
            down = jnp.where(first, state[kk], sv)
            up = jnp.where(last, fv, nv)
            rows[HALO - 1 - kk] = jnp.where(low, down, up)
    for i in range(NI):
        xts[i] = rows[i]
    for p in range(NI // 2):
        pair = [rows[2 * p], rows[2 * p + 1]]
        where = pl.ds(p * 2 * HALO, 2 * HALO)
        mw[where, :] = jnp.concatenate([t[:HALO] for t in pair], axis=0)
        me[where, :] = jnp.concatenate([t[CL - HALO :] for t in pair], axis=0)


def split3(value):
    a = value.astype(BF16)
    rest = value - a.astype(F32)
    b = rest.astype(BF16)
    c = (rest - b.astype(F32)).astype(BF16)
    return a, b, c


def one_hots(cells):
    n = cells.shape[1]
    column = jnp.bitwise_and(cells, CL - 1)
    row = jnp.right_shift(cells, 7)
    hot = jnp.where(lax.broadcasted_iota(jnp.int32, (CL, n), 0) == column, 1.0, 0.0).astype(BF16)
    return hot, lax.broadcasted_iota(jnp.int32, (RW, n), 0) == row


def gather(table, hot, mask):
    parts = split3(table)
    got = sum(jnp.dot(p, hot, preferred_element_type=F32) for p in parts)
    return [
        jnp.sum(jnp.where(mask, got[f * RW : (f + 1) * RW], 0.0), axis=0, keepdims=True)
        for f in range(table.shape[0] // RW)
    ]


def scatter(values, hot, mask):
    parts = [split3(v) for v in values]
    rows = [
        jnp.where(mask, parts[f][s].astype(F32), 0.0).astype(BF16)
        for s in range(3)
        for f in range(len(values))
    ]
    return lax.dot_general(
        jnp.concatenate(rows, axis=0), hot, (((1,), (1,)), ((), ())), preferred_element_type=F32
    )


def bulk_fluxes(air_vals, sea_vals):
    temp_air, humid_air, wind_east, wind_north = air_vals
    sea_temp, current_east, current_north = sea_vals
    shear_east = wind_east - current_east
    shear_north = wind_north - current_north
    wind_speed = jnp.sqrt(shear_east * shear_east + shear_north * shear_north + 0.25)
    richardson = (temp_air - sea_temp) / (wind_speed * wind_speed)
    heat_coeff = 0.1 + 0.4 * jax.nn.sigmoid(-2.0 * richardson)
    drag_coeff = 0.2 + 0.1 * jnp.tanh(wind_speed)
    sensible = heat_coeff * wind_speed * (sea_temp - temp_air)
    latent = heat_coeff * wind_speed * (0.5 * jnp.exp(0.3 * sea_temp) - humid_air)
    return [
        sensible,
        latent,
        drag_coeff * wind_speed * shear_east,
        drag_coeff * wind_speed * shear_north,
    ]


def flux_kernel(air, sea, air_cells, sea_cells, weights, atmos_flux, payload, vals):
    slots = air_cells.shape[1]

    def look(q, carry):
        hot, mask = one_hots(air_cells[pl.ds(q, 1), :])
        for f, v in enumerate(gather(air[...], hot, mask)):
            vals[f, pl.ds(q, 1), :] = v
        hot, mask = one_hots(sea_cells[pl.ds(q, 1), :])
        for f, v in enumerate(gather(sea[q], hot, mask)):
            vals[4 + f, pl.ds(q, 1), :] = v
        return carry

    lax.fori_loop(0, 9, look, 0)
    fluxes = bulk_fluxes(
        [vals[f, 0:9] for f in range(4)],
        [vals[4, 0:9], current_scale * vals[5, 0:9], current_scale * vals[6, 0:9]],
    )
    for f in range(4):
        payload[f] = weights[1] * fluxes[f]
        vals[f, 0:9] = weights[0] * fluxes[f]

    def place(q, total):
        hot, mask = one_hots(air_cells[pl.ds(q, 1), :])
        return total + scatter([vals[f, pl.ds(q, 1), :] for f in range(4)], hot, mask)

    total = lax.fori_loop(0, 9, place, jnp.zeros((12 * RW, CL), F32))
    atmos_flux[...] = total[0 : 4 * RW] + total[4 * RW : 8 * RW] + total[8 * RW :]


def ocean_flux_kernel(cells, values, mask, surface, stress, fields):
    def place(q, total):
        hot, rows = one_hots(cells[pl.ds(q, 1), :])
        return total + scatter([values[f, pl.ds(q, 1), :] for f in range(4)], hot, rows)

    total = lax.fori_loop(0, 9, place, jnp.zeros((12 * RW, CL), F32))
    flux = total[0 : 4 * RW] + total[4 * RW : 8 * RW] + total[8 * RW :]
    sea = mask[...]
    part = [flux[f * RW : (f + 1) * RW] for f in range(4)]
    stress[0] = sea * part[2]
    stress[1] = sea * part[3]
    for f in range(5):
        fields[f] = surface[f]
    fields[5] = -ocean_gain * sea * (part[0] + part[1])
    fields[6] = ocean_gain * sea * part[1]


def surface_join_kernel(own, south, north, fold, flags, out):
    first = flags[0] > 0
    last = flags[1] > 0
    for f in range(7):
        out[f, 0:DEEP] = south[f]
        out[f, DEEP : DEEP + RW] = own[f]
        out[f, DEEP + RW :] = north[f]

    @pl.when(first)
    def _():
        for f in range(7):
            sign = -1.0 if f == 3 else 1.0
            for k in range(DEEP):
                out[f, DEEP - 1 - k : DEEP - k] = sign * own[f, k : k + 1]

    @pl.when(last)
    def _():
        for f in range(7):
            sign = -1.0 if f in (2, 3) else 1.0
            turned = sign * reversed_lanes(fold[f])
            for k in range(DEEP):
                out[f, DEEP + RW + k : DEEP + RW + k + 1] = turned[DEEP - 1 - k : DEEP - k]


def surface_kernel(own, west, east, out, cw, ce, cs, cn, cf):
    low = lax.broadcasted_iota(jnp.int32, (SR, CL), 1) < CL // 2

    def wide(f):
        return jnp.concatenate([own[f], jnp.where(low, east[f], west[f])], axis=1)

    u, v, k = wide(2), wide(3), wide(4)
    cw[...] = jnp.maximum(u, 0.0) + k
    ce[...] = jnp.maximum(-u, 0.0) + k
    cs[...] = jnp.maximum(v, 0.0) + k
    cn[...] = jnp.maximum(-v, 0.0) + k
    cf[0] = wide(5)
    cf[1] = wide(6)

    def step(n, pair):
        new = []
        for t, x in enumerate(pair):
            west_x = pltpu.roll(x, 1, 1)
            east_x = pltpu.roll(x, 2 * CL - 1, 1)
            south_x = pltpu.roll(x, 1, 0)
            north_x = pltpu.roll(x, SR - 1, 0)
            new.append(
                x
                + cw[...] * (west_x - x)
                + ce[...] * (east_x - x)
                + cs[...] * (south_x - x)
                + cn[...] * (north_x - x)
                + cf[t]
            )
        return tuple(new)

    pair = lax.fori_loop(0, ITERS, step, (wide(0), wide(1)))
    for t in range(2):
        out[t] = pair[t][DEEP : DEEP + RW, 0:CL]


def atmos_kernel(state, kappa, flux, out):
    f = pl.program_id(0)
    gain = jnp.where(f < 2, atmos_gain, -atmos_gain).astype(F32)
    levels = state.shape[1]
    for g in range(RW // 8):
        rows = slice(8 * g, 8 * g + 8)
        k = kappa[rows, :]
        x = [state[0, l, rows, :] for l in range(levels)]
        x[0] = x[0] + gain * flux[0, rows, :]
        for _ in range(ATM_SUB):
            x = [
                x[l]
                + k * (x[min(l + 1, levels - 1)] + x[max(l - 1, 0)] - 2.0 * x[l])
                for l in range(levels)
            ]
        for l in range(levels):
            out[0, l, rows, :] = x[l]


def atmosphere(atmos_state, atmos_kappa, flux):
    fields, levels = atmos_state.shape[:2]
    block = pl.BlockSpec((1, levels, RW, CL), lambda f: (f, 0, 0, 0))
    return pl.pallas_call(
        atmos_kernel,
        grid=(fields,),
        in_specs=[
            block,
            pl.BlockSpec((RW, CL), lambda f: (0, 0)),
            pl.BlockSpec((1, RW, CL), lambda f: (f, 0, 0)),
        ],
        out_specs=block,
        out_shape=jax.ShapeDtypeStruct(atmos_state.shape, F32),
        cost_estimate=pl.CostEstimate(
            flops=5_000_000, bytes_accessed=4_200_000, transcendentals=0
        ),
    )(atmos_state, atmos_kappa, flux)


def to_columns_2(runs, own_axis):
    pick = [lax.index_in_dim(runs, b, own_axis, keepdims=False) for b in range(3)]
    return jnp.stack([to_east(pick[2]), pick[1], to_west(pick[0])], axis=own_axis)


def local(
    atmos_state,
    atmos_kappa,
    ocean_tracers,
    ocean_flow,
    ocean_kappa,
    sea_mask,
    xgrid_atmos_cell,
    xgrid_ocean_cell,
    xgrid_weights,
):
    slots = xgrid_atmos_cell.shape[2]
    position = lax.axis_index("face") * lax.axis_size("gy") + lax.axis_index("gy")
    flags = jnp.stack([position == 0, position == sizes()[0] - 1]).astype(jnp.int32)
    sea = sea_mask.astype(F32)

    top_fields = jnp.stack([ocean_tracers[0, 0], ocean_flow[0, 0], ocean_flow[1, 0]])
    values = top_fields.reshape(3 * RW, CL)
    lists = xgrid_ocean_cell.astype(F32).reshape(3, 3, slots // CL, CL)

    def lines(a):
        return a.reshape(-1, CL)

    up = to_north(jnp.concatenate([values, lines(lists[2])], axis=0))
    down = to_south(jnp.concatenate([values, lines(lists[0])], axis=0))
    n_val = 3 * RW
    three = jnp.concatenate([up[:n_val], values, down[:n_val]], axis=0)
    run_rows = jnp.stack([up[n_val:], lines(lists[1]), down[n_val:]]).reshape(3, 3, -1, CL)
    east_in = to_east(jnp.concatenate([three, lines(run_rows[:, 2])], axis=0))
    west_in = to_west(jnp.concatenate([three, lines(run_rows[:, 0])], axis=0))
    sea_blocks = jnp.stack(
        [east_in[: 3 * n_val], three, west_in[: 3 * n_val]], axis=0
    ).reshape(3, 3, n_val, CL)
    sea_blocks = sea_blocks.transpose(1, 0, 2, 3).reshape(9, n_val, CL)
    in_lists = jnp.stack(
        [lines(a) for a in (east_in[3 * n_val :], run_rows[:, 1], west_in[3 * n_val :])]
    )
    in_lists = in_lists.reshape(3, 3, slots).transpose(1, 0, 2).reshape(9, slots)
    in_lists = in_lists.astype(jnp.int32)

    tracers2 = ocean_tracers.reshape(-1, CL)
    flow2 = ocean_flow.reshape(-1, CL)
    kappa2 = ocean_kappa.reshape(-1, CL)
    edge = shape(HALO, 5 * LV, CL)
    top, bottom = call(edge_kernel, (edge, edge), (tracers2, flow2, kappa2, sea))
    south, north, fold = to_north(top), to_south(bottom), across_fold(top)

    atmos_flux, payload = call(
        flux_kernel,
        (shape(4 * RW, CL), shape(4, 9, slots)),
        (
            atmos_state[:, 0].reshape(4 * RW, CL),
            sea_blocks,
            xgrid_atmos_cell.reshape(9, slots),
            xgrid_ocean_cell.reshape(9, slots),
            xgrid_weights.reshape(2, 9, slots),
        ),
        scratch=[pltpu.VMEM((7, 16, slots), F32)],
        flops=20_000_000,
    )
    payload = payload.reshape(4, 3, 3, slots)
    pay = jnp.stack([to_north(payload[:, 2]), payload[:, 1], to_south(payload[:, 0])], axis=1)
    pay = to_columns_2(pay, 2).reshape(4, 9, slots)
    atmos_next = atmosphere(atmos_state, atmos_kappa, atmos_flux.reshape(4, RW, CL))

    ext = shape(NI, CL, CL)
    side = shape(4, NI * HALO, CL)
    xts, xu, xv, xk, mw, me = call(
        build_kernel,
        (ext, ext, ext, ext, side, side),
        (tracers2, flow2, kappa2, sea, bottom, south, north, fold, flags),
    )
    ww, we = to_east(me), to_west(mw)
    buffers = [pltpu.VMEM((NI, WIDTH, CL), F32)] * 6
    pair = shape(HALO // 2, CL, CL)
    state, top, bottom = call(
        functools.partial(deep_kernel, False),
        (shape(RW // 2, CL, CL), pair, pair),
        (xts, xu, xv, xk, ww, we),
        scratch=buffers,
        flops=60_000_000,
    )
    south, north, fold = to_north(top), to_south(bottom), across_fold(top)

    surface = jnp.concatenate(
        [ocean_tracers[:, 0], sea * ocean_flow[:, 0], (sea * ocean_kappa[0])[None]], axis=0
    )
    ocean_stress, fields = call(
        ocean_flux_kernel,
        (shape(2, RW, CL), shape(7, RW, CL)),
        (in_lists, pay, sea, surface),
        flops=8_000_000,
    )
    s_top, s_bottom = fields[:, RW - DEEP :], fields[:, :DEEP]
    joined = call(
        surface_join_kernel,
        shape(7, SR, CL),
        (fields, to_north(s_top), to_south(s_bottom), across_fold(s_top), flags),
    )
    wide = pltpu.VMEM((SR, 2 * CL), F32)
    level_0 = call(
        surface_kernel,
        shape(2, RW, CL),
        (joined, to_east(joined), to_west(joined)),
        scratch=[wide, wide, wide, wide, pltpu.VMEM((2, SR, 2 * CL), F32)],
        flops=10_000_000,
    )

    thin = shape(NI * HALO, CL)
    xts, mw, me = call(join_kernel, (ext, thin, thin), (state, south, north, fold, flags))
    ocean_next = call(
        functools.partial(deep_kernel, True),
        shape(2 * LV * RW, CL),
        (xts, xu, xv, xk, ww, we, to_east(me), to_west(mw), level_0),
        scratch=buffers,
        flops=60_000_000,
    )
    return (atmos_next, ocean_next.reshape(ocean_tracers.shape), ocean_stress)


def solution(mesh):
    placed = (
        P(None, None, ("face", "gy"), "gx"),
        P(("face", "gy"), "gx"),
        P(None, None, ("face", "gy"), "gx"),
        P(None, None, ("face", "gy"), "gx"),
        P(None, ("face", "gy"), "gx"),
        P(("face", "gy"), "gx"),
        P(("face", "gy"), "gx", None),
        P(("face", "gy"), "gx", None),
        P(None, ("face", "gy"), "gx", None),
    )
    return jax.shard_map(
        local,
        mesh=mesh,
        in_specs=placed,
        out_specs=(
            P(None, None, ("face", "gy"), "gx"),
            P(None, None, ("face", "gy"), "gx"),
            P(None, ("face", "gy"), "gx"),
        ),
        check_vma=False,
    )
```

time: 1040 us -> 212 us (0.20)
  other arithmetic: 497 us -> 5.85 us
  local copies, waits for them, and re-layouts: 366 us -> 17.6 us
  Pallas kernels: 0 us -> 84.1 us
  waiting for transfers between devices: 94.5 us -> 45.4 us
    mul x31 -> x1, other arithmetic: 115 us -> 0.77 us  [local(): sea * ocean_flow[:, 0]]
    scatter-add x26 -> x0, other arithmetic: 102 us -> none  [the longest x1 51.1 us: local(): atmos_flux = jnp.zeros((4, atmos_cells), jnp.float32).at[:, atmos_slots]....]
    while x354 -> x0, local copies, waits for them, and re-layouts: 93.4 us -> none
    add x53 -> x0, other arithmetic: 92.8 us -> none  [the longest x24 63.2 us: tendency(): change + diffusion * (west_cells + east_cells + south_cells + north_cells...]
    pallas_call x0 -> x10, Pallas kernels: none -> 84.1 us  [the longest x9 79.7 us: call(): pl.pallas_call(kernel, out_shape=outs, in_specs=[SMEM if a.dtype == jnp.i...]
    slice x54 -> x10, local copies, waits for them, and re-layouts: 84 us -> 2.14 us  [the longest x1 1.48 us: local(): atmos_state[:, 0].reshape(4 * RW, CL)]
    max x24 -> x0, other arithmetic: 73.7 us -> none  [tendency(): jnp.maximum(-north_flow, 0.0) * (north_cells - tracers)]
    gather x4 -> x0, local copies, waits for them, and re-layouts: 72.9 us -> none  [the longest x2 36.9 us: local(): packed = jnp.take(surface, ocean_lists, axis=1).reshape(3, 3, 3, slot_count)]
  transfers between devices with their start and end apart: 61 -> 23, of which waited for: 25 -> 6; matrix products, arithmetic and copies ran while one was open for 34% -> 7% of each run, Pallas kernels for 0% -> 20%
where the time goes in v1:
time: 212 us; the launch traced here: 211 us
  Pallas kernels  84.1 us (40%)
  starting transfers between devices  56.7 us (27%)
  waiting for transfers between devices  45.4 us (21%)
  local copies, waits for them, and re-layouts  17.6 us (8%)
  other arithmetic  5.85 us (3%)
    pallas_call x9, Pallas kernels, call(): pl.pallas_call(kernel, out_shape=outs, in_specs=[SMEM if a.dtype == jnp.i...  79.7 us
    ppermute x5, waiting for transfers between devices, to_north(): return lax.ppermute(value, AXES, pairs)  28.7 us
    ppermute x5, starting transfers between devices, to_north(): return lax.ppermute(value, AXES, pairs)  25.6 us
    ppermute x5, starting transfers between devices, to_south(): return lax.ppermute(value, AXES, pairs)  15.6 us
    ppermute x5, starting transfers between devices, to_west(): return lax.ppermute(value, 'gx', [(x, (x - 1) % nx) for x in range(nx)])  13.4 us
    ppermute x5, waiting for transfers between devices, to_south(): return lax.ppermute(value, AXES, pairs)  11.5 us
    unnamed x41, local copies, waits for them, and re-layouts  7.76 us
    ppermute x5, waiting for transfers between devices, to_east(): return lax.ppermute(value, 'gx', [(x, (x + 1) % nx) for x in range(nx)])  5.28 us
  transfers between devices with their start and end apart: 23, of which 6 were waited for; matrix products, arithmetic and copies ran while one was open for 7% of the time, Pallas kernels for 20%

profile of v1, /device:TPU:4, one launch (start us, length us, event | category | flops | bytes accessed | tf_op | source)
XLA Modules:
  0.0 210.8 jit_solution(16137342822993491649)
XLA Ops:
  0.7 1.4 convert_element_type.17.mask
  2.0 5.0 %shard_map.114 = (f32[12,160,128]{2,1,0:T(8,128)}, f32[12,160,128]{2,1,0:T(8,128)}) custom-call(f32[2048,128]{1,0:T(8,128)} %bitcast.74, f32[2048,128]{1,0:T(8,128)} %bitcast.72, f32[1024,128]{1,0:T(8,128)} %bitcast.76, f32[32,128]{1,0:T(8,128)} %convert_element_type.17.mask), custom_call_target="tpu_custom_call" | custom-call | flops 1000000 | bytes 1000000 | tf_op jit(solution)/shard_map/pallas_call | solution.py:38
  7.1 5.8 %collective-permute-start.4 = (f32[12,160,128]{2,1,0:T(8,128)}, f32[12,160,128]{2,1,0:T(8,128)S(1)}, u32[]{:S(2)}, u32[]{:S(2)}) collective-permute-start(f32[12,160,128]{2,1,0:T(8,128)} %get-tuple-element.23), channel_id=1, source_target_pairs={{0,1},{8,9},{16,17},{24,25},{32,33},{40,41},{48,49},{56,57},{1,2},... | collective-permute-start | bytes 2949128 | tf_op jit(solution)/shard_map/ppermute | solution.py:66
  12.8 0.7 collective-permute-start.6
  13.6 0.8 slice_bitcast_fusion.7
  14.4 2.5 %collective-permute-start.1 = (f32[120,128]{1,0:T(8,128)S(1)}, f32[120,128]{1,0:T(8,128)S(1)}, u32[]{:S(2)}, u32[]{:S(2)}) collective-permute-start(f32[120,128]{1,0:T(8,128)S(1)} %get-tuple-element.52), channel_id=1, source_target_pairs={{1,0},{9,8},{17,16},{25,24},{33,32},{41,40},{49,48},{57,56},{2,1},... | collective-permute-start | bytes 184328 | tf_op jit(solution)/shard_map/ppermute | solution.py:72
  16.9 4.9 %collective-permute-start = (f32[120,128]{1,0:T(8,128)S(1)}, f32[120,128]{1,0:T(8,128)S(1)}, u32[]{:S(2)}, u32[]{:S(2)}) collective-permute-start(f32[120,128]{1,0:T(8,128)S(1)} %get-tuple-element.51), channel_id=1, source_target_pairs={{0,1},{8,9},{16,17},{24,25},{32,33},{40,41},{48,49},{56,57},{1,2},... | collective-permute-start | bytes 184328 | tf_op jit(solution)/shard_map/ppermute | solution.py:66
  21.8 3.4 %collective-permute-start.5 = (f32[12,160,128]{2,1,0:T(8,128)}, f32[12,160,128]{2,1,0:T(8,128)S(1)}, u32[]{:S(2)}, u32[]{:S(2)}) collective-permute-start(f32[12,160,128]{2,1,0:T(8,128)} %get-tuple-element.22.own), channel_id=1, source_target_pairs={{1,0},{9,8},{17,16},{25,24},{33,32},{41,40},{49,48},{57,56},{2,1},... | collective-permute-start | bytes 2949128 | tf_op jit(solution)/shard_map/ppermute | solution.py:72
  25.2 0.8 bitcast_multiply_fusion
  25.9 0.8 slice_bitcast_fusion.4
  26.7 0.7 fusion.1
  27.4 10.3 %collective-permute-done.1 = f32[120,128]{1,0:T(8,128)S(1)} collective-permute-done((f32[120,128]{1,0:T(8,128)S(1)}, f32[120,128]{1,0:T(8,128)S(1)}, u32[]{:S(2)}, u32[]{:S(2)}) %collective-permute-start.1) | collective-permute-done | bytes 61472 | tf_op jit(solution)/shard_map/ppermute | solution.py:72
  37.8 20.0 %collective-permute-done = f32[120,128]{1,0:T(8,128)S(1)} collective-permute-done((f32[120,128]{1,0:T(8,128)S(1)}, f32[120,128]{1,0:T(8,128)S(1)}, u32[]{:S(2)}, u32[]{:S(2)}) %collective-permute-start) | collective-permute-done | bytes 61472 | tf_op jit(solution)/shard_map/ppermute | solution.py:66
  57.8 0.6 fusion.4
  58.4 0.7 pad_maximum_fusion.1
  59.1 1.6 collective-permute-start.3
  60.7 0.6 add_convert_fusion.flags
  61.4 0.6 reshape.76.sea_cells
  62.0 1.6 copy.20.weights
  63.6 1.5 slice.90
  65.1 1.4 reshape.75.air_cells
  66.5 0.3 collective-permute-done.2
  66.9 0.8 pad_maximum_fusion
  67.7 10.4 %shard_map.112 = (f32[128,128]{1,0:T(8,128)}, f32[4,9,1024]{2,1,0:T(8,128)}) custom-call(f32[128,128]{1,0:T(8,128)} %bitcast.88, f32[9,96,128]{2,1,0:T(8,128)} %bitcast.78, s32[9,1024]{1,0:T(8,128)} %reshape.75.air_cells, s32[9,1024]{1,0:T(8,128)} %reshape.76.sea_cells, f32[2,9,1024]{2,1,0:T(8,128)} %copy.20.weights), custom_call_target="tpu_custom_call" | custom-call | flops 20000000 | bytes 1000000 | tf_op jit(solution)/shard_map/pallas_call | solution.py:38
  78.1 1.0 copy.21
  79.1 5.9 %collective-permute-start.14 = (f32[4,3,1024]{2,0,1:T(4,128)S(1)}, f32[4,3,1024]{2,0,1:T(4,128)S(1)}, u32[]{:S(2)}, u32[]{:S(2)}) collective-permute-start(f32[4,3,1024]{2,0,1:T(4,128)S(1)} %get-tuple-element.44), channel_id=1, source_target_pairs={{0,1},{8,9},{16,17},{24,25},{32,33},{40,41},{48,49},{56,57},{1,2},... | collective-permute-start | bytes 147464 | tf_op jit(solution)/shard_map/ppermute | solution.py:66
  85.1 2.4 %collective-permute-start.15 = (f32[4,3,1024]{2,0,1:T(4,128)S(1)}, f32[4,3,1024]{2,0,1:T(4,128)S(1)}, u32[]{:S(2)}, u32[]{:S(2)}) collective-permute-start(f32[4,3,1024]{2,0,1:T(4,128)S(1)} %get-tuple-element.45), channel_id=1, source_target_pairs={{1,0},{9,8},{17,16},{25,24},{33,32},{41,40},{49,48},{57,56},{2,1},... | collective-permute-start | bytes 147464 | tf_op jit(solution)/shard_map/ppermute | solution.py:72
  87.5 0.9 copy-done.2
  88.4 0.4 copy-done.4
  88.8 0.9 copy-done.3
  89.7 10.4 %shard_map.115 = (f32[28,128,128]{2,1,0:T(8,128)}, f32[28,128,128]{2,1,0:T(8,128)}, f32[28,128,128]{2,1,0:T(8,128)}, f32[28,128,128]{2,1,0:T(8,128)}, f32[4,336,128]{2,1,0:T(8,128)}, /*index=5*/f32[4,336,128]{2,1,0:T(8,128)}) custom-call(f32[2048,128]{1,0:T(8,128)} %bitcast.75, f32[2048,128]{1,0:T(8,128)} %bitcast.73, f32[1024,128]{1,0:T(8,128)} %bitcast.77, ...), custom_call_target="tpu_custom_call" | custom-call | flops 1000000 | bytes 1000000 | tf_op jit(solution)/shard_map/pallas_call | solution.py:38
  100.2 3.0 %collective-permute-start.8 = (f32[4,336,128]{2,1,0:T(8,128)}, f32[4,336,128]{2,1,0:T(8,128)S(1)}, u32[]{:S(2)}, u32[]{:S(2)}) collective-permute-start(f32[4,336,128]{2,1,0:T(8,128)} %get-tuple-element.29), channel_id=1, source_target_pairs={{0,56},{8,0},{16,8},{24,16},{32,24},{40,32},{48,40},{56,48},{1,57}... | collective-permute-start | bytes 2064392 | tf_op jit(solution)/shard_map/ppermute | solution.py:88
  103.1 0.6 pad_maximum_fusion.7.surface
  103.9 2.9 %collective-permute-start.17 = (f32[4,3,1024]{2,0,1:T(4,128)S(1)}, f32[4,3,1024]{2,0,1:T(4,128)S(1)}, u32[]{:S(2)}, u32[]{:S(2)}) collective-permute-start(f32[4,3,1024]{2,0,1:T(4,128)S(1)} %get-tuple-element.42), channel_id=1, source_target_pairs={{0,56},{8,0},{16,8},{24,16},{32,24},{40,32},{48,40},{56,48},{1,57}... | collective-permute-start | bytes 147464 | tf_op jit(solution)/shard_map/ppermute | solution.py:88
  106.9 0.6 convert_element_type.21.cells
  107.5 5.0 %collective-permute-done.16 = f32[4,3,1024]{2,0,1:T(4,128)S(1)} collective-permute-done((f32[4,3,1024]{2,0,1:T(4,128)S(1)}, f32[4,3,1024]{2,0,1:T(4,128)S(1)}, u32[]{:S(2)}, u32[]{:S(2)}) %collective-permute-start.16) | collective-permute-done | bytes 49184 | tf_op jit(solution)/shard_map/ppermute | solution.py:83
  112.5 0.8 copy.25.values
  113.3 5.2 %shard_map.118 = (f32[2,32,128]{2,1,0:T(8,128)}, f32[7,32,128]{2,1,0:T(8,128)}) custom-call(s32[9,1024]{1,0:T(8,128)} %convert_element_type.21.cells, f32[4,9,1024]{2,1,0:T(8,128)} %copy.25.values, f32[32,128]{1,0:T(8,128)} %convert_element_type.17.mask, f32[5,32,128]{2,1,0:T(8,128)} %pad_maximum_fusion.7.surface), custom_call_target="tpu_custom_call" | custom-call | flops 8000000 | bytes 1000000 | tf_op jit(solution)/shard_map/pallas_call | solution.py:38
  118.5 0.9 copy-done
  119.4 0.3 copy-done.1
  119.7 17.9 %shard_map.116 = (f32[16,128,128]{2,1,0:T(8,128)}, f32[6,128,128]{2,1,0:T(8,128)}, f32[6,128,128]{2,1,0:T(8,128)}) custom-call(f32[28,128,128]{2,1,0:T(8,128)} %get-tuple-element.24.refs_0_, f32[28,128,128]{2,1,0:T(8,128)} %get-tuple-element.25.refs_1_, f32[28,128,128]{2,1,0:T(8,128)} %get-tuple-element.26.refs_2_, ...), custom_call_target="tpu_custom_call" | custom-call | flops 60000000 | bytes 1000000 | tf_op jit(solution)/shard_map/pallas_call | solution.py:38
  137.6 0.7 collective-permute-start.11
  138.3 5.0 %collective-permute-start.9 = (f32[6,128,128]{2,1,0:T(8,128)}, f32[6,128,128]{2,1,0:T(8,128)S(1)}, u32[]{:S(2)}, u32[]{:S(2)}) collective-permute-start(f32[6,128,128]{2,1,0:T(8,128)} %get-tuple-element.31), channel_id=1, source_target_pairs={{0,1},{8,9},{16,17},{24,25},{32,33},{40,41},{48,49},{56,57},{1,2},... | collective-permute-start | bytes 1179656 | tf_op jit(solution)/shard_map/ppermute | solution.py:66
  143.3 3.3 %collective-permute-start.10 = (f32[6,128,128]{2,1,0:T(8,128)}, f32[6,128,128]{2,1,0:T(8,128)S(1)}, u32[]{:S(2)}, u32[]{:S(2)}) collective-permute-start(f32[6,128,128]{2,1,0:T(8,128)} %get-tuple-element.32), channel_id=1, source_target_pairs={{1,0},{9,8},{17,16},{25,24},{33,32},{41,40},{49,48},{57,56},{2,1},... | collective-permute-start | bytes 1179656 | tf_op jit(solution)/shard_map/ppermute | solution.py:72
  146.6 4.1 %collective-permute-start.18 = (f32[7,24,128]{2,1,0:T(8,128)S(1)}, f32[7,24,128]{2,1,0:T(8,128)S(1)}, u32[]{:S(2)}, u32[]{:S(2)}) collective-permute-start(f32[7,24,128]{2,1,0:T(8,128)S(1)} %get-tuple-element.50), channel_id=1, source_target_pairs={{0,1},{8,9},{16,17},{24,25},{32,33},{40,41},{48,49},{56,57},{1,2},... | collective-permute-start | bytes 258056 | tf_op jit(solution)/shard_map/ppermute | solution.py:66
  150.7 4.2 %collective-permute-start.19 = (f32[7,24,128]{2,1,0:T(8,128)S(1)}, f32[7,24,128]{2,1,0:T(8,128)S(1)}, u32[]{:S(2)}, u32[]{:S(2)}) collective-permute-start(f32[7,24,128]{2,1,0:T(8,128)S(1)} %get-tuple-element.49), channel_id=1, source_target_pairs={{1,0},{9,8},{17,16},{25,24},{33,32},{41,40},{49,48},{57,56},{2,1},... | collective-permute-start | bytes 258056 | tf_op jit(solution)/shard_map/ppermute | solution.py:72
  154.8 8.7 %collective-permute-done.18.south = f32[7,24,128]{2,1,0:T(8,128)S(1)} collective-permute-done((f32[7,24,128]{2,1,0:T(8,128)S(1)}, f32[7,24,128]{2,1,0:T(8,128)S(1)}, u32[]{:S(2)}, u32[]{:S(2)}) %collective-permute-start.18) | collective-permute-done | bytes 86048 | tf_op jit(solution)/shard_map/ppermute | solution.py:66
  163.5 0.7 collective-permute-start.20
  164.2 1.1 collective-permute-done.19.north
  165.3 0.6 copy-done.16
  166.0 0.6 copy-done.17
  166.6 1.8 shard_map.119.own
  168.4 2.9 %collective-permute-start.22 = (f32[7,80,128]{2,1,0:T(8,128)}, f32[7,80,128]{2,1,0:T(8,128)S(1)}, u32[]{:S(2)}, u32[]{:S(2)}) collective-permute-start(f32[7,80,128]{2,1,0:T(8,128)} %shard_map.119.own), channel_id=1, source_target_pairs={{0,56},{8,0},{16,8},{24,16},{32,24},{40,32},{48,40},{56,48},{1,57}... | collective-permute-start | bytes 860168 | tf_op jit(solution)/shard_map/ppermute | solution.py:88
  171.4 0.7 copy-done.9
  172.1 0.1 copy-done.7
  172.2 0.1 copy-done.8
  172.3 3.5 %shard_map.117 = (f32[28,128,128]{2,1,0:T(8,128)}, f32[336,128]{1,0:T(8,128)}, f32[336,128]{1,0:T(8,128)}) custom-call(f32[16,128,128]{2,1,0:T(8,128)} %get-tuple-element.30.state, f32[6,128,128]{2,1,0:T(8,128)} %copy-done.8, f32[6,128,128]{2,1,0:T(8,128)} %copy-done.9, f32[6,128,128]{2,1,0:T(8,128)} %copy-done.7, s32[2]{0:T(128)} %add_convert_fusion.flags), custom_call_target="tpu_custom_call" | custom-call | flops 1000000 | bytes 1000000 | tf_op jit(solution)/shard_map/pallas_call | solution.py:38
  175.9 3.0 %collective-permute-start.13 = (f32[336,128]{1,0:T(8,128)}, f32[336,128]{1,0:T(8,128)S(1)}, u32[]{:S(2)}, u32[]{:S(2)}) collective-permute-start(f32[336,128]{1,0:T(8,128)} %get-tuple-element.35), channel_id=1, source_target_pairs={{0,56},{8,0},{16,8},{24,16},{32,24},{40,32},{48,40},{56,48},{1,57}... | collective-permute-start | bytes 516104 | tf_op jit(solution)/shard_map/ppermute | solution.py:88
  178.8 4.4 %shard_map.113 = f32[4,32,32,128]{3,2,1,0:T(8,128)} custom-call(f32[4,32,32,128]{3,2,1,0:T(8,128)} %state.1, f32[32,128]{1,0:T(8,128)} %kappa.1, f32[4,32,128]{2,1,0:T(8,128)} %bitcast.90), custom_call_target="tpu_custom_call" | custom-call | flops 5000000 | bytes 4200000 | tf_op jit(solution)/shard_map/pallas_call | solution.py:496
  183.2 0.7 copy-done.10
  183.9 0.7 copy-done.11
  184.7 5.9 %shard_map.120.refs_8_ = f32[2,32,128]{2,1,0:T(8,128)} custom-call(f32[7,80,128]{2,1,0:T(8,128)} %shard_map.119.own, f32[7,80,128]{2,1,0:T(8,128)} %copy-done.10, f32[7,80,128]{2,1,0:T(8,128)} %copy-done.11), custom_call_target="tpu_custom_call" | custom-call | flops 10000000 | bytes 1000000 | tf_op jit(solution)/shard_map/pallas_call | solution.py:38
  190.6 0.6 copy-done.13
  191.3 19.5 %shard_map.121 = f32[2048,128]{1,0:T(8,128)} custom-call(f32[28,128,128]{2,1,0:T(8,128)} %get-tuple-element.33.refs_0_, f32[28,128,128]{2,1,0:T(8,128)} %get-tuple-element.25.refs_1_, f32[28,128,128]{2,1,0:T(8,128)} %get-tuple-element.26.refs_2_, f32[28,128,128]{2,1,0:T(8,128)} %get-tuple-element.27.refs_3_, f32[4,336,128]{2,1,0:T(8,128)} %copy-done, ...), custom_call_target="tpu_custom_call" | custom-call | flops 60000000 | bytes 1000000 | tf_op jit(solution)/shard_map/pallas_call | solution.py:38
  (72 shorter events, 0.5 us)
Async XLA Ops:
  0.6 26.1 %copy-start.18 = (s32[32,128]{1,0:T(8,128)S(1)}, s32[32,128]{1,0:T(8,128)}, u32[]{:S(2)}) copy-start(s32[32,128]{1,0:T(8,128)} %param.14) | copy-start | bytes 49156
  0.6 13.7 %copy-start.12 = (s32[3,3,1024]{2,1,0:T(4,128)S(1)}, s32[3,3,1024]{2,1,0:T(4,128)}, u32[]{:S(2)}) copy-start(s32[3,3,1024]{2,1,0:T(4,128)} %param.16) | copy-start | bytes 110596
  2.0 23.1 %copy-start.6 = (f32[32,128]{1,0:T(8,128)S(1)}, f32[32,128]{1,0:T(8,128)}, u32[]{:S(2)}) copy-start(f32[32,128]{1,0:T(8,128)} %convert_element_type.17.mask) | copy-start | bytes 49156
  7.1 80.4 %collective-permute-start.4 = (f32[12,160,128]{2,1,0:T(8,128)}, f32[12,160,128]{2,1,0:T(8,128)S(1)}, u32[]{:S(2)}, u32[]{:S(2)}) collective-permute-start(f32[12,160,128]{2,1,0:T(8,128)} %get-tuple-element.23), channel_id=1, source_target_pairs={{0,1},{8,9},{16,17},{24,25},{32,33},{40,41},{48,49},{56,57},{1,2},... | collective-permute-start | bytes 2949128 | tf_op jit(solution)/shard_map/ppermute | solution.py:66
  12.8 74.6 %collective-permute-start.6 = (f32[12,160,128]{2,1,0:T(8,128)}, f32[12,160,128]{2,1,0:T(8,128)S(1)}, u32[]{:S(2)}, u32[]{:S(2)}) collective-permute-start(f32[12,160,128]{2,1,0:T(8,128)} %get-tuple-element.23), channel_id=1, source_target_pairs={{71,127},{79,119},{87,111},{95,103},{103,95},{111,87},{119,79},{12... | collective-permute-start | bytes 2949128 | tf_op jit(solution)/shard_map/ppermute | solution.py:78
  14.4 23.3 %collective-permute-start.1 = (f32[120,128]{1,0:T(8,128)S(1)}, f32[120,128]{1,0:T(8,128)S(1)}, u32[]{:S(2)}, u32[]{:S(2)}) collective-permute-start(f32[120,128]{1,0:T(8,128)S(1)} %get-tuple-element.52), channel_id=1, source_target_pairs={{1,0},{9,8},{17,16},{25,24},{33,32},{41,40},{49,48},{57,56},{2,1},... | collective-permute-start | bytes 184328 | tf_op jit(solution)/shard_map/ppermute | solution.py:72
  16.9 40.8 %collective-permute-start = (f32[120,128]{1,0:T(8,128)S(1)}, f32[120,128]{1,0:T(8,128)S(1)}, u32[]{:S(2)}, u32[]{:S(2)}) collective-permute-start(f32[120,128]{1,0:T(8,128)S(1)} %get-tuple-element.51), channel_id=1, source_target_pairs={{0,1},{8,9},{16,17},{24,25},{32,33},{40,41},{48,49},{56,57},{1,2},... | collective-permute-start | bytes 184328 | tf_op jit(solution)/shard_map/ppermute | solution.py:66
  21.8 65.6 %collective-permute-start.5 = (f32[12,160,128]{2,1,0:T(8,128)}, f32[12,160,128]{2,1,0:T(8,128)S(1)}, u32[]{:S(2)}, u32[]{:S(2)}) collective-permute-start(f32[12,160,128]{2,1,0:T(8,128)} %get-tuple-element.22.own), channel_id=1, source_target_pairs={{1,0},{9,8},{17,16},{25,24},{33,32},{41,40},{49,48},{57,56},{2,1},... | collective-permute-start | bytes 2949128 | tf_op jit(solution)/shard_map/ppermute | solution.py:72
  59.1 7.4 %collective-permute-start.3 = (f32[312,128]{1,0:T(8,128)}, f32[312,128]{1,0:T(8,128)S(1)}, u32[]{:S(2)}, u32[]{:S(2)}) collective-permute-start(f32[312,128]{1,0:T(8,128)} %get-tuple-element.48), channel_id=1, source_target_pairs={{0,56},{8,0},{16,8},{24,16},{32,24},{40,32},{48,40},{56,48},{1,57}... | collective-permute-start | bytes 479240 | tf_op jit(solution)/shard_map/ppermute | solution.py:88
  60.7 6.1 %collective-permute-start.2 = (f32[312,128]{1,0:T(8,128)}, f32[312,128]{1,0:T(8,128)S(1)}, u32[]{:S(2)}, u32[]{:S(2)}) collective-permute-start(f32[312,128]{1,0:T(8,128)} %get-tuple-element.47), channel_id=1, source_target_pairs={{0,8},{8,16},{16,24},{24,32},{32,40},{40,48},{48,56},{56,0},{1,9},... | collective-permute-start | bytes 479240 | tf_op jit(solution)/shard_map/ppermute | solution.py:83
  79.1 24.6 %collective-permute-start.14 = (f32[4,3,1024]{2,0,1:T(4,128)S(1)}, f32[4,3,1024]{2,0,1:T(4,128)S(1)}, u32[]{:S(2)}, u32[]{:S(2)}) collective-permute-start(f32[4,3,1024]{2,0,1:T(4,128)S(1)} %get-tuple-element.44), channel_id=1, source_target_pairs={{0,1},{8,9},{16,17},{24,25},{32,33},{40,41},{48,49},{56,57},{1,2},... | collective-permute-start | bytes 147464 | tf_op jit(solution)/shard_map/ppermute | solution.py:66
  85.1 21.8 %copy-start.19 = (f32[3,1,8,128]{3,2,1,0:T(8,128)S(1)}, f32[3,1,8,128]{3,2,1,0:T(8,128)}, u32[]{:S(2)}) copy-start(f32[3,1,8,128]{3,2,1,0:T(8,128)} %get-tuple-element.56) | copy-start | bytes 36868
  85.1 18.7 %collective-permute-start.15 = (f32[4,3,1024]{2,0,1:T(4,128)S(1)}, f32[4,3,1024]{2,0,1:T(4,128)S(1)}, u32[]{:S(2)}, u32[]{:S(2)}) collective-permute-start(f32[4,3,1024]{2,0,1:T(4,128)S(1)} %get-tuple-element.45), channel_id=1, source_target_pairs={{1,0},{9,8},{17,16},{25,24},{33,32},{41,40},{49,48},{57,56},{2,1},... | collective-permute-start | bytes 147464 | tf_op jit(solution)/shard_map/ppermute | solution.py:72
  87.4 1.0 copy-start.2
  87.5 1.3 copy-start.4
  88.8 0.9 copy-start.3
  100.2 18.4 %collective-permute-start.7 = (f32[4,336,128]{2,1,0:T(8,128)}, f32[4,336,128]{2,1,0:T(8,128)S(1)}, u32[]{:S(2)}, u32[]{:S(2)}) collective-permute-start(f32[4,336,128]{2,1,0:T(8,128)} %get-tuple-element.28), channel_id=1, source_target_pairs={{0,8},{8,16},{16,24},{24,32},{32,40},{40,48},{48,56},{56,0},{1,9},... | collective-permute-start | bytes 2064392 | tf_op jit(solution)/shard_map/ppermute | solution.py:83
  100.2 18.4 %collective-permute-start.8 = (f32[4,336,128]{2,1,0:T(8,128)}, f32[4,336,128]{2,1,0:T(8,128)S(1)}, u32[]{:S(2)}, u32[]{:S(2)}) collective-permute-start(f32[4,336,128]{2,1,0:T(8,128)} %get-tuple-element.29), channel_id=1, source_target_pairs={{0,56},{8,0},{16,8},{24,16},{32,24},{40,32},{48,40},{56,48},{1,57}... | collective-permute-start | bytes 2064392 | tf_op jit(solution)/shard_map/ppermute | solution.py:88
  103.8 8.6 %collective-permute-start.16 = (f32[4,3,1024]{2,0,1:T(4,128)S(1)}, f32[4,3,1024]{2,0,1:T(4,128)S(1)}, u32[]{:S(2)}, u32[]{:S(2)}) collective-permute-start(f32[4,3,1024]{2,0,1:T(4,128)S(1)} %get-tuple-element.41), channel_id=1, source_target_pairs={{0,8},{8,16},{16,24},{24,32},{32,40},{40,48},{48,56},{56,0},{1,9},... | collective-permute-start | bytes 147464 | tf_op jit(solution)/shard_map/ppermute | solution.py:83
  103.9 8.6 %collective-permute-start.17 = (f32[4,3,1024]{2,0,1:T(4,128)S(1)}, f32[4,3,1024]{2,0,1:T(4,128)S(1)}, u32[]{:S(2)}, u32[]{:S(2)}) collective-permute-start(f32[4,3,1024]{2,0,1:T(4,128)S(1)} %get-tuple-element.42), channel_id=1, source_target_pairs={{0,56},{8,0},{16,8},{24,16},{32,24},{40,32},{48,40},{56,48},{1,57}... | collective-permute-start | bytes 147464 | tf_op jit(solution)/shard_map/ppermute | solution.py:88
  118.5 0.9 copy-start
  118.5 1.2 copy-start.1
  119.7 26.9 %copy-start.5 = (f32[7,32,128]{2,1,0:T(8,128)S(1)}, f32[7,32,128]{2,1,0:T(8,128)}, u32[]{:S(2)}) copy-start(f32[7,32,128]{2,1,0:T(8,128)} %get-tuple-element.37.own) | copy-start | bytes 344068
  137.6 33.7 %collective-permute-start.11 = (f32[6,128,128]{2,1,0:T(8,128)}, f32[6,128,128]{2,1,0:T(8,128)S(1)}, u32[]{:S(2)}, u32[]{:S(2)}) collective-permute-start(f32[6,128,128]{2,1,0:T(8,128)} %get-tuple-element.31), channel_id=1, source_target_pairs={{71,127},{79,119},{87,111},{95,103},{103,95},{111,87},{119,79},{12... | collective-permute-start | bytes 1179656 | tf_op jit(solution)/shard_map/ppermute | solution.py:78
  138.3 33.1 %collective-permute-start.9 = (f32[6,128,128]{2,1,0:T(8,128)}, f32[6,128,128]{2,1,0:T(8,128)S(1)}, u32[]{:S(2)}, u32[]{:S(2)}) collective-permute-start(f32[6,128,128]{2,1,0:T(8,128)} %get-tuple-element.31), channel_id=1, source_target_pairs={{0,1},{8,9},{16,17},{24,25},{32,33},{40,41},{48,49},{56,57},{1,2},... | collective-permute-start | bytes 1179656 | tf_op jit(solution)/shard_map/ppermute | solution.py:66
  143.3 28.0 %collective-permute-start.10 = (f32[6,128,128]{2,1,0:T(8,128)}, f32[6,128,128]{2,1,0:T(8,128)S(1)}, u32[]{:S(2)}, u32[]{:S(2)}) collective-permute-start(f32[6,128,128]{2,1,0:T(8,128)} %get-tuple-element.32), channel_id=1, source_target_pairs={{1,0},{9,8},{17,16},{25,24},{33,32},{41,40},{49,48},{57,56},{2,1},... | collective-permute-start | bytes 1179656 | tf_op jit(solution)/shard_map/ppermute | solution.py:72
  146.6 16.9 %collective-permute-start.18 = (f32[7,24,128]{2,1,0:T(8,128)S(1)}, f32[7,24,128]{2,1,0:T(8,128)S(1)}, u32[]{:S(2)}, u32[]{:S(2)}) collective-permute-start(f32[7,24,128]{2,1,0:T(8,128)S(1)} %get-tuple-element.50), channel_id=1, source_target_pairs={{0,1},{8,9},{16,17},{24,25},{32,33},{40,41},{48,49},{56,57},{1,2},... | collective-permute-start | bytes 258056 | tf_op jit(solution)/shard_map/ppermute | solution.py:66
  150.7 14.6 %collective-permute-start.19 = (f32[7,24,128]{2,1,0:T(8,128)S(1)}, f32[7,24,128]{2,1,0:T(8,128)S(1)}, u32[]{:S(2)}, u32[]{:S(2)}) collective-permute-start(f32[7,24,128]{2,1,0:T(8,128)S(1)} %get-tuple-element.49), channel_id=1, source_target_pairs={{1,0},{9,8},{17,16},{25,24},{33,32},{41,40},{49,48},{57,56},{2,1},... | collective-permute-start | bytes 258056 | tf_op jit(solution)/shard_map/ppermute | solution.py:72
  163.5 1.8 copy-start.15
  163.5 1.8 collective-permute-start.20
  165.3 0.6 copy-start.16
  166.0 0.6 copy-start.17
  168.4 14.9 %collective-permute-start.21 = (f32[7,80,128]{2,1,0:T(8,128)}, f32[7,80,128]{2,1,0:T(8,128)S(1)}, u32[]{:S(2)}, u32[]{:S(2)}) collective-permute-start(f32[7,80,128]{2,1,0:T(8,128)} %shard_map.119.own), channel_id=1, source_target_pairs={{0,8},{8,16},{16,24},{24,32},{32,40},{40,48},{48,56},{56,0},{1,9},... | collective-permute-start | bytes 860168 | tf_op jit(solution)/shard_map/ppermute | solution.py:83
  168.4 14.9 %collective-permute-start.22 = (f32[7,80,128]{2,1,0:T(8,128)}, f32[7,80,128]{2,1,0:T(8,128)S(1)}, u32[]{:S(2)}, u32[]{:S(2)}) collective-permute-start(f32[7,80,128]{2,1,0:T(8,128)} %shard_map.119.own), channel_id=1, source_target_pairs={{0,56},{8,0},{16,8},{24,16},{32,24},{40,32},{48,40},{56,48},{1,57}... | collective-permute-start | bytes 860168 | tf_op jit(solution)/shard_map/ppermute | solution.py:88
  171.3 0.7 copy-start.9
  171.3 0.9 copy-start.7
  171.4 1.0 copy-start.8
  175.9 14.7 %collective-permute-start.12 = (f32[336,128]{1,0:T(8,128)}, f32[336,128]{1,0:T(8,128)S(1)}, u32[]{:S(2)}, u32[]{:S(2)}) collective-permute-start(f32[336,128]{1,0:T(8,128)} %get-tuple-element.34), channel_id=1, source_target_pairs={{0,8},{8,16},{16,24},{24,32},{32,40},{40,48},{48,56},{56,0},{1,9},... | collective-permute-start | bytes 516104 | tf_op jit(solution)/shard_map/ppermute | solution.py:83
  175.9 14.7 %collective-permute-start.13 = (f32[336,128]{1,0:T(8,128)}, f32[336,128]{1,0:T(8,128)S(1)}, u32[]{:S(2)}, u32[]{:S(2)}) collective-permute-start(f32[336,128]{1,0:T(8,128)} %get-tuple-element.35), channel_id=1, source_target_pairs={{0,56},{8,0},{16,8},{24,16},{32,24},{40,32},{48,40},{56,48},{1,57}... | collective-permute-start | bytes 516104 | tf_op jit(solution)/shard_map/ppermute | solution.py:88
  183.2 0.7 copy-start.10
  183.9 0.7 copy-start.11
  190.5 0.7 copy-start.13
  190.6 0.7 copy-start.14

commit v2 on v1

v2 whole, which is shorter than its diff:
```python
import functools

import jax
import jax.numpy as jnp
from jax import lax
from jax.experimental import pallas as pl
from jax.experimental.pallas import tpu as pltpu
from jax.sharding import PartitionSpec as P

ITERS = 24
ATM_SUB = 4

current_scale = 2.0
atmos_gain = 0.5
ocean_gain = 0.02

AXES = ("face", "gx", "gy")
F32 = jnp.float32
BF16 = jnp.bfloat16
LV = 32
RW = 32
CL = 128
HALO = 12
ROUNDS = ITERS // HALO
NI = RW // 2 + HALO
NC = CL + 2 * HALO
JB = NC // 8
OFF = 24 - HALO
WIDTH = 168
DEEP = ITERS
SR = RW + 2 * DEEP
VALS = 3 * RW
LINES = 8
EDGE_MIB, OWN_MIB, DEEP_MIB = 60, 20, 20

VMEM = pl.BlockSpec(memory_space=pltpu.VMEM)
SMEM = pl.BlockSpec(memory_space=pltpu.SMEM)


def call(kernel, outs, args, scratch=(), flops=1_000_000, mib=16, blocks=()):
    specs = [SMEM if a.dtype == jnp.int32 and a.ndim == 1 else VMEM for a in args]
    for n, block in dict(blocks).items():
        specs[n] = pl.BlockSpec(block, lambda _, rank=len(block): (0,) * rank)
    return pl.pallas_call(
        kernel,
        grid=(1,) if blocks else (),
        out_shape=outs,
        in_specs=specs,
        out_specs=jax.tree.map(lambda _: VMEM, outs),
        scratch_shapes=list(scratch),
        compiler_params=pltpu.CompilerParams(vmem_limit_bytes=mib * 2**20),
        cost_estimate=pl.CostEstimate(flops=flops, bytes_accessed=1_000_000, transcendentals=0),
    )(*args)


def shape(*dims):
    return jax.ShapeDtypeStruct(dims, F32)


def block_id(r, x):
    gx, gy = lax.axis_size("gx"), lax.axis_size("gy")
    return (r // gy) * gx * gy + x * gy + r % gy


def sizes():
    return lax.axis_size("face") * lax.axis_size("gy"), lax.axis_size("gx")


def to_north(value):
    nr, nx = sizes()
    pairs = [(block_id(r, x), block_id(r + 1, x)) for r in range(nr - 1) for x in range(nx)]
    return lax.ppermute(value, AXES, pairs)


def to_south(value):
    nr, nx = sizes()
    pairs = [(block_id(r, x), block_id(r - 1, x)) for r in range(1, nr) for x in range(nx)]
    return lax.ppermute(value, AXES, pairs)


def across_fold(value):
    nr, nx = sizes()
    pairs = [(block_id(nr - 1, x), block_id(nr - 1, nx - 1 - x)) for x in range(nx)]
    return lax.ppermute(value, AXES, pairs)


def to_east(value):
    nx = lax.axis_size("gx")
    return lax.ppermute(value, "gx", [(x, (x + 1) % nx) for x in range(nx)])


def to_west(value):
    nx = lax.axis_size("gx")
    return lax.ppermute(value, "gx", [(x, (x - 1) % nx) for x in range(nx)])


def reversed_lanes(value):
    index = CL - 1 - lax.broadcasted_iota(jnp.int32, value.shape, 1)
    return jnp.take_along_axis(value, index, axis=1, mode="promise_in_bounds")


def level_rows(ref, base, row):
    return ref[pl.ds(base + row, LV, stride=RW), :]


def edge_kernel(tracers, flow, kappa, mask, top, bottom):
    def body(k, carry):
        for out, row in ((bottom, k), (top, RW - 1 - k)):
            sea = mask[pl.ds(row, 1), :].astype(F32)
            out[k, 0:LV] = level_rows(tracers, 0, row)
            out[k, LV : 2 * LV] = level_rows(tracers, LV * RW, row)
            out[k, 2 * LV : 3 * LV] = sea * level_rows(flow, 0, row)
            out[k, 3 * LV : 4 * LV] = sea * level_rows(flow, LV * RW, row)
            out[k, 4 * LV : 5 * LV] = sea * level_rows(kappa, 0, row)
        return carry

    lax.fori_loop(0, HALO, body, 0)


def columns(low, high, sign=1.0):
    a, b = low
    c, d = high
    return jnp.concatenate([a, b, c, d] if sign > 0 else [a, b, -c, -d], axis=0).T


def emit_columns(p, pairs, x, mw, me):
    for f in range(4):
        pair = []
        for n in range(2):
            low, high = pairs[n]
            if f == 0:
                t = columns((low[0], low[1]), (high[0], high[1]))
            else:
                t = columns((low[f + 1],) * 2, (high[f + 1],) * 2, -1.0 if f == 2 else 1.0)
            x[f, 2 * p + n] = t
            pair.append(t)
        rows = pl.ds(pl.multiple_of(p * 2 * HALO, 8), 2 * HALO)
        mw[f, rows, :] = jnp.concatenate([t[:HALO] for t in pair], axis=0)
        me[f, rows, :] = jnp.concatenate([t[CL - HALO :] for t in pair], axis=0)


def own_kernel(tracers, flow, kappa, mask, x, mw, me):
    def inner(p, carry):
        pairs = []
        for n in range(2):
            sides = []
            for row in (2 * p + n, RW - 1 - (2 * p + n)):
                sea = mask[pl.ds(row, 1), :].astype(F32)
                sides.append(
                    [
                        level_rows(tracers, 0, row),
                        level_rows(tracers, LV * RW, row),
                        sea * level_rows(flow, 0, row),
                        sea * level_rows(flow, LV * RW, row),
                        sea * level_rows(kappa, 0, row),
                    ]
                )
            pairs.append(tuple(sides))
        emit_columns(p, pairs, x, mw, me)
        return carry

    lax.fori_loop(0, RW // 4, inner, 0)


def halo_kernel(own, south, north, fold, flags, x, mw, me):
    first = flags[0] > 0
    last = flags[1] > 0

    def halo(p, carry):
        pairs = []
        for n in range(2):
            k = HALO - 1 - (2 * p + n)
            low, high = [], []
            for f in range(5):
                part = slice(f * LV, (f + 1) * LV)
                mirror = own[k, part]
                turned = reversed_lanes(fold[k, part])
                if f == 3:
                    mirror = -mirror
                if f in (2, 3):
                    turned = -turned
                low.append(jnp.where(first, mirror, south[k, part]))
                high.append(jnp.where(last, turned, north[k, part]))
            pairs.append((low, high))
        emit_columns(p, pairs, x, mw, me)
        return carry

    lax.fori_loop(0, HALO // 2, halo, 0)


def deep_kernel(final, *refs):
    xh, xo, wh, wo, eh, eo = refs[:6]
    if final:
        xts, mine, w2, e2, out = refs[6:11]
        scratch = refs[11:]
        surface_steps(mine, w2, e2, out, scratch[6:])
        scratch = scratch[:6]
    else:
        fields, state, top, bottom = refs[6:10]
        scratch = refs[10:]
    s0, s1, cw, ce, cd, cu = scratch
    mid = slice(24, 24 + CL)

    def coefficients(i, where, u, v, k):
        cw[i, where] = jnp.maximum(u, 0.0) + k
        ce[i, where] = jnp.maximum(-u, 0.0) + k
        cd[i, where] = jnp.maximum(v, 0.0) + k
        cu[i, where] = jnp.maximum(-v, 0.0) + k

    def fill(x, w, e, start):
        def body(p, carry):
            rows = pl.ds(pl.multiple_of(p * 2 * HALO, 8), 2 * HALO)
            west = [w[f, rows, :] for f in range(4)]
            east = [e[f, rows, :] for f in range(4)]
            if final:
                rows = pl.ds(pl.multiple_of((p + start // 2) * 2 * HALO, 8), 2 * HALO)
                west[0] = w2[rows, :]
                east[0] = e2[rows, :]
            for n in range(2):
                i = 2 * p + n
                part = slice(n * HALO, (n + 1) * HALO)
                s0[start + i, mid] = xts[start + i] if final else x[0, i]
                coefficients(start + i, mid, x[1, i], x[2, i], x[3, i])
                for side, where in (
                    (west, slice(24 - HALO, 24)),
                    (east, slice(24 + CL, 24 + CL + HALO)),
                ):
                    s0[start + i, where] = side[0][part]
                    coefficients(start + i, where, side[1][part], side[2][part], side[3][part])
            return carry

        lax.fori_loop(0, x.shape[1] // 2, body, 0)

    fill(xh, wh, eh, 0)
    fill(xo, wo, eo, HALO)

    def at(ref, i, j):
        return ref[i, pl.ds(OFF + j, 8, stride=JB), :]

    def rows(src, dst, i, count):
        lines = [[at(src, i + n, j - 1) for j in range(2)] for n in range(count)]
        for j in range(JB):
            for n in range(count):
                lines[n].append(at(src, i + n, j + 1))
            for n in range(count):
                west, centre, east = lines[n][j : j + 3]
                down = lines[n - 1][j + 1] if n else at(src, i - 1, j)
                if count == 1:
                    up = pltpu.roll(centre, CL // 2, 1)
                else:
                    up = lines[n + 1][j + 1] if n + 1 < count else at(src, i + count, j)
                k = i + n
                dst[k, pl.ds(OFF + j, 8, stride=JB), :] = (
                    centre
                    + at(cw, k, j) * (west - centre)
                    + at(ce, k, j) * (east - centre)
                    + at(cd, k, j) * (down - centre)
                    + at(cu, k, j) * (up - centre)
                )

    def step(src, dst, s):
        def body(p, carry):
            rows(src, dst, 2 * p + 1, 2)
            return carry

        lax.fori_loop(s, NI // 2 - 1, body, 0)
        rows(src, dst, NI - 1, 1)

    def two(n, carry):
        step(s0, s1, n)
        step(s1, s0, n)
        return carry

    lax.fori_loop(0, HALO // 2, two, 0)

    if final:

        def write(i, carry):
            t = s0[i + HALO, mid].T
            for h, r in ((0, i), (1, RW - 1 - i)):
                for tracer in range(2):
                    base = h * 2 * LV + tracer * LV + 1
                    out[pl.ds(tracer * LV * RW + RW + r, LV - 1, stride=RW), :] = t[
                        base : base + LV - 1
                    ]
            return carry

        lax.fori_loop(0, RW // 2, write, 0)
    else:
        low = lax.broadcasted_iota(jnp.int32, (CL, CL), 1) < CL // 2
        for i in range(RW // 2):
            state[i] = s0[i + HALO, mid]
        half = HALO // 2
        for k in range(half):
            near, far = s0[HALO + k, mid], s0[HALO + k + half, mid]
            where = slice(k * CL, (k + 1) * CL)
            top[where] = jnp.where(low, pltpu.roll(near, CL // 2, 1), far)
            bottom[where] = jnp.where(low, near, pltpu.roll(far, CL // 2, 1))
        for f in range(7):
            where = slice(half * CL + f * DEEP, half * CL + (f + 1) * DEEP)
            top[where] = fields[f, RW - DEEP :]
            bottom[where] = fields[f, :DEEP]


def join_kernel(state, fields, south, north, fold, flags, xts, mw, me, joined):
    first = flags[0] > 0
    last = flags[1] > 0
    low = lax.broadcasted_iota(jnp.int32, (CL, CL), 1) < CL // 2
    half = HALO // 2
    flip = jnp.where(
        lax.broadcasted_iota(jnp.int32, (CL, CL), 0)
        + lax.broadcasted_iota(jnp.int32, (CL, CL), 1)
        == CL - 1,
        1.0,
        0.0,
    ).astype(F32)
    rows = {}
    for i in range(RW // 2):
        rows[HALO + i] = state[i]
    for k in range(half):
        where = slice(k * CL, (k + 1) * CL)
        s, n = south[where], north[where]
        f = jnp.dot(flip, fold[where], precision=lax.Precision.HIGHEST, preferred_element_type=F32)
        s_roll, n_roll, f_roll = (pltpu.roll(v, CL // 2, 1) for v in (s, n, f))
        for kk, sv, nv, fv in ((k, s, n_roll, f_roll), (k + half, s_roll, n, f)):
            down = jnp.where(first, state[kk], sv)
            up = jnp.where(last, fv, nv)
            rows[HALO - 1 - kk] = jnp.where(low, down, up)
    for i in range(NI):
        xts[i] = rows[i]
    for p in range(NI // 2):
        pair = [rows[2 * p], rows[2 * p + 1]]
        where = pl.ds(p * 2 * HALO, 2 * HALO)
        mw[where, :] = jnp.concatenate([t[:HALO] for t in pair], axis=0)
        me[where, :] = jnp.concatenate([t[CL - HALO :] for t in pair], axis=0)

    base = half * CL
    for f in range(7):
        part = slice(base + f * DEEP, base + (f + 1) * DEEP)
        joined[f, 0:DEEP] = south[part]
        joined[f, DEEP : DEEP + RW] = fields[f]
        joined[f, DEEP + RW :] = north[part]

    @pl.when(first)
    def _():
        for f in range(7):
            sign = -1.0 if f == 3 else 1.0
            for k in range(DEEP):
                joined[f, DEEP - 1 - k : DEEP - k] = sign * fields[f, k : k + 1]

    @pl.when(last)
    def _():
        for f in range(7):
            sign = -1.0 if f in (2, 3) else 1.0
            turned = sign * reversed_lanes(fold[base + f * DEEP : base + (f + 1) * DEEP])
            for k in range(DEEP):
                joined[f, DEEP + RW + k : DEEP + RW + k + 1] = turned[DEEP - 1 - k : DEEP - k]

    low = lax.broadcasted_iota(jnp.int32, (SR // 2, CL), 1) < CL // 2
    for f in range(7):
        a, b = joined[f, : SR // 2], joined[f, SR // 2 :]
        where = slice(NI * HALO + f * SR // 2, NI * HALO + (f + 1) * SR // 2)
        mw[where] = jnp.where(low, a, pltpu.roll(b, CL // 2, 1))
        me[where] = jnp.where(low, pltpu.roll(a, CL // 2, 1), b)


def surface_steps(mine, w2, e2, out, scratch):
    cw, ce, cs, cn, cf = scratch
    low = lax.broadcasted_iota(jnp.int32, (SR // 2, CL), 1) < CL // 2

    def wide(f):
        where = slice(NI * HALO + f * SR // 2, NI * HALO + (f + 1) * SR // 2)
        east, west = e2[where], w2[where]
        near = jnp.where(low, east, pltpu.roll(west, CL // 2, 1))
        far = jnp.where(low, pltpu.roll(east, CL // 2, 1), west)
        return jnp.concatenate([mine[f], jnp.concatenate([near, far], axis=0)], axis=1)

    u, v, k = wide(2), wide(3), wide(4)
    cw[...] = jnp.maximum(u, 0.0) + k
    ce[...] = jnp.maximum(-u, 0.0) + k
    cs[...] = jnp.maximum(v, 0.0) + k
    cn[...] = jnp.maximum(-v, 0.0) + k
    cf[0] = wide(5)
    cf[1] = wide(6)

    def step(n, pair):
        new = []
        for t, x in enumerate(pair):
            west_x = pltpu.roll(x, 1, 1)
            east_x = pltpu.roll(x, 2 * CL - 1, 1)
            south_x = pltpu.roll(x, 1, 0)
            north_x = pltpu.roll(x, SR - 1, 0)
            new.append(
                x
                + cw[...] * (west_x - x)
                + ce[...] * (east_x - x)
                + cs[...] * (south_x - x)
                + cn[...] * (north_x - x)
                + cf[t]
            )
        return tuple(new)

    pair = lax.fori_loop(0, ITERS, step, (wide(0), wide(1)))
    for t in range(2):
        out[t * LV * RW : t * LV * RW + RW] = pair[t][DEEP : DEEP + RW, 0:CL]


def split3(value):
    a = value.astype(BF16)
    rest = value - a.astype(F32)
    b = rest.astype(BF16)
    c = (rest - b.astype(F32)).astype(BF16)
    return a, b, c


def one_hots(cells):
    n = cells.shape[1]
    column = jnp.bitwise_and(cells, CL - 1)
    row = jnp.right_shift(cells, 7)
    hot = jnp.where(lax.broadcasted_iota(jnp.int32, (CL, n), 0) == column, 1.0, 0.0).astype(BF16)
    return hot, lax.broadcasted_iota(jnp.int32, (RW, n), 0) == row


def gather(table, hot, mask):
    parts = split3(table)
    got = sum(jnp.dot(p, hot, preferred_element_type=F32) for p in parts)
    return [
        jnp.sum(jnp.where(mask, got[f * RW : (f + 1) * RW], 0.0), axis=0, keepdims=True)
        for f in range(table.shape[0] // RW)
    ]


def scatter(values, hot, mask):
    parts = [split3(v) for v in values]
    rows = [
        jnp.where(mask, parts[f][s].astype(F32), 0.0).astype(BF16)
        for s in range(3)
        for f in range(len(values))
    ]
    return lax.dot_general(
        jnp.concatenate(rows, axis=0), hot, (((1,), (1,)), ((), ())), preferred_element_type=F32
    )


def bulk_fluxes(air_vals, sea_vals):
    temp_air, humid_air, wind_east, wind_north = air_vals
    sea_temp, current_east, current_north = sea_vals
    shear_east = wind_east - current_east
    shear_north = wind_north - current_north
    wind_speed = jnp.sqrt(shear_east * shear_east + shear_north * shear_north + 0.25)
    richardson = (temp_air - sea_temp) / (wind_speed * wind_speed)
    heat_coeff = 0.1 + 0.4 * jax.nn.sigmoid(-2.0 * richardson)
    drag_coeff = 0.2 + 0.1 * jnp.tanh(wind_speed)
    sensible = heat_coeff * wind_speed * (sea_temp - temp_air)
    latent = heat_coeff * wind_speed * (0.5 * jnp.exp(0.3 * sea_temp) - humid_air)
    return [
        sensible,
        latent,
        drag_coeff * wind_speed * shear_east,
        drag_coeff * wind_speed * shear_north,
    ]


def spread_kernel(tracers, flow, cells, up, mine, down):
    for out, a in ((up, 2), (mine, 1), (down, 0)):
        out[0:RW] = tracers[0, 0]
        out[RW : 2 * RW] = flow[0, 0]
        out[2 * RW : 3 * RW] = flow[1, 0]
        for b in range(3):
            run = cells[a, b : b + 1, :].astype(F32)
            for n in range(run.shape[1] // CL):
                line = VALS + b * LINES + n
                out[line : line + 1] = run[:, n * CL : (n + 1) * CL]


def relay_kernel(up, mine, down, east, west):
    for a, source in enumerate((up, mine, down)):
        for out, b in ((east, 2), (west, 0)):
            out[a * VALS : (a + 1) * VALS] = source[0:VALS]
            line = VALS + b * LINES
            out[3 * VALS + a * LINES : 3 * VALS + (a + 1) * LINES] = source[line : line + LINES]


def flux_kernel(
    air, up, mine, down, west, east, air_cells, sea_cells, weights, flux, north, own, south, vals, sea
):
    for a, source in enumerate((up, mine, down)):
        sea[3 * a] = west[a * VALS : (a + 1) * VALS]
        sea[3 * a + 1] = source[0:VALS]
        sea[3 * a + 2] = east[a * VALS : (a + 1) * VALS]
    table = jnp.concatenate([air[f, 0] for f in range(4)], axis=0)

    def run(ref, q):
        return ref[lax.div(q, 3), pl.ds(lax.rem(q, 3), 1), :]

    def look(q, carry):
        hot, mask = one_hots(run(air_cells, q))
        for f, v in enumerate(gather(table, hot, mask)):
            vals[f, pl.ds(q, 1), :] = v
        hot, mask = one_hots(run(sea_cells, q))
        for f, v in enumerate(gather(sea[q], hot, mask)):
            vals[4 + f, pl.ds(q, 1), :] = v
        for n in range(2):
            vals[7 + n, pl.ds(q, 1), :] = weights[
                n, lax.div(q, 3), pl.ds(lax.rem(q, 3), 1), :
            ]
        return carry

    lax.fori_loop(0, 9, look, 0)
    fluxes = bulk_fluxes(
        [vals[f, 0:9] for f in range(4)],
        [vals[4, 0:9], current_scale * vals[5, 0:9], current_scale * vals[6, 0:9]],
    )
    for f in range(4):
        pay = vals[8, 0:9] * fluxes[f]
        for a, out in enumerate((south, own, north)):
            out[f] = pay[3 * a : 3 * a + 3]
        vals[f, 0:9] = vals[7, 0:9] * fluxes[f]

    def place(q, total):
        hot, mask = one_hots(run(air_cells, q))
        return total + scatter([vals[f, pl.ds(q, 1), :] for f in range(4)], hot, mask)

    total = lax.fori_loop(0, 9, place, jnp.zeros((12 * RW, CL), F32))
    total = total[0 : 4 * RW] + total[4 * RW : 8 * RW] + total[8 * RW :]
    for f in range(4):
        flux[f] = total[f * RW : (f + 1) * RW]


def ocean_flux_kernel(
    up, mine, down, west, east, pay_up, pay_mine, pay_down, pay_west, pay_east,
    mask, tracers, flow, kappa, stress, fields, cells, vals,
):
    def line(ref, start):
        rows = ref[start : start + LINES]
        return jnp.concatenate([rows[n : n + 1] for n in range(LINES)], axis=1).astype(jnp.int32)

    for a, (lists, pay) in enumerate(((up, pay_up), (mine, pay_mine), (down, pay_down))):
        cells[3 * a : 3 * a + 1] = line(west, 3 * VALS + a * LINES)
        cells[3 * a + 1 : 3 * a + 2] = line(lists, VALS + LINES)
        cells[3 * a + 2 : 3 * a + 3] = line(east, 3 * VALS + a * LINES)
        for f in range(4):
            vals[f, 3 * a : 3 * a + 1] = pay_west[f, a : a + 1]
            vals[f, 3 * a + 1 : 3 * a + 2] = pay[f, 1:2]
            vals[f, 3 * a + 2 : 3 * a + 3] = pay_east[f, a : a + 1]

    def place(q, total):
        hot, rows = one_hots(cells[pl.ds(q, 1), :])
        return total + scatter([vals[f, pl.ds(q, 1), :] for f in range(4)], hot, rows)

    total = lax.fori_loop(0, 9, place, jnp.zeros((12 * RW, CL), F32))
    flux = total[0 : 4 * RW] + total[4 * RW : 8 * RW] + total[8 * RW :]
    sea = mask[...].astype(F32)
    part = [flux[f * RW : (f + 1) * RW] for f in range(4)]
    stress[0] = sea * part[2]
    stress[1] = sea * part[3]
    fields[0] = tracers[0, 0]
    fields[1] = tracers[1, 0]
    fields[2] = sea * flow[0, 0]
    fields[3] = sea * flow[1, 0]
    fields[4] = sea * kappa[0]
    fields[5] = -ocean_gain * sea * (part[0] + part[1])
    fields[6] = ocean_gain * sea * part[1]


def atmos_kernel(state, kappa, flux, out):
    f = pl.program_id(0)
    gain = jnp.where(f < 2, atmos_gain, -atmos_gain).astype(F32)
    levels = state.shape[1]
    for g in range(RW // 8):
        rows = slice(8 * g, 8 * g + 8)
        k = kappa[rows, :]
        x = [state[0, l, rows, :] for l in range(levels)]
        x[0] = x[0] + gain * flux[0, rows, :]
        for _ in range(ATM_SUB):
            x = [
                x[l]
                + k * (x[min(l + 1, levels - 1)] + x[max(l - 1, 0)] - 2.0 * x[l])
                for l in range(levels)
            ]
        for l in range(levels):
            out[0, l, rows, :] = x[l]


def atmosphere(atmos_state, atmos_kappa, flux):
    fields, levels = atmos_state.shape[:2]
    block = pl.BlockSpec((1, levels, RW, CL), lambda f: (f, 0, 0, 0))
    return pl.pallas_call(
        atmos_kernel,
        grid=(fields,),
        in_specs=[
            block,
            pl.BlockSpec((RW, CL), lambda f: (0, 0)),
            pl.BlockSpec((1, RW, CL), lambda f: (f, 0, 0)),
        ],
        out_specs=block,
        out_shape=jax.ShapeDtypeStruct(atmos_state.shape, F32),
        compiler_params=pltpu.CompilerParams(vmem_limit_bytes=8 * 2**20),
        cost_estimate=pl.CostEstimate(
            flops=5_000_000, bytes_accessed=4_200_000, transcendentals=0
        ),
    )(atmos_state, atmos_kappa, flux)


def local(
    atmos_state,
    atmos_kappa,
    ocean_tracers,
    ocean_flow,
    ocean_kappa,
    sea_mask,
    xgrid_atmos_cell,
    xgrid_ocean_cell,
    xgrid_weights,
):
    slots = xgrid_atmos_cell.shape[2]
    position = lax.axis_index("face") * lax.axis_size("gy") + lax.axis_index("gy")
    flags = jnp.stack([position == 0, position == sizes()[0] - 1]).astype(jnp.int32)
    level = (1, RW, CL)

    message = shape(VALS + 3 * LINES, CL)
    for_up, mine, for_down = call(
        spread_kernel,
        (message,) * 3,
        (ocean_tracers, ocean_flow, xgrid_ocean_cell),
        blocks={0: (1, *level), 1: (2, *level)},
        mib=60,
    )
    up, down = to_north(for_up), to_south(for_down)

    tracers2 = ocean_tracers.reshape(-1, CL)
    flow2 = ocean_flow.reshape(-1, CL)
    kappa2 = ocean_kappa.reshape(-1, CL)
    edge = shape(HALO, 5 * LV, CL)
    top, bottom = call(edge_kernel, (edge, edge), (tracers2, flow2, kappa2, sea_mask), mib=EDGE_MIB)
    up, down, top, bottom = lax.optimization_barrier((up, down, top, bottom))
    south, north, fold = to_north(top), to_south(bottom), across_fold(top)

    relay = shape(3 * (VALS + LINES), CL)
    for_east, for_west = call(relay_kernel, (relay,) * 2, (up, mine, down))
    west_in, east_in = to_east(for_east), to_west(for_west)

    xo, mw, me = call(
        own_kernel,
        (shape(4, RW // 2, CL, CL),) + (shape(4, RW // 2 * HALO, CL),) * 2,
        (tracers2, flow2, kappa2, sea_mask),
        flops=10_000_000,
        mib=OWN_MIB,
    )
    wo, eo = to_east(me), to_west(mw)

    run = shape(4, 3, slots)
    atmos_flux, pay_n, pay_o, pay_s = call(
        flux_kernel,
        (shape(4, RW, CL), run, run, run),
        (
            atmos_state,
            up,
            mine,
            down,
            west_in,
            east_in,
            xgrid_atmos_cell,
            xgrid_ocean_cell,
            xgrid_weights,
        ),
        scratch=[pltpu.VMEM((9, 16, slots), F32), pltpu.VMEM((9, VALS, CL), F32)],
        flops=20_000_000,
        blocks={0: (4, *level)},
    )
    pay_up, pay_down = to_north(pay_n), to_south(pay_s)
    pays = (pay_up, pay_o, pay_down)
    pay_west = to_east(jnp.concatenate([p[:, 2:3] for p in pays], axis=1))
    pay_east = to_west(jnp.concatenate([p[:, 0:1] for p in pays], axis=1))
    atmos_next = atmosphere(atmos_state, atmos_kappa, atmos_flux)

    xh, mw, me = call(
        halo_kernel,
        (shape(4, HALO, CL, CL),) + (shape(4, HALO * HALO, CL),) * 2,
        (bottom, south, north, fold, flags),
        flops=10_000_000,
        mib=OWN_MIB,
    )
    wh, eh = to_east(me), to_west(mw)

    ocean_stress, fields = call(
        ocean_flux_kernel,
        (shape(2, RW, CL), shape(7, RW, CL)),
        (
            up, mine, down, west_in, east_in, pay_up, pay_o, pay_down, pay_west, pay_east,
            sea_mask, ocean_tracers, ocean_flow, ocean_kappa,
        ),
        scratch=[pltpu.VMEM((16, slots), jnp.int32), pltpu.VMEM((4, 16, slots), F32)],
        flops=8_000_000,
        blocks={11: (2, *level), 12: (2, *level), 13: level},
    )

    buffers = [pltpu.VMEM((NI, WIDTH, CL), F32)] * 6
    pair = shape(HALO // 2 * CL + 7 * DEEP, CL)
    state, top, bottom = call(
        functools.partial(deep_kernel, False),
        (shape(RW // 2, CL, CL), pair, pair),
        (xh, xo, wh, wo, eh, eo, fields),
        scratch=buffers,
        flops=60_000_000,
        mib=DEEP_MIB,
    )
    south, north, fold = to_north(top), to_south(bottom), across_fold(top)

    side = shape(NI * HALO + 7 * SR // 2, CL)
    xts, mw, me, joined = call(
        join_kernel,
        (shape(NI, CL, CL), side, side, shape(7, SR, CL)),
        (state, fields, south, north, fold, flags),
    )
    wide = pltpu.VMEM((SR, 2 * CL), F32)
    ocean_next = call(
        functools.partial(deep_kernel, True),
        shape(2 * LV * RW, CL),
        (xh, xo, wh, wo, eh, eo, xts, joined, to_east(me), to_west(mw)),
        scratch=buffers + [wide] * 4 + [pltpu.VMEM((2, SR, 2 * CL), F32)],
        flops=80_000_000,
        mib=DEEP_MIB,
    )
    return (atmos_next, ocean_next.reshape(ocean_tracers.shape), ocean_stress)


def solution(mesh):
    placed = (
        P(None, None, ("face", "gy"), "gx"),
        P(("face", "gy"), "gx"),
        P(None, None, ("face", "gy"), "gx"),
        P(None, None, ("face", "gy"), "gx"),
        P(None, ("face", "gy"), "gx"),
        P(("face", "gy"), "gx"),
        P(("face", "gy"), "gx", None),
        P(("face", "gy"), "gx", None),
        P(None, ("face", "gy"), "gx", None),
    )
    return jax.shard_map(
        local,
        mesh=mesh,
        in_specs=placed,
        out_specs=(
            P(None, None, ("face", "gy"), "gx"),
            P(None, None, ("face", "gy"), "gx"),
            P(None, ("face", "gy"), "gx"),
        ),
        check_vma=False,
    )
```

time: 212 us -> 155 us (0.73)
  Pallas kernels: 84.1 us -> 59.7 us
  local copies, waits for them, and re-layouts: 17.6 us -> 0.18 us
  starting transfers between devices: 56.7 us -> 45.8 us
  other arithmetic: 5.85 us -> 0.18 us
    pallas_call x9 -> x10, Pallas kernels: 79.7 us -> 57 us  [call(): pl.pallas_call(kernel, grid=(1,) if blocks else (), out_shape=outs, in_sp...]
    ppermute x5 -> x4, starting transfers between devices: 25.6 us -> 16.4 us  [to_north(): return lax.ppermute(value, AXES, pairs)]
    unnamed x41 -> x23, local copies, waits for them, and re-layouts: 7.76 us -> 0.1 us
    ppermute x5 -> x4, waiting for transfers between devices: 11.5 us -> 4.92 us  [to_south(): return lax.ppermute(value, AXES, pairs)]
    ppermute x5, starting transfers between devices: 13.4 us -> 7.14 us  [to_west(): return lax.ppermute(value, 'gx', [(x, (x - 1) % nx) for x in range(nx)])]
    reshape x4 -> x0, local copies, waits for them, and re-layouts: 4.44 us -> none  [the longest x1 1.57 us: local(): xgrid_weights.reshape(2, 9, slots)]
    ppermute x5 -> x4, waiting for transfers between devices: 28.7 us -> 32.3 us  [to_north(): return lax.ppermute(value, AXES, pairs)]
    ppermute x5, waiting for transfers between devices: 5.28 us -> 7.86 us  [to_east(): return lax.ppermute(value, 'gx', [(x, (x + 1) % nx) for x in range(nx)])]
  transfers between devices with their start and end apart: 23 -> 20, of which waited for: 6 -> 8; matrix products, arithmetic and copies ran while one was open for 7% -> 0% of each run, Pallas kernels for 20% -> 18%
where the time goes in v2:
time: 155 us; the launch traced here: 154 us
  Pallas kernels  59.7 us (39%)
  waiting for transfers between devices  47 us (30%)
  starting transfers between devices  45.8 us (30%)
    pallas_call x10, Pallas kernels, call(): pl.pallas_call(kernel, grid=(1,) if blocks else (), out_shape=outs, in_sp...  57 us
    ppermute x4, waiting for transfers between devices, to_north(): return lax.ppermute(value, AXES, pairs)  32.3 us
    ppermute x4, starting transfers between devices, to_south(): return lax.ppermute(value, AXES, pairs)  18.1 us
    ppermute x4, starting transfers between devices, to_north(): return lax.ppermute(value, AXES, pairs)  16.4 us
    ppermute x5, waiting for transfers between devices, to_east(): return lax.ppermute(value, 'gx', [(x, (x + 1) % nx) for x in range(nx)])  7.86 us
    ppermute x5, starting transfers between devices, to_west(): return lax.ppermute(value, 'gx', [(x, (x - 1) % nx) for x in range(nx)])  7.14 us
    ppermute x4, waiting for transfers between devices, to_south(): return lax.ppermute(value, AXES, pairs)  4.92 us
  transfers between devices with their start and end apart: 20, of which 8 were waited for; matrix products, arithmetic and copies ran while one was open for 0% of the time, Pallas kernels for 18%

profile of v2, /device:TPU:4, one launch (start us, length us, event | category | flops | bytes accessed | tf_op | source)
XLA Modules:
  0.0 153.8 jit_solution(8965592309568495405)
XLA Ops:
  0.6 0.0 copy-start
  0.6 0.0 copy-start.1
  0.7 0.0 copy-start.3
  0.7 0.0 copy-start.7
  0.7 0.0 copy-start.10
  0.7 1.7 %shard_map.112 = (f32[120,128]{1,0:T(8,128)}, f32[120,128]{1,0:T(8,128)}, f32[120,128]{1,0:T(8,128)}) custom-call(f32[2,32,32,128]{3,2,1,0:T(8,128)} %tracers.3, f32[2,32,32,128]{3,2,1,0:T(8,128)} %flow.3, s32[3,3,1024]{2,1,0:T(4,128)} %sea_cells.1), custom_call_target="tpu_custom_call" | custom-call | flops 1000000 | bytes 1000000 | tf_op jit(solution)/shard_map/pallas_call | solution.py:44
  2.4 5.9 %collective-permute-start = (f32[120,128]{1,0:T(8,128)}, f32[120,128]{1,0:T(8,128)S(1)}, u32[]{:S(2)}, u32[]{:S(2)}) collective-permute-start(f32[120,128]{1,0:T(8,128)} %get-tuple-element.33), channel_id=1, source_target_pairs={{0,1},{8,9},{16,17},{24,25},{32,33},{40,41},{48,49},{56,57},{1,2},... | collective-permute-start | bytes 184328 | tf_op jit(solution)/shard_map/ppermute | solution.py:72
  8.3 2.5 %collective-permute-start.1 = (f32[120,128]{1,0:T(8,128)}, f32[120,128]{1,0:T(8,128)S(1)}, u32[]{:S(2)}, u32[]{:S(2)}) collective-permute-start(f32[120,128]{1,0:T(8,128)} %get-tuple-element.34), channel_id=1, source_target_pairs={{1,0},{9,8},{17,16},{25,24},{33,32},{41,40},{49,48},{57,56},{2,1},... | collective-permute-start | bytes 184328 | tf_op jit(solution)/shard_map/ppermute | solution.py:78
  10.8 5.0 %shard_map.113 = (f32[12,160,128]{2,1,0:T(8,128)}, f32[12,160,128]{2,1,0:T(8,128)}) custom-call(f32[2048,128]{1,0:T(8,128)} %bitcast.6, f32[2048,128]{1,0:T(8,128)} %bitcast.8, f32[1024,128]{1,0:T(8,128)} %bitcast.10, s32[32,128]{1,0:T(8,128)} %mask.5), custom_call_target="tpu_custom_call" | custom-call | flops 1000000 | bytes 1000000 | tf_op jit(solution)/shard_map/pallas_call | solution.py:44
  15.8 0.0 collective-permute-done.up
  15.8 0.3 collective-permute-done.1.down
  16.1 4.7 %collective-permute-start.4 = (f32[12,160,128]{2,1,0:T(8,128)}, f32[12,160,128]{2,1,0:T(8,128)}, u32[]{:S(2)}, u32[]{:S(2)}) collective-permute-start(f32[12,160,128]{2,1,0:T(8,128)} %get-tuple-element.44), channel_id=1, source_target_pairs={{0,1},{8,9},{16,17},{24,25},{32,33},{40,41},{48,49},{56,57},{1,2},... | collective-permute-start | bytes 2949128 | tf_op jit(solution)/shard_map/ppermute | solution.py:72
  20.9 3.5 %collective-permute-start.5 = (f32[12,160,128]{2,1,0:T(8,128)}, f32[12,160,128]{2,1,0:T(8,128)}, u32[]{:S(2)}, u32[]{:S(2)}) collective-permute-start(f32[12,160,128]{2,1,0:T(8,128)} %get-tuple-element.43.own), channel_id=1, source_target_pairs={{1,0},{9,8},{17,16},{25,24},{33,32},{41,40},{49,48},{57,56},{2,1},... | collective-permute-start | bytes 2949128 | tf_op jit(solution)/shard_map/ppermute | solution.py:78
  24.4 1.6 %collective-permute-start.6 = (f32[12,160,128]{2,1,0:T(8,128)}, f32[12,160,128]{2,1,0:T(8,128)}, u32[]{:S(2)}, u32[]{:S(2)}) collective-permute-start(f32[12,160,128]{2,1,0:T(8,128)} %get-tuple-element.44), channel_id=1, source_target_pairs={{71,127},{79,119},{87,111},{95,103},{103,95},{111,87},{119,79},{12... | collective-permute-start | bytes 2949128 | tf_op jit(solution)/shard_map/ppermute | solution.py:84
  26.0 0.0 copy-done.5
  26.0 0.7 shard_map.114
  26.7 0.0 collective-permute-start.2
  26.7 3.0 %collective-permute-start.3 = (f32[312,128]{1,0:T(8,128)S(1)}, f32[312,128]{1,0:T(8,128)S(1)}, u32[]{:S(2)}, u32[]{:S(2)}) collective-permute-start(f32[312,128]{1,0:T(8,128)S(1)} %get-tuple-element.41), channel_id=1, source_target_pairs={{0,56},{8,0},{16,8},{24,16},{32,24},{40,32},{48,40},{56,48},{1,57}... | collective-permute-start | bytes 479240 | tf_op jit(solution)/shard_map/ppermute | solution.py:94
  29.7 0.0 copy-done.10
  29.7 0.0 copy-done
  29.7 0.0 copy-done.1
  29.8 0.0 copy-start.2
  29.8 2.7 %shard_map.118 = (f32[4,16,128,128]{3,2,1,0:T(8,128)S(1)}, f32[4,192,128]{2,1,0:T(8,128)S(1)}, f32[4,192,128]{2,1,0:T(8,128)S(1)}) custom-call(f32[2048,128]{1,0:T(8,128)S(1)} %bitcast.7, f32[2048,128]{1,0:T(8,128)S(1)} %bitcast.9, f32[1024,128]{1,0:T(8,128)S(1)} %bitcast.11, s32[32,128]{1,0:T(8,128)S(1)} %copy-done.7), custom_call_target="tpu_custom_call" | custom-call | flops 10000000 | bytes 1000000 | tf_op jit(solution)/shard_map/pallas_call | solution.py:44
  32.5 0.0 copy-start.4
  32.5 0.1 add_convert_fusion.flags
  32.6 0.3 collective-permute-done.2.west
  32.8 0.0 collective-permute-start.10
  32.8 0.0 collective-permute-done.3.east
  32.9 9.3 %shard_map.115 = (f32[4,32,128]{2,1,0:T(8,128)S(1)}, f32[4,3,1024]{2,1,0:T(4,128)S(1)}, f32[4,3,1024]{2,1,0:T(4,128)S(1)}, f32[4,3,1024]{2,1,0:T(4,128)S(1)}) custom-call(f32[4,32,32,128]{3,2,1,0:T(8,128)S(1)} %copy-done.2, f32[120,128]{1,0:T(8,128)S(1)} %collective-permute-done.up, f32[120,128]{1,0:T(8,128)S(1)} %copy-done.5, ...), custom_call_target="tpu_custom_call" | custom-call | flops 20000000 | bytes 1000000 | tf_op jit(solution)/shard_map/pallas_call | solution.py:44
  42.2 3.8 %collective-permute-start.11 = (f32[4,3,1024]{2,1,0:T(4,128)S(1)}, f32[4,3,1024]{2,1,0:T(4,128)S(1)}, u32[]{:S(2)}, u32[]{:S(2)}) collective-permute-start(f32[4,3,1024]{2,1,0:T(4,128)S(1)} %get-tuple-element.51), channel_id=1, source_target_pairs={{0,1},{8,9},{16,17},{24,25},{32,33},{40,41},{48,49},{56,57},{1,2},... | collective-permute-start | bytes 147464 | tf_op jit(solution)/shard_map/ppermute | solution.py:72
  46.1 17.9 %collective-permute-done.11.pay_up = f32[4,3,1024]{2,1,0:T(4,128)S(1)} collective-permute-done((f32[4,3,1024]{2,1,0:T(4,128)S(1)}, f32[4,3,1024]{2,1,0:T(4,128)S(1)}, u32[]{:S(2)}, u32[]{:S(2)}) %collective-permute-start.11) | collective-permute-done | bytes 49184 | tf_op jit(solution)/shard_map/ppermute | solution.py:72
  64.0 5.9 %collective-permute-start.12 = (f32[4,3,1024]{2,1,0:T(4,128)S(1)}, f32[4,3,1024]{2,1,0:T(4,128)S(1)}, u32[]{:S(2)}, u32[]{:S(2)}) collective-permute-start(f32[4,3,1024]{2,1,0:T(4,128)S(1)} %get-tuple-element.53), channel_id=1, source_target_pairs={{1,0},{9,8},{17,16},{25,24},{33,32},{41,40},{49,48},{57,56},{2,1},... | collective-permute-start | bytes 147464 | tf_op jit(solution)/shard_map/ppermute | solution.py:78
  69.9 0.0 collective-permute-done.4.south
  69.9 0.0 collective-permute-start.8
  69.9 0.0 collective-permute-done.5.north
  69.9 0.0 collective-permute-done.6.fold
  69.9 3.5 %shard_map.117 = (f32[4,12,128,128]{3,2,1,0:T(8,128)S(1)}, f32[4,144,128]{2,1,0:T(8,128)S(1)}, f32[4,144,128]{2,1,0:T(8,128)S(1)}) custom-call(f32[12,160,128]{2,1,0:T(8,128)S(1)} %copy-done.4, f32[12,160,128]{2,1,0:T(8,128)} %collective-permute-done.4.south, f32[12,160,128]{2,1,0:T(8,128)} %collective-permute-done.5.north, ...), custom_call_target="tpu_custom_call" | custom-call | flops 10000000 | bytes 1000000 | tf_op jit(solution)/shard_map/pallas_call | solution.py:44
  73.4 1.7 %collective-permute-start.7 = (f32[4,144,128]{2,1,0:T(8,128)S(1)}, f32[4,144,128]{2,1,0:T(8,128)S(1)}, u32[]{:S(2)}, u32[]{:S(2)}) collective-permute-start(f32[4,144,128]{2,1,0:T(8,128)S(1)} %get-tuple-element.47), channel_id=1, source_target_pairs={{0,8},{8,16},{16,24},{24,32},{32,40},{40,48},{48,56},{56,0},{1,9},... | collective-permute-start | bytes 884744 | tf_op jit(solution)/shard_map/ppermute | solution.py:89
  75.1 1.3 collective-permute-start.9
  76.4 0.0 collective-permute-done.12.pay_down
  76.5 0.0 collective-permute-start.13
  76.5 5.6 %collective-permute-done.13.pay_west = f32[4,3,1024]{2,1,0:T(4,128)S(1)} collective-permute-done((f32[4,3,1024]{2,1,0:T(4,128)S(1)}, f32[4,3,1024]{2,1,0:T(4,128)S(1)}, u32[]{:S(2)}, u32[]{:S(2)}) %collective-permute-start.13) | collective-permute-done | bytes 49184 | tf_op jit(solution)/shard_map/ppermute | solution.py:89
  82.2 0.0 collective-permute-start.14
  82.2 1.9 %collective-permute-done.14.pay_east = f32[4,3,1024]{2,1,0:T(4,128)S(1)} collective-permute-done((f32[4,3,1024]{2,1,0:T(4,128)S(1)}, f32[4,3,1024]{2,1,0:T(4,128)S(1)}, u32[]{:S(2)}, u32[]{:S(2)}) %collective-permute-start.14) | collective-permute-done | bytes 49184 | tf_op jit(solution)/shard_map/ppermute | solution.py:94
  84.1 4.2 %shard_map.119 = (f32[2,32,128]{2,1,0:T(8,128)}, f32[7,32,128]{2,1,0:T(8,128)S(1)}) custom-call(f32[120,128]{1,0:T(8,128)S(1)} %collective-permute-done.up, f32[120,128]{1,0:T(8,128)S(1)} %copy-done.5, f32[120,128]{1,0:T(8,128)S(1)} %collective-permute-done.1.down, f32[312,128]{1,0:T(8,128)S(1)} %collective-permute-done.2.west, ...), custom_call_target="tpu_custom_call" | custom-call | flops 8000000 | bytes 1000000 | tf_op jit(solution)/shard_map/pallas_call | solution.py:44
  88.3 0.0 collective-permute-done.10.refs_5_
  88.3 0.0 collective-permute-done.8.refs_3_
  88.3 0.0 collective-permute-done.7.refs_2_
  88.3 0.0 collective-permute-done.9.refs_4_
  88.3 10.7 %shard_map.120 = (f32[16,128,128]{2,1,0:T(8,128)S(1)}, f32[936,128]{1,0:T(8,128)S(1)}, f32[936,128]{1,0:T(8,128)S(1)}) custom-call(f32[4,12,128,128]{3,2,1,0:T(8,128)S(1)} %get-tuple-element.45.refs_0_, f32[4,16,128,128]{3,2,1,0:T(8,128)S(1)} %get-tuple-element.46.refs_1_, f32[4,144,128]{2,1,0:T(8,128)S(1)} %collective-permute-done.7.refs_2_, ...), custom_call_target="tpu_custom_call" | custom-call | flops 60000000 | bytes 1000000 | tf_op jit(solution)/shard_map/pallas_call | solution.py:44
  99.0 0.0 copy-start.9
  99.1 2.0 %collective-permute-start.15 = (f32[936,128]{1,0:T(8,128)S(1)}, f32[936,128]{1,0:T(8,128)S(1)}, u32[]{:S(2)}, u32[]{:S(2)}) collective-permute-start(f32[936,128]{1,0:T(8,128)S(1)} %get-tuple-element.56), channel_id=1, source_target_pairs={{0,1},{8,9},{16,17},{24,25},{32,33},{40,41},{48,49},{56,57},{1,2},... | collective-permute-start | bytes 1437704 | tf_op jit(solution)/shard_map/ppermute | solution.py:72
  101.0 6.3 %collective-permute-start.16 = (f32[936,128]{1,0:T(8,128)S(1)}, f32[936,128]{1,0:T(8,128)S(1)}, u32[]{:S(2)}, u32[]{:S(2)}) collective-permute-start(f32[936,128]{1,0:T(8,128)S(1)} %get-tuple-element.57), channel_id=1, source_target_pairs={{1,0},{9,8},{17,16},{25,24},{33,32},{41,40},{49,48},{57,56},{2,1},... | collective-permute-start | bytes 1437704 | tf_op jit(solution)/shard_map/ppermute | solution.py:78
  107.3 0.7 collective-permute-start.17
  108.0 14.4 %collective-permute-done.15.south = f32[936,128]{1,0:T(8,128)S(1)} collective-permute-done((f32[936,128]{1,0:T(8,128)S(1)}, f32[936,128]{1,0:T(8,128)S(1)}, u32[]{:S(2)}, u32[]{:S(2)}) %collective-permute-start.15) | collective-permute-done | bytes 479264 | tf_op jit(solution)/shard_map/ppermute | solution.py:72
  122.4 4.6 %collective-permute-done.16.north = f32[936,128]{1,0:T(8,128)S(1)} collective-permute-done((f32[936,128]{1,0:T(8,128)S(1)}, f32[936,128]{1,0:T(8,128)S(1)}, u32[]{:S(2)}, u32[]{:S(2)}) %collective-permute-start.16) | collective-permute-done | bytes 479264 | tf_op jit(solution)/shard_map/ppermute | solution.py:78
  127.0 0.0 collective-permute-done.17.fold
  127.0 1.3 shard_map.121
  128.3 0.1 collective-permute-start.18
  128.4 2.9 %collective-permute-start.19 = (f32[616,128]{1,0:T(8,128)S(1)}, f32[616,128]{1,0:T(8,128)S(1)}, u32[]{:S(2)}, u32[]{:S(2)}) collective-permute-start(f32[616,128]{1,0:T(8,128)S(1)} %get-tuple-element.61), channel_id=1, source_target_pairs={{0,56},{8,0},{16,8},{24,16},{32,24},{40,32},{48,40},{56,48},{1,57}... | collective-permute-start | bytes 946184 | tf_op jit(solution)/shard_map/ppermute | solution.py:94
  131.3 2.6 %shard_map.116 = f32[4,32,32,128]{3,2,1,0:T(8,128)} custom-call(f32[4,32,32,128]{3,2,1,0:T(8,128)S(1)} %copy-done.2, f32[32,128]{1,0:T(8,128)S(1)} %copy-done.9, f32[4,32,128]{2,1,0:T(8,128)S(1)} %get-tuple-element.42.flux), custom_call_target="tpu_custom_call" | custom-call | flops 5000000 | bytes 4200000 | tf_op jit(solution)/shard_map/pallas_call | solution.py:588
  134.0 2.0 %collective-permute-done.18.refs_8_ = f32[616,128]{1,0:T(8,128)S(1)} collective-permute-done((f32[616,128]{1,0:T(8,128)S(1)}, f32[616,128]{1,0:T(8,128)S(1)}, u32[]{:S(2)}, u32[]{:S(2)}) %collective-permute-start.18) | collective-permute-done | bytes 315424 | tf_op jit(solution)/shard_map/ppermute | solution.py:89
  135.9 0.0 collective-permute-done.19.refs_9_
  135.9 17.8 %shard_map.122 = f32[2048,128]{1,0:T(8,128)} custom-call(f32[4,12,128,128]{3,2,1,0:T(8,128)S(1)} %get-tuple-element.45.refs_0_, f32[4,16,128,128]{3,2,1,0:T(8,128)S(1)} %get-tuple-element.46.refs_1_, f32[4,144,128]{2,1,0:T(8,128)S(1)} %collective-permute-done.7.refs_2_, f32[4,192,128]{2,1,0:T(8,128)S(1)} %collective-permute-done.8.refs_3_, ...), custom_call_target="tpu_custom_call" | custom-call | flops 80000000 | bytes 1000000 | tf_op jit(solution)/shard_map/pallas_call | solution.py:44
  (16 shorter events, 0.2 us)
Async XLA Ops:
  0.6 29.1 %copy-start = (f32[2,32,32,128]{3,2,1,0:T(8,128)S(1)}, f32[2,32,32,128]{3,2,1,0:T(8,128)}, u32[]{:S(2)}) copy-start(f32[2,32,32,128]{3,2,1,0:T(8,128)} %tracers.3) | copy-start | bytes 3145732
  0.6 29.1 %copy-start.1 = (f32[2,32,32,128]{3,2,1,0:T(8,128)S(1)}, f32[2,32,32,128]{3,2,1,0:T(8,128)}, u32[]{:S(2)}) copy-start(f32[2,32,32,128]{3,2,1,0:T(8,128)} %flow.3) | copy-start | bytes 3145732
  0.7 29.1 %copy-start.3 = (f32[32,32,128]{2,1,0:T(8,128)S(1)}, f32[32,32,128]{2,1,0:T(8,128)}, u32[]{:S(2)}) copy-start(f32[32,32,128]{2,1,0:T(8,128)} %kappa.3) | copy-start | bytes 1572868
  0.7 29.1 %copy-start.7 = (s32[32,128]{1,0:T(8,128)S(1)}, s32[32,128]{1,0:T(8,128)}, u32[]{:S(2)}) copy-start(s32[32,128]{1,0:T(8,128)} %mask.5) | copy-start | bytes 49156
  0.7 29.0 %copy-start.10 = (f32[2,3,3,1024]{3,0,2,1:T(2,128)S(1)}, f32[2,3,3,1024]{3,0,2,1:T(2,128)}, u32[]{:S(2)}) copy-start(f32[2,3,3,1024]{3,0,2,1:T(2,128)} %param.17) | copy-start | bytes 221188
  2.4 23.6 %copy-start.5 = (f32[120,128]{1,0:T(8,128)S(1)}, f32[120,128]{1,0:T(8,128)}, u32[]{:S(2)}) copy-start(f32[120,128]{1,0:T(8,128)} %get-tuple-element.38.mine) | copy-start | bytes 184324
  2.4 13.4 %collective-permute-start = (f32[120,128]{1,0:T(8,128)}, f32[120,128]{1,0:T(8,128)S(1)}, u32[]{:S(2)}, u32[]{:S(2)}) collective-permute-start(f32[120,128]{1,0:T(8,128)} %get-tuple-element.33), channel_id=1, source_target_pairs={{0,1},{8,9},{16,17},{24,25},{32,33},{40,41},{48,49},{56,57},{1,2},... | collective-permute-start | bytes 184328 | tf_op jit(solution)/shard_map/ppermute | solution.py:72
  8.3 7.8 %collective-permute-start.1 = (f32[120,128]{1,0:T(8,128)}, f32[120,128]{1,0:T(8,128)S(1)}, u32[]{:S(2)}, u32[]{:S(2)}) collective-permute-start(f32[120,128]{1,0:T(8,128)} %get-tuple-element.34), channel_id=1, source_target_pairs={{1,0},{9,8},{17,16},{25,24},{33,32},{41,40},{49,48},{57,56},{2,1},... | collective-permute-start | bytes 184328 | tf_op jit(solution)/shard_map/ppermute | solution.py:78
  15.8 17.0 %copy-start.6 = (s32[3,3,1024]{2,1,0:T(4,128)S(1)}, s32[3,3,1024]{2,1,0:T(4,128)}, u32[]{:S(2)}) copy-start(s32[3,3,1024]{2,1,0:T(4,128)} %sea_cells.1) | copy-start | bytes 110596
  15.8 17.0 %copy-start.8 = (s32[3,3,1024]{2,1,0:T(4,128)S(1)}, s32[3,3,1024]{2,1,0:T(4,128)}, u32[]{:S(2)}) copy-start(s32[3,3,1024]{2,1,0:T(4,128)} %air_cells.1) | copy-start | bytes 110596
  16.1 53.7 %collective-permute-start.4 = (f32[12,160,128]{2,1,0:T(8,128)}, f32[12,160,128]{2,1,0:T(8,128)}, u32[]{:S(2)}, u32[]{:S(2)}) collective-permute-start(f32[12,160,128]{2,1,0:T(8,128)} %get-tuple-element.44), channel_id=1, source_target_pairs={{0,1},{8,9},{16,17},{24,25},{32,33},{40,41},{48,49},{56,57},{1,2},... | collective-permute-start | bytes 2949128 | tf_op jit(solution)/shard_map/ppermute | solution.py:72
  20.9 49.0 %collective-permute-start.5 = (f32[12,160,128]{2,1,0:T(8,128)}, f32[12,160,128]{2,1,0:T(8,128)}, u32[]{:S(2)}, u32[]{:S(2)}) collective-permute-start(f32[12,160,128]{2,1,0:T(8,128)} %get-tuple-element.43.own), channel_id=1, source_target_pairs={{1,0},{9,8},{17,16},{25,24},{33,32},{41,40},{49,48},{57,56},{2,1},... | collective-permute-start | bytes 2949128 | tf_op jit(solution)/shard_map/ppermute | solution.py:78
  24.4 45.5 %collective-permute-start.6 = (f32[12,160,128]{2,1,0:T(8,128)}, f32[12,160,128]{2,1,0:T(8,128)}, u32[]{:S(2)}, u32[]{:S(2)}) collective-permute-start(f32[12,160,128]{2,1,0:T(8,128)} %get-tuple-element.44), channel_id=1, source_target_pairs={{71,127},{79,119},{87,111},{95,103},{103,95},{111,87},{119,79},{12... | collective-permute-start | bytes 2949128 | tf_op jit(solution)/shard_map/ppermute | solution.py:84
  26.7 6.1 %collective-permute-start.2 = (f32[312,128]{1,0:T(8,128)}, f32[312,128]{1,0:T(8,128)S(1)}, u32[]{:S(2)}, u32[]{:S(2)}) collective-permute-start(f32[312,128]{1,0:T(8,128)} %get-tuple-element.40), channel_id=1, source_target_pairs={{0,8},{8,16},{16,24},{24,32},{32,40},{40,48},{48,56},{56,0},{1,9},... | collective-permute-start | bytes 479240 | tf_op jit(solution)/shard_map/ppermute | solution.py:89
  26.7 6.1 %collective-permute-start.3 = (f32[312,128]{1,0:T(8,128)S(1)}, f32[312,128]{1,0:T(8,128)S(1)}, u32[]{:S(2)}, u32[]{:S(2)}) collective-permute-start(f32[312,128]{1,0:T(8,128)S(1)} %get-tuple-element.41), channel_id=1, source_target_pairs={{0,56},{8,0},{16,8},{24,16},{32,24},{40,32},{48,40},{56,48},{1,57}... | collective-permute-start | bytes 479240 | tf_op jit(solution)/shard_map/ppermute | solution.py:94
  29.8 3.1 %copy-start.2 = (f32[4,32,32,128]{3,2,1,0:T(8,128)S(1)}, f32[4,32,32,128]{3,2,1,0:T(8,128)}, u32[]{:S(2)}) copy-start(f32[4,32,32,128]{3,2,1,0:T(8,128)} %state.1) | copy-start | bytes 6291460
  32.5 37.5 %copy-start.4 = (f32[12,160,128]{2,1,0:T(8,128)S(1)}, f32[12,160,128]{2,1,0:T(8,128)}, u32[]{:S(2)}) copy-start(f32[12,160,128]{2,1,0:T(8,128)} %get-tuple-element.43.own) | copy-start | bytes 2949124
  32.8 55.5 %collective-permute-start.10 = (f32[4,192,128]{2,1,0:T(8,128)S(1)}, f32[4,192,128]{2,1,0:T(8,128)S(1)}, u32[]{:S(2)}, u32[]{:S(2)}) collective-permute-start(f32[4,192,128]{2,1,0:T(8,128)S(1)} %get-tuple-element.50), channel_id=1, source_target_pairs={{0,56},{8,0},{16,8},{24,16},{32,24},{40,32},{48,40},{56,48},{1,57}... | collective-permute-start | bytes 1179656 | tf_op jit(solution)/shard_map/ppermute | solution.py:94
  42.2 21.7 %collective-permute-start.11 = (f32[4,3,1024]{2,1,0:T(4,128)S(1)}, f32[4,3,1024]{2,1,0:T(4,128)S(1)}, u32[]{:S(2)}, u32[]{:S(2)}) collective-permute-start(f32[4,3,1024]{2,1,0:T(4,128)S(1)} %get-tuple-element.51), channel_id=1, source_target_pairs={{0,1},{8,9},{16,17},{24,25},{32,33},{40,41},{48,49},{56,57},{1,2},... | collective-permute-start | bytes 147464 | tf_op jit(solution)/shard_map/ppermute | solution.py:72
  64.0 12.4 %collective-permute-start.12 = (f32[4,3,1024]{2,1,0:T(4,128)S(1)}, f32[4,3,1024]{2,1,0:T(4,128)S(1)}, u32[]{:S(2)}, u32[]{:S(2)}) collective-permute-start(f32[4,3,1024]{2,1,0:T(4,128)S(1)} %get-tuple-element.53), channel_id=1, source_target_pairs={{1,0},{9,8},{17,16},{25,24},{33,32},{41,40},{49,48},{57,56},{2,1},... | collective-permute-start | bytes 147464 | tf_op jit(solution)/shard_map/ppermute | solution.py:78
  69.9 18.5 %collective-permute-start.8 = (f32[4,192,128]{2,1,0:T(8,128)S(1)}, f32[4,192,128]{2,1,0:T(8,128)S(1)}, u32[]{:S(2)}, u32[]{:S(2)}) collective-permute-start(f32[4,192,128]{2,1,0:T(8,128)S(1)} %get-tuple-element.48), channel_id=1, source_target_pairs={{0,8},{8,16},{16,24},{24,32},{32,40},{40,48},{48,56},{56,0},{1,9},... | collective-permute-start | bytes 1179656 | tf_op jit(solution)/shard_map/ppermute | solution.py:89
  73.4 14.9 %collective-permute-start.7 = (f32[4,144,128]{2,1,0:T(8,128)S(1)}, f32[4,144,128]{2,1,0:T(8,128)S(1)}, u32[]{:S(2)}, u32[]{:S(2)}) collective-permute-start(f32[4,144,128]{2,1,0:T(8,128)S(1)} %get-tuple-element.47), channel_id=1, source_target_pairs={{0,8},{8,16},{16,24},{24,32},{32,40},{40,48},{48,56},{56,0},{1,9},... | collective-permute-start | bytes 884744 | tf_op jit(solution)/shard_map/ppermute | solution.py:89
  75.1 13.3 %collective-permute-start.9 = (f32[4,144,128]{2,1,0:T(8,128)S(1)}, f32[4,144,128]{2,1,0:T(8,128)S(1)}, u32[]{:S(2)}, u32[]{:S(2)}) collective-permute-start(f32[4,144,128]{2,1,0:T(8,128)S(1)} %get-tuple-element.49), channel_id=1, source_target_pairs={{0,56},{8,0},{16,8},{24,16},{32,24},{40,32},{48,40},{56,48},{1,57}... | collective-permute-start | bytes 884744 | tf_op jit(solution)/shard_map/ppermute | solution.py:94
  76.5 5.7 %collective-permute-start.13 = (f32[4,3,1024]{2,1,0:T(4,128)S(1)}, f32[4,3,1024]{2,1,0:T(4,128)S(1)}, u32[]{:S(2)}, u32[]{:S(2)}) collective-permute-start(f32[4,3,1024]{2,1,0:T(4,128)S(1)} %pad_maximum_fusion), channel_id=1, source_target_pairs={{0,8},{8,16},{16,24},{24,32},{32,40},{40,48},{48,56},{56,0},{1,9},... | collective-permute-start | bytes 147464 | tf_op jit(solution)/shard_map/ppermute | solution.py:89
  82.2 1.9 %collective-permute-start.14 = (f32[4,3,1024]{2,1,0:T(4,128)S(1)}, f32[4,3,1024]{2,1,0:T(4,128)S(1)}, u32[]{:S(2)}, u32[]{:S(2)}) collective-permute-start(f32[4,3,1024]{2,1,0:T(4,128)S(1)} %pad_maximum_fusion.1), channel_id=1, source_target_pairs={{0,56},{8,0},{16,8},{24,16},{32,24},{40,32},{48,40},{56,48},{1,57}... | collective-permute-start | bytes 147464 | tf_op jit(solution)/shard_map/ppermute | solution.py:94
  99.0 32.3 %copy-start.9 = (f32[32,128]{1,0:T(8,128)S(1)}, f32[32,128]{1,0:T(8,128)}, u32[]{:S(2)}) copy-start(f32[32,128]{1,0:T(8,128)} %kappa.2) | copy-start | bytes 49156
  99.1 23.4 %collective-permute-start.15 = (f32[936,128]{1,0:T(8,128)S(1)}, f32[936,128]{1,0:T(8,128)S(1)}, u32[]{:S(2)}, u32[]{:S(2)}) collective-permute-start(f32[936,128]{1,0:T(8,128)S(1)} %get-tuple-element.56), channel_id=1, source_target_pairs={{0,1},{8,9},{16,17},{24,25},{32,33},{40,41},{48,49},{56,57},{1,2},... | collective-permute-start | bytes 1437704 | tf_op jit(solution)/shard_map/ppermute | solution.py:72
  101.0 26.0 %collective-permute-start.16 = (f32[936,128]{1,0:T(8,128)S(1)}, f32[936,128]{1,0:T(8,128)S(1)}, u32[]{:S(2)}, u32[]{:S(2)}) collective-permute-start(f32[936,128]{1,0:T(8,128)S(1)} %get-tuple-element.57), channel_id=1, source_target_pairs={{1,0},{9,8},{17,16},{25,24},{33,32},{41,40},{49,48},{57,56},{2,1},... | collective-permute-start | bytes 1437704 | tf_op jit(solution)/shard_map/ppermute | solution.py:78
  107.3 19.7 %collective-permute-start.17 = (f32[936,128]{1,0:T(8,128)S(1)}, f32[936,128]{1,0:T(8,128)S(1)}, u32[]{:S(2)}, u32[]{:S(2)}) collective-permute-start(f32[936,128]{1,0:T(8,128)S(1)} %get-tuple-element.56), channel_id=1, source_target_pairs={{71,127},{79,119},{87,111},{95,103},{103,95},{111,87},{119,79},{12... | collective-permute-start | bytes 1437704 | tf_op jit(solution)/shard_map/ppermute | solution.py:84
  128.3 7.6 %collective-permute-start.18 = (f32[616,128]{1,0:T(8,128)S(1)}, f32[616,128]{1,0:T(8,128)S(1)}, u32[]{:S(2)}, u32[]{:S(2)}) collective-permute-start(f32[616,128]{1,0:T(8,128)S(1)} %get-tuple-element.60), channel_id=1, source_target_pairs={{0,8},{8,16},{16,24},{24,32},{32,40},{40,48},{48,56},{56,0},{1,9},... | collective-permute-start | bytes 946184 | tf_op jit(solution)/shard_map/ppermute | solution.py:89
  128.4 7.5 %collective-permute-start.19 = (f32[616,128]{1,0:T(8,128)S(1)}, f32[616,128]{1,0:T(8,128)S(1)}, u32[]{:S(2)}, u32[]{:S(2)}) collective-permute-start(f32[616,128]{1,0:T(8,128)S(1)} %get-tuple-element.61), channel_id=1, source_target_pairs={{0,56},{8,0},{16,8},{24,16},{32,24},{40,32},{48,40},{56,48},{1,57}... | collective-permute-start | bytes 946184 | tf_op jit(solution)/shard_map/ppermute | solution.py:94

commit v3 on v2

--- a/solution.py
+++ b/solution.py
@@ -7,6 +7,7 @@
 from jax.experimental.pallas import tpu as pltpu
 from jax.sharding import PartitionSpec as P
 
+
 ITERS = 24
 ATM_SUB = 4
 
@@ -20,18 +21,17 @@
 LV = 32
 RW = 32
 CL = 128
-HALO = 12
-ROUNDS = ITERS // HALO
-NI = RW // 2 + HALO
-NC = CL + 2 * HALO
-JB = NC // 8
-OFF = 24 - HALO
-WIDTH = 168
+NEAR = 8
+FULL = 16
+EDGE = 24
+WIDTH = 176
 DEEP = ITERS
 SR = RW + 2 * DEEP
 VALS = 3 * RW
 LINES = 8
-EDGE_MIB, OWN_MIB, DEEP_MIB = 60, 20, 20
+DEEP_LINES = (RW // 2 + FULL) * FULL
+EDGE_MIB, OWN_MIB, FIRST_MIB, FINAL_MIB = 60, 20, 17, 22
+
 
 VMEM = pl.BlockSpec(memory_space=pltpu.VMEM)
 SMEM = pl.BlockSpec(memory_space=pltpu.SMEM)
@@ -103,18 +103,22 @@
     return ref[pl.ds(base + row, LV, stride=RW), :]
 
 
-def edge_kernel(tracers, flow, kappa, mask, top, bottom):
+def edge_kernel(start, tracers, flow, kappa, mask, top, bottom):
     def body(k, carry):
-        for out, row in ((bottom, k), (top, RW - 1 - k)):
+        for out, row in ((bottom, start + k), (top, RW - 1 - start - k)):
             sea = mask[pl.ds(row, 1), :].astype(F32)
-            out[k, 0:LV] = level_rows(tracers, 0, row)
-            out[k, LV : 2 * LV] = level_rows(tracers, LV * RW, row)
-            out[k, 2 * LV : 3 * LV] = sea * level_rows(flow, 0, row)
-            out[k, 3 * LV : 4 * LV] = sea * level_rows(flow, LV * RW, row)
-            out[k, 4 * LV : 5 * LV] = sea * level_rows(kappa, 0, row)
+            parts = [
+                sea * level_rows(flow, 0, row),
+                sea * level_rows(flow, LV * RW, row),
+                sea * level_rows(kappa, 0, row),
+            ]
+            if start == 0:
+                parts = [level_rows(tracers, 0, row), level_rows(tracers, LV * RW, row)] + parts
+            for f, part in enumerate(parts):
+                out[k, f * LV : (f + 1) * LV] = part
         return carry
 
-    lax.fori_loop(0, HALO, body, 0)
+    lax.fori_loop(0, NEAR, body, 0)
 
 
 def columns(low, high, sign=1.0):
@@ -123,28 +127,25 @@
     return jnp.concatenate([a, b, c, d] if sign > 0 else [a, b, -c, -d], axis=0).T
 
 
-def emit_columns(p, pairs, x, mw, me):
-    for f in range(4):
-        pair = []
-        for n in range(2):
-            low, high = pairs[n]
-            if f == 0:
-                t = columns((low[0], low[1]), (high[0], high[1]))
-            else:
-                t = columns((low[f + 1],) * 2, (high[f + 1],) * 2, -1.0 if f == 2 else 1.0)
-            x[f, 2 * p + n] = t
-            pair.append(t)
-        rows = pl.ds(pl.multiple_of(p * 2 * HALO, 8), 2 * HALO)
-        mw[f, rows, :] = jnp.concatenate([t[:HALO] for t in pair], axis=0)
-        me[f, rows, :] = jnp.concatenate([t[CL - HALO :] for t in pair], axis=0)
+def emit_columns(i, low, high, x, mw, me):
+    parts = []
+    if len(low) == 5:
+        parts.append(columns((low[0], low[1]), (high[0], high[1])))
+    for f, sign in ((-3, 1.0), (-2, -1.0), (-1, 1.0)):
+        parts.append(columns((low[f],) * 2, (high[f],) * 2, sign))
+    rows = pl.ds(pl.multiple_of(i * FULL, FULL), FULL)
+    for f, t in enumerate(parts):
+        x[f, i] = t
+        mw[f, rows, :] = t[:FULL]
+        me[f, rows, :] = t[CL - FULL :]
 
 
 def own_kernel(tracers, flow, kappa, mask, x, mw, me):
     def inner(p, carry):
-        pairs = []
         for n in range(2):
+            i = 2 * p + n
             sides = []
-            for row in (2 * p + n, RW - 1 - (2 * p + n)):
+            for row in (i, RW - 1 - i):
                 sea = mask[pl.ds(row, 1), :].astype(F32)
                 sides.append(
                     [
@@ -155,8 +156,7 @@
                         sea * level_rows(kappa, 0, row),
                     ]
                 )
-            pairs.append(tuple(sides))
-        emit_columns(p, pairs, x, mw, me)
+            emit_columns(i, *sides, x, mw, me)
         return carry
 
     lax.fori_loop(0, RW // 4, inner, 0)
@@ -165,41 +165,47 @@
 def halo_kernel(own, south, north, fold, flags, x, mw, me):
     first = flags[0] > 0
     last = flags[1] > 0
+    count = own.shape[1] // LV
 
     def halo(p, carry):
-        pairs = []
         for n in range(2):
-            k = HALO - 1 - (2 * p + n)
+            i = 2 * p + n
+            k = NEAR - 1 - i
             low, high = [], []
-            for f in range(5):
+            for f in range(count):
                 part = slice(f * LV, (f + 1) * LV)
                 mirror = own[k, part]
                 turned = reversed_lanes(fold[k, part])
-                if f == 3:
+                if f == count - 2:
                     mirror = -mirror
-                if f in (2, 3):
+                if f in (count - 3, count - 2):
                     turned = -turned
                 low.append(jnp.where(first, mirror, south[k, part]))
                 high.append(jnp.where(last, turned, north[k, part]))
-            pairs.append((low, high))
-        emit_columns(p, pairs, x, mw, me)
+            emit_columns(i, low, high, x, mw, me)
         return carry
 
-    lax.fori_loop(0, HALO // 2, halo, 0)
+    lax.fori_loop(0, NEAR // 2, halo, 0)
 
 
 def deep_kernel(final, *refs):
-    xh, xo, wh, wo, eh, eo = refs[:6]
+    halo = FULL if final else NEAR
+    xo, wo, eo, xn, wn, en = refs[:6]
     if final:
-        xts, mine, w2, e2, out = refs[6:11]
-        scratch = refs[11:]
+        xf, wf, ef, xts, mine, w2, e2, out = refs[6:14]
+        scratch = refs[14:]
         surface_steps(mine, w2, e2, out, scratch[6:])
         scratch = scratch[:6]
     else:
         fields, state, top, bottom = refs[6:10]
         scratch = refs[10:]
     s0, s1, cw, ce, cd, cu = scratch
-    mid = slice(24, 24 + CL)
+    pairs = RW // 2 + halo
+    block = (CL + 2 * halo) // 8
+    begin = EDGE - halo
+    mid = slice(EDGE, EDGE + CL)
+    west_cols = slice(EDGE - halo, EDGE)
+    east_cols = slice(EDGE + CL, EDGE + CL + halo)
 
     def coefficients(i, where, u, v, k):
         cw[i, where] = jnp.maximum(u, 0.0) + k
@@ -208,38 +214,42 @@
         cu[i, where] = jnp.maximum(-v, 0.0) + k
 
     def fill(x, w, e, start):
+        lead = x.shape[0] - 3
+
         def body(p, carry):
-            rows = pl.ds(pl.multiple_of(p * 2 * HALO, 8), 2 * HALO)
-            west = [w[f, rows, :] for f in range(4)]
-            east = [e[f, rows, :] for f in range(4)]
-            if final:
-                rows = pl.ds(pl.multiple_of((p + start // 2) * 2 * HALO, 8), 2 * HALO)
-                west[0] = w2[rows, :]
-                east[0] = e2[rows, :]
             for n in range(2):
                 i = 2 * p + n
-                part = slice(n * HALO, (n + 1) * HALO)
-                s0[start + i, mid] = xts[start + i] if final else x[0, i]
-                coefficients(start + i, mid, x[1, i], x[2, i], x[3, i])
-                for side, where in (
-                    (west, slice(24 - HALO, 24)),
-                    (east, slice(24 + CL, 24 + CL + HALO)),
-                ):
-                    s0[start + i, where] = side[0][part]
-                    coefficients(start + i, where, side[1][part], side[2][part], side[3][part])
+                rows = pl.ds(pl.multiple_of(i * FULL, FULL), FULL)
+                to = start + i
+                coefficients(to, mid, x[lead, i], x[lead + 1, i], x[lead + 2, i])
+                west = [w[lead + f, rows, :][FULL - halo :] for f in range(3)]
+                east = [e[lead + f, rows, :][:halo] for f in range(3)]
+                coefficients(to, west_cols, *west)
+                coefficients(to, east_cols, *east)
+                if final:
+                    rows = pl.ds(pl.multiple_of(to * FULL, FULL), FULL)
+                    s0[to, mid] = xts[to]
+                    s0[to, west_cols] = w2[rows, :]
+                    s0[to, east_cols] = e2[rows, :]
+                else:
+                    s0[to, mid] = x[0, i]
+                    s0[to, west_cols] = w[0, rows, :][FULL - halo :]
+                    s0[to, east_cols] = e[0, rows, :][:halo]
             return carry
 
         lax.fori_loop(0, x.shape[1] // 2, body, 0)
 
-    fill(xh, wh, eh, 0)
-    fill(xo, wo, eo, HALO)
+    if final:
+        fill(xf, wf, ef, 0)
+    fill(xn, wn, en, halo - NEAR)
+    fill(xo, wo, eo, halo)
 
     def at(ref, i, j):
-        return ref[i, pl.ds(OFF + j, 8, stride=JB), :]
+        return ref[i, pl.ds(begin + j, 8, stride=block), :]
 
     def rows(src, dst, i, count):
         lines = [[at(src, i + n, j - 1) for j in range(2)] for n in range(count)]
-        for j in range(JB):
+        for j in range(block):
             for n in range(count):
                 lines[n].append(at(src, i + n, j + 1))
             for n in range(count):
@@ -250,7 +260,7 @@
                 else:
                     up = lines[n + 1][j + 1] if n + 1 < count else at(src, i + count, j)
                 k = i + n
-                dst[k, pl.ds(OFF + j, 8, stride=JB), :] = (
+                dst[k, pl.ds(begin + j, 8, stride=block), :] = (
                     centre
                     + at(cw, k, j) * (west - centre)
                     + at(ce, k, j) * (east - centre)
@@ -263,20 +273,20 @@
             rows(src, dst, 2 * p + 1, 2)
             return carry
 
-        lax.fori_loop(s, NI // 2 - 1, body, 0)
-        rows(src, dst, NI - 1, 1)
+        lax.fori_loop(s, pairs // 2 - 1, body, 0)
+        rows(src, dst, pairs - 1, 1)
 
     def two(n, carry):
         step(s0, s1, n)
         step(s1, s0, n)
         return carry
 
-    lax.fori_loop(0, HALO // 2, two, 0)
+    lax.fori_loop(0, halo // 2, two, 0)
 
     if final:
 
         def write(i, carry):
-            t = s0[i + HALO, mid].T
+            t = s0[i + halo, mid].T
             for h, r in ((0, i), (1, RW - 1 - i)):
                 for tracer in range(2):
                     base = h * 2 * LV + tracer * LV + 1
@@ -289,10 +299,10 @@
     else:
         low = lax.broadcasted_iota(jnp.int32, (CL, CL), 1) < CL // 2
         for i in range(RW // 2):
-            state[i] = s0[i + HALO, mid]
-        half = HALO // 2
+            state[i] = s0[i + halo, mid]
+        half = FULL // 2
         for k in range(half):
-            near, far = s0[HALO + k, mid], s0[HALO + k + half, mid]
+            near, far = s0[halo + k, mid], s0[halo + k + half, mid]
             where = slice(k * CL, (k + 1) * CL)
             top[where] = jnp.where(low, pltpu.roll(near, CL // 2, 1), far)
             bottom[where] = jnp.where(low, near, pltpu.roll(far, CL // 2, 1))
@@ -306,7 +316,7 @@
     first = flags[0] > 0
     last = flags[1] > 0
     low = lax.broadcasted_iota(jnp.int32, (CL, CL), 1) < CL // 2
-    half = HALO // 2
+    half = FULL // 2
     flip = jnp.where(
         lax.broadcasted_iota(jnp.int32, (CL, CL), 0)
         + lax.broadcasted_iota(jnp.int32, (CL, CL), 1)
@@ -316,7 +326,7 @@
     ).astype(F32)
     rows = {}
     for i in range(RW // 2):
-        rows[HALO + i] = state[i]
+        rows[FULL + i] = state[i]
     for k in range(half):
         where = slice(k * CL, (k + 1) * CL)
         s, n = south[where], north[where]
@@ -325,14 +335,13 @@
         for kk, sv, nv, fv in ((k, s, n_roll, f_roll), (k + half, s_roll, n, f)):
             down = jnp.where(first, state[kk], sv)
             up = jnp.where(last, fv, nv)
-            rows[HALO - 1 - kk] = jnp.where(low, down, up)
-    for i in range(NI):
+            rows[FULL - 1 - kk] = jnp.where(low, down, up)
+    count = RW // 2 + FULL
+    for i in range(count):
+        where = pl.ds(i * FULL, FULL)
         xts[i] = rows[i]
-    for p in range(NI // 2):
-        pair = [rows[2 * p], rows[2 * p + 1]]
-        where = pl.ds(p * 2 * HALO, 2 * HALO)
-        mw[where, :] = jnp.concatenate([t[:HALO] for t in pair], axis=0)
-        me[where, :] = jnp.concatenate([t[CL - HALO :] for t in pair], axis=0)
+        mw[where, :] = rows[i][:FULL]
+        me[where, :] = rows[i][CL - FULL :]
 
     base = half * CL
     for f in range(7):
@@ -359,7 +368,7 @@
     low = lax.broadcasted_iota(jnp.int32, (SR // 2, CL), 1) < CL // 2
     for f in range(7):
         a, b = joined[f, : SR // 2], joined[f, SR // 2 :]
-        where = slice(NI * HALO + f * SR // 2, NI * HALO + (f + 1) * SR // 2)
+        where = slice(DEEP_LINES + f * SR // 2, DEEP_LINES + (f + 1) * SR // 2)
         mw[where] = jnp.where(low, a, pltpu.roll(b, CL // 2, 1))
         me[where] = jnp.where(low, pltpu.roll(a, CL // 2, 1), b)
 
@@ -369,7 +378,7 @@
     low = lax.broadcasted_iota(jnp.int32, (SR // 2, CL), 1) < CL // 2
 
     def wide(f):
-        where = slice(NI * HALO + f * SR // 2, NI * HALO + (f + 1) * SR // 2)
+        where = slice(DEEP_LINES + f * SR // 2, DEEP_LINES + (f + 1) * SR // 2)
         east, west = e2[where], w2[where]
         near = jnp.where(low, east, pltpu.roll(west, CL // 2, 1))
         far = jnp.where(low, pltpu.roll(east, CL // 2, 1), west)
@@ -628,26 +637,29 @@
     )
     up, down = to_north(for_up), to_south(for_down)
 
-    tracers2 = ocean_tracers.reshape(-1, CL)
-    flow2 = ocean_flow.reshape(-1, CL)
-    kappa2 = ocean_kappa.reshape(-1, CL)
-    edge = shape(HALO, 5 * LV, CL)
-    top, bottom = call(edge_kernel, (edge, edge), (tracers2, flow2, kappa2, sea_mask), mib=EDGE_MIB)
-    up, down, top, bottom = lax.optimization_barrier((up, down, top, bottom))
+    deep_args = (
+        ocean_tracers.reshape(-1, CL),
+        ocean_flow.reshape(-1, CL),
+        ocean_kappa.reshape(-1, CL),
+        sea_mask,
+    )
+    near = shape(NEAR, 5 * LV, CL)
+    top, bottom = call(functools.partial(edge_kernel, 0), (near, near), deep_args, mib=EDGE_MIB)
     south, north, fold = to_north(top), to_south(bottom), across_fold(top)
 
     relay = shape(3 * (VALS + LINES), CL)
     for_east, for_west = call(relay_kernel, (relay,) * 2, (up, mine, down))
     west_in, east_in = to_east(for_east), to_west(for_west)
 
-    xo, mw, me = call(
-        own_kernel,
-        (shape(4, RW // 2, CL, CL),) + (shape(4, RW // 2 * HALO, CL),) * 2,
-        (tracers2, flow2, kappa2, sea_mask),
-        flops=10_000_000,
-        mib=OWN_MIB,
-    )
+    def extended(fields, count):
+        return (shape(fields, count, CL, CL),) + (shape(fields, count * FULL, CL),) * 2
+
+    xo, mw, me = call(own_kernel, extended(4, RW // 2), deep_args, flops=10_000_000, mib=OWN_MIB)
     wo, eo = to_east(me), to_west(mw)
+    far = shape(NEAR, 3 * LV, CL)
+    far_top, far_bottom = call(
+        functools.partial(edge_kernel, NEAR), (far, far), deep_args, mib=OWN_MIB
+    )
 
     run = shape(4, 3, slots)
     atmos_flux, pay_n, pay_o, pay_s = call(
@@ -674,14 +686,24 @@
     pay_east = to_west(jnp.concatenate([p[:, 0:1] for p in pays], axis=1))
     atmos_next = atmosphere(atmos_state, atmos_kappa, atmos_flux)
 
-    xh, mw, me = call(
+    xn, mw, me = call(
         halo_kernel,
-        (shape(4, HALO, CL, CL),) + (shape(4, HALO * HALO, CL),) * 2,
+        extended(4, NEAR),
         (bottom, south, north, fold, flags),
-        flops=10_000_000,
+        flops=5_000_000,
         mib=OWN_MIB,
     )
-    wh, eh = to_east(me), to_west(mw)
+    wn, en = to_east(me), to_west(mw)
+
+    far_args = (to_north(far_top), to_south(far_bottom), across_fold(far_top))
+    xf, mw, me = call(
+        halo_kernel,
+        extended(3, NEAR),
+        (far_bottom, *far_args, flags),
+        flops=5_000_000,
+        mib=OWN_MIB,
+    )
+    wf, ef = to_east(me), to_west(mw)
 
     ocean_stress, fields = call(
         ocean_flux_kernel,
@@ -695,32 +717,34 @@
         blocks={11: (2, *level), 12: (2, *level), 13: level},
     )
 
-    buffers = [pltpu.VMEM((NI, WIDTH, CL), F32)] * 6
-    pair = shape(HALO // 2 * CL + 7 * DEEP, CL)
+    def buffers(halo):
+        return [pltpu.VMEM((RW // 2 + halo, WIDTH, CL), F32)] * 6
+
+    pair = shape(FULL // 2 * CL + 7 * DEEP, CL)
     state, top, bottom = call(
         functools.partial(deep_kernel, False),
         (shape(RW // 2, CL, CL), pair, pair),
-        (xh, xo, wh, wo, eh, eo, fields),
-        scratch=buffers,
-        flops=60_000_000,
-        mib=DEEP_MIB,
+        (xo, wo, eo, xn, wn, en, fields),
+        scratch=buffers(NEAR),
+        flops=40_000_000,
+        mib=FIRST_MIB,
     )
     south, north, fold = to_north(top), to_south(bottom), across_fold(top)
 
-    side = shape(NI * HALO + 7 * SR // 2, CL)
+    side = shape(DEEP_LINES + 7 * SR // 2, CL)
     xts, mw, me, joined = call(
         join_kernel,
-        (shape(NI, CL, CL), side, side, shape(7, SR, CL)),
+        (shape(RW // 2 + FULL, CL, CL), side, side, shape(7, SR, CL)),
         (state, fields, south, north, fold, flags),
     )
     wide = pltpu.VMEM((SR, 2 * CL), F32)
     ocean_next = call(
         functools.partial(deep_kernel, True),
         shape(2 * LV * RW, CL),
-        (xh, xo, wh, wo, eh, eo, xts, joined, to_east(me), to_west(mw)),
-        scratch=buffers + [wide] * 4 + [pltpu.VMEM((2, SR, 2 * CL), F32)],
+        (xo, wo, eo, xn, wn, en, xf, wf, ef, xts, joined, to_east(me), to_west(mw)),
+        scratch=buffers(FULL) + [wide] * 4 + [pltpu.VMEM((2, SR, 2 * CL), F32)],
         flops=80_000_000,
-        mib=DEEP_MIB,
+        mib=FINAL_MIB,
     )
     return (atmos_next, ocean_next.reshape(ocean_tracers.shape), ocean_stress)
 
@@ -737,6 +761,7 @@
         P(("face", "gy"), "gx", None),
         P(None, ("face", "gy"), "gx", None),
     )
+
     return jax.shard_map(
         local,
         mesh=mesh,

time: 155 us -> 168 us (1.084)
  starting transfers between devices: 45.8 us -> 55.3 us
  Pallas kernels: 59.7 us -> 62.9 us
    ppermute x4 -> x5, waiting for transfers between devices: 32.3 us -> 23 us  [to_north(): return lax.ppermute(value, AXES, pairs)]
    ppermute x4 -> x5, waiting for transfers between devices: 4.92 us -> 13.2 us  [to_south(): return lax.ppermute(value, AXES, pairs)]
    ppermute x4 -> x5, starting transfers between devices: 18.1 us -> 23.6 us  [to_south(): return lax.ppermute(value, AXES, pairs)]
    ppermute x5 -> x6, starting transfers between devices: 7.14 us -> 10.8 us  [to_west(): return lax.ppermute(value, 'gx', [(x, (x - 1) % nx) for x in range(nx)])]
    pallas_call x10 -> x12, Pallas kernels: 57 us -> 60.2 us  [call(): pl.pallas_call(kernel, grid=(1,) if blocks else (), out_shape=outs, in_sp...]
    ppermute x4 -> x5, starting transfers between devices: 16.4 us -> 17.5 us  [to_north(): return lax.ppermute(value, AXES, pairs)]
    ppermute x5 -> x6, waiting for transfers between devices: 7.86 us -> 7.99 us  [to_east(): return lax.ppermute(value, 'gx', [(x, (x + 1) % nx) for x in range(nx)])]
  transfers between devices with their start and end apart: 20 -> 25, of which waited for: 8 -> 11; matrix products, arithmetic and copies ran while one was open for 0% -> 1% of each run, Pallas kernels for 18% -> 19%
where the time goes in v3:
time: 168 us; the launch traced here: 167 us
  Pallas kernels  62.9 us (37%)
  starting transfers between devices  55.3 us (33%)
  waiting for transfers between devices  46.1 us (27%)
  local copies, waits for them, and re-layouts  1.68 us (1%)
    pallas_call x12, Pallas kernels, call(): pl.pallas_call(kernel, grid=(1,) if blocks else (), out_shape=outs, in_sp...  60.2 us
    ppermute x5, starting transfers between devices, to_south(): return lax.ppermute(value, AXES, pairs)  23.6 us
    ppermute x5, waiting for transfers between devices, to_north(): return lax.ppermute(value, AXES, pairs)  23 us
    ppermute x5, starting transfers between devices, to_north(): return lax.ppermute(value, AXES, pairs)  17.5 us
    ppermute x5, waiting for transfers between devices, to_south(): return lax.ppermute(value, AXES, pairs)  13.2 us
    ppermute x6, starting transfers between devices, to_west(): return lax.ppermute(value, 'gx', [(x, (x - 1) % nx) for x in range(nx)])  10.8 us
    ppermute x6, waiting for transfers between devices, to_east(): return lax.ppermute(value, 'gx', [(x, (x + 1) % nx) for x in range(nx)])  7.99 us
  transfers between devices with their start and end apart: 25, of which 11 were waited for; matrix products, arithmetic and copies ran while one was open for 1% of the time, Pallas kernels for 19%

profile of v3, /device:TPU:4, one launch (start us, length us, event | category | flops | bytes accessed | tf_op | source)
XLA Modules:
  0.0 167.1 jit_solution(6734990207086305176)
XLA Ops:
  0.6 0.0 copy-start
  0.6 0.0 copy-start.1
  0.7 0.0 copy-start.2
  0.7 1.7 %shard_map.112 = (f32[120,128]{1,0:T(8,128)}, f32[120,128]{1,0:T(8,128)}, f32[120,128]{1,0:T(8,128)}) custom-call(f32[2,32,32,128]{3,2,1,0:T(8,128)} %tracers.3, f32[2,32,32,128]{3,2,1,0:T(8,128)} %flow.3, s32[3,3,1024]{2,1,0:T(4,128)} %sea_cells.1), custom_call_target="tpu_custom_call" | custom-call | flops 1000000 | bytes 1000000 | tf_op jit(solution)/shard_map/pallas_call | solution.py:44
  2.3 5.8 %collective-permute-start = (f32[120,128]{1,0:T(8,128)}, f32[120,128]{1,0:T(8,128)S(1)}, u32[]{:S(2)}, u32[]{:S(2)}) collective-permute-start(f32[120,128]{1,0:T(8,128)} %get-tuple-element.34), channel_id=1, source_target_pairs={{0,1},{8,9},{16,17},{24,25},{32,33},{40,41},{48,49},{56,57},{1,2},... | collective-permute-start | bytes 184328 | tf_op jit(solution)/shard_map/ppermute | solution.py:72
  8.1 2.5 %collective-permute-start.1 = (f32[120,128]{1,0:T(8,128)}, f32[120,128]{1,0:T(8,128)S(1)}, u32[]{:S(2)}, u32[]{:S(2)}) collective-permute-start(f32[120,128]{1,0:T(8,128)} %get-tuple-element.36), channel_id=1, source_target_pairs={{1,0},{9,8},{17,16},{25,24},{33,32},{41,40},{49,48},{57,56},{2,1},... | collective-permute-start | bytes 184328 | tf_op jit(solution)/shard_map/ppermute | solution.py:78
  10.6 0.5 collective-permute-done.up
  11.1 4.9 %collective-permute-done.1.down = f32[120,128]{1,0:T(8,128)S(1)} collective-permute-done((f32[120,128]{1,0:T(8,128)}, f32[120,128]{1,0:T(8,128)S(1)}, u32[]{:S(2)}, u32[]{:S(2)}) %collective-permute-start.1) | collective-permute-done | bytes 61472 | tf_op jit(solution)/shard_map/ppermute | solution.py:78
  16.0 0.8 copy-done.5
  16.8 0.8 shard_map.113
  17.6 3.0 %collective-permute-start.3 = (f32[312,128]{1,0:T(8,128)}, f32[312,128]{1,0:T(8,128)}, u32[]{:S(2)}, u32[]{:S(2)}) collective-permute-start(f32[312,128]{1,0:T(8,128)} %get-tuple-element.38), channel_id=1, source_target_pairs={{0,56},{8,0},{16,8},{24,16},{32,24},{40,32},{48,40},{56,48},{1,57}... | collective-permute-start | bytes 479240 | tf_op jit(solution)/shard_map/ppermute | solution.py:94
  20.5 4.1 %shard_map.117 = (f32[8,160,128]{2,1,0:T(8,128)}, f32[8,160,128]{2,1,0:T(8,128)}) custom-call(f32[2048,128]{1,0:T(8,128)} %bitcast.6, f32[2048,128]{1,0:T(8,128)} %bitcast.9, f32[1024,128]{1,0:T(8,128)} %bitcast.12, s32[32,128]{1,0:T(8,128)} %mask.7), custom_call_target="tpu_custom_call" | custom-call | flops 1000000 | bytes 1000000 | tf_op jit(solution)/shard_map/pallas_call | solution.py:44
  24.7 3.1 %collective-permute-start.6 = (f32[8,160,128]{2,1,0:T(8,128)}, f32[8,160,128]{2,1,0:T(8,128)S(1)}, u32[]{:S(2)}, u32[]{:S(2)}) collective-permute-start(f32[8,160,128]{2,1,0:T(8,128)} %get-tuple-element.44), channel_id=1, source_target_pairs={{0,1},{8,9},{16,17},{24,25},{32,33},{40,41},{48,49},{56,57},{1,2},... | collective-permute-start | bytes 1966088 | tf_op jit(solution)/shard_map/ppermute | solution.py:72
  27.7 1.5 collective-permute-start.8
  29.3 5.1 %collective-permute-start.7 = (f32[8,160,128]{2,1,0:T(8,128)}, f32[8,160,128]{2,1,0:T(8,128)}, u32[]{:S(2)}, u32[]{:S(2)}) collective-permute-start(f32[8,160,128]{2,1,0:T(8,128)} %get-tuple-element.43.own), channel_id=1, source_target_pairs={{1,0},{9,8},{17,16},{25,24},{33,32},{41,40},{49,48},{57,56},{2,1},... | collective-permute-start | bytes 1966088 | tf_op jit(solution)/shard_map/ppermute | solution.py:78
  34.4 0.7 copy.12.weights
  35.1 0.0 copy-start.3
  35.2 0.0 copy-start.13
  35.2 0.0 copy-start.14
  35.2 2.9 %shard_map.116 = (f32[4,16,128,128]{3,2,1,0:T(8,128)S(1)}, f32[4,256,128]{2,1,0:T(8,128)S(1)}, f32[4,256,128]{2,1,0:T(8,128)S(1)}) custom-call(f32[2048,128]{1,0:T(8,128)S(1)} %bitcast.7, f32[2048,128]{1,0:T(8,128)S(1)} %bitcast.10, f32[1024,128]{1,0:T(8,128)S(1)} %bitcast.13, s32[32,128]{1,0:T(8,128)S(1)} %copy-done.12), custom_call_target="tpu_custom_call" | custom-call | flops 10000000 | bytes 1000000 | tf_op jit(solution)/shard_map/pallas_call | solution.py:44
  38.1 0.0 copy-start.4
  38.1 0.1 add_convert_fusion.flags
  38.2 0.0 collective-permute-done.2.west
  38.2 0.0 collective-permute-done.3.east
  38.3 10.3 %shard_map.114 = (f32[4,32,128]{2,1,0:T(8,128)S(1)}, f32[4,3,1024]{2,1,0:T(4,128)S(1)}, f32[4,3,1024]{2,1,0:T(4,128)S(1)}, f32[4,3,1024]{2,1,0:T(4,128)S(1)}) custom-call(f32[4,32,32,128]{3,2,1,0:T(8,128)S(1)} %copy-done.3, f32[120,128]{1,0:T(8,128)S(1)} %copy-done.8, f32[120,128]{1,0:T(8,128)S(1)} %copy-done.6, f32[120,128]{1,0:T(8,128)S(1)} %copy-done.10, ...), custom_call_target="tpu_custom_call" | custom-call | flops 20000000 | bytes 1000000 | tf_op jit(solution)/shard_map/pallas_call | solution.py:44
  48.6 2.2 %collective-permute-start.16 = (f32[4,3,1024]{2,1,0:T(4,128)S(1)}, f32[4,3,1024]{2,1,0:T(4,128)S(1)}, u32[]{:S(2)}, u32[]{:S(2)}) collective-permute-start(f32[4,3,1024]{2,1,0:T(4,128)S(1)} %get-tuple-element.53), channel_id=1, source_target_pairs={{0,1},{8,9},{16,17},{24,25},{32,33},{40,41},{48,49},{56,57},{1,2},... | collective-permute-start | bytes 147464 | tf_op jit(solution)/shard_map/ppermute | solution.py:72
  50.8 6.1 %collective-permute-start.17 = (f32[4,3,1024]{2,1,0:T(4,128)S(1)}, f32[4,3,1024]{2,1,0:T(4,128)S(1)}, u32[]{:S(2)}, u32[]{:S(2)}) collective-permute-start(f32[4,3,1024]{2,1,0:T(4,128)S(1)} %get-tuple-element.55), channel_id=1, source_target_pairs={{1,0},{9,8},{17,16},{25,24},{33,32},{41,40},{49,48},{57,56},{2,1},... | collective-permute-start | bytes 147464 | tf_op jit(solution)/shard_map/ppermute | solution.py:78
  56.9 0.4 collective-permute-done.16.pay_up
  57.2 4.2 %collective-permute-done.17.pay_down = f32[4,3,1024]{2,1,0:T(4,128)S(1)} collective-permute-done((f32[4,3,1024]{2,1,0:T(4,128)S(1)}, f32[4,3,1024]{2,1,0:T(4,128)S(1)}, u32[]{:S(2)}, u32[]{:S(2)}) %collective-permute-start.17) | collective-permute-done | bytes 49184 | tf_op jit(solution)/shard_map/ppermute | solution.py:78
  61.4 1.4 collective-permute-start.5
  62.9 0.0 collective-permute-done.8.fold
  62.9 2.4 %shard_map.118 = (f32[4,8,128,128]{3,2,1,0:T(8,128)S(1)}, f32[4,128,128]{2,1,0:T(8,128)S(1)}, f32[4,128,128]{2,1,0:T(8,128)S(1)}) custom-call(f32[8,160,128]{2,1,0:T(8,128)S(1)} %copy-done.4, f32[8,160,128]{2,1,0:T(8,128)S(1)} %collective-permute-done.6.south, f32[8,160,128]{2,1,0:T(8,128)} %collective-permute-done.7.north, ...), custom_call_target="tpu_custom_call" | custom-call | flops 5000000 | bytes 1000000 | tf_op jit(solution)/shard_map/pallas_call | solution.py:44
  65.3 0.5 collective-permute-start.10
  65.8 0.0 collective-permute-start.9
  65.9 0.3 collective-permute-start.18
  66.3 7.3 %collective-permute-done.18.pay_west = f32[4,3,1024]{2,1,0:T(4,128)S(1)} collective-permute-done((f32[4,3,1024]{2,1,0:T(4,128)S(1)}, f32[4,3,1024]{2,1,0:T(4,128)S(1)}, u32[]{:S(2)}, u32[]{:S(2)}) %collective-permute-start.18) | collective-permute-done | bytes 49184 | tf_op jit(solution)/shard_map/ppermute | solution.py:89
  73.5 1.9 %collective-permute-done.19.pay_east = f32[4,3,1024]{2,1,0:T(4,128)S(1)} collective-permute-done((f32[4,3,1024]{2,1,0:T(4,128)S(1)}, f32[4,3,1024]{2,1,0:T(4,128)S(1)}, u32[]{:S(2)}, u32[]{:S(2)}) %collective-permute-start.19) | collective-permute-done | bytes 49184 | tf_op jit(solution)/shard_map/ppermute | solution.py:94
  75.4 5.2 %shard_map.121 = (f32[2,32,128]{2,1,0:T(8,128)}, f32[7,32,128]{2,1,0:T(8,128)S(1)}) custom-call(f32[120,128]{1,0:T(8,128)S(1)} %copy-done.8, f32[120,128]{1,0:T(8,128)S(1)} %copy-done.6, f32[120,128]{1,0:T(8,128)S(1)} %copy-done.10, f32[312,128]{1,0:T(8,128)S(1)} %collective-permute-done.2.west, f32[312,128]{1,0:T(8,128)} %collective-permute-done.3.east, ...), custom_call_target="tpu_custom_call" | custom-call | flops 8000000 | bytes 1000000 | tf_op jit(solution)/shard_map/pallas_call | solution.py:44
  80.6 0.0 collective-permute-done.4.refs_1_
  80.6 0.0 collective-permute-done.5.refs_2_
  80.6 0.0 collective-permute-done.10.refs_5_
  80.6 0.0 collective-permute-done.9.refs_4_
  80.6 6.5 %shard_map.122 = (f32[16,128,128]{2,1,0:T(8,128)S(1)}, f32[1192,128]{1,0:T(8,128)S(1)}, f32[1192,128]{1,0:T(8,128)S(1)}) custom-call(f32[4,16,128,128]{3,2,1,0:T(8,128)S(1)} %get-tuple-element.40.refs_0_, f32[4,256,128]{2,1,0:T(8,128)S(1)} %collective-permute-done.4.refs_1_, f32[4,256,128]{2,1,0:T(8,128)S(1)} %collective-permute-done.5.refs_2_, ...), custom_call_target="tpu_custom_call" | custom-call | flops 40000000 | bytes 1000000 | tf_op jit(solution)/shard_map/pallas_call | solution.py:44
  87.2 3.7 %collective-permute-start.20 = (f32[1192,128]{1,0:T(8,128)S(1)}, f32[1192,128]{1,0:T(8,128)S(1)}, u32[]{:S(2)}, u32[]{:S(2)}) collective-permute-start(f32[1192,128]{1,0:T(8,128)S(1)} %get-tuple-element.58), channel_id=1, source_target_pairs={{0,1},{8,9},{16,17},{24,25},{32,33},{40,41},{48,49},{56,57},{1,2},... | collective-permute-start | bytes 1830920 | tf_op jit(solution)/shard_map/ppermute | solution.py:72
  90.9 4.5 %collective-permute-start.21 = (f32[1192,128]{1,0:T(8,128)S(1)}, f32[1192,128]{1,0:T(8,128)S(1)}, u32[]{:S(2)}, u32[]{:S(2)}) collective-permute-start(f32[1192,128]{1,0:T(8,128)S(1)} %get-tuple-element.59), channel_id=1, source_target_pairs={{1,0},{9,8},{17,16},{25,24},{33,32},{41,40},{49,48},{57,56},{2,1},... | collective-permute-start | bytes 1830920 | tf_op jit(solution)/shard_map/ppermute | solution.py:78
  95.4 0.7 collective-permute-start.22
  96.1 0.7 shard_map.119
  96.9 2.8 %collective-permute-start.11 = (f32[8,96,128]{2,1,0:T(8,128)S(1)}, f32[8,96,128]{2,1,0:T(8,128)S(1)}, u32[]{:S(2)}, u32[]{:S(2)}) collective-permute-start(f32[8,96,128]{2,1,0:T(8,128)S(1)} %get-tuple-element.49), channel_id=1, source_target_pairs={{0,1},{8,9},{16,17},{24,25},{32,33},{40,41},{48,49},{56,57},{1,2},... | collective-permute-start | bytes 1179656 | tf_op jit(solution)/shard_map/ppermute | solution.py:72
  99.7 5.4 %collective-permute-start.12 = (f32[8,96,128]{2,1,0:T(8,128)S(1)}, f32[8,96,128]{2,1,0:T(8,128)S(1)}, u32[]{:S(2)}, u32[]{:S(2)}) collective-permute-start(f32[8,96,128]{2,1,0:T(8,128)S(1)} %get-tuple-element.48.own), channel_id=1, source_target_pairs={{1,0},{9,8},{17,16},{25,24},{33,32},{41,40},{49,48},{57,56},{2,1},... | collective-permute-start | bytes 1179656 | tf_op jit(solution)/shard_map/ppermute | solution.py:78
  105.1 21.4 %collective-permute-done.20.south = f32[1192,128]{1,0:T(8,128)S(1)} collective-permute-done((f32[1192,128]{1,0:T(8,128)S(1)}, f32[1192,128]{1,0:T(8,128)S(1)}, u32[]{:S(2)}, u32[]{:S(2)}) %collective-permute-start.20) | collective-permute-done | bytes 610336 | tf_op jit(solution)/shard_map/ppermute | solution.py:72
  126.5 0.7 collective-permute-start.13
  127.2 1.0 collective-permute-done.21.north
  128.2 1.5 shard_map.123
  129.7 0.0 collective-permute-start.23
  129.7 2.9 %collective-permute-start.24 = (f32[792,128]{1,0:T(8,128)S(1)}, f32[792,128]{1,0:T(8,128)S(1)}, u32[]{:S(2)}, u32[]{:S(2)}) collective-permute-start(f32[792,128]{1,0:T(8,128)S(1)} %get-tuple-element.63), channel_id=1, source_target_pairs={{0,56},{8,0},{16,8},{24,16},{32,24},{40,32},{48,40},{56,48},{1,57}... | collective-permute-start | bytes 1216520 | tf_op jit(solution)/shard_map/ppermute | solution.py:94
  132.7 0.8 collective-permute-done.11.south
  133.5 3.1 %collective-permute-done.12.north = f32[8,96,128]{2,1,0:T(8,128)S(1)} collective-permute-done((f32[8,96,128]{2,1,0:T(8,128)S(1)}, f32[8,96,128]{2,1,0:T(8,128)S(1)}, u32[]{:S(2)}, u32[]{:S(2)}) %collective-permute-start.12) | collective-permute-done | bytes 393248 | tf_op jit(solution)/shard_map/ppermute | solution.py:78
  136.6 1.5 shard_map.120
  138.0 0.0 collective-permute-start.14
  138.1 2.9 %collective-permute-start.15 = (f32[3,128,128]{2,1,0:T(8,128)S(1)}, f32[3,128,128]{2,1,0:T(8,128)S(1)}, u32[]{:S(2)}, u32[]{:S(2)}) collective-permute-start(f32[3,128,128]{2,1,0:T(8,128)S(1)} %get-tuple-element.52), channel_id=1, source_target_pairs={{0,56},{8,0},{16,8},{24,16},{32,24},{40,32},{48,40},{56,48},{1,57}... | collective-permute-start | bytes 589832 | tf_op jit(solution)/shard_map/ppermute | solution.py:94
  141.0 2.6 %shard_map.115 = f32[4,32,32,128]{3,2,1,0:T(8,128)} custom-call(f32[4,32,32,128]{3,2,1,0:T(8,128)S(1)} %copy-done.3, f32[32,128]{1,0:T(8,128)S(1)} %copy-done.15, f32[4,32,128]{2,1,0:T(8,128)S(1)} %get-tuple-element.39.flux), custom_call_target="tpu_custom_call" | custom-call | flops 5000000 | bytes 4200000 | tf_op jit(solution)/shard_map/pallas_call | solution.py:597
  143.7 0.7 collective-permute-done.14.refs_7_
  144.4 0.0 collective-permute-done.15.refs_8_
  144.4 22.7 %shard_map.124 = f32[2048,128]{1,0:T(8,128)} custom-call(f32[4,16,128,128]{3,2,1,0:T(8,128)S(1)} %get-tuple-element.40.refs_0_, f32[4,256,128]{2,1,0:T(8,128)S(1)} %collective-permute-done.4.refs_1_, f32[4,256,128]{2,1,0:T(8,128)S(1)} %collective-permute-done.5.refs_2_, f32[4,8,128,128]{3,2,1,0:T(8,128)S(1)} %get-tuple-element.45.refs_3_, ...), custom_call_target="tpu_custom_call" | custom-call | flops 80000000 | bytes 1000000 | tf_op jit(solution)/shard_map/pallas_call | solution.py:44
  (40 shorter events, 0.3 us)
Async XLA Ops:
  0.6 34.5 %copy-start = (f32[2,32,32,128]{3,2,1,0:T(8,128)S(1)}, f32[2,32,32,128]{3,2,1,0:T(8,128)}, u32[]{:S(2)}) copy-start(f32[2,32,32,128]{3,2,1,0:T(8,128)} %tracers.3) | copy-start | bytes 3145732
  0.6 34.5 %copy-start.1 = (f32[2,32,32,128]{3,2,1,0:T(8,128)S(1)}, f32[2,32,32,128]{3,2,1,0:T(8,128)}, u32[]{:S(2)}) copy-start(f32[2,32,32,128]{3,2,1,0:T(8,128)} %flow.3) | copy-start | bytes 3145732
  0.7 34.5 %copy-start.2 = (f32[32,32,128]{2,1,0:T(8,128)S(1)}, f32[32,32,128]{2,1,0:T(8,128)}, u32[]{:S(2)}) copy-start(f32[32,32,128]{2,1,0:T(8,128)} %kappa.3) | copy-start | bytes 1572868
  2.3 8.7 %collective-permute-start = (f32[120,128]{1,0:T(8,128)}, f32[120,128]{1,0:T(8,128)S(1)}, u32[]{:S(2)}, u32[]{:S(2)}) collective-permute-start(f32[120,128]{1,0:T(8,128)} %get-tuple-element.34), channel_id=1, source_target_pairs={{0,1},{8,9},{16,17},{24,25},{32,33},{40,41},{48,49},{56,57},{1,2},... | collective-permute-start | bytes 184328 | tf_op jit(solution)/shard_map/ppermute | solution.py:72
  8.1 7.8 %collective-permute-start.1 = (f32[120,128]{1,0:T(8,128)}, f32[120,128]{1,0:T(8,128)S(1)}, u32[]{:S(2)}, u32[]{:S(2)}) collective-permute-start(f32[120,128]{1,0:T(8,128)} %get-tuple-element.36), channel_id=1, source_target_pairs={{1,0},{9,8},{17,16},{25,24},{33,32},{41,40},{49,48},{57,56},{2,1},... | collective-permute-start | bytes 184328 | tf_op jit(solution)/shard_map/ppermute | solution.py:78
  11.1 9.5 %copy-start.7 = (f32[120,128]{1,0:T(8,128)}, f32[120,128]{1,0:T(8,128)S(1)}, u32[]{:S(2)}) copy-start(f32[120,128]{1,0:T(8,128)S(1)} %collective-permute-done.up) | copy-start | bytes 184324
  16.0 4.6 %copy-start.9 = (f32[120,128]{1,0:T(8,128)}, f32[120,128]{1,0:T(8,128)S(1)}, u32[]{:S(2)}) copy-start(f32[120,128]{1,0:T(8,128)S(1)} %collective-permute-done.1.down) | copy-start | bytes 184324
  16.0 0.9 copy-start.5
  16.8 17.6 %copy-start.16 = (f32[2,3,3,1024]{3,0,2,1:T(2,128)S(1)}, f32[2,3,3,1024]{3,0,2,1:T(2,128)}, u32[]{:S(2)}) copy-start(f32[2,3,3,1024]{3,0,2,1:T(2,128)} %param.17) | copy-start | bytes 221188
  16.8 18.3 %copy-start.12 = (s32[32,128]{1,0:T(8,128)S(1)}, s32[32,128]{1,0:T(8,128)}, u32[]{:S(2)}) copy-start(s32[32,128]{1,0:T(8,128)} %mask.7) | copy-start | bytes 49156
  17.6 20.6 %collective-permute-start.2 = (f32[312,128]{1,0:T(8,128)}, f32[312,128]{1,0:T(8,128)S(1)}, u32[]{:S(2)}, u32[]{:S(2)}) collective-permute-start(f32[312,128]{1,0:T(8,128)} %get-tuple-element.37), channel_id=1, source_target_pairs={{0,8},{8,16},{16,24},{24,32},{32,40},{40,48},{48,56},{56,0},{1,9},... | collective-permute-start | bytes 479240 | tf_op jit(solution)/shard_map/ppermute | solution.py:89
  17.6 20.6 %collective-permute-start.3 = (f32[312,128]{1,0:T(8,128)}, f32[312,128]{1,0:T(8,128)}, u32[]{:S(2)}, u32[]{:S(2)}) collective-permute-start(f32[312,128]{1,0:T(8,128)} %get-tuple-element.38), channel_id=1, source_target_pairs={{0,56},{8,0},{16,8},{24,16},{32,24},{40,32},{48,40},{56,48},{1,57}... | collective-permute-start | bytes 479240 | tf_op jit(solution)/shard_map/ppermute | solution.py:94
  20.5 17.7 %copy-start.6 = (f32[120,128]{1,0:T(8,128)S(1)}, f32[120,128]{1,0:T(8,128)}, u32[]{:S(2)}) copy-start(f32[120,128]{1,0:T(8,128)} %get-tuple-element.35.mine) | copy-start | bytes 184324
  24.7 38.2 %collective-permute-start.6 = (f32[8,160,128]{2,1,0:T(8,128)}, f32[8,160,128]{2,1,0:T(8,128)S(1)}, u32[]{:S(2)}, u32[]{:S(2)}) collective-permute-start(f32[8,160,128]{2,1,0:T(8,128)} %get-tuple-element.44), channel_id=1, source_target_pairs={{0,1},{8,9},{16,17},{24,25},{32,33},{40,41},{48,49},{56,57},{1,2},... | collective-permute-start | bytes 1966088 | tf_op jit(solution)/shard_map/ppermute | solution.py:72
  27.7 35.2 %collective-permute-start.8 = (f32[8,160,128]{2,1,0:T(8,128)}, f32[8,160,128]{2,1,0:T(8,128)}, u32[]{:S(2)}, u32[]{:S(2)}) collective-permute-start(f32[8,160,128]{2,1,0:T(8,128)} %get-tuple-element.44), channel_id=1, source_target_pairs={{71,127},{79,119},{87,111},{95,103},{103,95},{111,87},{119,79},{12... | collective-permute-start | bytes 1966088 | tf_op jit(solution)/shard_map/ppermute | solution.py:84
  29.3 33.6 %collective-permute-start.7 = (f32[8,160,128]{2,1,0:T(8,128)}, f32[8,160,128]{2,1,0:T(8,128)}, u32[]{:S(2)}, u32[]{:S(2)}) collective-permute-start(f32[8,160,128]{2,1,0:T(8,128)} %get-tuple-element.43.own), channel_id=1, source_target_pairs={{1,0},{9,8},{17,16},{25,24},{33,32},{41,40},{49,48},{57,56},{2,1},... | collective-permute-start | bytes 1966088 | tf_op jit(solution)/shard_map/ppermute | solution.py:78
  35.1 3.1 %copy-start.3 = (f32[4,32,32,128]{3,2,1,0:T(8,128)S(1)}, f32[4,32,32,128]{3,2,1,0:T(8,128)}, u32[]{:S(2)}) copy-start(f32[4,32,32,128]{3,2,1,0:T(8,128)} %state.1) | copy-start | bytes 6291460
  35.1 3.1 %copy-start.8 = (f32[120,128]{1,0:T(8,128)S(1)}, f32[120,128]{1,0:T(8,128)}, u32[]{:S(2)}) copy-start(f32[120,128]{1,0:T(8,128)} %copy-done.7) | copy-start | bytes 184324
  35.1 3.1 %copy-start.10 = (f32[120,128]{1,0:T(8,128)S(1)}, f32[120,128]{1,0:T(8,128)}, u32[]{:S(2)}) copy-start(f32[120,128]{1,0:T(8,128)} %copy-done.9) | copy-start | bytes 184324
  35.1 3.1 %copy-start.11 = (f32[2,3,3,1024]{3,2,1,0:T(4,128)S(1)}, f32[2,3,3,1024]{3,2,1,0:T(4,128)}, u32[]{:S(2)}) copy-start(f32[2,3,3,1024]{3,2,1,0:T(4,128)} %copy.12.weights) | copy-start | bytes 221188
  35.2 3.1 %copy-start.13 = (s32[3,3,1024]{2,1,0:T(4,128)S(1)}, s32[3,3,1024]{2,1,0:T(4,128)}, u32[]{:S(2)}) copy-start(s32[3,3,1024]{2,1,0:T(4,128)} %sea_cells.1) | copy-start | bytes 110596
  35.2 3.1 %copy-start.14 = (s32[3,3,1024]{2,1,0:T(4,128)S(1)}, s32[3,3,1024]{2,1,0:T(4,128)}, u32[]{:S(2)}) copy-start(s32[3,3,1024]{2,1,0:T(4,128)} %air_cells.1) | copy-start | bytes 110596
  38.1 24.8 %copy-start.4 = (f32[8,160,128]{2,1,0:T(8,128)S(1)}, f32[8,160,128]{2,1,0:T(8,128)}, u32[]{:S(2)}) copy-start(f32[8,160,128]{2,1,0:T(8,128)} %get-tuple-element.43.own) | copy-start | bytes 1966084
  48.6 8.7 %collective-permute-start.16 = (f32[4,3,1024]{2,1,0:T(4,128)S(1)}, f32[4,3,1024]{2,1,0:T(4,128)S(1)}, u32[]{:S(2)}, u32[]{:S(2)}) collective-permute-start(f32[4,3,1024]{2,1,0:T(4,128)S(1)} %get-tuple-element.53), channel_id=1, source_target_pairs={{0,1},{8,9},{16,17},{24,25},{32,33},{40,41},{48,49},{56,57},{1,2},... | collective-permute-start | bytes 147464 | tf_op jit(solution)/shard_map/ppermute | solution.py:72
  50.8 10.6 %collective-permute-start.17 = (f32[4,3,1024]{2,1,0:T(4,128)S(1)}, f32[4,3,1024]{2,1,0:T(4,128)S(1)}, u32[]{:S(2)}, u32[]{:S(2)}) collective-permute-start(f32[4,3,1024]{2,1,0:T(4,128)S(1)} %get-tuple-element.55), channel_id=1, source_target_pairs={{1,0},{9,8},{17,16},{25,24},{33,32},{41,40},{49,48},{57,56},{2,1},... | collective-permute-start | bytes 147464 | tf_op jit(solution)/shard_map/ppermute | solution.py:78
  57.2 23.4 %collective-permute-start.4 = (f32[4,256,128]{2,1,0:T(8,128)S(1)}, f32[4,256,128]{2,1,0:T(8,128)S(1)}, u32[]{:S(2)}, u32[]{:S(2)}) collective-permute-start(f32[4,256,128]{2,1,0:T(8,128)S(1)} %get-tuple-element.41), channel_id=1, source_target_pairs={{0,8},{8,16},{16,24},{24,32},{32,40},{40,48},{48,56},{56,0},{1,9},... | collective-permute-start | bytes 1572872 | tf_op jit(solution)/shard_map/ppermute | solution.py:89
  61.4 19.2 %collective-permute-start.5 = (f32[4,256,128]{2,1,0:T(8,128)S(1)}, f32[4,256,128]{2,1,0:T(8,128)S(1)}, u32[]{:S(2)}, u32[]{:S(2)}) collective-permute-start(f32[4,256,128]{2,1,0:T(8,128)S(1)} %get-tuple-element.42), channel_id=1, source_target_pairs={{0,56},{8,0},{16,8},{24,16},{32,24},{40,32},{48,40},{56,48},{1,57}... | collective-permute-start | bytes 1572872 | tf_op jit(solution)/shard_map/ppermute | solution.py:94
  65.3 15.3 %collective-permute-start.10 = (f32[4,128,128]{2,1,0:T(8,128)S(1)}, f32[4,128,128]{2,1,0:T(8,128)S(1)}, u32[]{:S(2)}, u32[]{:S(2)}) collective-permute-start(f32[4,128,128]{2,1,0:T(8,128)S(1)} %get-tuple-element.47), channel_id=1, source_target_pairs={{0,56},{8,0},{16,8},{24,16},{32,24},{40,32},{48,40},{56,48},{1,57}... | collective-permute-start | bytes 786440 | tf_op jit(solution)/shard_map/ppermute | solution.py:94
  65.8 14.8 %collective-permute-start.9 = (f32[4,128,128]{2,1,0:T(8,128)S(1)}, f32[4,128,128]{2,1,0:T(8,128)S(1)}, u32[]{:S(2)}, u32[]{:S(2)}) collective-permute-start(f32[4,128,128]{2,1,0:T(8,128)S(1)} %get-tuple-element.46), channel_id=1, source_target_pairs={{0,8},{8,16},{16,24},{24,32},{32,40},{40,48},{48,56},{56,0},{1,9},... | collective-permute-start | bytes 786440 | tf_op jit(solution)/shard_map/ppermute | solution.py:89
  65.9 7.6 %collective-permute-start.18 = (f32[4,3,1024]{2,1,0:T(4,128)S(1)}, f32[4,3,1024]{2,1,0:T(4,128)S(1)}, u32[]{:S(2)}, u32[]{:S(2)}) collective-permute-start(f32[4,3,1024]{2,1,0:T(4,128)S(1)} %pad_maximum_fusion), channel_id=1, source_target_pairs={{0,8},{8,16},{16,24},{24,32},{32,40},{40,48},{48,56},{56,0},{1,9},... | collective-permute-start | bytes 147464 | tf_op jit(solution)/shard_map/ppermute | solution.py:89
  73.5 1.9 %collective-permute-start.19 = (f32[4,3,1024]{2,1,0:T(4,128)S(1)}, f32[4,3,1024]{2,1,0:T(4,128)S(1)}, u32[]{:S(2)}, u32[]{:S(2)}) collective-permute-start(f32[4,3,1024]{2,1,0:T(4,128)S(1)} %pad_maximum_fusion.1), channel_id=1, source_target_pairs={{0,56},{8,0},{16,8},{24,16},{32,24},{40,32},{48,40},{56,48},{1,57}... | collective-permute-start | bytes 147464 | tf_op jit(solution)/shard_map/ppermute | solution.py:94
  87.2 39.3 %collective-permute-start.20 = (f32[1192,128]{1,0:T(8,128)S(1)}, f32[1192,128]{1,0:T(8,128)S(1)}, u32[]{:S(2)}, u32[]{:S(2)}) collective-permute-start(f32[1192,128]{1,0:T(8,128)S(1)} %get-tuple-element.58), channel_id=1, source_target_pairs={{0,1},{8,9},{16,17},{24,25},{32,33},{40,41},{48,49},{56,57},{1,2},... | collective-permute-start | bytes 1830920 | tf_op jit(solution)/shard_map/ppermute | solution.py:72
  90.9 37.4 %collective-permute-start.21 = (f32[1192,128]{1,0:T(8,128)S(1)}, f32[1192,128]{1,0:T(8,128)S(1)}, u32[]{:S(2)}, u32[]{:S(2)}) collective-permute-start(f32[1192,128]{1,0:T(8,128)S(1)} %get-tuple-element.59), channel_id=1, source_target_pairs={{1,0},{9,8},{17,16},{25,24},{33,32},{41,40},{49,48},{57,56},{2,1},... | collective-permute-start | bytes 1830920 | tf_op jit(solution)/shard_map/ppermute | solution.py:78
  95.4 32.8 %collective-permute-start.22 = (f32[1192,128]{1,0:T(8,128)S(1)}, f32[1192,128]{1,0:T(8,128)S(1)}, u32[]{:S(2)}, u32[]{:S(2)}) collective-permute-start(f32[1192,128]{1,0:T(8,128)S(1)} %get-tuple-element.58), channel_id=1, source_target_pairs={{71,127},{79,119},{87,111},{95,103},{103,95},{111,87},{119,79},{12... | collective-permute-start | bytes 1830920 | tf_op jit(solution)/shard_map/ppermute | solution.py:84
  96.9 36.6 %collective-permute-start.11 = (f32[8,96,128]{2,1,0:T(8,128)S(1)}, f32[8,96,128]{2,1,0:T(8,128)S(1)}, u32[]{:S(2)}, u32[]{:S(2)}) collective-permute-start(f32[8,96,128]{2,1,0:T(8,128)S(1)} %get-tuple-element.49), channel_id=1, source_target_pairs={{0,1},{8,9},{16,17},{24,25},{32,33},{40,41},{48,49},{56,57},{1,2},... | collective-permute-start | bytes 1179656 | tf_op jit(solution)/shard_map/ppermute | solution.py:72
  99.7 36.9 %collective-permute-start.12 = (f32[8,96,128]{2,1,0:T(8,128)S(1)}, f32[8,96,128]{2,1,0:T(8,128)S(1)}, u32[]{:S(2)}, u32[]{:S(2)}) collective-permute-start(f32[8,96,128]{2,1,0:T(8,128)S(1)} %get-tuple-element.48.own), channel_id=1, source_target_pairs={{1,0},{9,8},{17,16},{25,24},{33,32},{41,40},{49,48},{57,56},{2,1},... | collective-permute-start | bytes 1179656 | tf_op jit(solution)/shard_map/ppermute | solution.py:78
  126.5 10.1 %collective-permute-start.13 = (f32[8,96,128]{2,1,0:T(8,128)S(1)}, f32[8,96,128]{2,1,0:T(8,128)S(1)}, u32[]{:S(2)}, u32[]{:S(2)}) collective-permute-start(f32[8,96,128]{2,1,0:T(8,128)S(1)} %get-tuple-element.49), channel_id=1, source_target_pairs={{71,127},{79,119},{87,111},{95,103},{103,95},{111,87},{119,79},{12... | collective-permute-start | bytes 1179656 | tf_op jit(solution)/shard_map/ppermute | solution.py:84
  128.2 12.8 %copy-start.15 = (f32[32,128]{1,0:T(8,128)S(1)}, f32[32,128]{1,0:T(8,128)}, u32[]{:S(2)}) copy-start(f32[32,128]{1,0:T(8,128)} %kappa.2) | copy-start | bytes 49156
  129.7 14.7 %collective-permute-start.23 = (f32[792,128]{1,0:T(8,128)S(1)}, f32[792,128]{1,0:T(8,128)S(1)}, u32[]{:S(2)}, u32[]{:S(2)}) collective-permute-start(f32[792,128]{1,0:T(8,128)S(1)} %get-tuple-element.62), channel_id=1, source_target_pairs={{0,8},{8,16},{16,24},{24,32},{32,40},{40,48},{48,56},{56,0},{1,9},... | collective-permute-start | bytes 1216520 | tf_op jit(solution)/shard_map/ppermute | solution.py:89
  129.7 14.6 %collective-permute-start.24 = (f32[792,128]{1,0:T(8,128)S(1)}, f32[792,128]{1,0:T(8,128)S(1)}, u32[]{:S(2)}, u32[]{:S(2)}) collective-permute-start(f32[792,128]{1,0:T(8,128)S(1)} %get-tuple-element.63), channel_id=1, source_target_pairs={{0,56},{8,0},{16,8},{24,16},{32,24},{40,32},{48,40},{56,48},{1,57}... | collective-permute-start | bytes 1216520 | tf_op jit(solution)/shard_map/ppermute | solution.py:94
  138.0 6.3 %collective-permute-start.14 = (f32[3,128,128]{2,1,0:T(8,128)S(1)}, f32[3,128,128]{2,1,0:T(8,128)S(1)}, u32[]{:S(2)}, u32[]{:S(2)}) collective-permute-start(f32[3,128,128]{2,1,0:T(8,128)S(1)} %get-tuple-element.51), channel_id=1, source_target_pairs={{0,8},{8,16},{16,24},{24,32},{32,40},{40,48},{48,56},{56,0},{1,9},... | collective-permute-start | bytes 589832 | tf_op jit(solution)/shard_map/ppermute | solution.py:89
  138.1 6.3 %collective-permute-start.15 = (f32[3,128,128]{2,1,0:T(8,128)S(1)}, f32[3,128,128]{2,1,0:T(8,128)S(1)}, u32[]{:S(2)}, u32[]{:S(2)}) collective-permute-start(f32[3,128,128]{2,1,0:T(8,128)S(1)} %get-tuple-element.52), channel_id=1, source_target_pairs={{0,56},{8,0},{16,8},{24,16},{32,24},{40,32},{48,40},{56,48},{1,57}... | collective-permute-start | bytes 589832 | tf_op jit(solution)/shard_map/ppermute | solution.py:94

commit v4 on v3

--- a/solution.py
+++ b/solution.py
@@ -30,7 +30,9 @@
 VALS = 3 * RW
 LINES = 8
 DEEP_LINES = (RW // 2 + FULL) * FULL
-EDGE_MIB, OWN_MIB, FIRST_MIB, FINAL_MIB = 60, 20, 17, 22
+FAR_LINES = NEAR * 3 * LV
+FAR_COLS = 3 * NEAR * FULL
+EDGE_MIB, OWN_MIB, FIRST_MIB, FINAL_MIB, FLUX_MIB = 12, 14, 15, 20, 10
 
 
 VMEM = pl.BlockSpec(memory_space=pltpu.VMEM)
@@ -115,7 +117,8 @@
             if start == 0:
                 parts = [level_rows(tracers, 0, row), level_rows(tracers, LV * RW, row)] + parts
             for f, part in enumerate(parts):
-                out[k, f * LV : (f + 1) * LV] = part
+                where = pl.multiple_of((k * len(parts) + f) * LV, LV)
+                out[pl.ds(where, LV), :] = part
         return carry
 
     lax.fori_loop(0, NEAR, body, 0)
@@ -133,11 +136,11 @@
         parts.append(columns((low[0], low[1]), (high[0], high[1])))
     for f, sign in ((-3, 1.0), (-2, -1.0), (-1, 1.0)):
         parts.append(columns((low[f],) * 2, (high[f],) * 2, sign))
-    rows = pl.ds(pl.multiple_of(i * FULL, FULL), FULL)
     for f, t in enumerate(parts):
+        rows = pl.ds(pl.multiple_of((f * x.shape[1] + i) * FULL, FULL), FULL)
         x[f, i] = t
-        mw[f, rows, :] = t[:FULL]
-        me[f, rows, :] = t[CL - FULL :]
+        mw[rows, :] = t[:FULL]
+        me[rows, :] = t[CL - FULL :]
 
 
 def own_kernel(tracers, flow, kappa, mask, x, mw, me):
@@ -162,43 +165,51 @@
     lax.fori_loop(0, RW // 4, inner, 0)
 
 
-def halo_kernel(own, south, north, fold, flags, x, mw, me):
+def halo_kernel(count, own, south, north, fold, flags, x, mw, me):
     first = flags[0] > 0
     last = flags[1] > 0
-    count = own.shape[1] // LV
 
     def halo(p, carry):
         for n in range(2):
             i = 2 * p + n
-            k = NEAR - 1 - i
             low, high = [], []
             for f in range(count):
-                part = slice(f * LV, (f + 1) * LV)
-                mirror = own[k, part]
-                turned = reversed_lanes(fold[k, part])
+                part = pl.ds(pl.multiple_of(((NEAR - 1 - i) * count + f) * LV, LV), LV)
+                mirror = own[part, :]
+                turned = reversed_lanes(fold[part, :])
                 if f == count - 2:
                     mirror = -mirror
                 if f in (count - 3, count - 2):
                     turned = -turned
-                low.append(jnp.where(first, mirror, south[k, part]))
-                high.append(jnp.where(last, turned, north[k, part]))
+                low.append(jnp.where(first, mirror, south[part, :]))
+                high.append(jnp.where(last, turned, north[part, :]))
             emit_columns(i, low, high, x, mw, me)
         return carry
 
     lax.fori_loop(0, NEAR // 2, halo, 0)
+
+
+def far_halo_kernel(own, south, north, fold, flags, x, mw, me):
+    halo_kernel(3, own, south, north, fold, flags, x, mw, me)
+    for a, source in enumerate((south, own, north)):
+        for f in range(4):
+            for out, b in ((me, 2), (mw, 0)):
+                line = FAR_LINES + (f * 3 + b) * LINES
+                to = FAR_COLS + (a * 4 + f) * LINES
+                out[to : to + LINES] = source[line : line + LINES]
 
 
 def deep_kernel(final, *refs):
     halo = FULL if final else NEAR
     xo, wo, eo, xn, wn, en = refs[:6]
     if final:
-        xf, wf, ef, xts, mine, w2, e2, out = refs[6:14]
-        scratch = refs[14:]
-        surface_steps(mine, w2, e2, out, scratch[6:])
+        xf, wf, ef, xts, w2, e2, mine, w3, e3, out = refs[6:16]
+        scratch = refs[16:]
+        surface_steps(mine, w3, e3, out, scratch[6:])
         scratch = scratch[:6]
     else:
-        fields, state, top, bottom = refs[6:10]
-        scratch = refs[10:]
+        state, top, bottom = refs[6:9]
+        scratch = refs[9:]
     s0, s1, cw, ce, cd, cu = scratch
     pairs = RW // 2 + halo
     block = (CL + 2 * halo) // 8
@@ -219,11 +230,14 @@
         def body(p, carry):
             for n in range(2):
                 i = 2 * p + n
-                rows = pl.ds(pl.multiple_of(i * FULL, FULL), FULL)
+                lines = [
+                    pl.ds(pl.multiple_of((f * x.shape[1] + i) * FULL, FULL), FULL)
+                    for f in range(lead + 3)
+                ]
                 to = start + i
                 coefficients(to, mid, x[lead, i], x[lead + 1, i], x[lead + 2, i])
-                west = [w[lead + f, rows, :][FULL - halo :] for f in range(3)]
-                east = [e[lead + f, rows, :][:halo] for f in range(3)]
+                west = [w[lines[lead + f], :][FULL - halo :] for f in range(3)]
+                east = [e[lines[lead + f], :][:halo] for f in range(3)]
                 coefficients(to, west_cols, *west)
                 coefficients(to, east_cols, *east)
                 if final:
@@ -233,8 +247,8 @@
                     s0[to, east_cols] = e2[rows, :]
                 else:
                     s0[to, mid] = x[0, i]
-                    s0[to, west_cols] = w[0, rows, :][FULL - halo :]
-                    s0[to, east_cols] = e[0, rows, :][:halo]
+                    s0[to, west_cols] = w[lines[0], :][FULL - halo :]
+                    s0[to, east_cols] = e[lines[0], :][:halo]
             return carry
 
         lax.fori_loop(0, x.shape[1] // 2, body, 0)
@@ -306,13 +320,9 @@
             where = slice(k * CL, (k + 1) * CL)
             top[where] = jnp.where(low, pltpu.roll(near, CL // 2, 1), far)
             bottom[where] = jnp.where(low, near, pltpu.roll(far, CL // 2, 1))
-        for f in range(7):
-            where = slice(half * CL + f * DEEP, half * CL + (f + 1) * DEEP)
-            top[where] = fields[f, RW - DEEP :]
-            bottom[where] = fields[f, :DEEP]
-
-
-def join_kernel(state, fields, south, north, fold, flags, xts, mw, me, joined):
+
+
+def join_kernel(state, south, north, fold, flags, xts, mw, me):
     first = flags[0] > 0
     last = flags[1] > 0
     low = lax.broadcasted_iota(jnp.int32, (CL, CL), 1) < CL // 2
@@ -343,9 +353,12 @@
         mw[where, :] = rows[i][:FULL]
         me[where, :] = rows[i][CL - FULL :]
 
-    base = half * CL
+
+def surface_join_kernel(fields, south, north, fold, flags, joined, mw, me):
+    first = flags[0] > 0
+    last = flags[1] > 0
     for f in range(7):
-        part = slice(base + f * DEEP, base + (f + 1) * DEEP)
+        part = slice(f * DEEP, (f + 1) * DEEP)
         joined[f, 0:DEEP] = south[part]
         joined[f, DEEP : DEEP + RW] = fields[f]
         joined[f, DEEP + RW :] = north[part]
@@ -361,14 +374,14 @@
     def _():
         for f in range(7):
             sign = -1.0 if f in (2, 3) else 1.0
-            turned = sign * reversed_lanes(fold[base + f * DEEP : base + (f + 1) * DEEP])
+            turned = sign * reversed_lanes(fold[f * DEEP : (f + 1) * DEEP])
             for k in range(DEEP):
                 joined[f, DEEP + RW + k : DEEP + RW + k + 1] = turned[DEEP - 1 - k : DEEP - k]
 
     low = lax.broadcasted_iota(jnp.int32, (SR // 2, CL), 1) < CL // 2
     for f in range(7):
         a, b = joined[f, : SR // 2], joined[f, SR // 2 :]
-        where = slice(DEEP_LINES + f * SR // 2, DEEP_LINES + (f + 1) * SR // 2)
+        where = slice(f * SR // 2, (f + 1) * SR // 2)
         mw[where] = jnp.where(low, a, pltpu.roll(b, CL // 2, 1))
         me[where] = jnp.where(low, pltpu.roll(a, CL // 2, 1), b)
 
@@ -378,7 +391,7 @@
     low = lax.broadcasted_iota(jnp.int32, (SR // 2, CL), 1) < CL // 2
 
     def wide(f):
-        where = slice(DEEP_LINES + f * SR // 2, DEEP_LINES + (f + 1) * SR // 2)
+        where = slice(f * SR // 2, (f + 1) * SR // 2)
         east, west = e2[where], w2[where]
         near = jnp.where(low, east, pltpu.roll(west, CL // 2, 1))
         far = jnp.where(low, pltpu.roll(east, CL // 2, 1), west)
@@ -491,7 +504,8 @@
 
 
 def flux_kernel(
-    air, up, mine, down, west, east, air_cells, sea_cells, weights, flux, north, own, south, vals, sea
+    air, up, mine, down, west, east, air_cells, sea_cells, weights, far_top, far_bottom,
+    flux, north, own, south, vals, sea,
 ):
     for a, source in enumerate((up, mine, down)):
         sea[3 * a] = west[a * VALS : (a + 1) * VALS]
@@ -520,10 +534,16 @@
         [vals[f, 0:9] for f in range(4)],
         [vals[4, 0:9], current_scale * vals[5, 0:9], current_scale * vals[6, 0:9]],
     )
+    north[0:FAR_LINES] = far_top[...]
+    south[0:FAR_LINES] = far_bottom[...]
+    own[0:FAR_LINES] = far_bottom[...]
     for f in range(4):
         pay = vals[8, 0:9] * fluxes[f]
         for a, out in enumerate((south, own, north)):
-            out[f] = pay[3 * a : 3 * a + 3]
+            for b in range(3):
+                for n in range(LINES):
+                    line = FAR_LINES + (f * 3 + b) * LINES + n
+                    out[line : line + 1] = pay[3 * a + b : 3 * a + b + 1, n * CL : (n + 1) * CL]
         vals[f, 0:9] = vals[7, 0:9] * fluxes[f]
 
     def place(q, total):
@@ -538,20 +558,25 @@
 
 def ocean_flux_kernel(
     up, mine, down, west, east, pay_up, pay_mine, pay_down, pay_west, pay_east,
-    mask, tracers, flow, kappa, stress, fields, cells, vals,
+    mask, tracers, flow, kappa, stress, fields, top, bottom, cells, vals,
 ):
     def line(ref, start):
         rows = ref[start : start + LINES]
-        return jnp.concatenate([rows[n : n + 1] for n in range(LINES)], axis=1).astype(jnp.int32)
+        return jnp.concatenate([rows[n : n + 1] for n in range(LINES)], axis=1)
 
     for a, (lists, pay) in enumerate(((up, pay_up), (mine, pay_mine), (down, pay_down))):
-        cells[3 * a : 3 * a + 1] = line(west, 3 * VALS + a * LINES)
-        cells[3 * a + 1 : 3 * a + 2] = line(lists, VALS + LINES)
-        cells[3 * a + 2 : 3 * a + 3] = line(east, 3 * VALS + a * LINES)
+        for b, (ref, start) in enumerate(
+            ((west, 3 * VALS + a * LINES), (lists, VALS + LINES), (east, 3 * VALS + a * LINES))
+        ):
+            q = 3 * a + b
+            cells[q : q + 1] = line(ref, start).astype(jnp.int32)
         for f in range(4):
-            vals[f, 3 * a : 3 * a + 1] = pay_west[f, a : a + 1]
-            vals[f, 3 * a + 1 : 3 * a + 2] = pay[f, 1:2]
-            vals[f, 3 * a + 2 : 3 * a + 3] = pay_east[f, a : a + 1]
+            along = FAR_COLS + (a * 4 + f) * LINES
+            for b, (ref, start) in enumerate(
+                ((pay_west, along), (pay, FAR_LINES + (f * 3 + 1) * LINES), (pay_east, along))
+            ):
+                q = 3 * a + b
+                vals[f, q : q + 1] = line(ref, start)
 
     def place(q, total):
         hot, rows = one_hots(cells[pl.ds(q, 1), :])
@@ -570,6 +595,9 @@
     fields[4] = sea * kappa[0]
     fields[5] = -ocean_gain * sea * (part[0] + part[1])
     fields[6] = ocean_gain * sea * part[1]
+    for f in range(7):
+        top[f * DEEP : (f + 1) * DEEP] = fields[f, RW - DEEP :]
+        bottom[f * DEEP : (f + 1) * DEEP] = fields[f, :DEEP]
 
 
 def atmos_kernel(state, kappa, flux, out):
@@ -643,51 +671,44 @@
         ocean_kappa.reshape(-1, CL),
         sea_mask,
     )
-    near = shape(NEAR, 5 * LV, CL)
-    top, bottom = call(functools.partial(edge_kernel, 0), (near, near), deep_args, mib=EDGE_MIB)
+    near = shape(NEAR * 5 * LV, CL)
+    top, bottom = call(
+        functools.partial(edge_kernel, 0), (near, near), deep_args, mib=EDGE_MIB
+    )
     south, north, fold = to_north(top), to_south(bottom), across_fold(top)
 
     relay = shape(3 * (VALS + LINES), CL)
     for_east, for_west = call(relay_kernel, (relay,) * 2, (up, mine, down))
     west_in, east_in = to_east(for_east), to_west(for_west)
 
-    def extended(fields, count):
-        return (shape(fields, count, CL, CL),) + (shape(fields, count * FULL, CL),) * 2
+    def extended(fields, count, extra=0):
+        return (shape(fields, count, CL, CL),) + (shape(fields * count * FULL + extra, CL),) * 2
 
     xo, mw, me = call(own_kernel, extended(4, RW // 2), deep_args, flops=10_000_000, mib=OWN_MIB)
     wo, eo = to_east(me), to_west(mw)
-    far = shape(NEAR, 3 * LV, CL)
+    far = shape(FAR_LINES, CL)
     far_top, far_bottom = call(
         functools.partial(edge_kernel, NEAR), (far, far), deep_args, mib=OWN_MIB
     )
 
-    run = shape(4, 3, slots)
+    load = shape(FAR_LINES + 12 * LINES, CL)
     atmos_flux, pay_n, pay_o, pay_s = call(
         flux_kernel,
-        (shape(4, RW, CL), run, run, run),
+        (shape(4, RW, CL), load, load, load),
         (
-            atmos_state,
-            up,
-            mine,
-            down,
-            west_in,
-            east_in,
-            xgrid_atmos_cell,
-            xgrid_ocean_cell,
-            xgrid_weights,
+            atmos_state, up, mine, down, west_in, east_in,
+            xgrid_atmos_cell, xgrid_ocean_cell, xgrid_weights, far_top, far_bottom,
         ),
         scratch=[pltpu.VMEM((9, 16, slots), F32), pltpu.VMEM((9, VALS, CL), F32)],
         flops=20_000_000,
         blocks={0: (4, *level)},
-    )
-    pay_up, pay_down = to_north(pay_n), to_south(pay_s)
-    pays = (pay_up, pay_o, pay_down)
-    pay_west = to_east(jnp.concatenate([p[:, 2:3] for p in pays], axis=1))
-    pay_east = to_west(jnp.concatenate([p[:, 0:1] for p in pays], axis=1))
+        mib=FLUX_MIB,
+    )
+    pay_up, pay_down, pay_fold = to_north(pay_n), to_south(pay_s), across_fold(pay_n)
     atmos_next = atmosphere(atmos_state, atmos_kappa, atmos_flux)
 
     xn, mw, me = call(
-        halo_kernel,
+        functools.partial(halo_kernel, 5),
         extended(4, NEAR),
         (bottom, south, north, fold, flags),
         flops=5_000_000,
@@ -695,53 +716,59 @@
     )
     wn, en = to_east(me), to_west(mw)
 
-    far_args = (to_north(far_top), to_south(far_bottom), across_fold(far_top))
+    def buffers(halo):
+        return [pltpu.VMEM((RW // 2 + halo, WIDTH, CL), F32)] * 6
+
+    pair = shape(FULL // 2 * CL, CL)
+    state, top, bottom = call(
+        functools.partial(deep_kernel, False),
+        (shape(RW // 2, CL, CL), pair, pair),
+        (xo, wo, eo, xn, wn, en),
+        scratch=buffers(NEAR),
+        flops=40_000_000,
+        mib=FIRST_MIB,
+    )
+    south, north, fold = to_north(top), to_south(bottom), across_fold(top)
+
     xf, mw, me = call(
-        halo_kernel,
-        extended(3, NEAR),
-        (far_bottom, *far_args, flags),
+        far_halo_kernel,
+        extended(3, NEAR, 12 * LINES),
+        (pay_o, pay_up, pay_down, pay_fold, flags),
         flops=5_000_000,
         mib=OWN_MIB,
     )
     wf, ef = to_east(me), to_west(mw)
-
-    ocean_stress, fields = call(
+    edge = shape(7 * DEEP, CL)
+    ocean_stress, fields, s_top, s_bottom = call(
         ocean_flux_kernel,
-        (shape(2, RW, CL), shape(7, RW, CL)),
+        (shape(2, RW, CL), shape(7, RW, CL), edge, edge),
         (
-            up, mine, down, west_in, east_in, pay_up, pay_o, pay_down, pay_west, pay_east,
+            up, mine, down, west_in, east_in, pay_up, pay_o, pay_down, wf, ef,
             sea_mask, ocean_tracers, ocean_flow, ocean_kappa,
         ),
         scratch=[pltpu.VMEM((16, slots), jnp.int32), pltpu.VMEM((4, 16, slots), F32)],
         flops=8_000_000,
         blocks={11: (2, *level), 12: (2, *level), 13: level},
-    )
-
-    def buffers(halo):
-        return [pltpu.VMEM((RW // 2 + halo, WIDTH, CL), F32)] * 6
-
-    pair = shape(FULL // 2 * CL + 7 * DEEP, CL)
-    state, top, bottom = call(
-        functools.partial(deep_kernel, False),
-        (shape(RW // 2, CL, CL), pair, pair),
-        (xo, wo, eo, xn, wn, en, fields),
-        scratch=buffers(NEAR),
-        flops=40_000_000,
-        mib=FIRST_MIB,
-    )
-    south, north, fold = to_north(top), to_south(bottom), across_fold(top)
-
-    side = shape(DEEP_LINES + 7 * SR // 2, CL)
-    xts, mw, me, joined = call(
+        mib=FLUX_MIB,
+    )
+    s_args = (to_north(s_top), to_south(s_bottom), across_fold(s_top))
+
+    side = shape(DEEP_LINES, CL)
+    xts, mw, me = call(
         join_kernel,
-        (shape(RW // 2 + FULL, CL, CL), side, side, shape(7, SR, CL)),
-        (state, fields, south, north, fold, flags),
+        (shape(RW // 2 + FULL, CL, CL), side, side),
+        (state, south, north, fold, flags),
+    )
+    w2, e2 = to_east(me), to_west(mw)
+    side = shape(7 * SR // 2, CL)
+    joined, sw, se = call(
+        surface_join_kernel, (shape(7, SR, CL), side, side), (fields, *s_args, flags)
     )
     wide = pltpu.VMEM((SR, 2 * CL), F32)
     ocean_next = call(
         functools.partial(deep_kernel, True),
         shape(2 * LV * RW, CL),
-        (xo, wo, eo, xn, wn, en, xf, wf, ef, xts, joined, to_east(me), to_west(mw)),
+        (xo, wo, eo, xn, wn, en, xf, wf, ef, xts, w2, e2, joined, to_east(se), to_west(sw)),
         scratch=buffers(FULL) + [wide] * 4 + [pltpu.VMEM((2, SR, 2 * CL), F32)],
         flops=80_000_000,
         mib=FINAL_MIB,
@@ -762,6 +789,7 @@
         P(None, ("face", "gy"), "gx", None),
     )
 
+
     return jax.shard_map(
         local,
         mesh=mesh,

time: 168 us -> 175 us (1.042)
  waiting for transfers between devices: 46.1 us -> 35.2 us
  local copies, waits for them, and re-layouts: 1.68 us -> 11.5 us
  starting transfers between devices: 55.3 us -> 60.2 us
  Pallas kernels: 62.9 us -> 64.7 us
    unnamed x35 -> x55, local copies, waits for them, and re-layouts: 1.6 us -> 11.5 us
    ppermute x5, waiting for transfers between devices: 13.2 us -> 5.76 us  [to_south(): return lax.ppermute(value, AXES, pairs)]
    ppermute x6, waiting for transfers between devices: 7.99 us -> 2.53 us  [to_east(): return lax.ppermute(value, 'gx', [(x, (x + 1) % nx) for x in range(nx)])]
    ppermute x5, starting transfers between devices: 17.5 us -> 21.7 us  [to_north(): return lax.ppermute(value, AXES, pairs)]
    ppermute x5, starting transfers between devices: 23.6 us -> 19.6 us  [to_south(): return lax.ppermute(value, AXES, pairs)]
    ppermute x6, starting transfers between devices: 10.8 us -> 14.7 us  [to_west(): return lax.ppermute(value, 'gx', [(x, (x - 1) % nx) for x in range(nx)])]
    ppermute x5, waiting for transfers between devices: 23 us -> 26.9 us  [to_north(): return lax.ppermute(value, AXES, pairs)]
    ppermute x6, waiting for transfers between devices: 1.92 us -> 0.02 us  [to_west(): return lax.ppermute(value, 'gx', [(x, (x - 1) % nx) for x in range(nx)])]
  transfers between devices with their start and end apart: 25 -> 26, of which waited for: 11 -> 7; matrix products, arithmetic and copies ran while one was open for 1% -> 0% of each run, Pallas kernels for 19% -> 22%
where the time goes in v4:
time: 175 us; the launch traced here: 173 us
  Pallas kernels  64.7 us (37%)
  starting transfers between devices  60.2 us (34%)
  waiting for transfers between devices  35.2 us (20%)
  local copies, waits for them, and re-layouts  11.5 us (7%)
    pallas_call x13, Pallas kernels, call(): pl.pallas_call(kernel, grid=(1,) if blocks else (), out_shape=outs, in_sp...  62.1 us
    ppermute x5, waiting for transfers between devices, to_north(): return lax.ppermute(value, AXES, pairs)  26.9 us
    ppermute x5, starting transfers between devices, to_north(): return lax.ppermute(value, AXES, pairs)  21.7 us
    ppermute x5, starting transfers between devices, to_south(): return lax.ppermute(value, AXES, pairs)  19.6 us
    ppermute x6, starting transfers between devices, to_west(): return lax.ppermute(value, 'gx', [(x, (x - 1) % nx) for x in range(nx)])  14.7 us
    unnamed x55, local copies, waits for them, and re-layouts  11.5 us
    ppermute x5, waiting for transfers between devices, to_south(): return lax.ppermute(value, AXES, pairs)  5.76 us
    ppermute x4, starting transfers between devices, across_fold(): return lax.ppermute(value, AXES, pairs)  3.57 us
  transfers between devices with their start and end apart: 26, of which 7 were waited for; matrix products, arithmetic and copies ran while one was open for 0% of the time, Pallas kernels for 22%

profile of v4, /device:TPU:4, one launch (start us, length us, event | category | flops | bytes accessed | tf_op | source)
XLA Modules:
  0.0 172.8 jit_solution(14838113760554412101)
XLA Ops:
  0.6 0.0 copy-start
  0.6 1.2 copy-done
  1.9 1.2 copy-done.2
  3.1 1.0 copy-done.9
  4.1 0.7 copy-done.17
  4.9 2.5 %shard_map.118 = (f32[1280,128]{1,0:T(8,128)}, f32[1280,128]{1,0:T(8,128)}) custom-call(f32[2048,128]{1,0:T(8,128)S(1)} %bitcast.6, f32[2048,128]{1,0:T(8,128)S(1)} %bitcast.9, f32[1024,128]{1,0:T(8,128)S(1)} %bitcast.12, s32[32,128]{1,0:T(8,128)S(1)} %copy-done.17), custom_call_target="tpu_custom_call" | custom-call | flops 1000000 | bytes 1000000 | tf_op jit(solution)/shard_map/pallas_call | solution.py:46
  7.3 5.8 %collective-permute-start.6 = (f32[1280,128]{1,0:T(8,128)}, f32[1280,128]{1,0:T(8,128)}, u32[]{:S(2)}, u32[]{:S(2)}) collective-permute-start(f32[1280,128]{1,0:T(8,128)} %get-tuple-element.50), channel_id=1, source_target_pairs={{0,1},{8,9},{16,17},{24,25},{32,33},{40,41},{48,49},{56,57},{1,2},... | collective-permute-start | bytes 1966088 | tf_op jit(solution)/shard_map/ppermute | solution.py:74
  13.1 0.0 copy-start.26
  13.1 2.6 %collective-permute-start.7 = (f32[1280,128]{1,0:T(8,128)}, f32[1280,128]{1,0:T(8,128)}, u32[]{:S(2)}, u32[]{:S(2)}) collective-permute-start(f32[1280,128]{1,0:T(8,128)} %get-tuple-element.49.own), channel_id=1, source_target_pairs={{1,0},{9,8},{17,16},{25,24},{33,32},{41,40},{49,48},{57,56},{2,1},... | collective-permute-start | bytes 1966088 | tf_op jit(solution)/shard_map/ppermute | solution.py:80
  15.7 1.5 collective-permute-start.8
  17.2 1.6 shard_map.112
  18.8 4.9 %collective-permute-start = (f32[120,128]{1,0:T(8,128)}, f32[120,128]{1,0:T(8,128)S(1)}, u32[]{:S(2)}, u32[]{:S(2)}) collective-permute-start(f32[120,128]{1,0:T(8,128)} %get-tuple-element.38), channel_id=1, source_target_pairs={{0,1},{8,9},{16,17},{24,25},{32,33},{40,41},{48,49},{56,57},{1,2},... | collective-permute-start | bytes 184328 | tf_op jit(solution)/shard_map/ppermute | solution.py:74
  23.7 3.4 %collective-permute-start.1 = (f32[120,128]{1,0:T(8,128)}, f32[120,128]{1,0:T(8,128)S(1)}, u32[]{:S(2)}, u32[]{:S(2)}) collective-permute-start(f32[120,128]{1,0:T(8,128)} %get-tuple-element.40), channel_id=1, source_target_pairs={{1,0},{9,8},{17,16},{25,24},{33,32},{41,40},{49,48},{57,56},{2,1},... | collective-permute-start | bytes 184328 | tf_op jit(solution)/shard_map/ppermute | solution.py:80
  27.1 17.0 %collective-permute-done.up = f32[120,128]{1,0:T(8,128)S(1)} collective-permute-done((f32[120,128]{1,0:T(8,128)}, f32[120,128]{1,0:T(8,128)S(1)}, u32[]{:S(2)}, u32[]{:S(2)}) %collective-permute-start) | collective-permute-done | bytes 61472 | tf_op jit(solution)/shard_map/ppermute | solution.py:74
  44.1 0.9 collective-permute-done.1.down
  45.0 0.8 copy-done.13
  45.9 0.0 collective-permute-start.2
  45.9 0.0 copy-start.19
  45.9 0.0 copy-start.22
  45.9 2.9 %collective-permute-start.3 = (f32[312,128]{1,0:T(8,128)S(1)}, f32[312,128]{1,0:T(8,128)S(1)}, u32[]{:S(2)}, u32[]{:S(2)}) collective-permute-start(f32[312,128]{1,0:T(8,128)S(1)} %get-tuple-element.42), channel_id=1, source_target_pairs={{0,56},{8,0},{16,8},{24,16},{32,24},{40,32},{48,40},{56,48},{1,57}... | collective-permute-start | bytes 479240 | tf_op jit(solution)/shard_map/ppermute | solution.py:96
  48.8 3.9 %shard_map.117 = (f32[4,16,128,128]{3,2,1,0:T(8,128)S(1)}, f32[1024,128]{1,0:T(8,128)}, f32[1024,128]{1,0:T(8,128)}) custom-call(f32[2048,128]{1,0:T(8,128)S(1)} %bitcast.7, f32[2048,128]{1,0:T(8,128)S(1)} %bitcast.10, f32[1024,128]{1,0:T(8,128)S(1)} %bitcast.13, s32[32,128]{1,0:T(8,128)S(1)} %copy-done.18), custom_call_target="tpu_custom_call" | custom-call | flops 10000000 | bytes 1000000 | tf_op jit(solution)/shard_map/pallas_call | solution.py:46
  52.8 2.0 %copy-done.4 = f32[4,16,128,128]{3,2,1,0:T(8,128)} copy-done((f32[4,16,128,128]{3,2,1,0:T(8,128)}, f32[4,16,128,128]{3,2,1,0:T(8,128)S(1)}, u32[]{:S(2)}) %copy-start.4) | copy-done | bytes 4194328
  54.8 0.0 collective-permute-done.2.west
  54.8 0.0 collective-permute-start.4
  54.8 0.0 collective-permute-done.3.east
  54.8 3.0 %collective-permute-start.5 = (f32[1024,128]{1,0:T(8,128)}, f32[1024,128]{1,0:T(8,128)}, u32[]{:S(2)}, u32[]{:S(2)}) collective-permute-start(f32[1024,128]{1,0:T(8,128)} %get-tuple-element.48), channel_id=1, source_target_pairs={{0,56},{8,0},{16,8},{24,16},{32,24},{40,32},{48,40},{56,48},{1,57}... | collective-permute-start | bytes 1572872 | tf_op jit(solution)/shard_map/ppermute | solution.py:96
  57.8 0.7 shard_map.114
  58.5 9.8 %shard_map.115 = (f32[4,32,128]{2,1,0:T(8,128)S(1)}, f32[864,128]{1,0:T(8,128)}, f32[864,128]{1,0:T(8,128)S(1)}, f32[864,128]{1,0:T(8,128)S(1)}) custom-call(f32[4,32,32,128]{3,2,1,0:T(8,128)S(1)} %copy-done.7, f32[120,128]{1,0:T(8,128)S(1)} %collective-permute-done.up, f32[120,128]{1,0:T(8,128)S(1)} %copy-done.13, ...), custom_call_target="tpu_custom_call" | custom-call | flops 20000000 | bytes 1000000 | tf_op jit(solution)/shard_map/pallas_call | solution.py:46
  68.4 0.8 copy-done.11
  69.2 0.6 copy-done.20
  69.8 0.7 copy-done.24
  70.6 4.9 %collective-permute-start.11 = (f32[864,128]{1,0:T(8,128)}, f32[864,128]{1,0:T(8,128)}, u32[]{:S(2)}, u32[]{:S(2)}) collective-permute-start(f32[864,128]{1,0:T(8,128)} %get-tuple-element.55), channel_id=1, source_target_pairs={{0,1},{8,9},{16,17},{24,25},{32,33},{40,41},{48,49},{56,57},{1,2},... | collective-permute-start | bytes 1327112 | tf_op jit(solution)/shard_map/ppermute | solution.py:74
  75.5 0.1 add_convert_fusion.flags
  75.5 2.8 %shard_map.119 = (f32[4,8,128,128]{3,2,1,0:T(8,128)S(1)}, f32[512,128]{1,0:T(8,128)S(1)}, f32[512,128]{1,0:T(8,128)S(1)}) custom-call(f32[1280,128]{1,0:T(8,128)} %get-tuple-element.49.own, f32[1280,128]{1,0:T(8,128)} %collective-permute-done.6.south, f32[1280,128]{1,0:T(8,128)} %collective-permute-done.7.north, f32[1280,128]{1,0:T(8,128)} %collective-permute-done.8.fold, ...), custom_call_target="tpu_custom_call" | custom-call | flops 5000000 | bytes 1000000 | tf_op jit(solution)/shard_map/pallas_call | solution.py:46
  78.3 0.0 collective-permute-start.10
  78.4 0.5 collective-permute-start.9
  78.9 3.4 %collective-permute-start.12 = (f32[864,128]{1,0:T(8,128)S(1)}, f32[864,128]{1,0:T(8,128)S(1)}, u32[]{:S(2)}, u32[]{:S(2)}) collective-permute-start(f32[864,128]{1,0:T(8,128)S(1)} %copy-done.25), channel_id=1, source_target_pairs={{1,0},{9,8},{17,16},{25,24},{33,32},{41,40},{49,48},{57,56},{2,1},... | collective-permute-start | bytes 1327112 | tf_op jit(solution)/shard_map/ppermute | solution.py:80
  82.2 0.7 collective-permute-start.13
  82.9 2.4 %collective-permute-done.9.refs_4_ = f32[512,128]{1,0:T(8,128)S(1)} collective-permute-done((f32[512,128]{1,0:T(8,128)S(1)}, f32[512,128]{1,0:T(8,128)S(1)}, u32[]{:S(2)}, u32[]{:S(2)}) %collective-permute-start.9) | collective-permute-done | bytes 262176 | tf_op jit(solution)/shard_map/ppermute | solution.py:91
  85.4 2.2 %copy-done.5 = f32[4,16,128,128]{3,2,1,0:T(8,128)S(1)} copy-done((f32[4,16,128,128]{3,2,1,0:T(8,128)S(1)}, f32[4,16,128,128]{3,2,1,0:T(8,128)}, u32[]{:S(2)}) %copy-start.5) | copy-done | bytes 4194328
  87.6 7.6 %shard_map.121 = (f32[16,128,128]{2,1,0:T(8,128)S(1)}, f32[1024,128]{1,0:T(8,128)S(1)}, f32[1024,128]{1,0:T(8,128)S(1)}) custom-call(f32[4,16,128,128]{3,2,1,0:T(8,128)S(1)} %copy-done.5, f32[1024,128]{1,0:T(8,128)S(1)} %collective-permute-done.4.refs_1_, f32[1024,128]{1,0:T(8,128)} %collective-permute-done.5.refs_2_, ...), custom_call_target="tpu_custom_call" | custom-call | flops 40000000 | bytes 1000000 | tf_op jit(solution)/shard_map/pallas_call | solution.py:46
  95.2 3.1 %collective-permute-start.16 = (f32[1024,128]{1,0:T(8,128)S(1)}, f32[1024,128]{1,0:T(8,128)S(1)}, u32[]{:S(2)}, u32[]{:S(2)}) collective-permute-start(f32[1024,128]{1,0:T(8,128)S(1)} %get-tuple-element.61), channel_id=1, source_target_pairs={{0,1},{8,9},{16,17},{24,25},{32,33},{40,41},{48,49},{56,57},{1,2},... | collective-permute-start | bytes 1572872 | tf_op jit(solution)/shard_map/ppermute | solution.py:74
  98.3 5.1 %collective-permute-start.17 = (f32[1024,128]{1,0:T(8,128)S(1)}, f32[1024,128]{1,0:T(8,128)S(1)}, u32[]{:S(2)}, u32[]{:S(2)}) collective-permute-start(f32[1024,128]{1,0:T(8,128)S(1)} %get-tuple-element.62), channel_id=1, source_target_pairs={{1,0},{9,8},{17,16},{25,24},{33,32},{41,40},{49,48},{57,56},{2,1},... | collective-permute-start | bytes 1572872 | tf_op jit(solution)/shard_map/ppermute | solution.py:80
  103.5 0.7 collective-permute-start.18
  104.2 2.0 %shard_map.120 = (f32[3,8,128,128]{3,2,1,0:T(8,128)S(1)}, f32[480,128]{1,0:T(8,128)S(1)}, f32[480,128]{1,0:T(8,128)S(1)}) custom-call(f32[864,128]{1,0:T(8,128)S(1)} %copy-done.12, f32[864,128]{1,0:T(8,128)} %collective-permute-done.11.south.pay_up, f32[864,128]{1,0:T(8,128)S(1)} %collective-permute-done.12.north.pay_down, ...), custom_call_target="tpu_custom_call" | custom-call | flops 5000000 | bytes 1000000 | tf_op jit(solution)/shard_map/pallas_call | solution.py:46
  106.2 0.0 collective-permute-start.14
  106.2 2.9 %collective-permute-start.15 = (f32[480,128]{1,0:T(8,128)S(1)}, f32[480,128]{1,0:T(8,128)S(1)}, u32[]{:S(2)}, u32[]{:S(2)}) collective-permute-start(f32[480,128]{1,0:T(8,128)S(1)} %get-tuple-element.59), channel_id=1, source_target_pairs={{0,56},{8,0},{16,8},{24,16},{32,24},{40,32},{48,40},{56,48},{1,57}... | collective-permute-start | bytes 737288 | tf_op jit(solution)/shard_map/ppermute | solution.py:96
  109.2 9.9 %collective-permute-done.16.south = f32[1024,128]{1,0:T(8,128)S(1)} collective-permute-done((f32[1024,128]{1,0:T(8,128)S(1)}, f32[1024,128]{1,0:T(8,128)S(1)}, u32[]{:S(2)}, u32[]{:S(2)}) %collective-permute-start.16) | collective-permute-done | bytes 524320 | tf_op jit(solution)/shard_map/ppermute | solution.py:74
  119.1 2.8 %collective-permute-done.17.north = f32[1024,128]{1,0:T(8,128)S(1)} collective-permute-done((f32[1024,128]{1,0:T(8,128)S(1)}, f32[1024,128]{1,0:T(8,128)S(1)}, u32[]{:S(2)}, u32[]{:S(2)}) %collective-permute-start.17) | collective-permute-done | bytes 524320 | tf_op jit(solution)/shard_map/ppermute | solution.py:80
  121.9 1.3 shard_map.122
  123.2 0.0 collective-permute-start.19
  123.3 0.0 copy-start.23
  123.3 2.9 %collective-permute-start.20 = (f32[512,128]{1,0:T(8,128)S(1)}, f32[512,128]{1,0:T(8,128)S(1)}, u32[]{:S(2)}, u32[]{:S(2)}) collective-permute-start(f32[512,128]{1,0:T(8,128)S(1)} %get-tuple-element.65), channel_id=1, source_target_pairs={{0,56},{8,0},{16,8},{24,16},{32,24},{40,32},{48,40},{56,48},{1,57}... | collective-permute-start | bytes 786440 | tf_op jit(solution)/shard_map/ppermute | solution.py:96
  126.2 5.4 %shard_map.123 = (f32[2,32,128]{2,1,0:T(8,128)}, f32[7,32,128]{2,1,0:T(8,128)S(1)}, f32[168,128]{1,0:T(8,128)S(1)}, f32[168,128]{1,0:T(8,128)S(1)}) custom-call(f32[120,128]{1,0:T(8,128)S(1)} %collective-permute-done.up, f32[120,128]{1,0:T(8,128)S(1)} %copy-done.14, f32[120,128]{1,0:T(8,128)S(1)} %copy-done.16, f32[312,128]{1,0:T(8,128)S(1)} %collective-permute-done.2.west, ...), custom_call_target="tpu_custom_call" | custom-call | flops 8000000 | bytes 1000000 | tf_op jit(solution)/shard_map/pallas_call | solution.py:46
  131.6 3.1 %collective-permute-start.21 = (f32[168,128]{1,0:T(8,128)S(1)}, f32[168,128]{1,0:T(8,128)S(1)}, u32[]{:S(2)}, u32[]{:S(2)}) collective-permute-start(f32[168,128]{1,0:T(8,128)S(1)} %get-tuple-element.67), channel_id=1, source_target_pairs={{0,1},{8,9},{16,17},{24,25},{32,33},{40,41},{48,49},{56,57},{1,2},... | collective-permute-start | bytes 258056 | tf_op jit(solution)/shard_map/ppermute | solution.py:74
  134.7 5.2 %collective-permute-start.22 = (f32[168,128]{1,0:T(8,128)S(1)}, f32[168,128]{1,0:T(8,128)S(1)}, u32[]{:S(2)}, u32[]{:S(2)}) collective-permute-start(f32[168,128]{1,0:T(8,128)S(1)} %get-tuple-element.68), channel_id=1, source_target_pairs={{1,0},{9,8},{17,16},{25,24},{33,32},{41,40},{49,48},{57,56},{2,1},... | collective-permute-start | bytes 258056 | tf_op jit(solution)/shard_map/ppermute | solution.py:80
  139.8 0.7 collective-permute-start.23
  140.5 2.0 %collective-permute-done.22.north = f32[168,128]{1,0:T(8,128)S(1)} collective-permute-done((f32[168,128]{1,0:T(8,128)S(1)}, f32[168,128]{1,0:T(8,128)S(1)}, u32[]{:S(2)}, u32[]{:S(2)}) %collective-permute-start.22) | collective-permute-done | bytes 86048 | tf_op jit(solution)/shard_map/ppermute | solution.py:80
  142.6 0.7 shard_map.124
  143.3 0.0 collective-permute-start.24
  143.3 2.9 %collective-permute-start.25 = (f32[280,128]{1,0:T(8,128)S(1)}, f32[280,128]{1,0:T(8,128)S(1)}, u32[]{:S(2)}, u32[]{:S(2)}) collective-permute-start(f32[280,128]{1,0:T(8,128)S(1)} %get-tuple-element.71), channel_id=1, source_target_pairs={{0,56},{8,0},{16,8},{24,16},{32,24},{40,32},{48,40},{56,48},{1,57}... | collective-permute-start | bytes 430088 | tf_op jit(solution)/shard_map/ppermute | solution.py:96
  146.2 2.7 %shard_map.116 = f32[4,32,32,128]{3,2,1,0:T(8,128)} custom-call(f32[4,32,32,128]{3,2,1,0:T(8,128)S(1)} %copy-done.8, f32[32,128]{1,0:T(8,128)S(1)} %copy-done.23, f32[4,32,128]{2,1,0:T(8,128)S(1)} %copy-done.21), custom_call_target="tpu_custom_call" | custom-call | flops 5000000 | bytes 4200000 | tf_op jit(solution)/shard_map/pallas_call | solution.py:625
  148.9 0.1 collective-permute-done.24.refs_13_
  149.0 23.7 %shard_map.125 = f32[2048,128]{1,0:T(8,128)} custom-call(f32[4,16,128,128]{3,2,1,0:T(8,128)S(1)} %copy-done.6, f32[1024,128]{1,0:T(8,128)S(1)} %collective-permute-done.4.refs_1_, f32[1024,128]{1,0:T(8,128)} %collective-permute-done.5.refs_2_, f32[4,8,128,128]{3,2,1,0:T(8,128)S(1)} %get-tuple-element.51.refs_3_, ...), custom_call_target="tpu_custom_call" | custom-call | flops 80000000 | bytes 1000000 | tf_op jit(solution)/shard_map/pallas_call | solution.py:46
  (58 shorter events, 0.2 us)
Async XLA Ops:
  0.6 1.2 copy-start
  1.9 1.2 copy-start.2
  3.1 1.0 copy-start.9
  4.1 0.7 copy-start.17
  4.8 44.0 %copy-start.1 = (f32[2,32,32,128]{3,2,1,0:T(8,128)S(1)}, f32[2,32,32,128]{3,2,1,0:T(8,128)}, u32[]{:S(2)}) copy-start(f32[2,32,32,128]{3,2,1,0:T(8,128)} %tracers.3) | copy-start | bytes 3145732
  4.8 44.0 %copy-start.3 = (f32[2,32,32,128]{3,2,1,0:T(8,128)S(1)}, f32[2,32,32,128]{3,2,1,0:T(8,128)}, u32[]{:S(2)}) copy-start(f32[2,32,32,128]{3,2,1,0:T(8,128)} %flow.3) | copy-start | bytes 3145732
  4.8 44.0 %copy-start.10 = (f32[32,32,128]{2,1,0:T(8,128)S(1)}, f32[32,32,128]{2,1,0:T(8,128)}, u32[]{:S(2)}) copy-start(f32[32,32,128]{2,1,0:T(8,128)} %kappa.3) | copy-start | bytes 1572868
  4.8 44.0 %copy-start.18 = (s32[32,128]{1,0:T(8,128)S(1)}, s32[32,128]{1,0:T(8,128)}, u32[]{:S(2)}) copy-start(s32[32,128]{1,0:T(8,128)} %mask.7) | copy-start | bytes 49156
  7.3 63.2 %collective-permute-start.6 = (f32[1280,128]{1,0:T(8,128)}, f32[1280,128]{1,0:T(8,128)}, u32[]{:S(2)}, u32[]{:S(2)}) collective-permute-start(f32[1280,128]{1,0:T(8,128)} %get-tuple-element.50), channel_id=1, source_target_pairs={{0,1},{8,9},{16,17},{24,25},{32,33},{40,41},{48,49},{56,57},{1,2},... | collective-permute-start | bytes 1966088 | tf_op jit(solution)/shard_map/ppermute | solution.py:74
  13.1 44.6 %copy-start.26 = (f32[2,3,3,1024]{3,0,2,1:T(2,128)S(1)}, f32[2,3,3,1024]{3,0,2,1:T(2,128)}, u32[]{:S(2)}) copy-start(f32[2,3,3,1024]{3,0,2,1:T(2,128)} %param.17) | copy-start | bytes 221188
  13.1 62.4 %collective-permute-start.7 = (f32[1280,128]{1,0:T(8,128)}, f32[1280,128]{1,0:T(8,128)}, u32[]{:S(2)}, u32[]{:S(2)}) collective-permute-start(f32[1280,128]{1,0:T(8,128)} %get-tuple-element.49.own), channel_id=1, source_target_pairs={{1,0},{9,8},{17,16},{25,24},{33,32},{41,40},{49,48},{57,56},{2,1},... | collective-permute-start | bytes 1966088 | tf_op jit(solution)/shard_map/ppermute | solution.py:80
  15.7 59.8 %collective-permute-start.8 = (f32[1280,128]{1,0:T(8,128)}, f32[1280,128]{1,0:T(8,128)}, u32[]{:S(2)}, u32[]{:S(2)}) collective-permute-start(f32[1280,128]{1,0:T(8,128)} %get-tuple-element.50), channel_id=1, source_target_pairs={{71,127},{79,119},{87,111},{95,103},{103,95},{111,87},{119,79},{12... | collective-permute-start | bytes 1966088 | tf_op jit(solution)/shard_map/ppermute | solution.py:86
  18.8 25.3 %collective-permute-start = (f32[120,128]{1,0:T(8,128)}, f32[120,128]{1,0:T(8,128)S(1)}, u32[]{:S(2)}, u32[]{:S(2)}) collective-permute-start(f32[120,128]{1,0:T(8,128)} %get-tuple-element.38), channel_id=1, source_target_pairs={{0,1},{8,9},{16,17},{24,25},{32,33},{40,41},{48,49},{56,57},{1,2},... | collective-permute-start | bytes 184328 | tf_op jit(solution)/shard_map/ppermute | solution.py:74
  23.7 21.3 %collective-permute-start.1 = (f32[120,128]{1,0:T(8,128)}, f32[120,128]{1,0:T(8,128)S(1)}, u32[]{:S(2)}, u32[]{:S(2)}) collective-permute-start(f32[120,128]{1,0:T(8,128)} %get-tuple-element.40), channel_id=1, source_target_pairs={{1,0},{9,8},{17,16},{25,24},{33,32},{41,40},{49,48},{57,56},{2,1},... | collective-permute-start | bytes 184328 | tf_op jit(solution)/shard_map/ppermute | solution.py:80
  45.0 13.5 %copy-start.15 = (f32[120,128]{1,0:T(8,128)}, f32[120,128]{1,0:T(8,128)S(1)}, u32[]{:S(2)}) copy-start(f32[120,128]{1,0:T(8,128)S(1)} %collective-permute-done.1.down) | copy-start | bytes 184324
  45.0 0.9 copy-start.13
  45.9 8.9 %collective-permute-start.2 = (f32[312,128]{1,0:T(8,128)S(1)}, f32[312,128]{1,0:T(8,128)S(1)}, u32[]{:S(2)}, u32[]{:S(2)}) collective-permute-start(f32[312,128]{1,0:T(8,128)S(1)} %get-tuple-element.41), channel_id=1, source_target_pairs={{0,8},{8,16},{16,24},{24,32},{32,40},{40,48},{48,56},{56,0},{1,9},... | collective-permute-start | bytes 479240 | tf_op jit(solution)/shard_map/ppermute | solution.py:91
  45.9 12.6 %copy-start.7 = (f32[4,32,32,128]{3,2,1,0:T(8,128)S(1)}, f32[4,32,32,128]{3,2,1,0:T(8,128)}, u32[]{:S(2)}) copy-start(f32[4,32,32,128]{3,2,1,0:T(8,128)} %state.1) | copy-start | bytes 6291460
  45.9 12.6 %copy-start.19 = (s32[3,3,1024]{2,1,0:T(4,128)S(1)}, s32[3,3,1024]{2,1,0:T(4,128)}, u32[]{:S(2)}) copy-start(s32[3,3,1024]{2,1,0:T(4,128)} %sea_cells.1) | copy-start | bytes 110596
  45.9 12.6 %copy-start.22 = (s32[3,3,1024]{2,1,0:T(4,128)S(1)}, s32[3,3,1024]{2,1,0:T(4,128)}, u32[]{:S(2)}) copy-start(s32[3,3,1024]{2,1,0:T(4,128)} %air_cells.1) | copy-start | bytes 110596
  45.9 8.9 %collective-permute-start.3 = (f32[312,128]{1,0:T(8,128)S(1)}, f32[312,128]{1,0:T(8,128)S(1)}, u32[]{:S(2)}, u32[]{:S(2)}) collective-permute-start(f32[312,128]{1,0:T(8,128)S(1)} %get-tuple-element.42), channel_id=1, source_target_pairs={{0,56},{8,0},{16,8},{24,16},{32,24},{40,32},{48,40},{56,48},{1,57}... | collective-permute-start | bytes 479240 | tf_op jit(solution)/shard_map/ppermute | solution.py:96
  52.8 2.0 %copy-start.4 = (f32[4,16,128,128]{3,2,1,0:T(8,128)}, f32[4,16,128,128]{3,2,1,0:T(8,128)S(1)}, u32[]{:S(2)}) copy-start(f32[4,16,128,128]{3,2,1,0:T(8,128)S(1)} %get-tuple-element.46.refs_0_) | copy-start | bytes 12582916
  54.8 24.1 %collective-permute-start.4 = (f32[1024,128]{1,0:T(8,128)}, f32[1024,128]{1,0:T(8,128)S(1)}, u32[]{:S(2)}, u32[]{:S(2)}) collective-permute-start(f32[1024,128]{1,0:T(8,128)} %get-tuple-element.47), channel_id=1, source_target_pairs={{0,8},{8,16},{16,24},{24,32},{32,40},{40,48},{48,56},{56,0},{1,9},... | collective-permute-start | bytes 1572872 | tf_op jit(solution)/shard_map/ppermute | solution.py:91
  54.8 27.5 %collective-permute-start.5 = (f32[1024,128]{1,0:T(8,128)}, f32[1024,128]{1,0:T(8,128)}, u32[]{:S(2)}, u32[]{:S(2)}) collective-permute-start(f32[1024,128]{1,0:T(8,128)} %get-tuple-element.48), channel_id=1, source_target_pairs={{0,56},{8,0},{16,8},{24,16},{32,24},{40,32},{48,40},{56,48},{1,57}... | collective-permute-start | bytes 1572872 | tf_op jit(solution)/shard_map/ppermute | solution.py:96
  68.4 0.8 copy-start.11
  69.2 0.6 copy-start.20
  69.8 0.7 copy-start.24
  70.6 32.9 %collective-permute-start.11 = (f32[864,128]{1,0:T(8,128)}, f32[864,128]{1,0:T(8,128)}, u32[]{:S(2)}, u32[]{:S(2)}) collective-permute-start(f32[864,128]{1,0:T(8,128)} %get-tuple-element.55), channel_id=1, source_target_pairs={{0,1},{8,9},{16,17},{24,25},{32,33},{40,41},{48,49},{56,57},{1,2},... | collective-permute-start | bytes 1327112 | tf_op jit(solution)/shard_map/ppermute | solution.py:74
  75.4 3.4 %copy-start.25 = (f32[864,128]{1,0:T(8,128)S(1)}, f32[864,128]{1,0:T(8,128)}, u32[]{:S(2)}) copy-start(f32[864,128]{1,0:T(8,128)} %copy-done.24) | copy-start | bytes 1327108
  78.3 4.6 %collective-permute-start.10 = (f32[512,128]{1,0:T(8,128)S(1)}, f32[512,128]{1,0:T(8,128)S(1)}, u32[]{:S(2)}, u32[]{:S(2)}) collective-permute-start(f32[512,128]{1,0:T(8,128)S(1)} %get-tuple-element.53), channel_id=1, source_target_pairs={{0,56},{8,0},{16,8},{24,16},{32,24},{40,32},{48,40},{56,48},{1,57}... | collective-permute-start | bytes 786440 | tf_op jit(solution)/shard_map/ppermute | solution.py:96
  78.4 7.0 %collective-permute-start.9 = (f32[512,128]{1,0:T(8,128)S(1)}, f32[512,128]{1,0:T(8,128)S(1)}, u32[]{:S(2)}, u32[]{:S(2)}) collective-permute-start(f32[512,128]{1,0:T(8,128)S(1)} %get-tuple-element.52), channel_id=1, source_target_pairs={{0,8},{8,16},{16,24},{24,32},{32,40},{40,48},{48,56},{56,0},{1,9},... | collective-permute-start | bytes 786440 | tf_op jit(solution)/shard_map/ppermute | solution.py:91
  78.9 25.3 %collective-permute-start.12 = (f32[864,128]{1,0:T(8,128)S(1)}, f32[864,128]{1,0:T(8,128)S(1)}, u32[]{:S(2)}, u32[]{:S(2)}) collective-permute-start(f32[864,128]{1,0:T(8,128)S(1)} %copy-done.25), channel_id=1, source_target_pairs={{1,0},{9,8},{17,16},{25,24},{33,32},{41,40},{49,48},{57,56},{2,1},... | collective-permute-start | bytes 1327112 | tf_op jit(solution)/shard_map/ppermute | solution.py:80
  82.2 21.9 %collective-permute-start.13 = (f32[864,128]{1,0:T(8,128)}, f32[864,128]{1,0:T(8,128)S(1)}, u32[]{:S(2)}, u32[]{:S(2)}) collective-permute-start(f32[864,128]{1,0:T(8,128)} %get-tuple-element.55), channel_id=1, source_target_pairs={{71,127},{79,119},{87,111},{95,103},{103,95},{111,87},{119,79},{12... | collective-permute-start | bytes 1327112 | tf_op jit(solution)/shard_map/ppermute | solution.py:86
  85.4 2.2 %copy-start.5 = (f32[4,16,128,128]{3,2,1,0:T(8,128)S(1)}, f32[4,16,128,128]{3,2,1,0:T(8,128)}, u32[]{:S(2)}) copy-start(f32[4,16,128,128]{3,2,1,0:T(8,128)} %copy-done.4) | copy-start | bytes 12582916
  87.6 16.6 %copy-start.12 = (f32[864,128]{1,0:T(8,128)S(1)}, f32[864,128]{1,0:T(8,128)}, u32[]{:S(2)}) copy-start(f32[864,128]{1,0:T(8,128)} %copy-done.11) | copy-start | bytes 1327108
  95.2 23.9 %collective-permute-start.16 = (f32[1024,128]{1,0:T(8,128)S(1)}, f32[1024,128]{1,0:T(8,128)S(1)}, u32[]{:S(2)}, u32[]{:S(2)}) collective-permute-start(f32[1024,128]{1,0:T(8,128)S(1)} %get-tuple-element.61), channel_id=1, source_target_pairs={{0,1},{8,9},{16,17},{24,25},{32,33},{40,41},{48,49},{56,57},{1,2},... | collective-permute-start | bytes 1572872 | tf_op jit(solution)/shard_map/ppermute | solution.py:74
  98.3 23.6 %collective-permute-start.17 = (f32[1024,128]{1,0:T(8,128)S(1)}, f32[1024,128]{1,0:T(8,128)S(1)}, u32[]{:S(2)}, u32[]{:S(2)}) collective-permute-start(f32[1024,128]{1,0:T(8,128)S(1)} %get-tuple-element.62), channel_id=1, source_target_pairs={{1,0},{9,8},{17,16},{25,24},{33,32},{41,40},{49,48},{57,56},{2,1},... | collective-permute-start | bytes 1572872 | tf_op jit(solution)/shard_map/ppermute | solution.py:80
  103.5 18.4 %collective-permute-start.18 = (f32[1024,128]{1,0:T(8,128)S(1)}, f32[1024,128]{1,0:T(8,128)S(1)}, u32[]{:S(2)}, u32[]{:S(2)}) collective-permute-start(f32[1024,128]{1,0:T(8,128)S(1)} %get-tuple-element.61), channel_id=1, source_target_pairs={{71,127},{79,119},{87,111},{95,103},{103,95},{111,87},{119,79},{12... | collective-permute-start | bytes 1572872 | tf_op jit(solution)/shard_map/ppermute | solution.py:86
  104.2 22.0 %copy-start.14 = (f32[120,128]{1,0:T(8,128)S(1)}, f32[120,128]{1,0:T(8,128)}, u32[]{:S(2)}) copy-start(f32[120,128]{1,0:T(8,128)} %get-tuple-element.39.mine) | copy-start | bytes 184324
  104.2 22.0 %copy-start.16 = (f32[120,128]{1,0:T(8,128)S(1)}, f32[120,128]{1,0:T(8,128)}, u32[]{:S(2)}) copy-start(f32[120,128]{1,0:T(8,128)} %copy-done.15) | copy-start | bytes 184324
  106.2 20.0 %collective-permute-start.14 = (f32[480,128]{1,0:T(8,128)S(1)}, f32[480,128]{1,0:T(8,128)S(1)}, u32[]{:S(2)}, u32[]{:S(2)}) collective-permute-start(f32[480,128]{1,0:T(8,128)S(1)} %get-tuple-element.58), channel_id=1, source_target_pairs={{0,8},{8,16},{16,24},{24,32},{32,40},{40,48},{48,56},{56,0},{1,9},... | collective-permute-start | bytes 737288 | tf_op jit(solution)/shard_map/ppermute | solution.py:91
  106.2 20.0 %collective-permute-start.15 = (f32[480,128]{1,0:T(8,128)S(1)}, f32[480,128]{1,0:T(8,128)S(1)}, u32[]{:S(2)}, u32[]{:S(2)}) collective-permute-start(f32[480,128]{1,0:T(8,128)S(1)} %get-tuple-element.59), channel_id=1, source_target_pairs={{0,56},{8,0},{16,8},{24,16},{32,24},{40,32},{48,40},{56,48},{1,57}... | collective-permute-start | bytes 737288 | tf_op jit(solution)/shard_map/ppermute | solution.py:96
  123.2 25.8 %collective-permute-start.19 = (f32[512,128]{1,0:T(8,128)S(1)}, f32[512,128]{1,0:T(8,128)S(1)}, u32[]{:S(2)}, u32[]{:S(2)}) collective-permute-start(f32[512,128]{1,0:T(8,128)S(1)} %get-tuple-element.64), channel_id=1, source_target_pairs={{0,8},{8,16},{16,24},{24,32},{32,40},{40,48},{48,56},{56,0},{1,9},... | collective-permute-start | bytes 786440 | tf_op jit(solution)/shard_map/ppermute | solution.py:91
  123.3 23.0 %copy-start.8 = (f32[4,32,32,128]{3,2,1,0:T(8,128)S(1)}, f32[4,32,32,128]{3,2,1,0:T(8,128)}, u32[]{:S(2)}) copy-start(f32[4,32,32,128]{3,2,1,0:T(8,128)} %state.1) | copy-start | bytes 6291460
  123.3 23.0 %copy-start.21 = (f32[4,32,128]{2,1,0:T(8,128)S(1)}, f32[4,32,128]{2,1,0:T(8,128)}, u32[]{:S(2)}) copy-start(f32[4,32,128]{2,1,0:T(8,128)} %copy-done.20) | copy-start | bytes 196612
  123.3 23.0 %copy-start.23 = (f32[32,128]{1,0:T(8,128)S(1)}, f32[32,128]{1,0:T(8,128)}, u32[]{:S(2)}) copy-start(f32[32,128]{1,0:T(8,128)} %kappa.2) | copy-start | bytes 49156
  123.3 25.7 %collective-permute-start.20 = (f32[512,128]{1,0:T(8,128)S(1)}, f32[512,128]{1,0:T(8,128)S(1)}, u32[]{:S(2)}, u32[]{:S(2)}) collective-permute-start(f32[512,128]{1,0:T(8,128)S(1)} %get-tuple-element.65), channel_id=1, source_target_pairs={{0,56},{8,0},{16,8},{24,16},{32,24},{40,32},{48,40},{56,48},{1,57}... | collective-permute-start | bytes 786440 | tf_op jit(solution)/shard_map/ppermute | solution.py:96
  131.6 8.9 %collective-permute-start.21 = (f32[168,128]{1,0:T(8,128)S(1)}, f32[168,128]{1,0:T(8,128)S(1)}, u32[]{:S(2)}, u32[]{:S(2)}) collective-permute-start(f32[168,128]{1,0:T(8,128)S(1)} %get-tuple-element.67), channel_id=1, source_target_pairs={{0,1},{8,9},{16,17},{24,25},{32,33},{40,41},{48,49},{56,57},{1,2},... | collective-permute-start | bytes 258056 | tf_op jit(solution)/shard_map/ppermute | solution.py:74
  134.7 7.9 %collective-permute-start.22 = (f32[168,128]{1,0:T(8,128)S(1)}, f32[168,128]{1,0:T(8,128)S(1)}, u32[]{:S(2)}, u32[]{:S(2)}) collective-permute-start(f32[168,128]{1,0:T(8,128)S(1)} %get-tuple-element.68), channel_id=1, source_target_pairs={{1,0},{9,8},{17,16},{25,24},{33,32},{41,40},{49,48},{57,56},{2,1},... | collective-permute-start | bytes 258056 | tf_op jit(solution)/shard_map/ppermute | solution.py:80
  139.8 2.7 %collective-permute-start.23 = (f32[168,128]{1,0:T(8,128)S(1)}, f32[168,128]{1,0:T(8,128)S(1)}, u32[]{:S(2)}, u32[]{:S(2)}) collective-permute-start(f32[168,128]{1,0:T(8,128)S(1)} %get-tuple-element.67), channel_id=1, source_target_pairs={{71,127},{79,119},{87,111},{95,103},{103,95},{111,87},{119,79},{12... | collective-permute-start | bytes 258056 | tf_op jit(solution)/shard_map/ppermute | solution.py:86
  143.3 5.7 %collective-permute-start.24 = (f32[280,128]{1,0:T(8,128)S(1)}, f32[280,128]{1,0:T(8,128)S(1)}, u32[]{:S(2)}, u32[]{:S(2)}) collective-permute-start(f32[280,128]{1,0:T(8,128)S(1)} %get-tuple-element.70), channel_id=1, source_target_pairs={{0,8},{8,16},{16,24},{24,32},{32,40},{40,48},{48,56},{56,0},{1,9},... | collective-permute-start | bytes 430088 | tf_op jit(solution)/shard_map/ppermute | solution.py:91
  143.3 5.7 %collective-permute-start.25 = (f32[280,128]{1,0:T(8,128)S(1)}, f32[280,128]{1,0:T(8,128)S(1)}, u32[]{:S(2)}, u32[]{:S(2)}) collective-permute-start(f32[280,128]{1,0:T(8,128)S(1)} %get-tuple-element.71), channel_id=1, source_target_pairs={{0,56},{8,0},{16,8},{24,16},{32,24},{40,32},{48,40},{56,48},{1,57}... | collective-permute-start | bytes 430088 | tf_op jit(solution)/shard_map/ppermute | solution.py:96
  146.2 2.8 %copy-start.6 = (f32[4,16,128,128]{3,2,1,0:T(8,128)S(1)}, f32[4,16,128,128]{3,2,1,0:T(8,128)}, u32[]{:S(2)}) copy-start(f32[4,16,128,128]{3,2,1,0:T(8,128)} %copy-done.4) | copy-start | bytes 12582916

commit v5 on v4

--- a/solution.py
+++ b/solution.py
@@ -21,18 +21,16 @@
 LV = 32
 RW = 32
 CL = 128
-NEAR = 8
-FULL = 16
+HALO = 12
+SIDE = 16
 EDGE = 24
 WIDTH = 176
 DEEP = ITERS
 SR = RW + 2 * DEEP
-VALS = 3 * RW
+SEA = 3 * RW
+VALS = SEA + 4 * RW
 LINES = 8
-DEEP_LINES = (RW // 2 + FULL) * FULL
-FAR_LINES = NEAR * 3 * LV
-FAR_COLS = 3 * NEAR * FULL
-EDGE_MIB, OWN_MIB, FIRST_MIB, FINAL_MIB, FLUX_MIB = 12, 14, 15, 20, 10
+EDGE_MIB, OWN_MIB, FIRST_MIB, FINAL_MIB, FLUX_MIB = 12, 14, 17, 19, 10
 
 
 VMEM = pl.BlockSpec(memory_space=pltpu.VMEM)
@@ -105,23 +103,23 @@
     return ref[pl.ds(base + row, LV, stride=RW), :]
 
 
-def edge_kernel(start, tracers, flow, kappa, mask, top, bottom):
+def edge_kernel(tracers, flow, kappa, mask, top, bottom):
     def body(k, carry):
-        for out, row in ((bottom, start + k), (top, RW - 1 - start - k)):
+        for out, row in ((bottom, k), (top, RW - 1 - k)):
             sea = mask[pl.ds(row, 1), :].astype(F32)
-            parts = [
+            parts = (
+                level_rows(tracers, 0, row),
+                level_rows(tracers, LV * RW, row),
                 sea * level_rows(flow, 0, row),
                 sea * level_rows(flow, LV * RW, row),
                 sea * level_rows(kappa, 0, row),
-            ]
-            if start == 0:
-                parts = [level_rows(tracers, 0, row), level_rows(tracers, LV * RW, row)] + parts
+            )
             for f, part in enumerate(parts):
                 where = pl.multiple_of((k * len(parts) + f) * LV, LV)
                 out[pl.ds(where, LV), :] = part
         return carry
 
-    lax.fori_loop(0, NEAR, body, 0)
+    lax.fori_loop(0, HALO, body, 0)
 
 
 def columns(low, high, sign=1.0):
@@ -131,16 +129,14 @@
 
 
 def emit_columns(i, low, high, x, mw, me):
-    parts = []
-    if len(low) == 5:
-        parts.append(columns((low[0], low[1]), (high[0], high[1])))
-    for f, sign in ((-3, 1.0), (-2, -1.0), (-1, 1.0)):
+    parts = [columns((low[0], low[1]), (high[0], high[1]))]
+    for f, sign in ((2, 1.0), (3, -1.0), (4, 1.0)):
         parts.append(columns((low[f],) * 2, (high[f],) * 2, sign))
     for f, t in enumerate(parts):
-        rows = pl.ds(pl.multiple_of((f * x.shape[1] + i) * FULL, FULL), FULL)
+        rows = pl.ds(pl.multiple_of((f * x.shape[1] + i) * SIDE, SIDE), SIDE)
         x[f, i] = t
-        mw[rows, :] = t[:FULL]
-        me[rows, :] = t[CL - FULL :]
+        mw[rows, :] = t[:SIDE]
+        me[rows, :] = t[CL - SIDE :]
 
 
 def own_kernel(tracers, flow, kappa, mask, x, mw, me):
@@ -165,7 +161,7 @@
     lax.fori_loop(0, RW // 4, inner, 0)
 
 
-def halo_kernel(count, own, south, north, fold, flags, x, mw, me):
+def halo_kernel(own, south, north, fold, flags, x, mw, me):
     first = flags[0] > 0
     last = flags[1] > 0
 
@@ -173,40 +169,28 @@
         for n in range(2):
             i = 2 * p + n
             low, high = [], []
-            for f in range(count):
-                part = pl.ds(pl.multiple_of(((NEAR - 1 - i) * count + f) * LV, LV), LV)
+            for f in range(5):
+                part = pl.ds(pl.multiple_of(((HALO - 1 - i) * 5 + f) * LV, LV), LV)
                 mirror = own[part, :]
                 turned = reversed_lanes(fold[part, :])
-                if f == count - 2:
+                if f == 3:
                     mirror = -mirror
-                if f in (count - 3, count - 2):
+                if f in (2, 3):
                     turned = -turned
                 low.append(jnp.where(first, mirror, south[part, :]))
                 high.append(jnp.where(last, turned, north[part, :]))
             emit_columns(i, low, high, x, mw, me)
         return carry
 
-    lax.fori_loop(0, NEAR // 2, halo, 0)
-
-
-def far_halo_kernel(own, south, north, fold, flags, x, mw, me):
-    halo_kernel(3, own, south, north, fold, flags, x, mw, me)
-    for a, source in enumerate((south, own, north)):
-        for f in range(4):
-            for out, b in ((me, 2), (mw, 0)):
-                line = FAR_LINES + (f * 3 + b) * LINES
-                to = FAR_COLS + (a * 4 + f) * LINES
-                out[to : to + LINES] = source[line : line + LINES]
+    lax.fori_loop(0, HALO // 2, halo, 0)
 
 
 def deep_kernel(final, *refs):
-    halo = FULL if final else NEAR
+    halo = HALO
     xo, wo, eo, xn, wn, en = refs[:6]
     if final:
-        xf, wf, ef, xts, w2, e2, mine, w3, e3, out = refs[6:16]
-        scratch = refs[16:]
-        surface_steps(mine, w3, e3, out, scratch[6:])
-        scratch = scratch[:6]
+        xts, w2, e2, surface, out = refs[6:11]
+        scratch = refs[11:]
     else:
         state, top, bottom = refs[6:9]
         scratch = refs[9:]
@@ -225,37 +209,35 @@
         cu[i, where] = jnp.maximum(-v, 0.0) + k
 
     def fill(x, w, e, start):
-        lead = x.shape[0] - 3
+        lead = 1
 
         def body(p, carry):
             for n in range(2):
                 i = 2 * p + n
                 lines = [
-                    pl.ds(pl.multiple_of((f * x.shape[1] + i) * FULL, FULL), FULL)
+                    pl.ds(pl.multiple_of((f * x.shape[1] + i) * SIDE, SIDE), SIDE)
                     for f in range(lead + 3)
                 ]
                 to = start + i
                 coefficients(to, mid, x[lead, i], x[lead + 1, i], x[lead + 2, i])
-                west = [w[lines[lead + f], :][FULL - halo :] for f in range(3)]
+                west = [w[lines[lead + f], :][SIDE - halo :] for f in range(3)]
                 east = [e[lines[lead + f], :][:halo] for f in range(3)]
                 coefficients(to, west_cols, *west)
                 coefficients(to, east_cols, *east)
                 if final:
-                    rows = pl.ds(pl.multiple_of(to * FULL, FULL), FULL)
+                    rows = pl.ds(pl.multiple_of(to * SIDE, SIDE), SIDE)
                     s0[to, mid] = xts[to]
-                    s0[to, west_cols] = w2[rows, :]
-                    s0[to, east_cols] = e2[rows, :]
+                    s0[to, west_cols] = w2[rows, :][SIDE - halo :]
+                    s0[to, east_cols] = e2[rows, :][:halo]
                 else:
                     s0[to, mid] = x[0, i]
-                    s0[to, west_cols] = w[lines[0], :][FULL - halo :]
+                    s0[to, west_cols] = w[lines[0], :][SIDE - halo :]
                     s0[to, east_cols] = e[lines[0], :][:halo]
             return carry
 
         lax.fori_loop(0, x.shape[1] // 2, body, 0)
 
-    if final:
-        fill(xf, wf, ef, 0)
-    fill(xn, wn, en, halo - NEAR)
+    fill(xn, wn, en, 0)
     fill(xo, wo, eo, halo)
 
     def at(ref, i, j):
@@ -310,11 +292,13 @@
             return carry
 
         lax.fori_loop(0, RW // 2, write, 0)
+        for tracer in range(2):
+            out[tracer * LV * RW : tracer * LV * RW + RW] = surface[tracer]
     else:
         low = lax.broadcasted_iota(jnp.int32, (CL, CL), 1) < CL // 2
         for i in range(RW // 2):
             state[i] = s0[i + halo, mid]
-        half = FULL // 2
+        half = HALO // 2
         for k in range(half):
             near, far = s0[halo + k, mid], s0[halo + k + half, mid]
             where = slice(k * CL, (k + 1) * CL)
@@ -326,7 +310,7 @@
     first = flags[0] > 0
     last = flags[1] > 0
     low = lax.broadcasted_iota(jnp.int32, (CL, CL), 1) < CL // 2
-    half = FULL // 2
+    half = HALO // 2
     flip = jnp.where(
         lax.broadcasted_iota(jnp.int32, (CL, CL), 0)
         + lax.broadcasted_iota(jnp.int32, (CL, CL), 1)
@@ -336,7 +320,7 @@
     ).astype(F32)
     rows = {}
     for i in range(RW // 2):
-        rows[FULL + i] = state[i]
+        rows[HALO + i] = state[i]
     for k in range(half):
         where = slice(k * CL, (k + 1) * CL)
         s, n = south[where], north[where]
@@ -345,13 +329,13 @@
         for kk, sv, nv, fv in ((k, s, n_roll, f_roll), (k + half, s_roll, n, f)):
             down = jnp.where(first, state[kk], sv)
             up = jnp.where(last, fv, nv)
-            rows[FULL - 1 - kk] = jnp.where(low, down, up)
-    count = RW // 2 + FULL
+            rows[HALO - 1 - kk] = jnp.where(low, down, up)
+    count = RW // 2 + HALO
     for i in range(count):
-        where = pl.ds(i * FULL, FULL)
+        where = pl.ds(i * SIDE, SIDE)
         xts[i] = rows[i]
-        mw[where, :] = rows[i][:FULL]
-        me[where, :] = rows[i][CL - FULL :]
+        mw[where, :] = rows[i][:SIDE]
+        me[where, :] = rows[i][CL - SIDE :]
 
 
 def surface_join_kernel(fields, south, north, fold, flags, joined, mw, me):
@@ -386,8 +370,7 @@
         me[where] = jnp.where(low, pltpu.roll(a, CL // 2, 1), b)
 
 
-def surface_steps(mine, w2, e2, out, scratch):
-    cw, ce, cs, cn, cf = scratch
+def surface_kernel(mine, w2, e2, out, cw, ce, cs, cn, cf):
     low = lax.broadcasted_iota(jnp.int32, (SR // 2, CL), 1) < CL // 2
 
     def wide(f):
@@ -424,7 +407,7 @@
 
     pair = lax.fori_loop(0, ITERS, step, (wide(0), wide(1)))
     for t in range(2):
-        out[t * LV * RW : t * LV * RW + RW] = pair[t][DEEP : DEEP + RW, 0:CL]
+        out[t] = pair[t][DEEP : DEEP + RW, 0:CL]
 
 
 def split3(value):
@@ -435,17 +418,29 @@
     return a, b, c
 
 
-def one_hots(cells):
-    n = cells.shape[1]
-    column = jnp.bitwise_and(cells, CL - 1)
+def lane_blocks(value):
+    return [value[:, n : n + CL] for n in range(0, value.shape[1], CL)]
+
+
+def column_hot(cells, index):
+    column = jnp.bitwise_and(cells, CL - 1).astype(F32).astype(BF16)
+    one, zero = jnp.ones_like(index), jnp.zeros_like(index)
+    return jnp.concatenate(
+        [jnp.where(index == part, one, zero) for part in lane_blocks(column)], axis=1
+    )
+
+
+def row_mask(cells):
     row = jnp.right_shift(cells, 7)
-    hot = jnp.where(lax.broadcasted_iota(jnp.int32, (CL, n), 0) == column, 1.0, 0.0).astype(BF16)
-    return hot, lax.broadcasted_iota(jnp.int32, (RW, n), 0) == row
+    return lax.broadcasted_iota(jnp.int32, (RW, cells.shape[1]), 0) == row
 
 
 def gather(table, hot, mask):
-    parts = split3(table)
-    got = sum(jnp.dot(p, hot, preferred_element_type=F32) for p in parts)
+    got = jnp.dot(
+        jnp.concatenate(split3(table), axis=1),
+        jnp.concatenate([hot] * 3, axis=0),
+        preferred_element_type=F32,
+    )
     return [
         jnp.sum(jnp.where(mask, got[f * RW : (f + 1) * RW], 0.0), axis=0, keepdims=True)
         for f in range(table.shape[0] // RW)
@@ -454,11 +449,8 @@
 
 def scatter(values, hot, mask):
     parts = [split3(v) for v in values]
-    rows = [
-        jnp.where(mask, parts[f][s].astype(F32), 0.0).astype(BF16)
-        for s in range(3)
-        for f in range(len(values))
-    ]
+    where = jnp.where(mask, 1.0, 0.0).astype(BF16)
+    rows = [where * parts[f][s] for s in range(3) for f in range(len(values))]
     return lax.dot_general(
         jnp.concatenate(rows, axis=0), hot, (((1,), (1,)), ((), ())), preferred_element_type=F32
     )
@@ -483,50 +475,46 @@
     ]
 
 
-def spread_kernel(tracers, flow, cells, up, mine, down):
+def spread_kernel(tracers, flow, state, sea_cells, air_cells, weights, up, mine, down):
     for out, a in ((up, 2), (mine, 1), (down, 0)):
         out[0:RW] = tracers[0, 0]
         out[RW : 2 * RW] = flow[0, 0]
-        out[2 * RW : 3 * RW] = flow[1, 0]
+        out[2 * RW : SEA] = flow[1, 0]
+        for f in range(4):
+            out[SEA + f * RW : SEA + (f + 1) * RW] = state[f, 0]
         for b in range(3):
-            run = cells[a, b : b + 1, :].astype(F32)
-            for n in range(run.shape[1] // CL):
-                line = VALS + b * LINES + n
-                out[line : line + 1] = run[:, n * CL : (n + 1) * CL]
+            runs = (
+                sea_cells[a, b : b + 1, :].astype(F32),
+                air_cells[a, b : b + 1, :].astype(F32),
+                weights[a, b, 1:2, :],
+            )
+            for k, run in enumerate(runs):
+                for n, part in enumerate(lane_blocks(run)):
+                    line = VALS + (k * 3 + b) * LINES + n
+                    out[line : line + 1] = part
 
 
 def relay_kernel(up, mine, down, east, west):
     for a, source in enumerate((up, mine, down)):
         for out, b in ((east, 2), (west, 0)):
             out[a * VALS : (a + 1) * VALS] = source[0:VALS]
-            line = VALS + b * LINES
-            out[3 * VALS + a * LINES : 3 * VALS + (a + 1) * LINES] = source[line : line + LINES]
-
-
-def flux_kernel(
-    air, up, mine, down, west, east, air_cells, sea_cells, weights, far_top, far_bottom,
-    flux, north, own, south, vals, sea,
-):
-    for a, source in enumerate((up, mine, down)):
-        sea[3 * a] = west[a * VALS : (a + 1) * VALS]
-        sea[3 * a + 1] = source[0:VALS]
-        sea[3 * a + 2] = east[a * VALS : (a + 1) * VALS]
-    table = jnp.concatenate([air[f, 0] for f in range(4)], axis=0)
-
-    def run(ref, q):
-        return ref[lax.div(q, 3), pl.ds(lax.rem(q, 3), 1), :]
+            for k in range(3):
+                line = VALS + (k * 3 + b) * LINES
+                to = 3 * VALS + (a * 3 + k) * LINES
+                out[to : to + LINES] = source[line : line + LINES]
+
+
+def summed_fluxes(air, sea, air_cells, sea_cells, weight, onto_air, vals):
+    index = lax.broadcasted_iota(jnp.int32, (CL, CL), 0).astype(F32).astype(BF16)
 
     def look(q, carry):
-        hot, mask = one_hots(run(air_cells, q))
-        for f, v in enumerate(gather(table, hot, mask)):
+        cells = air_cells(q)
+        for f, v in enumerate(gather(air(q), column_hot(cells, index), row_mask(cells))):
             vals[f, pl.ds(q, 1), :] = v
-        hot, mask = one_hots(run(sea_cells, q))
-        for f, v in enumerate(gather(sea[q], hot, mask)):
+        cells = sea_cells(q)
+        for f, v in enumerate(gather(sea(q), column_hot(cells, index), row_mask(cells))):
             vals[4 + f, pl.ds(q, 1), :] = v
-        for n in range(2):
-            vals[7 + n, pl.ds(q, 1), :] = weights[
-                n, lax.div(q, 3), pl.ds(lax.rem(q, 3), 1), :
-            ]
+        vals[7, pl.ds(q, 1), :] = weight(q)
         return carry
 
     lax.fori_loop(0, 9, look, 0)
@@ -534,58 +522,73 @@
         [vals[f, 0:9] for f in range(4)],
         [vals[4, 0:9], current_scale * vals[5, 0:9], current_scale * vals[6, 0:9]],
     )
-    north[0:FAR_LINES] = far_top[...]
-    south[0:FAR_LINES] = far_bottom[...]
-    own[0:FAR_LINES] = far_bottom[...]
     for f in range(4):
-        pay = vals[8, 0:9] * fluxes[f]
-        for a, out in enumerate((south, own, north)):
-            for b in range(3):
-                for n in range(LINES):
-                    line = FAR_LINES + (f * 3 + b) * LINES + n
-                    out[line : line + 1] = pay[3 * a + b : 3 * a + b + 1, n * CL : (n + 1) * CL]
         vals[f, 0:9] = vals[7, 0:9] * fluxes[f]
 
     def place(q, total):
-        hot, mask = one_hots(run(air_cells, q))
-        return total + scatter([vals[f, pl.ds(q, 1), :] for f in range(4)], hot, mask)
+        cells = (air_cells if onto_air else sea_cells)(q)
+        rows = [vals[f, pl.ds(q, 1), :] for f in range(4)]
+        return total + scatter(rows, column_hot(cells, index), row_mask(cells))
 
     total = lax.fori_loop(0, 9, place, jnp.zeros((12 * RW, CL), F32))
     total = total[0 : 4 * RW] + total[4 * RW : 8 * RW] + total[8 * RW :]
+    return [total[f * RW : (f + 1) * RW] for f in range(4)]
+
+
+def air_flux_kernel(up, mine, down, west, east, air_cells, sea_cells, weights, flux, vals, sea):
+    for a, source in enumerate((up, mine, down)):
+        sea[3 * a] = west[a * VALS : a * VALS + SEA]
+        sea[3 * a + 1] = source[0:SEA]
+        sea[3 * a + 2] = east[a * VALS : a * VALS + SEA]
+
+    def run(ref):
+        return lambda q: ref[lax.div(q, 3), pl.ds(lax.rem(q, 3), 1), :]
+
+    parts = summed_fluxes(
+        lambda q: mine[SEA:VALS],
+        lambda q: sea[q],
+        run(air_cells),
+        run(sea_cells),
+        lambda q: weights[lax.div(q, 3), lax.rem(q, 3), 0:1, :],
+        True,
+        vals,
+    )
     for f in range(4):
-        flux[f] = total[f * RW : (f + 1) * RW]
-
-
-def ocean_flux_kernel(
-    up, mine, down, west, east, pay_up, pay_mine, pay_down, pay_west, pay_east,
-    mask, tracers, flow, kappa, stress, fields, top, bottom, cells, vals,
+        flux[f] = parts[f]
+
+
+def sea_flux_kernel(
+    up, mine, down, west, east, mask, tracers, flow, kappa,
+    stress, fields, top, bottom, vals, air, cells, weight,
 ):
     def line(ref, start):
         rows = ref[start : start + LINES]
         return jnp.concatenate([rows[n : n + 1] for n in range(LINES)], axis=1)
 
-    for a, (lists, pay) in enumerate(((up, pay_up), (mine, pay_mine), (down, pay_down))):
-        for b, (ref, start) in enumerate(
-            ((west, 3 * VALS + a * LINES), (lists, VALS + LINES), (east, 3 * VALS + a * LINES))
+    for a, source in enumerate((up, mine, down)):
+        for b, (ref, table, start, step) in enumerate(
+            (
+                (west, a * VALS, 3 * VALS + a * 3 * LINES, LINES),
+                (source, 0, VALS + LINES, 3 * LINES),
+                (east, a * VALS, 3 * VALS + a * 3 * LINES, LINES),
+            )
         ):
             q = 3 * a + b
-            cells[q : q + 1] = line(ref, start).astype(jnp.int32)
-        for f in range(4):
-            along = FAR_COLS + (a * 4 + f) * LINES
-            for b, (ref, start) in enumerate(
-                ((pay_west, along), (pay, FAR_LINES + (f * 3 + 1) * LINES), (pay_east, along))
-            ):
-                q = 3 * a + b
-                vals[f, q : q + 1] = line(ref, start)
-
-    def place(q, total):
-        hot, rows = one_hots(cells[pl.ds(q, 1), :])
-        return total + scatter([vals[f, pl.ds(q, 1), :] for f in range(4)], hot, rows)
-
-    total = lax.fori_loop(0, 9, place, jnp.zeros((12 * RW, CL), F32))
-    flux = total[0 : 4 * RW] + total[4 * RW : 8 * RW] + total[8 * RW :]
+            air[q] = ref[table + SEA : table + VALS]
+            for k in range(2):
+                cells[k, q : q + 1] = line(ref, start + k * step).astype(jnp.int32)
+            weight[q : q + 1] = line(ref, start + 2 * step)
+
+    part = summed_fluxes(
+        lambda q: air[q],
+        lambda q: mine[0:SEA],
+        lambda q: cells[1, pl.ds(q, 1), :],
+        lambda q: cells[0, pl.ds(q, 1), :],
+        lambda q: weight[pl.ds(q, 1), :],
+        False,
+        vals,
+    )
     sea = mask[...].astype(F32)
-    part = [flux[f * RW : (f + 1) * RW] for f in range(4)]
     stress[0] = sea * part[2]
     stress[1] = sea * part[3]
     fields[0] = tracers[0, 0]
@@ -654,13 +657,14 @@
     position = lax.axis_index("face") * lax.axis_size("gy") + lax.axis_index("gy")
     flags = jnp.stack([position == 0, position == sizes()[0] - 1]).astype(jnp.int32)
     level = (1, RW, CL)
-
-    message = shape(VALS + 3 * LINES, CL)
+    weights = xgrid_weights.transpose(1, 2, 0, 3)
+
+    message = shape(VALS + 9 * LINES, CL)
     for_up, mine, for_down = call(
         spread_kernel,
         (message,) * 3,
-        (ocean_tracers, ocean_flow, xgrid_ocean_cell),
-        blocks={0: (1, *level), 1: (2, *level)},
+        (ocean_tracers, ocean_flow, atmos_state, xgrid_ocean_cell, xgrid_atmos_cell, weights),
+        blocks={0: (1, *level), 1: (2, *level), 2: (4, *level)},
         mib=60,
     )
     up, down = to_north(for_up), to_south(for_down)
@@ -671,106 +675,99 @@
         ocean_kappa.reshape(-1, CL),
         sea_mask,
     )
-    near = shape(NEAR * 5 * LV, CL)
-    top, bottom = call(
-        functools.partial(edge_kernel, 0), (near, near), deep_args, mib=EDGE_MIB
-    )
-    south, north, fold = to_north(top), to_south(bottom), across_fold(top)
-
-    relay = shape(3 * (VALS + LINES), CL)
+    near = shape(HALO * 5 * LV, CL)
+    top, bottom = call(edge_kernel, (near, near), deep_args, mib=EDGE_MIB)
+    south, north = to_north(top), to_south(bottom)
+    fold = across_fold(top)
+
+    relay = shape(3 * (VALS + 3 * LINES), CL)
     for_east, for_west = call(relay_kernel, (relay,) * 2, (up, mine, down))
     west_in, east_in = to_east(for_east), to_west(for_west)
 
-    def extended(fields, count, extra=0):
-        return (shape(fields, count, CL, CL),) + (shape(fields * count * FULL + extra, CL),) * 2
-
-    xo, mw, me = call(own_kernel, extended(4, RW // 2), deep_args, flops=10_000_000, mib=OWN_MIB)
+    def extended(count):
+        return (shape(4, count, CL, CL),) + (shape(4 * count * SIDE, CL),) * 2
+
+    xo, mw, me = call(
+        own_kernel, extended(RW // 2), deep_args, flops=10_000_000, mib=OWN_MIB
+    )
     wo, eo = to_east(me), to_west(mw)
-    far = shape(FAR_LINES, CL)
-    far_top, far_bottom = call(
-        functools.partial(edge_kernel, NEAR), (far, far), deep_args, mib=OWN_MIB
-    )
-
-    load = shape(FAR_LINES + 12 * LINES, CL)
-    atmos_flux, pay_n, pay_o, pay_s = call(
-        flux_kernel,
-        (shape(4, RW, CL), load, load, load),
-        (
-            atmos_state, up, mine, down, west_in, east_in,
-            xgrid_atmos_cell, xgrid_ocean_cell, xgrid_weights, far_top, far_bottom,
-        ),
-        scratch=[pltpu.VMEM((9, 16, slots), F32), pltpu.VMEM((9, VALS, CL), F32)],
+
+    around = (up, mine, down, west_in, east_in)
+    vals = pltpu.VMEM((8, 16, slots), F32)
+    edge = shape(7 * DEEP, CL)
+    ocean_stress, fields, s_top, s_bottom = call(
+        sea_flux_kernel,
+        (shape(2, RW, CL), shape(7, RW, CL), edge, edge),
+        (*around, sea_mask, ocean_tracers, ocean_flow, ocean_kappa),
+        scratch=[
+            vals,
+            pltpu.VMEM((9, 4 * RW, CL), F32),
+            pltpu.VMEM((2, 16, slots), jnp.int32),
+            pltpu.VMEM((16, slots), F32),
+        ],
         flops=20_000_000,
-        blocks={0: (4, *level)},
+        blocks={6: (2, *level), 7: (2, *level), 8: level},
         mib=FLUX_MIB,
     )
-    pay_up, pay_down, pay_fold = to_north(pay_n), to_south(pay_s), across_fold(pay_n)
+    s_args = (to_north(s_top), to_south(s_bottom), across_fold(s_top))
+
+    atmos_flux = call(
+        air_flux_kernel,
+        shape(4, RW, CL),
+        (*around, xgrid_atmos_cell, xgrid_ocean_cell, weights),
+        scratch=[vals, pltpu.VMEM((9, SEA, CL), F32)],
+        flops=20_000_000,
+        mib=FLUX_MIB,
+    )
     atmos_next = atmosphere(atmos_state, atmos_kappa, atmos_flux)
 
     xn, mw, me = call(
-        functools.partial(halo_kernel, 5),
-        extended(4, NEAR),
+        halo_kernel,
+        extended(HALO),
         (bottom, south, north, fold, flags),
         flops=5_000_000,
         mib=OWN_MIB,
     )
     wn, en = to_east(me), to_west(mw)
-
-    def buffers(halo):
-        return [pltpu.VMEM((RW // 2 + halo, WIDTH, CL), F32)] * 6
-
-    pair = shape(FULL // 2 * CL, CL)
+    buffers = [pltpu.VMEM((RW // 2 + HALO, WIDTH, CL), F32)] * 6
+    pair = shape(HALO // 2 * CL, CL)
     state, top, bottom = call(
         functools.partial(deep_kernel, False),
         (shape(RW // 2, CL, CL), pair, pair),
         (xo, wo, eo, xn, wn, en),
-        scratch=buffers(NEAR),
+        scratch=buffers,
         flops=40_000_000,
         mib=FIRST_MIB,
     )
-    south, north, fold = to_north(top), to_south(bottom), across_fold(top)
-
-    xf, mw, me = call(
-        far_halo_kernel,
-        extended(3, NEAR, 12 * LINES),
-        (pay_o, pay_up, pay_down, pay_fold, flags),
-        flops=5_000_000,
-        mib=OWN_MIB,
-    )
-    wf, ef = to_east(me), to_west(mw)
-    edge = shape(7 * DEEP, CL)
-    ocean_stress, fields, s_top, s_bottom = call(
-        ocean_flux_kernel,
-        (shape(2, RW, CL), shape(7, RW, CL), edge, edge),
-        (
-            up, mine, down, west_in, east_in, pay_up, pay_o, pay_down, wf, ef,
-            sea_mask, ocean_tracers, ocean_flow, ocean_kappa,
-        ),
-        scratch=[pltpu.VMEM((16, slots), jnp.int32), pltpu.VMEM((4, 16, slots), F32)],
-        flops=8_000_000,
-        blocks={11: (2, *level), 12: (2, *level), 13: level},
-        mib=FLUX_MIB,
-    )
-    s_args = (to_north(s_top), to_south(s_bottom), across_fold(s_top))
-
-    side = shape(DEEP_LINES, CL)
-    xts, mw, me = call(
-        join_kernel,
-        (shape(RW // 2 + FULL, CL, CL), side, side),
-        (state, south, north, fold, flags),
-    )
-    w2, e2 = to_east(me), to_west(mw)
+    south, north = to_north(top), to_south(bottom)
+    fold = across_fold(top)
+
     side = shape(7 * SR // 2, CL)
     joined, sw, se = call(
         surface_join_kernel, (shape(7, SR, CL), side, side), (fields, *s_args, flags)
     )
+    w3, e3 = to_east(se), to_west(sw)
     wide = pltpu.VMEM((SR, 2 * CL), F32)
+    surface = call(
+        surface_kernel,
+        shape(2, RW, CL),
+        (joined, w3, e3),
+        scratch=[wide] * 4 + [pltpu.VMEM((2, SR, 2 * CL), F32)],
+        flops=10_000_000,
+    )
+
+    side = shape((RW // 2 + HALO) * SIDE, CL)
+    xts, mw, me = call(
+        join_kernel,
+        (shape(RW // 2 + HALO, CL, CL), side, side),
+        (state, south, north, fold, flags),
+    )
     ocean_next = call(
         functools.partial(deep_kernel, True),
         shape(2 * LV * RW, CL),
-        (xo, wo, eo, xn, wn, en, xf, wf, ef, xts, w2, e2, joined, to_east(se), to_west(sw)),
-        scratch=buffers(FULL) + [wide] * 4 + [pltpu.VMEM((2, SR, 2 * CL), F32)],
-        flops=80_000_000,
+        (xo, wo, eo, xn, wn, en, xts, to_east(me), to_west(mw), surface),
+        scratch=buffers,
+        flops=60_000_000,
         mib=FINAL_MIB,
     )
     return (atmos_next, ocean_next.reshape(ocean_tracers.shape), ocean_stress)

time: 175 us -> 162 us (0.926)
  starting transfers between devices: 60.2 us -> 50.5 us
  local copies, waits for them, and re-layouts: 11.5 us -> 8.4 us
    ppermute x5 -> x4, starting transfers between devices: 21.7 us -> 14.7 us  [to_north(): return lax.ppermute(value, AXES, pairs)]
    ppermute x5 -> x4, waiting for transfers between devices: 5.76 us -> 1.02 us  [to_south(): return lax.ppermute(value, AXES, pairs)]
    unnamed x55 -> x38, local copies, waits for them, and re-layouts: 11.5 us -> 8.4 us
    ppermute x6 -> x5, waiting for transfers between devices: 2.53 us -> 5.33 us  [to_east(): return lax.ppermute(value, 'gx', [(x, (x + 1) % nx) for x in range(nx)])]
    ppermute x5 -> x4, waiting for transfers between devices: 26.9 us -> 29.4 us  [to_north(): return lax.ppermute(value, AXES, pairs)]
    ppermute x5 -> x4, starting transfers between devices: 19.6 us -> 18.3 us  [to_south(): return lax.ppermute(value, AXES, pairs)]
    pallas_call x13 -> x12, Pallas kernels: 62.1 us -> 63 us  [call(): pl.pallas_call(kernel, grid=(1,) if blocks else (), out_shape=outs, in_sp...]
    ppermute x4 -> x3, starting transfers between devices: 3.57 us -> 2.96 us  [across_fold(): return lax.ppermute(value, AXES, pairs)]
  transfers between devices with their start and end apart: 26 -> 21, of which waited for: 7 -> 3; matrix products, arithmetic and copies ran while one was open for 0% -> 0% of each run, Pallas kernels for 22% -> 29%
where the time goes in v5:
time: 162 us; the launch traced here: 161 us
  Pallas kernels  65.6 us (40%)
  starting transfers between devices  50.5 us (31%)
  waiting for transfers between devices  35.8 us (22%)
  local copies, waits for them, and re-layouts  8.4 us (5%)
    pallas_call x12, Pallas kernels, call(): pl.pallas_call(kernel, grid=(1,) if blocks else (), out_shape=outs, in_sp...  63 us
    ppermute x4, waiting for transfers between devices, to_north(): return lax.ppermute(value, AXES, pairs)  29.4 us
    ppermute x4, starting transfers between devices, to_south(): return lax.ppermute(value, AXES, pairs)  18.3 us
    ppermute x4, starting transfers between devices, to_north(): return lax.ppermute(value, AXES, pairs)  14.7 us
    ppermute x5, starting transfers between devices, to_west(): return lax.ppermute(value, 'gx', [(x, (x - 1) % nx) for x in range(nx)])  14.4 us
    unnamed x38, local copies, waits for them, and re-layouts  8.4 us
    ppermute x5, waiting for transfers between devices, to_east(): return lax.ppermute(value, 'gx', [(x, (x + 1) % nx) for x in range(nx)])  5.33 us
  transfers between devices with their start and end apart: 21, of which 3 were waited for; matrix products, arithmetic and copies ran while one was open for 0% of the time, Pallas kernels for 29%

profile of v5, /device:TPU:4, one launch (start us, length us, event | category | flops | bytes accessed | tf_op | source)
XLA Modules:
  0.0 161.4 jit_solution(15454514728714832075)
XLA Ops:
  0.6 0.0 copy-start.3
  0.6 1.2 copy-done.3
  1.9 1.2 copy-done.6
  3.1 1.0 copy-done.10
  4.1 0.7 copy-done.16
  4.8 3.4 %shard_map.117 = (f32[1920,128]{1,0:T(8,128)}, f32[1920,128]{1,0:T(8,128)}) custom-call(f32[2048,128]{1,0:T(8,128)S(1)} %bitcast.7, f32[2048,128]{1,0:T(8,128)S(1)} %bitcast.9, f32[1024,128]{1,0:T(8,128)S(1)} %bitcast.11, s32[32,128]{1,0:T(8,128)S(1)} %copy-done.16), custom_call_target="tpu_custom_call" | custom-call | flops 1000000 | bytes 1000000 | tf_op jit(solution)/shard_map/pallas_call | solution.py:44
  8.2 5.8 %collective-permute-start.6 = (f32[1920,128]{1,0:T(8,128)}, f32[1920,128]{1,0:T(8,128)}, u32[]{:S(2)}, u32[]{:S(2)}) collective-permute-start(f32[1920,128]{1,0:T(8,128)} %get-tuple-element.38), channel_id=1, source_target_pairs={{0,1},{8,9},{16,17},{24,25},{32,33},{40,41},{48,49},{56,57},{1,2},... | collective-permute-start | bytes 2949128 | tf_op jit(solution)/shard_map/ppermute | solution.py:72
  14.0 2.5 %collective-permute-start.7 = (f32[1920,128]{1,0:T(8,128)}, f32[1920,128]{1,0:T(8,128)}, u32[]{:S(2)}, u32[]{:S(2)}) collective-permute-start(f32[1920,128]{1,0:T(8,128)} %get-tuple-element.37.own), channel_id=1, source_target_pairs={{1,0},{9,8},{17,16},{25,24},{33,32},{41,40},{49,48},{57,56},{2,1},... | collective-permute-start | bytes 2949128 | tf_op jit(solution)/shard_map/ppermute | solution.py:78
  16.5 1.6 collective-permute-start.8
  18.1 3.9 %shard_map.116 = (f32[4,16,128,128]{3,2,1,0:T(8,128)S(1)}, f32[1024,128]{1,0:T(8,128)}, f32[1024,128]{1,0:T(8,128)}) custom-call(f32[2048,128]{1,0:T(8,128)S(1)} %bitcast.8, f32[2048,128]{1,0:T(8,128)S(1)} %bitcast.10, f32[1024,128]{1,0:T(8,128)S(1)} %bitcast.12, s32[32,128]{1,0:T(8,128)S(1)} %copy-done.16), custom_call_target="tpu_custom_call" | custom-call | flops 10000000 | bytes 1000000 | tf_op jit(solution)/shard_map/pallas_call | solution.py:44
  22.0 2.0 %copy-done = f32[4,16,128,128]{3,2,1,0:T(8,128)} copy-done((f32[4,16,128,128]{3,2,1,0:T(8,128)}, f32[4,16,128,128]{3,2,1,0:T(8,128)S(1)}, u32[]{:S(2)}) %copy-start) | copy-done | bytes 4194328
  24.0 0.0 collective-permute-start.4
  24.0 3.0 %collective-permute-start.5 = (f32[1024,128]{1,0:T(8,128)}, f32[1024,128]{1,0:T(8,128)}, u32[]{:S(2)}, u32[]{:S(2)}) collective-permute-start(f32[1024,128]{1,0:T(8,128)} %get-tuple-element.36), channel_id=1, source_target_pairs={{0,56},{8,0},{16,8},{24,16},{32,24},{40,32},{48,40},{56,48},{1,57}... | collective-permute-start | bytes 1572872 | tf_op jit(solution)/shard_map/ppermute | solution.py:94
  26.9 0.1 add_convert_fusion.flags
  27.0 29.4 %collective-permute-done.6.south = f32[1920,128]{1,0:T(8,128)} collective-permute-done((f32[1920,128]{1,0:T(8,128)}, f32[1920,128]{1,0:T(8,128)}, u32[]{:S(2)}, u32[]{:S(2)}) %collective-permute-start.6) | collective-permute-done | bytes 983072 | tf_op jit(solution)/shard_map/ppermute | solution.py:72
  56.4 1.0 collective-permute-done.7.north
  57.4 0.0 collective-permute-done.8.fold
  57.4 4.6 %shard_map.118 = (f32[4,12,128,128]{3,2,1,0:T(8,128)S(1)}, f32[768,128]{1,0:T(8,128)}, f32[768,128]{1,0:T(8,128)}) custom-call(f32[1920,128]{1,0:T(8,128)} %get-tuple-element.37.own, f32[1920,128]{1,0:T(8,128)} %collective-permute-done.6.south, f32[1920,128]{1,0:T(8,128)} %collective-permute-done.7.north, f32[1920,128]{1,0:T(8,128)} %collective-permute-done.8.fold, ...), custom_call_target="tpu_custom_call" | custom-call | flops 5000000 | bytes 1000000 | tf_op jit(solution)/shard_map/pallas_call | solution.py:44
  61.9 2.6 %collective-permute-start.10 = (f32[768,128]{1,0:T(8,128)}, f32[768,128]{1,0:T(8,128)S(1)}, u32[]{:S(2)}, u32[]{:S(2)}) collective-permute-start(f32[768,128]{1,0:T(8,128)} %get-tuple-element.41), channel_id=1, source_target_pairs={{0,56},{8,0},{16,8},{24,16},{32,24},{40,32},{48,40},{56,48},{1,57}... | collective-permute-start | bytes 1179656 | tf_op jit(solution)/shard_map/ppermute | solution.py:94
  64.6 0.0 collective-permute-start.9
  64.6 1.9 %shard_map.112 = (f32[296,128]{1,0:T(8,128)}, f32[296,128]{1,0:T(8,128)}, f32[296,128]{1,0:T(8,128)}) custom-call(f32[2,32,32,128]{3,2,1,0:T(8,128)} %tracers.3, f32[2,32,32,128]{3,2,1,0:T(8,128)} %flow.3, f32[4,32,32,128]{3,2,1,0:T(8,128)} %state.3, s32[3,3,1024]{2,1,0:T(4,128)} %sea_cells.3, s32[3,3,1024]{2,1,0:T(4,128)} %air_cells.3, ...), custom_call_target="tpu_custom_call" | custom-call | flops 1000000 | bytes 1000000 | tf_op jit(solution)/shard_map/pallas_call | solution.py:44
  66.4 3.8 %collective-permute-start = (f32[296,128]{1,0:T(8,128)}, f32[296,128]{1,0:T(8,128)S(1)}, u32[]{:S(2)}, u32[]{:S(2)}) collective-permute-start(f32[296,128]{1,0:T(8,128)} %get-tuple-element.29), channel_id=1, source_target_pairs={{0,1},{8,9},{16,17},{24,25},{32,33},{40,41},{48,49},{56,57},{1,2},... | collective-permute-start | bytes 454664 | tf_op jit(solution)/shard_map/ppermute | solution.py:72
  70.3 0.0 collective-permute-done.4.refs_1_
  70.3 4.4 %collective-permute-start.1 = (f32[296,128]{1,0:T(8,128)}, f32[296,128]{1,0:T(8,128)S(1)}, u32[]{:S(2)}, u32[]{:S(2)}) collective-permute-start(f32[296,128]{1,0:T(8,128)} %get-tuple-element.31), channel_id=1, source_target_pairs={{1,0},{9,8},{17,16},{25,24},{33,32},{41,40},{49,48},{57,56},{2,1},... | collective-permute-start | bytes 454664 | tf_op jit(solution)/shard_map/ppermute | solution.py:78
  74.7 0.0 collective-permute-done.5.refs_2_
  74.7 0.0 collective-permute-done.10.refs_5_
  74.7 0.0 collective-permute-done.9.refs_4_
  74.7 2.2 %copy-done.1 = f32[4,16,128,128]{3,2,1,0:T(8,128)S(1)} copy-done((f32[4,16,128,128]{3,2,1,0:T(8,128)S(1)}, f32[4,16,128,128]{3,2,1,0:T(8,128)}, u32[]{:S(2)}) %copy-start.1) | copy-done | bytes 4194328
  76.9 0.0 copy-start.17
  76.9 12.0 %shard_map.119 = (f32[16,128,128]{2,1,0:T(8,128)S(1)}, f32[768,128]{1,0:T(8,128)S(1)}, f32[768,128]{1,0:T(8,128)S(1)}) custom-call(f32[4,16,128,128]{3,2,1,0:T(8,128)S(1)} %copy-done.1, f32[1024,128]{1,0:T(8,128)S(1)} %collective-permute-done.4.refs_1_, f32[1024,128]{1,0:T(8,128)} %collective-permute-done.5.refs_2_, ...), custom_call_target="tpu_custom_call" | custom-call | flops 40000000 | bytes 1000000 | tf_op jit(solution)/shard_map/pallas_call | solution.py:44
  88.9 3.0 %collective-permute-start.11 = (f32[768,128]{1,0:T(8,128)S(1)}, f32[768,128]{1,0:T(8,128)S(1)}, u32[]{:S(2)}, u32[]{:S(2)}) collective-permute-start(f32[768,128]{1,0:T(8,128)S(1)} %get-tuple-element.43), channel_id=1, source_target_pairs={{0,1},{8,9},{16,17},{24,25},{32,33},{40,41},{48,49},{56,57},{1,2},... | collective-permute-start | bytes 1179656 | tf_op jit(solution)/shard_map/ppermute | solution.py:72
  91.9 0.7 collective-permute-start.13
  92.6 5.3 %collective-permute-start.12 = (f32[768,128]{1,0:T(8,128)S(1)}, f32[768,128]{1,0:T(8,128)S(1)}, u32[]{:S(2)}, u32[]{:S(2)}) collective-permute-start(f32[768,128]{1,0:T(8,128)S(1)} %get-tuple-element.44), channel_id=1, source_target_pairs={{1,0},{9,8},{17,16},{25,24},{33,32},{41,40},{49,48},{57,56},{2,1},... | collective-permute-start | bytes 1179656 | tf_op jit(solution)/shard_map/ppermute | solution.py:78
  97.9 0.0 collective-permute-done.up
  97.9 0.0 collective-permute-done.1.down
  97.9 0.1 shard_map.113
  98.0 0.0 collective-permute-start.2
  98.0 2.9 %collective-permute-start.3 = (f32[744,128]{1,0:T(8,128)S(1)}, f32[744,128]{1,0:T(8,128)S(1)}, u32[]{:S(2)}, u32[]{:S(2)}) collective-permute-start(f32[744,128]{1,0:T(8,128)S(1)} %get-tuple-element.33), channel_id=1, source_target_pairs={{0,56},{8,0},{16,8},{24,16},{32,24},{40,32},{48,40},{56,48},{1,57}... | collective-permute-start | bytes 1142792 | tf_op jit(solution)/shard_map/ppermute | solution.py:94
  100.9 5.3 %collective-permute-done.2.west = f32[744,128]{1,0:T(8,128)S(1)} collective-permute-done((f32[744,128]{1,0:T(8,128)S(1)}, f32[744,128]{1,0:T(8,128)S(1)}, u32[]{:S(2)}, u32[]{:S(2)}) %collective-permute-start.2) | collective-permute-done | bytes 380960 | tf_op jit(solution)/shard_map/ppermute | solution.py:89
  106.3 0.0 collective-permute-done.3.east
  106.3 8.5 %shard_map.121 = (f32[2,32,128]{2,1,0:T(8,128)}, f32[7,32,128]{2,1,0:T(8,128)S(1)}, f32[168,128]{1,0:T(8,128)S(1)}, f32[168,128]{1,0:T(8,128)S(1)}) custom-call(f32[296,128]{1,0:T(8,128)S(1)} %collective-permute-done.up, f32[296,128]{1,0:T(8,128)S(1)} %copy-done.12, f32[296,128]{1,0:T(8,128)S(1)} %collective-permute-done.1.down, ...), custom_call_target="tpu_custom_call" | custom-call | flops 20000000 | bytes 1000000 | tf_op jit(solution)/shard_map/pallas_call | solution.py:44
  114.8 0.0 copy-start.18
  114.8 2.2 %collective-permute-start.16 = (f32[168,128]{1,0:T(8,128)S(1)}, f32[168,128]{1,0:T(8,128)S(1)}, u32[]{:S(2)}, u32[]{:S(2)}) collective-permute-start(f32[168,128]{1,0:T(8,128)S(1)} %get-tuple-element.49), channel_id=1, source_target_pairs={{0,1},{8,9},{16,17},{24,25},{32,33},{40,41},{48,49},{56,57},{1,2},... | collective-permute-start | bytes 258056 | tf_op jit(solution)/shard_map/ppermute | solution.py:72
  117.0 0.7 collective-permute-start.18
  117.7 0.0 collective-permute-done.11.south
  117.7 6.2 %collective-permute-start.17 = (f32[168,128]{1,0:T(8,128)S(1)}, f32[168,128]{1,0:T(8,128)S(1)}, u32[]{:S(2)}, u32[]{:S(2)}) collective-permute-start(f32[168,128]{1,0:T(8,128)S(1)} %get-tuple-element.50), channel_id=1, source_target_pairs={{1,0},{9,8},{17,16},{25,24},{33,32},{41,40},{49,48},{57,56},{2,1},... | collective-permute-start | bytes 258056 | tf_op jit(solution)/shard_map/ppermute | solution.py:78
  123.9 0.0 collective-permute-done.13.fold
  123.9 0.0 collective-permute-done.12.north
  123.9 1.2 shard_map.120
  125.1 0.0 collective-permute-start.14
  125.2 2.9 %collective-permute-start.15 = (f32[448,128]{1,0:T(8,128)S(1)}, f32[448,128]{1,0:T(8,128)S(1)}, u32[]{:S(2)}, u32[]{:S(2)}) collective-permute-start(f32[448,128]{1,0:T(8,128)S(1)} %get-tuple-element.47), channel_id=1, source_target_pairs={{0,56},{8,0},{16,8},{24,16},{32,24},{40,32},{48,40},{56,48},{1,57}... | collective-permute-start | bytes 688136 | tf_op jit(solution)/shard_map/ppermute | solution.py:94
  128.1 0.0 collective-permute-done.16.south
  128.1 0.0 collective-permute-done.18.fold
  128.1 0.0 collective-permute-done.17.north
  128.1 0.7 shard_map.122
  128.8 0.0 collective-permute-start.19
  128.8 2.9 %collective-permute-start.20 = (f32[280,128]{1,0:T(8,128)S(1)}, f32[280,128]{1,0:T(8,128)S(1)}, u32[]{:S(2)}, u32[]{:S(2)}) collective-permute-start(f32[280,128]{1,0:T(8,128)S(1)} %get-tuple-element.53), channel_id=1, source_target_pairs={{0,56},{8,0},{16,8},{24,16},{32,24},{40,32},{48,40},{56,48},{1,57}... | collective-permute-start | bytes 430088 | tf_op jit(solution)/shard_map/ppermute | solution.py:94
  131.8 7.9 %shard_map.114.flux = f32[4,32,128]{2,1,0:T(8,128)S(1)} custom-call(f32[296,128]{1,0:T(8,128)S(1)} %collective-permute-done.up, f32[296,128]{1,0:T(8,128)S(1)} %copy-done.12, f32[296,128]{1,0:T(8,128)S(1)} %collective-permute-done.1.down, f32[744,128]{1,0:T(8,128)S(1)} %collective-permute-done.2.west, f32[744,128]{1,0:T(8,128)S(1)} %collective-permute-done.3.east, ...), custom_call_target="tpu_custom_call" | custom-call | flops 20000000 | bytes 1000000 | tf_op jit(solution)/shard_map/pallas_call | solution.py:44
  139.7 2.7 %shard_map.115 = f32[4,32,32,128]{3,2,1,0:T(8,128)} custom-call(f32[4,32,32,128]{3,2,1,0:T(8,128)S(1)} %copy-done.9, f32[32,128]{1,0:T(8,128)S(1)} %copy-done.18, f32[4,32,128]{2,1,0:T(8,128)S(1)} %shard_map.114.flux), custom_call_target="tpu_custom_call" | custom-call | flops 5000000 | bytes 4200000 | tf_op jit(solution)/shard_map/pallas_call | solution.py:628
  142.4 0.0 collective-permute-done.19.w2
  142.4 0.0 collective-permute-done.20.e2
  142.4 4.2 %shard_map.123.refs_9_ = f32[2,32,128]{2,1,0:T(8,128)S(1)} custom-call(f32[7,80,128]{2,1,0:T(8,128)S(1)} %get-tuple-element.51.mine, f32[280,128]{1,0:T(8,128)S(1)} %collective-permute-done.19.w2, f32[280,128]{1,0:T(8,128)S(1)} %collective-permute-done.20.e2), custom_call_target="tpu_custom_call" | custom-call | flops 10000000 | bytes 1000000 | tf_op jit(solution)/shard_map/pallas_call | solution.py:44
  146.6 0.0 collective-permute-done.14.refs_7_
  146.7 14.7 %shard_map.124 = f32[2048,128]{1,0:T(8,128)} custom-call(f32[4,16,128,128]{3,2,1,0:T(8,128)S(1)} %copy-done.2, f32[1024,128]{1,0:T(8,128)S(1)} %collective-permute-done.4.refs_1_, f32[1024,128]{1,0:T(8,128)} %collective-permute-done.5.refs_2_, f32[4,12,128,128]{3,2,1,0:T(8,128)S(1)} %get-tuple-element.39.refs_3_, f32[768,128]{1,0:T(8,128)} %collective-permute-done.9.refs_4_, ...), custom_call_target="tpu_custom_call" | custom-call | flops 60000000 | bytes 1000000 | tf_op jit(solution)/shard_map/pallas_call | solution.py:44
  (30 shorter events, 0.1 us)
Async XLA Ops:
  0.6 1.2 copy-start.3
  1.9 1.2 copy-start.6
  3.1 1.0 copy-start.10
  4.1 0.7 copy-start.16
  4.8 13.2 %copy-start.4 = (f32[2,32,32,128]{3,2,1,0:T(8,128)S(1)}, f32[2,32,32,128]{3,2,1,0:T(8,128)}, u32[]{:S(2)}) copy-start(f32[2,32,32,128]{3,2,1,0:T(8,128)} %tracers.3) | copy-start | bytes 3145732
  4.8 13.2 %copy-start.7 = (f32[2,32,32,128]{3,2,1,0:T(8,128)S(1)}, f32[2,32,32,128]{3,2,1,0:T(8,128)}, u32[]{:S(2)}) copy-start(f32[2,32,32,128]{3,2,1,0:T(8,128)} %flow.3) | copy-start | bytes 3145732
  8.2 48.2 %collective-permute-start.6 = (f32[1920,128]{1,0:T(8,128)}, f32[1920,128]{1,0:T(8,128)}, u32[]{:S(2)}, u32[]{:S(2)}) collective-permute-start(f32[1920,128]{1,0:T(8,128)} %get-tuple-element.38), channel_id=1, source_target_pairs={{0,1},{8,9},{16,17},{24,25},{32,33},{40,41},{48,49},{56,57},{1,2},... | collective-permute-start | bytes 2949128 | tf_op jit(solution)/shard_map/ppermute | solution.py:72
  14.0 43.4 %collective-permute-start.7 = (f32[1920,128]{1,0:T(8,128)}, f32[1920,128]{1,0:T(8,128)}, u32[]{:S(2)}, u32[]{:S(2)}) collective-permute-start(f32[1920,128]{1,0:T(8,128)} %get-tuple-element.37.own), channel_id=1, source_target_pairs={{1,0},{9,8},{17,16},{25,24},{33,32},{41,40},{49,48},{57,56},{2,1},... | collective-permute-start | bytes 2949128 | tf_op jit(solution)/shard_map/ppermute | solution.py:78
  16.5 40.9 %collective-permute-start.8 = (f32[1920,128]{1,0:T(8,128)}, f32[1920,128]{1,0:T(8,128)}, u32[]{:S(2)}, u32[]{:S(2)}) collective-permute-start(f32[1920,128]{1,0:T(8,128)} %get-tuple-element.38), channel_id=1, source_target_pairs={{71,127},{79,119},{87,111},{95,103},{103,95},{111,87},{119,79},{12... | collective-permute-start | bytes 2949128 | tf_op jit(solution)/shard_map/ppermute | solution.py:84
  22.0 2.0 %copy-start = (f32[4,16,128,128]{3,2,1,0:T(8,128)}, f32[4,16,128,128]{3,2,1,0:T(8,128)S(1)}, u32[]{:S(2)}) copy-start(f32[4,16,128,128]{3,2,1,0:T(8,128)S(1)} %get-tuple-element.34.refs_0_) | copy-start | bytes 12582916
  24.0 46.3 %collective-permute-start.4 = (f32[1024,128]{1,0:T(8,128)}, f32[1024,128]{1,0:T(8,128)S(1)}, u32[]{:S(2)}, u32[]{:S(2)}) collective-permute-start(f32[1024,128]{1,0:T(8,128)} %get-tuple-element.35), channel_id=1, source_target_pairs={{0,8},{8,16},{16,24},{24,32},{32,40},{40,48},{48,56},{56,0},{1,9},... | collective-permute-start | bytes 1572872 | tf_op jit(solution)/shard_map/ppermute | solution.py:89
  24.0 50.7 %collective-permute-start.5 = (f32[1024,128]{1,0:T(8,128)}, f32[1024,128]{1,0:T(8,128)}, u32[]{:S(2)}, u32[]{:S(2)}) collective-permute-start(f32[1024,128]{1,0:T(8,128)} %get-tuple-element.36), channel_id=1, source_target_pairs={{0,56},{8,0},{16,8},{24,16},{32,24},{40,32},{48,40},{56,48},{1,57}... | collective-permute-start | bytes 1572872 | tf_op jit(solution)/shard_map/ppermute | solution.py:94
  61.9 12.8 %collective-permute-start.10 = (f32[768,128]{1,0:T(8,128)}, f32[768,128]{1,0:T(8,128)S(1)}, u32[]{:S(2)}, u32[]{:S(2)}) collective-permute-start(f32[768,128]{1,0:T(8,128)} %get-tuple-element.41), channel_id=1, source_target_pairs={{0,56},{8,0},{16,8},{24,16},{32,24},{40,32},{48,40},{56,48},{1,57}... | collective-permute-start | bytes 1179656 | tf_op jit(solution)/shard_map/ppermute | solution.py:94
  64.6 10.1 %collective-permute-start.9 = (f32[768,128]{1,0:T(8,128)}, f32[768,128]{1,0:T(8,128)}, u32[]{:S(2)}, u32[]{:S(2)}) collective-permute-start(f32[768,128]{1,0:T(8,128)} %get-tuple-element.40), channel_id=1, source_target_pairs={{0,8},{8,16},{16,24},{24,32},{32,40},{40,48},{48,56},{56,0},{1,9},... | collective-permute-start | bytes 1179656 | tf_op jit(solution)/shard_map/ppermute | solution.py:89
  66.4 31.5 %collective-permute-start = (f32[296,128]{1,0:T(8,128)}, f32[296,128]{1,0:T(8,128)S(1)}, u32[]{:S(2)}, u32[]{:S(2)}) collective-permute-start(f32[296,128]{1,0:T(8,128)} %get-tuple-element.29), channel_id=1, source_target_pairs={{0,1},{8,9},{16,17},{24,25},{32,33},{40,41},{48,49},{56,57},{1,2},... | collective-permute-start | bytes 454664 | tf_op jit(solution)/shard_map/ppermute | solution.py:72
  70.3 27.6 %collective-permute-start.1 = (f32[296,128]{1,0:T(8,128)}, f32[296,128]{1,0:T(8,128)S(1)}, u32[]{:S(2)}, u32[]{:S(2)}) collective-permute-start(f32[296,128]{1,0:T(8,128)} %get-tuple-element.31), channel_id=1, source_target_pairs={{1,0},{9,8},{17,16},{25,24},{33,32},{41,40},{49,48},{57,56},{2,1},... | collective-permute-start | bytes 454664 | tf_op jit(solution)/shard_map/ppermute | solution.py:78
  74.7 2.2 %copy-start.1 = (f32[4,16,128,128]{3,2,1,0:T(8,128)S(1)}, f32[4,16,128,128]{3,2,1,0:T(8,128)}, u32[]{:S(2)}) copy-start(f32[4,16,128,128]{3,2,1,0:T(8,128)} %copy-done) | copy-start | bytes 12582916
  76.9 21.0 %copy-start.12 = (f32[296,128]{1,0:T(8,128)S(1)}, f32[296,128]{1,0:T(8,128)}, u32[]{:S(2)}) copy-start(f32[296,128]{1,0:T(8,128)} %get-tuple-element.30.mine) | copy-start | bytes 454660
  76.9 29.4 %copy-start.5 = (f32[2,32,32,128]{3,2,1,0:T(8,128)S(1)}, f32[2,32,32,128]{3,2,1,0:T(8,128)}, u32[]{:S(2)}) copy-start(f32[2,32,32,128]{3,2,1,0:T(8,128)} %tracers.3) | copy-start | bytes 3145732
  76.9 29.4 %copy-start.8 = (f32[2,32,32,128]{3,2,1,0:T(8,128)S(1)}, f32[2,32,32,128]{3,2,1,0:T(8,128)}, u32[]{:S(2)}) copy-start(f32[2,32,32,128]{3,2,1,0:T(8,128)} %flow.3) | copy-start | bytes 3145732
  76.9 29.4 %copy-start.11 = (f32[32,32,128]{2,1,0:T(8,128)S(1)}, f32[32,32,128]{2,1,0:T(8,128)}, u32[]{:S(2)}) copy-start(f32[32,32,128]{2,1,0:T(8,128)} %kappa.3) | copy-start | bytes 1572868
  76.9 29.4 %copy-start.17 = (s32[32,128]{1,0:T(8,128)S(1)}, s32[32,128]{1,0:T(8,128)}, u32[]{:S(2)}) copy-start(s32[32,128]{1,0:T(8,128)} %mask.5) | copy-start | bytes 49156
  88.9 28.8 %collective-permute-start.11 = (f32[768,128]{1,0:T(8,128)S(1)}, f32[768,128]{1,0:T(8,128)S(1)}, u32[]{:S(2)}, u32[]{:S(2)}) collective-permute-start(f32[768,128]{1,0:T(8,128)S(1)} %get-tuple-element.43), channel_id=1, source_target_pairs={{0,1},{8,9},{16,17},{24,25},{32,33},{40,41},{48,49},{56,57},{1,2},... | collective-permute-start | bytes 1179656 | tf_op jit(solution)/shard_map/ppermute | solution.py:72
  91.9 32.0 %collective-permute-start.13 = (f32[768,128]{1,0:T(8,128)S(1)}, f32[768,128]{1,0:T(8,128)S(1)}, u32[]{:S(2)}, u32[]{:S(2)}) collective-permute-start(f32[768,128]{1,0:T(8,128)S(1)} %get-tuple-element.43), channel_id=1, source_target_pairs={{71,127},{79,119},{87,111},{95,103},{103,95},{111,87},{119,79},{12... | collective-permute-start | bytes 1179656 | tf_op jit(solution)/shard_map/ppermute | solution.py:84
  92.6 31.3 %collective-permute-start.12 = (f32[768,128]{1,0:T(8,128)S(1)}, f32[768,128]{1,0:T(8,128)S(1)}, u32[]{:S(2)}, u32[]{:S(2)}) collective-permute-start(f32[768,128]{1,0:T(8,128)S(1)} %get-tuple-element.44), channel_id=1, source_target_pairs={{1,0},{9,8},{17,16},{25,24},{33,32},{41,40},{49,48},{57,56},{2,1},... | collective-permute-start | bytes 1179656 | tf_op jit(solution)/shard_map/ppermute | solution.py:78
  98.0 8.3 %collective-permute-start.2 = (f32[744,128]{1,0:T(8,128)S(1)}, f32[744,128]{1,0:T(8,128)S(1)}, u32[]{:S(2)}, u32[]{:S(2)}) collective-permute-start(f32[744,128]{1,0:T(8,128)S(1)} %get-tuple-element.32), channel_id=1, source_target_pairs={{0,8},{8,16},{16,24},{24,32},{32,40},{40,48},{48,56},{56,0},{1,9},... | collective-permute-start | bytes 1142792 | tf_op jit(solution)/shard_map/ppermute | solution.py:89
  98.0 8.3 %collective-permute-start.3 = (f32[744,128]{1,0:T(8,128)S(1)}, f32[744,128]{1,0:T(8,128)S(1)}, u32[]{:S(2)}, u32[]{:S(2)}) collective-permute-start(f32[744,128]{1,0:T(8,128)S(1)} %get-tuple-element.33), channel_id=1, source_target_pairs={{0,56},{8,0},{16,8},{24,16},{32,24},{40,32},{48,40},{56,48},{1,57}... | collective-permute-start | bytes 1142792 | tf_op jit(solution)/shard_map/ppermute | solution.py:94
  114.8 17.0 %copy-start.13 = (f32[2,3,3,1024]{3,0,2,1:T(2,128)S(1)}, f32[2,3,3,1024]{3,0,2,1:T(2,128)}, u32[]{:S(2)}) copy-start(f32[2,3,3,1024]{3,0,2,1:T(2,128)} %param.17) | copy-start | bytes 221188
  114.8 17.0 %copy-start.14 = (s32[3,3,1024]{2,1,0:T(4,128)S(1)}, s32[3,3,1024]{2,1,0:T(4,128)}, u32[]{:S(2)}) copy-start(s32[3,3,1024]{2,1,0:T(4,128)} %sea_cells.3) | copy-start | bytes 110596
  114.8 17.0 %copy-start.15 = (s32[3,3,1024]{2,1,0:T(4,128)S(1)}, s32[3,3,1024]{2,1,0:T(4,128)}, u32[]{:S(2)}) copy-start(s32[3,3,1024]{2,1,0:T(4,128)} %air_cells.3) | copy-start | bytes 110596
  114.8 24.9 %copy-start.9 = (f32[4,32,32,128]{3,2,1,0:T(8,128)S(1)}, f32[4,32,32,128]{3,2,1,0:T(8,128)}, u32[]{:S(2)}) copy-start(f32[4,32,32,128]{3,2,1,0:T(8,128)} %state.3) | copy-start | bytes 6291460
  114.8 24.9 %copy-start.18 = (f32[32,128]{1,0:T(8,128)S(1)}, f32[32,128]{1,0:T(8,128)}, u32[]{:S(2)}) copy-start(f32[32,128]{1,0:T(8,128)} %kappa.2) | copy-start | bytes 49156
  114.8 13.3 %collective-permute-start.16 = (f32[168,128]{1,0:T(8,128)S(1)}, f32[168,128]{1,0:T(8,128)S(1)}, u32[]{:S(2)}, u32[]{:S(2)}) collective-permute-start(f32[168,128]{1,0:T(8,128)S(1)} %get-tuple-element.49), channel_id=1, source_target_pairs={{0,1},{8,9},{16,17},{24,25},{32,33},{40,41},{48,49},{56,57},{1,2},... | collective-permute-start | bytes 258056 | tf_op jit(solution)/shard_map/ppermute | solution.py:72
  117.0 11.1 %collective-permute-start.18 = (f32[168,128]{1,0:T(8,128)S(1)}, f32[168,128]{1,0:T(8,128)S(1)}, u32[]{:S(2)}, u32[]{:S(2)}) collective-permute-start(f32[168,128]{1,0:T(8,128)S(1)} %get-tuple-element.49), channel_id=1, source_target_pairs={{71,127},{79,119},{87,111},{95,103},{103,95},{111,87},{119,79},{12... | collective-permute-start | bytes 258056 | tf_op jit(solution)/shard_map/ppermute | solution.py:84
  117.7 10.4 %collective-permute-start.17 = (f32[168,128]{1,0:T(8,128)S(1)}, f32[168,128]{1,0:T(8,128)S(1)}, u32[]{:S(2)}, u32[]{:S(2)}) collective-permute-start(f32[168,128]{1,0:T(8,128)S(1)} %get-tuple-element.50), channel_id=1, source_target_pairs={{1,0},{9,8},{17,16},{25,24},{33,32},{41,40},{49,48},{57,56},{2,1},... | collective-permute-start | bytes 258056 | tf_op jit(solution)/shard_map/ppermute | solution.py:78
  125.1 21.5 %collective-permute-start.14 = (f32[448,128]{1,0:T(8,128)S(1)}, f32[448,128]{1,0:T(8,128)S(1)}, u32[]{:S(2)}, u32[]{:S(2)}) collective-permute-start(f32[448,128]{1,0:T(8,128)S(1)} %get-tuple-element.46), channel_id=1, source_target_pairs={{0,8},{8,16},{16,24},{24,32},{32,40},{40,48},{48,56},{56,0},{1,9},... | collective-permute-start | bytes 688136 | tf_op jit(solution)/shard_map/ppermute | solution.py:89
  125.2 21.5 %collective-permute-start.15 = (f32[448,128]{1,0:T(8,128)S(1)}, f32[448,128]{1,0:T(8,128)S(1)}, u32[]{:S(2)}, u32[]{:S(2)}) collective-permute-start(f32[448,128]{1,0:T(8,128)S(1)} %get-tuple-element.47), channel_id=1, source_target_pairs={{0,56},{8,0},{16,8},{24,16},{32,24},{40,32},{48,40},{56,48},{1,57}... | collective-permute-start | bytes 688136 | tf_op jit(solution)/shard_map/ppermute | solution.py:94
  128.8 13.6 %collective-permute-start.19 = (f32[280,128]{1,0:T(8,128)S(1)}, f32[280,128]{1,0:T(8,128)S(1)}, u32[]{:S(2)}, u32[]{:S(2)}) collective-permute-start(f32[280,128]{1,0:T(8,128)S(1)} %get-tuple-element.52), channel_id=1, source_target_pairs={{0,8},{8,16},{16,24},{24,32},{32,40},{40,48},{48,56},{56,0},{1,9},... | collective-permute-start | bytes 430088 | tf_op jit(solution)/shard_map/ppermute | solution.py:89
  128.8 13.5 %collective-permute-start.20 = (f32[280,128]{1,0:T(8,128)S(1)}, f32[280,128]{1,0:T(8,128)S(1)}, u32[]{:S(2)}, u32[]{:S(2)}) collective-permute-start(f32[280,128]{1,0:T(8,128)S(1)} %get-tuple-element.53), channel_id=1, source_target_pairs={{0,56},{8,0},{16,8},{24,16},{32,24},{40,32},{48,40},{56,48},{1,57}... | collective-permute-start | bytes 430088 | tf_op jit(solution)/shard_map/ppermute | solution.py:94
  139.7 7.0 %copy-start.2 = (f32[4,16,128,128]{3,2,1,0:T(8,128)S(1)}, f32[4,16,128,128]{3,2,1,0:T(8,128)}, u32[]{:S(2)}) copy-start(f32[4,16,128,128]{3,2,1,0:T(8,128)} %copy-done) | copy-start | bytes 12582916

commit v6 on v5

--- a/solution.py
+++ b/solution.py
@@ -24,13 +24,13 @@
 HALO = 12
 SIDE = 16
 EDGE = 24
-WIDTH = 176
+WIDTH = 168
 DEEP = ITERS
 SR = RW + 2 * DEEP
 SEA = 3 * RW
 VALS = SEA + 4 * RW
 LINES = 8
-EDGE_MIB, OWN_MIB, FIRST_MIB, FINAL_MIB, FLUX_MIB = 12, 14, 17, 19, 10
+EDGE_MIB, OWN_MIB, FIRST_MIB, FINAL_MIB, FLUX_MIB = 12, 14, 19, 21, 10
 
 
 VMEM = pl.BlockSpec(memory_space=pltpu.VMEM)
@@ -64,6 +64,11 @@
 
 def sizes():
     return lax.axis_size("face") * lax.axis_size("gy"), lax.axis_size("gx")
+
+
+def at_ends():
+    position = lax.axis_index("face") * lax.axis_size("gy") + lax.axis_index("gy")
+    return position == 0, position == sizes()[0] - 1
 
 
 def to_north(value):
@@ -161,9 +166,8 @@
     lax.fori_loop(0, RW // 4, inner, 0)
 
 
-def halo_kernel(own, south, north, fold, flags, x, mw, me):
-    first = flags[0] > 0
-    last = flags[1] > 0
+def halo_kernel(own, south, north, fold, x, mw, me):
+    first, last = at_ends()
 
     def halo(p, carry):
         for n in range(2):
@@ -194,7 +198,7 @@
     else:
         state, top, bottom = refs[6:9]
         scratch = refs[9:]
-    s0, s1, cw, ce, cd, cu = scratch
+    s0, s1, cc, cw, ce, cd, cu = scratch
     pairs = RW // 2 + halo
     block = (CL + 2 * halo) // 8
     begin = EDGE - halo
@@ -203,10 +207,13 @@
     east_cols = slice(EDGE + CL, EDGE + CL + halo)
 
     def coefficients(i, where, u, v, k):
-        cw[i, where] = jnp.maximum(u, 0.0) + k
-        ce[i, where] = jnp.maximum(-u, 0.0) + k
-        cd[i, where] = jnp.maximum(v, 0.0) + k
-        cu[i, where] = jnp.maximum(-v, 0.0) + k
+        a, b = jnp.maximum(u, 0.0) + k, jnp.maximum(-u, 0.0) + k
+        c, d = jnp.maximum(v, 0.0) + k, jnp.maximum(-v, 0.0) + k
+        cw[i, where] = a
+        ce[i, where] = b
+        cd[i, where] = c
+        cu[i, where] = d
+        cc[i, where] = 1.0 - ((a + b) + (c + d))
 
     def fill(x, w, e, start):
         lead = 1
@@ -257,11 +264,9 @@
                     up = lines[n + 1][j + 1] if n + 1 < count else at(src, i + count, j)
                 k = i + n
                 dst[k, pl.ds(begin + j, 8, stride=block), :] = (
-                    centre
-                    + at(cw, k, j) * (west - centre)
-                    + at(ce, k, j) * (east - centre)
-                    + at(cd, k, j) * (down - centre)
-                    + at(cu, k, j) * (up - centre)
+                    at(cc, k, j) * centre
+                    + (at(cw, k, j) * west + at(ce, k, j) * east)
+                    + (at(cd, k, j) * down + at(cu, k, j) * up)
                 )
 
     def step(src, dst, s):
@@ -306,9 +311,8 @@
             bottom[where] = jnp.where(low, near, pltpu.roll(far, CL // 2, 1))
 
 
-def join_kernel(state, south, north, fold, flags, xts, mw, me):
-    first = flags[0] > 0
-    last = flags[1] > 0
+def join_kernel(state, south, north, fold, xts, mw, me):
+    first, last = at_ends()
     low = lax.broadcasted_iota(jnp.int32, (CL, CL), 1) < CL // 2
     half = HALO // 2
     flip = jnp.where(
@@ -338,9 +342,8 @@
         me[where, :] = rows[i][CL - SIDE :]
 
 
-def surface_join_kernel(fields, south, north, fold, flags, joined, mw, me):
-    first = flags[0] > 0
-    last = flags[1] > 0
+def surface_join_kernel(fields, south, north, fold, joined, mw, me):
+    first, last = at_ends()
     for f in range(7):
         part = slice(f * DEEP, (f + 1) * DEEP)
         joined[f, 0:DEEP] = south[part]
@@ -654,8 +657,6 @@
     xgrid_weights,
 ):
     slots = xgrid_atmos_cell.shape[2]
-    position = lax.axis_index("face") * lax.axis_size("gy") + lax.axis_index("gy")
-    flags = jnp.stack([position == 0, position == sizes()[0] - 1]).astype(jnp.int32)
     level = (1, RW, CL)
     weights = xgrid_weights.transpose(1, 2, 0, 3)
 
@@ -724,12 +725,12 @@
     xn, mw, me = call(
         halo_kernel,
         extended(HALO),
-        (bottom, south, north, fold, flags),
+        (bottom, south, north, fold),
         flops=5_000_000,
         mib=OWN_MIB,
     )
     wn, en = to_east(me), to_west(mw)
-    buffers = [pltpu.VMEM((RW // 2 + HALO, WIDTH, CL), F32)] * 6
+    buffers = [pltpu.VMEM((RW // 2 + HALO, WIDTH, CL), F32)] * 7
     pair = shape(HALO // 2 * CL, CL)
     state, top, bottom = call(
         functools.partial(deep_kernel, False),
@@ -743,9 +744,7 @@
     fold = across_fold(top)
 
     side = shape(7 * SR // 2, CL)
-    joined, sw, se = call(
-        surface_join_kernel, (shape(7, SR, CL), side, side), (fields, *s_args, flags)
-    )
+    joined, sw, se = call(surface_join_kernel, (shape(7, SR, CL), side, side), (fields, *s_args))
     w3, e3 = to_east(se), to_west(sw)
     wide = pltpu.VMEM((SR, 2 * CL), F32)
     surface = call(
@@ -760,7 +759,7 @@
     xts, mw, me = call(
         join_kernel,
         (shape(RW // 2 + HALO, CL, CL), side, side),
-        (state, south, north, fold, flags),
+        (state, south, north, fold),
     )
     ocean_next = call(
         functools.partial(deep_kernel, True),

time: 162 us -> 157 us (0.969)
  Pallas kernels: 65.6 us -> 60.2 us
    pallas_call x12, Pallas kernels: 63 us -> 57.5 us  [call(): pl.pallas_call(kernel, grid=(1,) if blocks else (), out_shape=outs, in_sp...]
  transfers between devices with their start and end apart: 21 -> 21, of which waited for: 3 -> 3; matrix products, arithmetic and copies ran while one was open for 0% -> 0% of each run, Pallas kernels for 29% -> 28%
where the time goes in v6:
time: 157 us; the launch traced here: 156 us
  Pallas kernels  60.2 us (38%)
  starting transfers between devices  49.7 us (32%)
  waiting for transfers between devices  36.4 us (23%)
  local copies, waits for them, and re-layouts  8.4 us (5%)
    pallas_call x12, Pallas kernels, call(): pl.pallas_call(kernel, grid=(1,) if blocks else (), out_shape=outs, in_sp...  57.5 us
    ppermute x4, waiting for transfers between devices, to_north(): return lax.ppermute(value, AXES, pairs)  30.1 us
    ppermute x4, starting transfers between devices, to_south(): return lax.ppermute(value, AXES, pairs)  18.3 us
    ppermute x4, starting transfers between devices, to_north(): return lax.ppermute(value, AXES, pairs)  14.8 us
    ppermute x5, starting transfers between devices, to_west(): return lax.ppermute(value, 'gx', [(x, (x - 1) % nx) for x in range(nx)])  14.4 us
    unnamed x38, local copies, waits for them, and re-layouts  8.4 us
    ppermute x5, waiting for transfers between devices, to_east(): return lax.ppermute(value, 'gx', [(x, (x + 1) % nx) for x in range(nx)])  5.33 us
  transfers between devices with their start and end apart: 21, of which 3 were waited for; matrix products, arithmetic and copies ran while one was open for 0% of the time, Pallas kernels for 28%

profile of v6, /device:TPU:4, one launch (start us, length us, event | category | flops | bytes accessed | tf_op | source)
XLA Modules:
  0.0 155.7 jit_solution(16711916249091097116)
XLA Ops:
  0.6 0.0 copy-start.3
  0.6 1.2 copy-done.3
  1.9 1.2 copy-done.6
  3.1 1.0 copy-done.10
  4.1 0.7 copy-done.16
  4.8 2.1 %shard_map.117 = (f32[1920,128]{1,0:T(8,128)S(1)}, f32[1920,128]{1,0:T(8,128)S(1)}) custom-call(f32[2048,128]{1,0:T(8,128)S(1)} %bitcast.5, f32[2048,128]{1,0:T(8,128)S(1)} %bitcast.7, f32[1024,128]{1,0:T(8,128)S(1)} %bitcast.9, s32[32,128]{1,0:T(8,128)S(1)} %copy-done.16), custom_call_target="tpu_custom_call" | custom-call | flops 1000000 | bytes 1000000 | tf_op jit(solution)/shard_map/pallas_call | solution.py:44
  6.9 5.8 %collective-permute-start.6 = (f32[1920,128]{1,0:T(8,128)S(1)}, f32[1920,128]{1,0:T(8,128)S(1)}, u32[]{:S(2)}, u32[]{:S(2)}) collective-permute-start(f32[1920,128]{1,0:T(8,128)S(1)} %get-tuple-element.38), channel_id=1, source_target_pairs={{0,1},{8,9},{16,17},{24,25},{32,33},{40,41},{48,49},{56,57},{1,2},... | collective-permute-start | bytes 2949128 | tf_op jit(solution)/shard_map/ppermute | solution.py:77
  12.7 2.5 %collective-permute-start.7 = (f32[1920,128]{1,0:T(8,128)S(1)}, f32[1920,128]{1,0:T(8,128)S(1)}, u32[]{:S(2)}, u32[]{:S(2)}) collective-permute-start(f32[1920,128]{1,0:T(8,128)S(1)} %get-tuple-element.37.own), channel_id=1, source_target_pairs={{1,0},{9,8},{17,16},{25,24},{33,32},{41,40},{49,48},{57,56},{2,1},... | collective-permute-start | bytes 2949128 | tf_op jit(solution)/shard_map/ppermute | solution.py:83
  15.2 0.7 collective-permute-start.8
  16.0 3.9 %shard_map.116 = (f32[4,16,128,128]{3,2,1,0:T(8,128)S(1)}, f32[1024,128]{1,0:T(8,128)}, f32[1024,128]{1,0:T(8,128)}) custom-call(f32[2048,128]{1,0:T(8,128)S(1)} %bitcast.6, f32[2048,128]{1,0:T(8,128)S(1)} %bitcast.8, f32[1024,128]{1,0:T(8,128)S(1)} %bitcast.10, s32[32,128]{1,0:T(8,128)S(1)} %copy-done.17), custom_call_target="tpu_custom_call" | custom-call | flops 10000000 | bytes 1000000 | tf_op jit(solution)/shard_map/pallas_call | solution.py:44
  19.8 2.0 %copy-done = f32[4,16,128,128]{3,2,1,0:T(8,128)} copy-done((f32[4,16,128,128]{3,2,1,0:T(8,128)}, f32[4,16,128,128]{3,2,1,0:T(8,128)S(1)}, u32[]{:S(2)}) %copy-start) | copy-done | bytes 4194328
  21.8 0.0 collective-permute-start.4
  21.8 3.0 %collective-permute-start.5 = (f32[1024,128]{1,0:T(8,128)}, f32[1024,128]{1,0:T(8,128)}, u32[]{:S(2)}, u32[]{:S(2)}) collective-permute-start(f32[1024,128]{1,0:T(8,128)} %get-tuple-element.36), channel_id=1, source_target_pairs={{0,56},{8,0},{16,8},{24,16},{32,24},{40,32},{48,40},{56,48},{1,57}... | collective-permute-start | bytes 1572872 | tf_op jit(solution)/shard_map/ppermute | solution.py:99
  24.7 30.0 %collective-permute-done.6.south = f32[1920,128]{1,0:T(8,128)S(1)} collective-permute-done((f32[1920,128]{1,0:T(8,128)S(1)}, f32[1920,128]{1,0:T(8,128)S(1)}, u32[]{:S(2)}, u32[]{:S(2)}) %collective-permute-start.6) | collective-permute-done | bytes 983072 | tf_op jit(solution)/shard_map/ppermute | solution.py:77
  54.8 1.0 collective-permute-done.7.north
  55.8 0.0 collective-permute-done.8.fold
  55.8 2.5 %shard_map.118 = (f32[4,12,128,128]{3,2,1,0:T(8,128)S(1)}, f32[768,128]{1,0:T(8,128)}, f32[768,128]{1,0:T(8,128)}) custom-call(f32[1920,128]{1,0:T(8,128)S(1)} %get-tuple-element.37.own, f32[1920,128]{1,0:T(8,128)S(1)} %collective-permute-done.6.south, f32[1920,128]{1,0:T(8,128)S(1)} %collective-permute-done.7.north, f32[1920,128]{1,0:T(8,128)S(1)} %collective-permute-done.8.fold), custom_call_target="tpu_custom_call" | custom-call | flops 5000000 | bytes 1000000 | tf_op jit(solution)/shard_map/pallas_call | solution.py:44
  58.3 2.6 %collective-permute-start.10 = (f32[768,128]{1,0:T(8,128)}, f32[768,128]{1,0:T(8,128)S(1)}, u32[]{:S(2)}, u32[]{:S(2)}) collective-permute-start(f32[768,128]{1,0:T(8,128)} %get-tuple-element.41), channel_id=1, source_target_pairs={{0,56},{8,0},{16,8},{24,16},{32,24},{40,32},{48,40},{56,48},{1,57}... | collective-permute-start | bytes 1179656 | tf_op jit(solution)/shard_map/ppermute | solution.py:99
  60.9 0.0 collective-permute-start.9
  60.9 1.9 %shard_map.112 = (f32[296,128]{1,0:T(8,128)}, f32[296,128]{1,0:T(8,128)}, f32[296,128]{1,0:T(8,128)}) custom-call(f32[2,32,32,128]{3,2,1,0:T(8,128)} %tracers.3, f32[2,32,32,128]{3,2,1,0:T(8,128)} %flow.3, f32[4,32,32,128]{3,2,1,0:T(8,128)} %state.3, s32[3,3,1024]{2,1,0:T(4,128)} %sea_cells.3, s32[3,3,1024]{2,1,0:T(4,128)} %air_cells.3, ...), custom_call_target="tpu_custom_call" | custom-call | flops 1000000 | bytes 1000000 | tf_op jit(solution)/shard_map/pallas_call | solution.py:44
  62.8 3.8 %collective-permute-start = (f32[296,128]{1,0:T(8,128)}, f32[296,128]{1,0:T(8,128)S(1)}, u32[]{:S(2)}, u32[]{:S(2)}) collective-permute-start(f32[296,128]{1,0:T(8,128)} %get-tuple-element.29), channel_id=1, source_target_pairs={{0,1},{8,9},{16,17},{24,25},{32,33},{40,41},{48,49},{56,57},{1,2},... | collective-permute-start | bytes 454664 | tf_op jit(solution)/shard_map/ppermute | solution.py:77
  66.6 0.0 collective-permute-done.4.refs_1_
  66.6 4.4 %collective-permute-start.1 = (f32[296,128]{1,0:T(8,128)}, f32[296,128]{1,0:T(8,128)S(1)}, u32[]{:S(2)}, u32[]{:S(2)}) collective-permute-start(f32[296,128]{1,0:T(8,128)} %get-tuple-element.31), channel_id=1, source_target_pairs={{1,0},{9,8},{17,16},{25,24},{33,32},{41,40},{49,48},{57,56},{2,1},... | collective-permute-start | bytes 454664 | tf_op jit(solution)/shard_map/ppermute | solution.py:83
  71.0 0.0 collective-permute-done.5.refs_2_
  71.0 0.0 collective-permute-done.10.refs_5_
  71.1 0.0 collective-permute-done.9.refs_4_
  71.1 0.0 copy-start.1
  71.1 2.2 %copy-done.1 = f32[4,16,128,128]{3,2,1,0:T(8,128)S(1)} copy-done((f32[4,16,128,128]{3,2,1,0:T(8,128)S(1)}, f32[4,16,128,128]{3,2,1,0:T(8,128)}, u32[]{:S(2)}) %copy-start.1) | copy-done | bytes 4194328
  73.3 11.5 %shard_map.119 = (f32[16,128,128]{2,1,0:T(8,128)S(1)}, f32[768,128]{1,0:T(8,128)S(1)}, f32[768,128]{1,0:T(8,128)S(1)}) custom-call(f32[4,16,128,128]{3,2,1,0:T(8,128)S(1)} %copy-done.1, f32[1024,128]{1,0:T(8,128)S(1)} %collective-permute-done.4.refs_1_, f32[1024,128]{1,0:T(8,128)} %collective-permute-done.5.refs_2_, ...), custom_call_target="tpu_custom_call" | custom-call | flops 40000000 | bytes 1000000 | tf_op jit(solution)/shard_map/pallas_call | solution.py:44
  84.8 3.0 %collective-permute-start.11 = (f32[768,128]{1,0:T(8,128)S(1)}, f32[768,128]{1,0:T(8,128)S(1)}, u32[]{:S(2)}, u32[]{:S(2)}) collective-permute-start(f32[768,128]{1,0:T(8,128)S(1)} %get-tuple-element.43), channel_id=1, source_target_pairs={{0,1},{8,9},{16,17},{24,25},{32,33},{40,41},{48,49},{56,57},{1,2},... | collective-permute-start | bytes 1179656 | tf_op jit(solution)/shard_map/ppermute | solution.py:77
  87.7 0.7 collective-permute-start.13
  88.4 5.3 %collective-permute-start.12 = (f32[768,128]{1,0:T(8,128)S(1)}, f32[768,128]{1,0:T(8,128)S(1)}, u32[]{:S(2)}, u32[]{:S(2)}) collective-permute-start(f32[768,128]{1,0:T(8,128)S(1)} %get-tuple-element.44), channel_id=1, source_target_pairs={{1,0},{9,8},{17,16},{25,24},{33,32},{41,40},{49,48},{57,56},{2,1},... | collective-permute-start | bytes 1179656 | tf_op jit(solution)/shard_map/ppermute | solution.py:83
  93.7 0.0 collective-permute-done.up
  93.7 0.0 collective-permute-done.1.down
  93.8 0.1 shard_map.113
  93.8 0.0 collective-permute-start.2
  93.8 2.9 %collective-permute-start.3 = (f32[744,128]{1,0:T(8,128)S(1)}, f32[744,128]{1,0:T(8,128)S(1)}, u32[]{:S(2)}, u32[]{:S(2)}) collective-permute-start(f32[744,128]{1,0:T(8,128)S(1)} %get-tuple-element.33), channel_id=1, source_target_pairs={{0,56},{8,0},{16,8},{24,16},{32,24},{40,32},{48,40},{56,48},{1,57}... | collective-permute-start | bytes 1142792 | tf_op jit(solution)/shard_map/ppermute | solution.py:99
  96.8 5.3 %collective-permute-done.2.west = f32[744,128]{1,0:T(8,128)S(1)} collective-permute-done((f32[744,128]{1,0:T(8,128)S(1)}, f32[744,128]{1,0:T(8,128)S(1)}, u32[]{:S(2)}, u32[]{:S(2)}) %collective-permute-start.2) | collective-permute-done | bytes 380960 | tf_op jit(solution)/shard_map/ppermute | solution.py:94
  102.1 0.0 collective-permute-done.3.east
  102.1 8.5 %shard_map.121 = (f32[2,32,128]{2,1,0:T(8,128)}, f32[7,32,128]{2,1,0:T(8,128)S(1)}, f32[168,128]{1,0:T(8,128)S(1)}, f32[168,128]{1,0:T(8,128)S(1)}) custom-call(f32[296,128]{1,0:T(8,128)S(1)} %collective-permute-done.up, f32[296,128]{1,0:T(8,128)S(1)} %copy-done.12, f32[296,128]{1,0:T(8,128)S(1)} %collective-permute-done.1.down, ...), custom_call_target="tpu_custom_call" | custom-call | flops 20000000 | bytes 1000000 | tf_op jit(solution)/shard_map/pallas_call | solution.py:44
  110.6 0.0 copy-start.18
  110.7 2.2 %collective-permute-start.16 = (f32[168,128]{1,0:T(8,128)S(1)}, f32[168,128]{1,0:T(8,128)S(1)}, u32[]{:S(2)}, u32[]{:S(2)}) collective-permute-start(f32[168,128]{1,0:T(8,128)S(1)} %get-tuple-element.49), channel_id=1, source_target_pairs={{0,1},{8,9},{16,17},{24,25},{32,33},{40,41},{48,49},{56,57},{1,2},... | collective-permute-start | bytes 258056 | tf_op jit(solution)/shard_map/ppermute | solution.py:77
  112.8 0.7 collective-permute-start.18
  113.5 0.0 collective-permute-done.11.south
  113.5 6.2 %collective-permute-start.17 = (f32[168,128]{1,0:T(8,128)S(1)}, f32[168,128]{1,0:T(8,128)S(1)}, u32[]{:S(2)}, u32[]{:S(2)}) collective-permute-start(f32[168,128]{1,0:T(8,128)S(1)} %get-tuple-element.50), channel_id=1, source_target_pairs={{1,0},{9,8},{17,16},{25,24},{33,32},{41,40},{49,48},{57,56},{2,1},... | collective-permute-start | bytes 258056 | tf_op jit(solution)/shard_map/ppermute | solution.py:83
  119.7 0.0 collective-permute-done.13.fold
  119.7 0.0 collective-permute-done.12.north
  119.8 0.7 shard_map.120
  120.4 0.0 collective-permute-start.14
  120.5 2.9 %collective-permute-start.15 = (f32[448,128]{1,0:T(8,128)S(1)}, f32[448,128]{1,0:T(8,128)S(1)}, u32[]{:S(2)}, u32[]{:S(2)}) collective-permute-start(f32[448,128]{1,0:T(8,128)S(1)} %get-tuple-element.47), channel_id=1, source_target_pairs={{0,56},{8,0},{16,8},{24,16},{32,24},{40,32},{48,40},{56,48},{1,57}... | collective-permute-start | bytes 688136 | tf_op jit(solution)/shard_map/ppermute | solution.py:99
  123.4 0.0 collective-permute-done.16.south
  123.4 0.0 collective-permute-done.18.fold
  123.4 0.0 collective-permute-done.17.north
  123.4 0.2 shard_map.122
  123.6 0.0 collective-permute-start.19
  123.6 2.9 %collective-permute-start.20 = (f32[280,128]{1,0:T(8,128)S(1)}, f32[280,128]{1,0:T(8,128)S(1)}, u32[]{:S(2)}, u32[]{:S(2)}) collective-permute-start(f32[280,128]{1,0:T(8,128)S(1)} %get-tuple-element.53), channel_id=1, source_target_pairs={{0,56},{8,0},{16,8},{24,16},{32,24},{40,32},{48,40},{56,48},{1,57}... | collective-permute-start | bytes 430088 | tf_op jit(solution)/shard_map/ppermute | solution.py:99
  126.6 7.9 %shard_map.114.flux = f32[4,32,128]{2,1,0:T(8,128)S(1)} custom-call(f32[296,128]{1,0:T(8,128)S(1)} %collective-permute-done.up, f32[296,128]{1,0:T(8,128)S(1)} %copy-done.12, f32[296,128]{1,0:T(8,128)S(1)} %collective-permute-done.1.down, f32[744,128]{1,0:T(8,128)S(1)} %collective-permute-done.2.west, f32[744,128]{1,0:T(8,128)S(1)} %collective-permute-done.3.east, ...), custom_call_target="tpu_custom_call" | custom-call | flops 20000000 | bytes 1000000 | tf_op jit(solution)/shard_map/pallas_call | solution.py:44
  134.5 2.7 %shard_map.115 = f32[4,32,32,128]{3,2,1,0:T(8,128)} custom-call(f32[4,32,32,128]{3,2,1,0:T(8,128)S(1)} %copy-done.9, f32[32,128]{1,0:T(8,128)S(1)} %copy-done.18, f32[4,32,128]{2,1,0:T(8,128)S(1)} %shard_map.114.flux), custom_call_target="tpu_custom_call" | custom-call | flops 5000000 | bytes 4200000 | tf_op jit(solution)/shard_map/pallas_call | solution.py:631
  137.1 0.0 collective-permute-done.19.w2
  137.1 0.0 collective-permute-done.20.e2
  137.1 4.2 %shard_map.123.refs_9_ = f32[2,32,128]{2,1,0:T(8,128)S(1)} custom-call(f32[7,80,128]{2,1,0:T(8,128)S(1)} %get-tuple-element.51.mine, f32[280,128]{1,0:T(8,128)S(1)} %collective-permute-done.19.w2, f32[280,128]{1,0:T(8,128)S(1)} %collective-permute-done.20.e2), custom_call_target="tpu_custom_call" | custom-call | flops 10000000 | bytes 1000000 | tf_op jit(solution)/shard_map/pallas_call | solution.py:44
  141.4 0.0 collective-permute-done.14.refs_7_
  141.4 0.0 collective-permute-done.15.refs_8_
  141.4 14.2 %shard_map.124 = f32[2048,128]{1,0:T(8,128)} custom-call(f32[4,16,128,128]{3,2,1,0:T(8,128)S(1)} %copy-done.2, f32[1024,128]{1,0:T(8,128)S(1)} %collective-permute-done.4.refs_1_, f32[1024,128]{1,0:T(8,128)} %collective-permute-done.5.refs_2_, f32[4,12,128,128]{3,2,1,0:T(8,128)S(1)} %get-tuple-element.39.refs_3_, f32[768,128]{1,0:T(8,128)} %collective-permute-done.9.refs_4_, ...), custom_call_target="tpu_custom_call" | custom-call | flops 60000000 | bytes 1000000 | tf_op jit(solution)/shard_map/pallas_call | solution.py:44
  (29 shorter events, 0.1 us)
Async XLA Ops:
  0.6 1.2 copy-start.3
  1.9 1.2 copy-start.6
  3.1 1.0 copy-start.10
  4.1 0.7 copy-start.16
  4.8 11.1 %copy-start.4 = (f32[2,32,32,128]{3,2,1,0:T(8,128)S(1)}, f32[2,32,32,128]{3,2,1,0:T(8,128)}, u32[]{:S(2)}) copy-start(f32[2,32,32,128]{3,2,1,0:T(8,128)} %tracers.3) | copy-start | bytes 3145732
  4.8 11.1 %copy-start.7 = (f32[2,32,32,128]{3,2,1,0:T(8,128)S(1)}, f32[2,32,32,128]{3,2,1,0:T(8,128)}, u32[]{:S(2)}) copy-start(f32[2,32,32,128]{3,2,1,0:T(8,128)} %flow.3) | copy-start | bytes 3145732
  4.8 11.1 %copy-start.17 = (s32[32,128]{1,0:T(8,128)S(1)}, s32[32,128]{1,0:T(8,128)}, u32[]{:S(2)}) copy-start(s32[32,128]{1,0:T(8,128)} %mask.5) | copy-start | bytes 49156
  6.9 47.9 %collective-permute-start.6 = (f32[1920,128]{1,0:T(8,128)S(1)}, f32[1920,128]{1,0:T(8,128)S(1)}, u32[]{:S(2)}, u32[]{:S(2)}) collective-permute-start(f32[1920,128]{1,0:T(8,128)S(1)} %get-tuple-element.38), channel_id=1, source_target_pairs={{0,1},{8,9},{16,17},{24,25},{32,33},{40,41},{48,49},{56,57},{1,2},... | collective-permute-start | bytes 2949128 | tf_op jit(solution)/shard_map/ppermute | solution.py:77
  12.7 43.1 %collective-permute-start.7 = (f32[1920,128]{1,0:T(8,128)S(1)}, f32[1920,128]{1,0:T(8,128)S(1)}, u32[]{:S(2)}, u32[]{:S(2)}) collective-permute-start(f32[1920,128]{1,0:T(8,128)S(1)} %get-tuple-element.37.own), channel_id=1, source_target_pairs={{1,0},{9,8},{17,16},{25,24},{33,32},{41,40},{49,48},{57,56},{2,1},... | collective-permute-start | bytes 2949128 | tf_op jit(solution)/shard_map/ppermute | solution.py:83
  15.2 40.6 %collective-permute-start.8 = (f32[1920,128]{1,0:T(8,128)S(1)}, f32[1920,128]{1,0:T(8,128)S(1)}, u32[]{:S(2)}, u32[]{:S(2)}) collective-permute-start(f32[1920,128]{1,0:T(8,128)S(1)} %get-tuple-element.38), channel_id=1, source_target_pairs={{71,127},{79,119},{87,111},{95,103},{103,95},{111,87},{119,79},{12... | collective-permute-start | bytes 2949128 | tf_op jit(solution)/shard_map/ppermute | solution.py:89
  19.8 2.0 %copy-start = (f32[4,16,128,128]{3,2,1,0:T(8,128)}, f32[4,16,128,128]{3,2,1,0:T(8,128)S(1)}, u32[]{:S(2)}) copy-start(f32[4,16,128,128]{3,2,1,0:T(8,128)S(1)} %get-tuple-element.34.refs_0_) | copy-start | bytes 12582916
  21.8 44.8 %collective-permute-start.4 = (f32[1024,128]{1,0:T(8,128)}, f32[1024,128]{1,0:T(8,128)S(1)}, u32[]{:S(2)}, u32[]{:S(2)}) collective-permute-start(f32[1024,128]{1,0:T(8,128)} %get-tuple-element.35), channel_id=1, source_target_pairs={{0,8},{8,16},{16,24},{24,32},{32,40},{40,48},{48,56},{56,0},{1,9},... | collective-permute-start | bytes 1572872 | tf_op jit(solution)/shard_map/ppermute | solution.py:94
  21.8 49.2 %collective-permute-start.5 = (f32[1024,128]{1,0:T(8,128)}, f32[1024,128]{1,0:T(8,128)}, u32[]{:S(2)}, u32[]{:S(2)}) collective-permute-start(f32[1024,128]{1,0:T(8,128)} %get-tuple-element.36), channel_id=1, source_target_pairs={{0,56},{8,0},{16,8},{24,16},{32,24},{40,32},{48,40},{56,48},{1,57}... | collective-permute-start | bytes 1572872 | tf_op jit(solution)/shard_map/ppermute | solution.py:99
  58.3 12.8 %collective-permute-start.10 = (f32[768,128]{1,0:T(8,128)}, f32[768,128]{1,0:T(8,128)S(1)}, u32[]{:S(2)}, u32[]{:S(2)}) collective-permute-start(f32[768,128]{1,0:T(8,128)} %get-tuple-element.41), channel_id=1, source_target_pairs={{0,56},{8,0},{16,8},{24,16},{32,24},{40,32},{48,40},{56,48},{1,57}... | collective-permute-start | bytes 1179656 | tf_op jit(solution)/shard_map/ppermute | solution.py:99
  60.9 10.1 %collective-permute-start.9 = (f32[768,128]{1,0:T(8,128)}, f32[768,128]{1,0:T(8,128)}, u32[]{:S(2)}, u32[]{:S(2)}) collective-permute-start(f32[768,128]{1,0:T(8,128)} %get-tuple-element.40), channel_id=1, source_target_pairs={{0,8},{8,16},{16,24},{24,32},{32,40},{40,48},{48,56},{56,0},{1,9},... | collective-permute-start | bytes 1179656 | tf_op jit(solution)/shard_map/ppermute | solution.py:94
  62.8 30.9 %collective-permute-start = (f32[296,128]{1,0:T(8,128)}, f32[296,128]{1,0:T(8,128)S(1)}, u32[]{:S(2)}, u32[]{:S(2)}) collective-permute-start(f32[296,128]{1,0:T(8,128)} %get-tuple-element.29), channel_id=1, source_target_pairs={{0,1},{8,9},{16,17},{24,25},{32,33},{40,41},{48,49},{56,57},{1,2},... | collective-permute-start | bytes 454664 | tf_op jit(solution)/shard_map/ppermute | solution.py:77
  66.6 27.1 %collective-permute-start.1 = (f32[296,128]{1,0:T(8,128)}, f32[296,128]{1,0:T(8,128)S(1)}, u32[]{:S(2)}, u32[]{:S(2)}) collective-permute-start(f32[296,128]{1,0:T(8,128)} %get-tuple-element.31), channel_id=1, source_target_pairs={{1,0},{9,8},{17,16},{25,24},{33,32},{41,40},{49,48},{57,56},{2,1},... | collective-permute-start | bytes 454664 | tf_op jit(solution)/shard_map/ppermute | solution.py:83
  71.1 2.2 %copy-start.1 = (f32[4,16,128,128]{3,2,1,0:T(8,128)S(1)}, f32[4,16,128,128]{3,2,1,0:T(8,128)}, u32[]{:S(2)}) copy-start(f32[4,16,128,128]{3,2,1,0:T(8,128)} %copy-done) | copy-start | bytes 12582916
  73.3 20.5 %copy-start.12 = (f32[296,128]{1,0:T(8,128)S(1)}, f32[296,128]{1,0:T(8,128)}, u32[]{:S(2)}) copy-start(f32[296,128]{1,0:T(8,128)} %get-tuple-element.30.mine) | copy-start | bytes 454660
  73.3 28.9 %copy-start.5 = (f32[2,32,32,128]{3,2,1,0:T(8,128)S(1)}, f32[2,32,32,128]{3,2,1,0:T(8,128)}, u32[]{:S(2)}) copy-start(f32[2,32,32,128]{3,2,1,0:T(8,128)} %tracers.3) | copy-start | bytes 3145732
  73.3 28.9 %copy-start.8 = (f32[2,32,32,128]{3,2,1,0:T(8,128)S(1)}, f32[2,32,32,128]{3,2,1,0:T(8,128)}, u32[]{:S(2)}) copy-start(f32[2,32,32,128]{3,2,1,0:T(8,128)} %flow.3) | copy-start | bytes 3145732
  73.3 28.9 %copy-start.11 = (f32[32,32,128]{2,1,0:T(8,128)S(1)}, f32[32,32,128]{2,1,0:T(8,128)}, u32[]{:S(2)}) copy-start(f32[32,32,128]{2,1,0:T(8,128)} %kappa.3) | copy-start | bytes 1572868
  84.8 28.8 %collective-permute-start.11 = (f32[768,128]{1,0:T(8,128)S(1)}, f32[768,128]{1,0:T(8,128)S(1)}, u32[]{:S(2)}, u32[]{:S(2)}) collective-permute-start(f32[768,128]{1,0:T(8,128)S(1)} %get-tuple-element.43), channel_id=1, source_target_pairs={{0,1},{8,9},{16,17},{24,25},{32,33},{40,41},{48,49},{56,57},{1,2},... | collective-permute-start | bytes 1179656 | tf_op jit(solution)/shard_map/ppermute | solution.py:77
  87.7 32.0 %collective-permute-start.13 = (f32[768,128]{1,0:T(8,128)S(1)}, f32[768,128]{1,0:T(8,128)S(1)}, u32[]{:S(2)}, u32[]{:S(2)}) collective-permute-start(f32[768,128]{1,0:T(8,128)S(1)} %get-tuple-element.43), channel_id=1, source_target_pairs={{71,127},{79,119},{87,111},{95,103},{103,95},{111,87},{119,79},{12... | collective-permute-start | bytes 1179656 | tf_op jit(solution)/shard_map/ppermute | solution.py:89
  88.4 31.3 %collective-permute-start.12 = (f32[768,128]{1,0:T(8,128)S(1)}, f32[768,128]{1,0:T(8,128)S(1)}, u32[]{:S(2)}, u32[]{:S(2)}) collective-permute-start(f32[768,128]{1,0:T(8,128)S(1)} %get-tuple-element.44), channel_id=1, source_target_pairs={{1,0},{9,8},{17,16},{25,24},{33,32},{41,40},{49,48},{57,56},{2,1},... | collective-permute-start | bytes 1179656 | tf_op jit(solution)/shard_map/ppermute | solution.py:83
  93.8 8.3 %collective-permute-start.2 = (f32[744,128]{1,0:T(8,128)S(1)}, f32[744,128]{1,0:T(8,128)S(1)}, u32[]{:S(2)}, u32[]{:S(2)}) collective-permute-start(f32[744,128]{1,0:T(8,128)S(1)} %get-tuple-element.32), channel_id=1, source_target_pairs={{0,8},{8,16},{16,24},{24,32},{32,40},{40,48},{48,56},{56,0},{1,9},... | collective-permute-start | bytes 1142792 | tf_op jit(solution)/shard_map/ppermute | solution.py:94
  93.8 8.3 %collective-permute-start.3 = (f32[744,128]{1,0:T(8,128)S(1)}, f32[744,128]{1,0:T(8,128)S(1)}, u32[]{:S(2)}, u32[]{:S(2)}) collective-permute-start(f32[744,128]{1,0:T(8,128)S(1)} %get-tuple-element.33), channel_id=1, source_target_pairs={{0,56},{8,0},{16,8},{24,16},{32,24},{40,32},{48,40},{56,48},{1,57}... | collective-permute-start | bytes 1142792 | tf_op jit(solution)/shard_map/ppermute | solution.py:99
  110.6 15.9 %copy-start.13 = (f32[2,3,3,1024]{3,0,2,1:T(2,128)S(1)}, f32[2,3,3,1024]{3,0,2,1:T(2,128)}, u32[]{:S(2)}) copy-start(f32[2,3,3,1024]{3,0,2,1:T(2,128)} %param.17) | copy-start | bytes 221188
  110.6 15.9 %copy-start.14 = (s32[3,3,1024]{2,1,0:T(4,128)S(1)}, s32[3,3,1024]{2,1,0:T(4,128)}, u32[]{:S(2)}) copy-start(s32[3,3,1024]{2,1,0:T(4,128)} %sea_cells.3) | copy-start | bytes 110596
  110.6 15.9 %copy-start.15 = (s32[3,3,1024]{2,1,0:T(4,128)S(1)}, s32[3,3,1024]{2,1,0:T(4,128)}, u32[]{:S(2)}) copy-start(s32[3,3,1024]{2,1,0:T(4,128)} %air_cells.3) | copy-start | bytes 110596
  110.6 23.8 %copy-start.9 = (f32[4,32,32,128]{3,2,1,0:T(8,128)S(1)}, f32[4,32,32,128]{3,2,1,0:T(8,128)}, u32[]{:S(2)}) copy-start(f32[4,32,32,128]{3,2,1,0:T(8,128)} %state.3) | copy-start | bytes 6291460
  110.6 23.8 %copy-start.18 = (f32[32,128]{1,0:T(8,128)S(1)}, f32[32,128]{1,0:T(8,128)}, u32[]{:S(2)}) copy-start(f32[32,128]{1,0:T(8,128)} %kappa.2) | copy-start | bytes 49156
  110.7 12.8 %collective-permute-start.16 = (f32[168,128]{1,0:T(8,128)S(1)}, f32[168,128]{1,0:T(8,128)S(1)}, u32[]{:S(2)}, u32[]{:S(2)}) collective-permute-start(f32[168,128]{1,0:T(8,128)S(1)} %get-tuple-element.49), channel_id=1, source_target_pairs={{0,1},{8,9},{16,17},{24,25},{32,33},{40,41},{48,49},{56,57},{1,2},... | collective-permute-start | bytes 258056 | tf_op jit(solution)/shard_map/ppermute | solution.py:77
  112.8 10.6 %collective-permute-start.18 = (f32[168,128]{1,0:T(8,128)S(1)}, f32[168,128]{1,0:T(8,128)S(1)}, u32[]{:S(2)}, u32[]{:S(2)}) collective-permute-start(f32[168,128]{1,0:T(8,128)S(1)} %get-tuple-element.49), channel_id=1, source_target_pairs={{71,127},{79,119},{87,111},{95,103},{103,95},{111,87},{119,79},{12... | collective-permute-start | bytes 258056 | tf_op jit(solution)/shard_map/ppermute | solution.py:89
  113.5 9.9 %collective-permute-start.17 = (f32[168,128]{1,0:T(8,128)S(1)}, f32[168,128]{1,0:T(8,128)S(1)}, u32[]{:S(2)}, u32[]{:S(2)}) collective-permute-start(f32[168,128]{1,0:T(8,128)S(1)} %get-tuple-element.50), channel_id=1, source_target_pairs={{1,0},{9,8},{17,16},{25,24},{33,32},{41,40},{49,48},{57,56},{2,1},... | collective-permute-start | bytes 258056 | tf_op jit(solution)/shard_map/ppermute | solution.py:83
  120.4 21.0 %collective-permute-start.14 = (f32[448,128]{1,0:T(8,128)S(1)}, f32[448,128]{1,0:T(8,128)S(1)}, u32[]{:S(2)}, u32[]{:S(2)}) collective-permute-start(f32[448,128]{1,0:T(8,128)S(1)} %get-tuple-element.46), channel_id=1, source_target_pairs={{0,8},{8,16},{16,24},{24,32},{32,40},{40,48},{48,56},{56,0},{1,9},... | collective-permute-start | bytes 688136 | tf_op jit(solution)/shard_map/ppermute | solution.py:94
  120.5 20.9 %collective-permute-start.15 = (f32[448,128]{1,0:T(8,128)S(1)}, f32[448,128]{1,0:T(8,128)S(1)}, u32[]{:S(2)}, u32[]{:S(2)}) collective-permute-start(f32[448,128]{1,0:T(8,128)S(1)} %get-tuple-element.47), channel_id=1, source_target_pairs={{0,56},{8,0},{16,8},{24,16},{32,24},{40,32},{48,40},{56,48},{1,57}... | collective-permute-start | bytes 688136 | tf_op jit(solution)/shard_map/ppermute | solution.py:99
  123.6 13.6 %collective-permute-start.19 = (f32[280,128]{1,0:T(8,128)S(1)}, f32[280,128]{1,0:T(8,128)S(1)}, u32[]{:S(2)}, u32[]{:S(2)}) collective-permute-start(f32[280,128]{1,0:T(8,128)S(1)} %get-tuple-element.52), channel_id=1, source_target_pairs={{0,8},{8,16},{16,24},{24,32},{32,40},{40,48},{48,56},{56,0},{1,9},... | collective-permute-start | bytes 430088 | tf_op jit(solution)/shard_map/ppermute | solution.py:94
  123.6 13.5 %collective-permute-start.20 = (f32[280,128]{1,0:T(8,128)S(1)}, f32[280,128]{1,0:T(8,128)S(1)}, u32[]{:S(2)}, u32[]{:S(2)}) collective-permute-start(f32[280,128]{1,0:T(8,128)S(1)} %get-tuple-element.53), channel_id=1, source_target_pairs={{0,56},{8,0},{16,8},{24,16},{32,24},{40,32},{48,40},{56,48},{1,57}... | collective-permute-start | bytes 430088 | tf_op jit(solution)/shard_map/ppermute | solution.py:99
  134.4 7.0 %copy-start.2 = (f32[4,16,128,128]{3,2,1,0:T(8,128)S(1)}, f32[4,16,128,128]{3,2,1,0:T(8,128)}, u32[]{:S(2)}) copy-start(f32[4,16,128,128]{3,2,1,0:T(8,128)} %copy-done) | copy-start | bytes 12582916

commit v7 on v6

--- a/solution.py
+++ b/solution.py
@@ -21,16 +21,18 @@
 LV = 32
 RW = 32
 CL = 128
-HALO = 12
+NEAR = 8
 SIDE = 16
 EDGE = 24
-WIDTH = 168
+WIDTH = 176
 DEEP = ITERS
 SR = RW + 2 * DEEP
 SEA = 3 * RW
 VALS = SEA + 4 * RW
 LINES = 8
-EDGE_MIB, OWN_MIB, FIRST_MIB, FINAL_MIB, FLUX_MIB = 12, 14, 19, 21, 10
+FAR = NEAR * 3 * LV
+SURF = 7 * SR // 2
+EDGE_MIB, OWN_MIB, FIRST_MIB, FINAL_MIB, FLUX_MIB = 12, 14, 17, 23, 10
 
 
 VMEM = pl.BlockSpec(memory_space=pltpu.VMEM)
@@ -108,23 +110,23 @@
     return ref[pl.ds(base + row, LV, stride=RW), :]
 
 
-def edge_kernel(tracers, flow, kappa, mask, top, bottom):
+def edge_kernel(start, tracers, flow, kappa, mask, top, bottom):
     def body(k, carry):
-        for out, row in ((bottom, k), (top, RW - 1 - k)):
+        for out, row in ((bottom, start + k), (top, RW - 1 - start - k)):
             sea = mask[pl.ds(row, 1), :].astype(F32)
-            parts = (
-                level_rows(tracers, 0, row),
-                level_rows(tracers, LV * RW, row),
+            parts = [
                 sea * level_rows(flow, 0, row),
                 sea * level_rows(flow, LV * RW, row),
                 sea * level_rows(kappa, 0, row),
-            )
+            ]
+            if start == 0:
+                parts = [level_rows(tracers, 0, row), level_rows(tracers, LV * RW, row)] + parts
             for f, part in enumerate(parts):
                 where = pl.multiple_of((k * len(parts) + f) * LV, LV)
                 out[pl.ds(where, LV), :] = part
         return carry
 
-    lax.fori_loop(0, HALO, body, 0)
+    lax.fori_loop(0, NEAR, body, 0)
 
 
 def columns(low, high, sign=1.0):
@@ -133,12 +135,14 @@
     return jnp.concatenate([a, b, c, d] if sign > 0 else [a, b, -c, -d], axis=0).T
 
 
-def emit_columns(i, low, high, x, mw, me):
-    parts = [columns((low[0], low[1]), (high[0], high[1]))]
-    for f, sign in ((2, 1.0), (3, -1.0), (4, 1.0)):
+def emit_columns(i, low, high, x, mw, me, base=0):
+    parts = []
+    if len(low) == 5:
+        parts.append(columns((low[0], low[1]), (high[0], high[1])))
+    for f, sign in ((-3, 1.0), (-2, -1.0), (-1, 1.0)):
         parts.append(columns((low[f],) * 2, (high[f],) * 2, sign))
     for f, t in enumerate(parts):
-        rows = pl.ds(pl.multiple_of((f * x.shape[1] + i) * SIDE, SIDE), SIDE)
+        rows = pl.ds(pl.multiple_of(base + (f * x.shape[1] + i) * SIDE, 8), SIDE)
         x[f, i] = t
         mw[rows, :] = t[:SIDE]
         me[rows, :] = t[CL - SIDE :]
@@ -166,35 +170,36 @@
     lax.fori_loop(0, RW // 4, inner, 0)
 
 
-def halo_kernel(own, south, north, fold, x, mw, me):
+def halo_kernel(count, skip, base, own, south, north, fold, x, mw, me):
     first, last = at_ends()
 
     def halo(p, carry):
         for n in range(2):
             i = 2 * p + n
             low, high = [], []
-            for f in range(5):
-                part = pl.ds(pl.multiple_of(((HALO - 1 - i) * 5 + f) * LV, LV), LV)
-                mirror = own[part, :]
+            for f in range(count):
+                line = pl.multiple_of(((NEAR - 1 - i) * count + f) * LV, LV)
+                part = pl.ds(pl.multiple_of(skip + line, 8), LV)
+                mirror = own[pl.ds(line, LV), :]
                 turned = reversed_lanes(fold[part, :])
-                if f == 3:
+                if f == count - 2:
                     mirror = -mirror
-                if f in (2, 3):
+                if f in (count - 3, count - 2):
                     turned = -turned
                 low.append(jnp.where(first, mirror, south[part, :]))
                 high.append(jnp.where(last, turned, north[part, :]))
-            emit_columns(i, low, high, x, mw, me)
+            emit_columns(i, low, high, x, mw, me, base)
         return carry
 
-    lax.fori_loop(0, HALO // 2, halo, 0)
+    lax.fori_loop(0, NEAR // 2, halo, 0)
 
 
 def deep_kernel(final, *refs):
-    halo = HALO
+    halo = SIDE if final else NEAR
     xo, wo, eo, xn, wn, en = refs[:6]
     if final:
-        xts, w2, e2, surface, out = refs[6:11]
-        scratch = refs[11:]
+        xf, wf, ef, xts, w2, e2, surface, out = refs[6:14]
+        scratch = refs[14:]
     else:
         state, top, bottom = refs[6:9]
         scratch = refs[9:]
@@ -215,14 +220,14 @@
         cu[i, where] = d
         cc[i, where] = 1.0 - ((a + b) + (c + d))
 
-    def fill(x, w, e, start):
-        lead = 1
+    def fill(x, w, e, start, base=0):
+        lead = x.shape[0] - 3
 
         def body(p, carry):
             for n in range(2):
                 i = 2 * p + n
                 lines = [
-                    pl.ds(pl.multiple_of((f * x.shape[1] + i) * SIDE, SIDE), SIDE)
+                    pl.ds(pl.multiple_of(base + (f * x.shape[1] + i) * SIDE, 8), SIDE)
                     for f in range(lead + 3)
                 ]
                 to = start + i
@@ -244,7 +249,9 @@
 
         lax.fori_loop(0, x.shape[1] // 2, body, 0)
 
-    fill(xn, wn, en, 0)
+    if final:
+        fill(xf, wf, ef, 0, SURF)
+    fill(xn, wn, en, halo - NEAR)
     fill(xo, wo, eo, halo)
 
     def at(ref, i, j):
@@ -303,7 +310,7 @@
         low = lax.broadcasted_iota(jnp.int32, (CL, CL), 1) < CL // 2
         for i in range(RW // 2):
             state[i] = s0[i + halo, mid]
-        half = HALO // 2
+        half = SIDE // 2
         for k in range(half):
             near, far = s0[halo + k, mid], s0[halo + k + half, mid]
             where = slice(k * CL, (k + 1) * CL)
@@ -314,7 +321,7 @@
 def join_kernel(state, south, north, fold, xts, mw, me):
     first, last = at_ends()
     low = lax.broadcasted_iota(jnp.int32, (CL, CL), 1) < CL // 2
-    half = HALO // 2
+    half = SIDE // 2
     flip = jnp.where(
         lax.broadcasted_iota(jnp.int32, (CL, CL), 0)
         + lax.broadcasted_iota(jnp.int32, (CL, CL), 1)
@@ -324,7 +331,7 @@
     ).astype(F32)
     rows = {}
     for i in range(RW // 2):
-        rows[HALO + i] = state[i]
+        rows[SIDE + i] = state[i]
     for k in range(half):
         where = slice(k * CL, (k + 1) * CL)
         s, n = south[where], north[where]
@@ -333,8 +340,8 @@
         for kk, sv, nv, fv in ((k, s, n_roll, f_roll), (k + half, s_roll, n, f)):
             down = jnp.where(first, state[kk], sv)
             up = jnp.where(last, fv, nv)
-            rows[HALO - 1 - kk] = jnp.where(low, down, up)
-    count = RW // 2 + HALO
+            rows[SIDE - 1 - kk] = jnp.where(low, down, up)
+    count = RW // 2 + SIDE
     for i in range(count):
         where = pl.ds(i * SIDE, SIDE)
         xts[i] = rows[i]
@@ -342,7 +349,8 @@
         me[where, :] = rows[i][CL - SIDE :]
 
 
-def surface_join_kernel(fields, south, north, fold, joined, mw, me):
+def surface_join_kernel(fields, own, south, north, fold, joined, x, mw, me):
+    halo_kernel(3, 7 * DEEP, SURF, own, south, north, fold, x, mw, me)
     first, last = at_ends()
     for f in range(7):
         part = slice(f * DEEP, (f + 1) * DEEP)
@@ -561,7 +569,7 @@
 
 
 def sea_flux_kernel(
-    up, mine, down, west, east, mask, tracers, flow, kappa,
+    up, mine, down, west, east, mask, tracers, flow, kappa, far_top, far_bottom,
     stress, fields, top, bottom, vals, air, cells, weight,
 ):
     def line(ref, start):
@@ -604,6 +612,8 @@
     for f in range(7):
         top[f * DEEP : (f + 1) * DEEP] = fields[f, RW - DEEP :]
         bottom[f * DEEP : (f + 1) * DEEP] = fields[f, :DEEP]
+    top[7 * DEEP :] = far_top[...]
+    bottom[7 * DEEP :] = far_bottom[...]
 
 
 def atmos_kernel(state, kappa, flux, out):
@@ -676,8 +686,10 @@
         ocean_kappa.reshape(-1, CL),
         sea_mask,
     )
-    near = shape(HALO * 5 * LV, CL)
-    top, bottom = call(edge_kernel, (near, near), deep_args, mib=EDGE_MIB)
+    near = shape(NEAR * 5 * LV, CL)
+    top, bottom = call(
+        functools.partial(edge_kernel, 0), (near, near), deep_args, mib=EDGE_MIB
+    )
     south, north = to_north(top), to_south(bottom)
     fold = across_fold(top)
 
@@ -688,6 +700,11 @@
     def extended(count):
         return (shape(4, count, CL, CL),) + (shape(4 * count * SIDE, CL),) * 2
 
+    far = shape(FAR, CL)
+    far_top, far_bottom = call(
+        functools.partial(edge_kernel, NEAR), (far, far), deep_args, mib=EDGE_MIB
+    )
+
     xo, mw, me = call(
         own_kernel, extended(RW // 2), deep_args, flops=10_000_000, mib=OWN_MIB
     )
@@ -695,11 +712,13 @@
 
     around = (up, mine, down, west_in, east_in)
     vals = pltpu.VMEM((8, 16, slots), F32)
-    edge = shape(7 * DEEP, CL)
+    edge = shape(7 * DEEP + FAR, CL)
     ocean_stress, fields, s_top, s_bottom = call(
         sea_flux_kernel,
         (shape(2, RW, CL), shape(7, RW, CL), edge, edge),
-        (*around, sea_mask, ocean_tracers, ocean_flow, ocean_kappa),
+        (
+            *around, sea_mask, ocean_tracers, ocean_flow, ocean_kappa, far_top, far_bottom,
+        ),
         scratch=[
             vals,
             pltpu.VMEM((9, 4 * RW, CL), F32),
@@ -723,28 +742,36 @@
     atmos_next = atmosphere(atmos_state, atmos_kappa, atmos_flux)
 
     xn, mw, me = call(
-        halo_kernel,
-        extended(HALO),
+        functools.partial(halo_kernel, 5, 0, 0),
+        extended(NEAR),
         (bottom, south, north, fold),
         flops=5_000_000,
         mib=OWN_MIB,
     )
     wn, en = to_east(me), to_west(mw)
-    buffers = [pltpu.VMEM((RW // 2 + HALO, WIDTH, CL), F32)] * 7
-    pair = shape(HALO // 2 * CL, CL)
+
+    def buffers(halo):
+        return [pltpu.VMEM((RW // 2 + halo, WIDTH, CL), F32)] * 7
+
+    pair = shape(SIDE // 2 * CL, CL)
     state, top, bottom = call(
         functools.partial(deep_kernel, False),
         (shape(RW // 2, CL, CL), pair, pair),
         (xo, wo, eo, xn, wn, en),
-        scratch=buffers,
+        scratch=buffers(NEAR),
         flops=40_000_000,
         mib=FIRST_MIB,
     )
     south, north = to_north(top), to_south(bottom)
     fold = across_fold(top)
 
-    side = shape(7 * SR // 2, CL)
-    joined, sw, se = call(surface_join_kernel, (shape(7, SR, CL), side, side), (fields, *s_args))
+    side = shape(SURF + 3 * NEAR * SIDE, CL)
+    joined, xf, sw, se = call(
+        surface_join_kernel,
+        (shape(7, SR, CL), shape(3, NEAR, CL, CL), side, side),
+        (fields, far_bottom, *s_args),
+        mib=OWN_MIB,
+    )
     w3, e3 = to_east(se), to_west(sw)
     wide = pltpu.VMEM((SR, 2 * CL), F32)
     surface = call(
@@ -755,17 +782,17 @@
         flops=10_000_000,
     )
 
-    side = shape((RW // 2 + HALO) * SIDE, CL)
+    side = shape((RW // 2 + SIDE) * SIDE, CL)
     xts, mw, me = call(
         join_kernel,
-        (shape(RW // 2 + HALO, CL, CL), side, side),
+        (shape(RW // 2 + SIDE, CL, CL), side, side),
         (state, south, north, fold),
     )
     ocean_next = call(
         functools.partial(deep_kernel, True),
         shape(2 * LV * RW, CL),
-        (xo, wo, eo, xn, wn, en, xts, to_east(me), to_west(mw), surface),
-        scratch=buffers,
+        (xo, wo, eo, xn, wn, en, xf, w3, e3, xts, to_east(me), to_west(mw), surface),
+        scratch=buffers(SIDE),
         flops=60_000_000,
         mib=FINAL_MIB,
     )

time: 157 us -> 144 us (0.917)
  waiting for transfers between devices: 36.4 us -> 28.9 us
  local copies, waits for them, and re-layouts: 8.4 us -> 5.17 us
  Pallas kernels: 60.2 us -> 58.3 us
    ppermute x4, waiting for transfers between devices: 30.1 us -> 14.5 us  [to_north(): return lax.ppermute(value, AXES, pairs)]
    ppermute x4, waiting for transfers between devices: 1.02 us -> 14.4 us  [to_south(): return lax.ppermute(value, AXES, pairs)]
    ppermute x5, waiting for transfers between devices: 5.33 us -> 0.04 us  [to_east(): return lax.ppermute(value, 'gx', [(x, (x + 1) % nx) for x in range(nx)])]
    unnamed x38 -> x30, local copies, waits for them, and re-layouts: 8.4 us -> 5.17 us
    ppermute x5, starting transfers between devices: 14.4 us -> 11.7 us  [to_west(): return lax.ppermute(value, 'gx', [(x, (x - 1) % nx) for x in range(nx)])]
    pallas_call x12 -> x13, Pallas kernels: 57.5 us -> 55.6 us  [call(): pl.pallas_call(kernel, grid=(1,) if blocks else (), out_shape=outs, in_sp...]
  transfers between devices with their start and end apart: 21 -> 21, of which waited for: 3 -> 5; matrix products, arithmetic and copies ran while one was open for 0% -> 0% of each run, Pallas kernels for 28% -> 27%
where the time goes in v7:
time: 144 us; the launch traced here: 143 us
  Pallas kernels  58.3 us (40%)
  starting transfers between devices  49.8 us (35%)
  waiting for transfers between devices  28.9 us (20%)
  local copies, waits for them, and re-layouts  5.17 us (4%)
    pallas_call x13, Pallas kernels, call(): pl.pallas_call(kernel, grid=(1,) if blocks else (), out_shape=outs, in_sp...  55.6 us
    ppermute x4, starting transfers between devices, to_south(): return lax.ppermute(value, AXES, pairs)  19.1 us
    ppermute x4, starting transfers between devices, to_north(): return lax.ppermute(value, AXES, pairs)  16.2 us
    ppermute x4, waiting for transfers between devices, to_north(): return lax.ppermute(value, AXES, pairs)  14.5 us
    ppermute x4, waiting for transfers between devices, to_south(): return lax.ppermute(value, AXES, pairs)  14.4 us
    ppermute x5, starting transfers between devices, to_west(): return lax.ppermute(value, 'gx', [(x, (x - 1) % nx) for x in range(nx)])  11.7 us
    unnamed x30, local copies, waits for them, and re-layouts  5.17 us
  transfers between devices with their start and end apart: 21, of which 5 were waited for; matrix products, arithmetic and copies ran while one was open for 0% of the time, Pallas kernels for 27%

profile of v7, /device:TPU:4, one launch (start us, length us, event | category | flops | bytes accessed | tf_op | source)
XLA Modules:
  0.0 143.1 jit_solution(12142981695519144854)
XLA Ops:
  0.6 0.0 copy-start
  0.6 1.2 copy-done
  1.9 1.2 copy-done.2
  3.1 1.0 copy-done.5
  4.1 0.7 copy-done.10
  4.8 2.2 %shard_map.117 = (f32[1280,128]{1,0:T(8,128)}, f32[1280,128]{1,0:T(8,128)S(1)}) custom-call(f32[2048,128]{1,0:T(8,128)S(1)} %bitcast.5, f32[2048,128]{1,0:T(8,128)S(1)} %bitcast.8, f32[1024,128]{1,0:T(8,128)S(1)} %bitcast.11, s32[32,128]{1,0:T(8,128)S(1)} %copy-done.10), custom_call_target="tpu_custom_call" | custom-call | flops 1000000 | bytes 1000000 | tf_op jit(solution)/shard_map/pallas_call | solution.py:46
  7.1 5.8 %collective-permute-start.6 = (f32[1280,128]{1,0:T(8,128)}, f32[1280,128]{1,0:T(8,128)S(1)}, u32[]{:S(2)}, u32[]{:S(2)}) collective-permute-start(f32[1280,128]{1,0:T(8,128)} %get-tuple-element.41), channel_id=1, source_target_pairs={{0,1},{8,9},{16,17},{24,25},{32,33},{40,41},{48,49},{56,57},{1,2},... | collective-permute-start | bytes 1966088 | tf_op jit(solution)/shard_map/ppermute | solution.py:79
  12.8 0.0 copy-start.1
  12.9 0.0 copy-start.3
  12.9 0.0 copy-start.6
  12.9 0.0 copy-start.11
  12.9 2.0 %shard_map.112 = (f32[296,128]{1,0:T(8,128)}, f32[296,128]{1,0:T(8,128)}, f32[296,128]{1,0:T(8,128)}) custom-call(f32[2,32,32,128]{3,2,1,0:T(8,128)} %tracers.3, f32[2,32,32,128]{3,2,1,0:T(8,128)} %flow.3, f32[4,32,32,128]{3,2,1,0:T(8,128)} %state.3, s32[3,3,1024]{2,1,0:T(4,128)} %sea_cells.3, s32[3,3,1024]{2,1,0:T(4,128)} %air_cells.3, ...), custom_call_target="tpu_custom_call" | custom-call | flops 1000000 | bytes 1000000 | tf_op jit(solution)/shard_map/pallas_call | solution.py:46
  14.9 2.2 %collective-permute-start = (f32[296,128]{1,0:T(8,128)}, f32[296,128]{1,0:T(8,128)S(1)}, u32[]{:S(2)}, u32[]{:S(2)}) collective-permute-start(f32[296,128]{1,0:T(8,128)} %get-tuple-element.32), channel_id=1, source_target_pairs={{0,1},{8,9},{16,17},{24,25},{32,33},{40,41},{48,49},{56,57},{1,2},... | collective-permute-start | bytes 454664 | tf_op jit(solution)/shard_map/ppermute | solution.py:79
  17.1 6.0 %collective-permute-start.1 = (f32[296,128]{1,0:T(8,128)}, f32[296,128]{1,0:T(8,128)S(1)}, u32[]{:S(2)}, u32[]{:S(2)}) collective-permute-start(f32[296,128]{1,0:T(8,128)} %get-tuple-element.34), channel_id=1, source_target_pairs={{1,0},{9,8},{17,16},{25,24},{33,32},{41,40},{49,48},{57,56},{2,1},... | collective-permute-start | bytes 454664 | tf_op jit(solution)/shard_map/ppermute | solution.py:85
  23.1 10.5 %collective-permute-done.up = f32[296,128]{1,0:T(8,128)S(1)} collective-permute-done((f32[296,128]{1,0:T(8,128)}, f32[296,128]{1,0:T(8,128)S(1)}, u32[]{:S(2)}, u32[]{:S(2)}) %collective-permute-start) | collective-permute-done | bytes 151584 | tf_op jit(solution)/shard_map/ppermute | solution.py:79
  33.6 0.9 collective-permute-done.1.down
  34.5 0.9 copy-done.7
  35.4 0.1 shard_map.113
  35.5 0.0 collective-permute-start.2
  35.5 2.9 %collective-permute-start.3 = (f32[744,128]{1,0:T(8,128)S(1)}, f32[744,128]{1,0:T(8,128)S(1)}, u32[]{:S(2)}, u32[]{:S(2)}) collective-permute-start(f32[744,128]{1,0:T(8,128)S(1)} %get-tuple-element.36), channel_id=1, source_target_pairs={{0,56},{8,0},{16,8},{24,16},{32,24},{40,32},{48,40},{56,48},{1,57}... | collective-permute-start | bytes 1142792 | tf_op jit(solution)/shard_map/ppermute | solution.py:101
  38.5 4.8 %collective-permute-start.7 = (f32[1280,128]{1,0:T(8,128)S(1)}, f32[1280,128]{1,0:T(8,128)S(1)}, u32[]{:S(2)}, u32[]{:S(2)}) collective-permute-start(f32[1280,128]{1,0:T(8,128)S(1)} %get-tuple-element.40.own), channel_id=1, source_target_pairs={{1,0},{9,8},{17,16},{25,24},{33,32},{41,40},{49,48},{57,56},{2,1},... | collective-permute-start | bytes 1966088 | tf_op jit(solution)/shard_map/ppermute | solution.py:85
  43.3 0.7 collective-permute-start.8
  44.1 2.9 %shard_map.116 = (f32[4,16,128,128]{3,2,1,0:T(8,128)S(1)}, f32[1024,128]{1,0:T(8,128)S(1)}, f32[1024,128]{1,0:T(8,128)S(1)}) custom-call(f32[2048,128]{1,0:T(8,128)S(1)} %bitcast.6, f32[2048,128]{1,0:T(8,128)S(1)} %bitcast.9, f32[1024,128]{1,0:T(8,128)S(1)} %bitcast.12, s32[32,128]{1,0:T(8,128)S(1)} %copy-done.11), custom_call_target="tpu_custom_call" | custom-call | flops 10000000 | bytes 1000000 | tf_op jit(solution)/shard_map/pallas_call | solution.py:46
  47.0 0.0 collective-permute-done.2.west
  47.0 0.0 collective-permute-start.4
  47.0 0.0 collective-permute-done.3.east
  47.0 2.9 %collective-permute-start.5 = (f32[1024,128]{1,0:T(8,128)S(1)}, f32[1024,128]{1,0:T(8,128)S(1)}, u32[]{:S(2)}, u32[]{:S(2)}) collective-permute-start(f32[1024,128]{1,0:T(8,128)S(1)} %get-tuple-element.39), channel_id=1, source_target_pairs={{0,56},{8,0},{16,8},{24,16},{32,24},{40,32},{48,40},{56,48},{1,57}... | collective-permute-start | bytes 1572872 | tf_op jit(solution)/shard_map/ppermute | solution.py:101
  50.0 0.7 shard_map.119
  50.7 8.6 %shard_map.120 = (f32[2,32,128]{2,1,0:T(8,128)}, f32[7,32,128]{2,1,0:T(8,128)S(1)}, f32[936,128]{1,0:T(8,128)S(1)}, f32[936,128]{1,0:T(8,128)S(1)}) custom-call(f32[296,128]{1,0:T(8,128)S(1)} %collective-permute-done.up, f32[296,128]{1,0:T(8,128)S(1)} %copy-done.7, f32[296,128]{1,0:T(8,128)S(1)} %collective-permute-done.1.down, ...), custom_call_target="tpu_custom_call" | custom-call | flops 20000000 | bytes 1000000 | tf_op jit(solution)/shard_map/pallas_call | solution.py:46
  59.3 0.0 collective-permute-done.6.south
  59.3 2.5 %collective-permute-start.11 = (f32[936,128]{1,0:T(8,128)S(1)}, f32[936,128]{1,0:T(8,128)S(1)}, u32[]{:S(2)}, u32[]{:S(2)}) collective-permute-start(f32[936,128]{1,0:T(8,128)S(1)} %get-tuple-element.48), channel_id=1, source_target_pairs={{0,1},{8,9},{16,17},{24,25},{32,33},{40,41},{48,49},{56,57},{1,2},... | collective-permute-start | bytes 1437704 | tf_op jit(solution)/shard_map/ppermute | solution.py:79
  61.7 0.0 collective-permute-done.7.north
  61.7 0.0 collective-permute-done.8.fold
  61.8 1.1 shard_map.118
  62.8 0.0 collective-permute-start.10
  62.9 0.5 collective-permute-start.9
  63.4 0.0 collective-permute-done.4.refs_1_
  63.4 0.7 collective-permute-start.13
  64.1 0.0 collective-permute-done.5.refs_2_
  64.1 5.8 %collective-permute-start.12 = (f32[936,128]{1,0:T(8,128)S(1)}, f32[936,128]{1,0:T(8,128)S(1)}, u32[]{:S(2)}, u32[]{:S(2)}) collective-permute-start(f32[936,128]{1,0:T(8,128)S(1)} %get-tuple-element.49), channel_id=1, source_target_pairs={{1,0},{9,8},{17,16},{25,24},{33,32},{41,40},{49,48},{57,56},{2,1},... | collective-permute-start | bytes 1437704 | tf_op jit(solution)/shard_map/ppermute | solution.py:85
  69.9 0.0 collective-permute-done.9.refs_4_
  69.9 6.3 %shard_map.122 = (f32[16,128,128]{2,1,0:T(8,128)S(1)}, f32[1024,128]{1,0:T(8,128)S(1)}, f32[1024,128]{1,0:T(8,128)S(1)}) custom-call(f32[4,16,128,128]{3,2,1,0:T(8,128)S(1)} %get-tuple-element.37.refs_0_, f32[1024,128]{1,0:T(8,128)S(1)} %collective-permute-done.4.refs_1_, f32[1024,128]{1,0:T(8,128)S(1)} %collective-permute-done.5.refs_2_, ...), custom_call_target="tpu_custom_call" | custom-call | flops 40000000 | bytes 1000000 | tf_op jit(solution)/shard_map/pallas_call | solution.py:46
  76.2 5.8 %collective-permute-start.16 = (f32[1024,128]{1,0:T(8,128)S(1)}, f32[1024,128]{1,0:T(8,128)S(1)}, u32[]{:S(2)}, u32[]{:S(2)}) collective-permute-start(f32[1024,128]{1,0:T(8,128)S(1)} %get-tuple-element.54), channel_id=1, source_target_pairs={{0,1},{8,9},{16,17},{24,25},{32,33},{40,41},{48,49},{56,57},{1,2},... | collective-permute-start | bytes 1572872 | tf_op jit(solution)/shard_map/ppermute | solution.py:79
  82.0 2.4 %collective-permute-start.17 = (f32[1024,128]{1,0:T(8,128)S(1)}, f32[1024,128]{1,0:T(8,128)S(1)}, u32[]{:S(2)}, u32[]{:S(2)}) collective-permute-start(f32[1024,128]{1,0:T(8,128)S(1)} %get-tuple-element.55), channel_id=1, source_target_pairs={{1,0},{9,8},{17,16},{25,24},{33,32},{41,40},{49,48},{57,56},{2,1},... | collective-permute-start | bytes 1572872 | tf_op jit(solution)/shard_map/ppermute | solution.py:85
  84.5 0.7 collective-permute-start.18
  85.2 0.0 collective-permute-done.13.fold
  85.2 10.4 %collective-permute-done.12.north = f32[936,128]{1,0:T(8,128)S(1)} collective-permute-done((f32[936,128]{1,0:T(8,128)S(1)}, f32[936,128]{1,0:T(8,128)S(1)}, u32[]{:S(2)}, u32[]{:S(2)}) %collective-permute-start.12) | collective-permute-done | bytes 479264 | tf_op jit(solution)/shard_map/ppermute | solution.py:85
  95.6 1.1 shard_map.121
  96.7 0.0 copy-start.4
  96.7 0.0 copy-start.14
  96.7 0.0 collective-permute-start.14
  96.7 2.9 %collective-permute-start.15 = (f32[664,128]{1,0:T(8,128)S(1)}, f32[664,128]{1,0:T(8,128)S(1)}, u32[]{:S(2)}, u32[]{:S(2)}) collective-permute-start(f32[664,128]{1,0:T(8,128)S(1)} %get-tuple-element.52), channel_id=1, source_target_pairs={{0,56},{8,0},{16,8},{24,16},{32,24},{40,32},{48,40},{56,48},{1,57}... | collective-permute-start | bytes 1019912 | tf_op jit(solution)/shard_map/ppermute | solution.py:101
  99.7 4.0 %collective-permute-done.16.south = f32[1024,128]{1,0:T(8,128)S(1)} collective-permute-done((f32[1024,128]{1,0:T(8,128)S(1)}, f32[1024,128]{1,0:T(8,128)S(1)}, u32[]{:S(2)}, u32[]{:S(2)}) %collective-permute-start.16) | collective-permute-done | bytes 524320 | tf_op jit(solution)/shard_map/ppermute | solution.py:79
  103.6 3.1 %collective-permute-done.17.north = f32[1024,128]{1,0:T(8,128)S(1)} collective-permute-done((f32[1024,128]{1,0:T(8,128)S(1)}, f32[1024,128]{1,0:T(8,128)S(1)}, u32[]{:S(2)}, u32[]{:S(2)}) %collective-permute-start.17) | collective-permute-done | bytes 524320 | tf_op jit(solution)/shard_map/ppermute | solution.py:85
  106.7 0.8 shard_map.123
  107.6 0.1 collective-permute-start.19
  107.6 2.9 %collective-permute-start.20 = (f32[512,128]{1,0:T(8,128)S(1)}, f32[512,128]{1,0:T(8,128)S(1)}, u32[]{:S(2)}, u32[]{:S(2)}) collective-permute-start(f32[512,128]{1,0:T(8,128)S(1)} %get-tuple-element.58), channel_id=1, source_target_pairs={{0,56},{8,0},{16,8},{24,16},{32,24},{40,32},{48,40},{56,48},{1,57}... | collective-permute-start | bytes 786440 | tf_op jit(solution)/shard_map/ppermute | solution.py:101
  110.5 7.9 %shard_map.114.flux = f32[4,32,128]{2,1,0:T(8,128)S(1)} custom-call(f32[296,128]{1,0:T(8,128)S(1)} %collective-permute-done.up, f32[296,128]{1,0:T(8,128)S(1)} %copy-done.8, f32[296,128]{1,0:T(8,128)S(1)} %collective-permute-done.1.down, f32[744,128]{1,0:T(8,128)S(1)} %collective-permute-done.2.west, f32[744,128]{1,0:T(8,128)S(1)} %collective-permute-done.3.east, ...), custom_call_target="tpu_custom_call" | custom-call | flops 20000000 | bytes 1000000 | tf_op jit(solution)/shard_map/pallas_call | solution.py:46
  118.4 2.7 %shard_map.115 = f32[4,32,32,128]{3,2,1,0:T(8,128)} custom-call(f32[4,32,32,128]{3,2,1,0:T(8,128)S(1)} %copy-done.4, f32[32,128]{1,0:T(8,128)S(1)} %copy-done.14, f32[4,32,128]{2,1,0:T(8,128)S(1)} %shard_map.114.flux), custom_call_target="tpu_custom_call" | custom-call | flops 5000000 | bytes 4200000 | tf_op jit(solution)/shard_map/pallas_call | solution.py:641
  121.1 0.0 collective-permute-done.14.w2.refs_7_
  121.1 0.0 collective-permute-done.15.e2.refs_8_
  121.1 4.2 %shard_map.124.refs_12_ = f32[2,32,128]{2,1,0:T(8,128)S(1)} custom-call(f32[7,80,128]{2,1,0:T(8,128)S(1)} %get-tuple-element.59.mine, f32[664,128]{1,0:T(8,128)S(1)} %collective-permute-done.14.w2.refs_7_, f32[664,128]{1,0:T(8,128)S(1)} %collective-permute-done.15.e2.refs_8_), custom_call_target="tpu_custom_call" | custom-call | flops 10000000 | bytes 1000000 | tf_op jit(solution)/shard_map/pallas_call | solution.py:46
  125.4 0.0 collective-permute-done.20.refs_11_
  125.4 17.7 %shard_map.125 = f32[2048,128]{1,0:T(8,128)} custom-call(f32[4,16,128,128]{3,2,1,0:T(8,128)S(1)} %get-tuple-element.37.refs_0_, f32[1024,128]{1,0:T(8,128)S(1)} %collective-permute-done.4.refs_1_, f32[1024,128]{1,0:T(8,128)S(1)} %collective-permute-done.5.refs_2_, f32[4,8,128,128]{3,2,1,0:T(8,128)S(1)} %get-tuple-element.42.refs_3_, ...), custom_call_target="tpu_custom_call" | custom-call | flops 60000000 | bytes 1000000 | tf_op jit(solution)/shard_map/pallas_call | solution.py:46
  (22 shorter events, 0.0 us)
Async XLA Ops:
  0.6 1.2 copy-start
  1.9 1.2 copy-start.2
  3.1 1.0 copy-start.5
  4.1 0.7 copy-start.10
  7.1 52.2 %collective-permute-start.6 = (f32[1280,128]{1,0:T(8,128)}, f32[1280,128]{1,0:T(8,128)S(1)}, u32[]{:S(2)}, u32[]{:S(2)}) collective-permute-start(f32[1280,128]{1,0:T(8,128)} %get-tuple-element.41), channel_id=1, source_target_pairs={{0,1},{8,9},{16,17},{24,25},{32,33},{40,41},{48,49},{56,57},{1,2},... | collective-permute-start | bytes 1966088 | tf_op jit(solution)/shard_map/ppermute | solution.py:79
  12.8 31.2 %copy-start.1 = (f32[2,32,32,128]{3,2,1,0:T(8,128)S(1)}, f32[2,32,32,128]{3,2,1,0:T(8,128)}, u32[]{:S(2)}) copy-start(f32[2,32,32,128]{3,2,1,0:T(8,128)} %tracers.3) | copy-start | bytes 3145732
  12.9 31.2 %copy-start.3 = (f32[2,32,32,128]{3,2,1,0:T(8,128)S(1)}, f32[2,32,32,128]{3,2,1,0:T(8,128)}, u32[]{:S(2)}) copy-start(f32[2,32,32,128]{3,2,1,0:T(8,128)} %flow.3) | copy-start | bytes 3145732
  12.9 31.2 %copy-start.6 = (f32[32,32,128]{2,1,0:T(8,128)S(1)}, f32[32,32,128]{2,1,0:T(8,128)}, u32[]{:S(2)}) copy-start(f32[32,32,128]{2,1,0:T(8,128)} %kappa.3) | copy-start | bytes 1572868
  12.9 31.2 %copy-start.11 = (s32[32,128]{1,0:T(8,128)S(1)}, s32[32,128]{1,0:T(8,128)}, u32[]{:S(2)}) copy-start(s32[32,128]{1,0:T(8,128)} %mask.7) | copy-start | bytes 49156
  14.9 18.7 %collective-permute-start = (f32[296,128]{1,0:T(8,128)}, f32[296,128]{1,0:T(8,128)S(1)}, u32[]{:S(2)}, u32[]{:S(2)}) collective-permute-start(f32[296,128]{1,0:T(8,128)} %get-tuple-element.32), channel_id=1, source_target_pairs={{0,1},{8,9},{16,17},{24,25},{32,33},{40,41},{48,49},{56,57},{1,2},... | collective-permute-start | bytes 454664 | tf_op jit(solution)/shard_map/ppermute | solution.py:79
  17.1 17.4 %collective-permute-start.1 = (f32[296,128]{1,0:T(8,128)}, f32[296,128]{1,0:T(8,128)S(1)}, u32[]{:S(2)}, u32[]{:S(2)}) collective-permute-start(f32[296,128]{1,0:T(8,128)} %get-tuple-element.34), channel_id=1, source_target_pairs={{1,0},{9,8},{17,16},{25,24},{33,32},{41,40},{49,48},{57,56},{2,1},... | collective-permute-start | bytes 454664 | tf_op jit(solution)/shard_map/ppermute | solution.py:85
  34.5 0.9 copy-start.7
  35.5 11.5 %collective-permute-start.2 = (f32[744,128]{1,0:T(8,128)S(1)}, f32[744,128]{1,0:T(8,128)S(1)}, u32[]{:S(2)}, u32[]{:S(2)}) collective-permute-start(f32[744,128]{1,0:T(8,128)S(1)} %get-tuple-element.35), channel_id=1, source_target_pairs={{0,8},{8,16},{16,24},{24,32},{32,40},{40,48},{48,56},{56,0},{1,9},... | collective-permute-start | bytes 1142792 | tf_op jit(solution)/shard_map/ppermute | solution.py:96
  35.5 11.5 %collective-permute-start.3 = (f32[744,128]{1,0:T(8,128)S(1)}, f32[744,128]{1,0:T(8,128)S(1)}, u32[]{:S(2)}, u32[]{:S(2)}) collective-permute-start(f32[744,128]{1,0:T(8,128)S(1)} %get-tuple-element.36), channel_id=1, source_target_pairs={{0,56},{8,0},{16,8},{24,16},{32,24},{40,32},{48,40},{56,48},{1,57}... | collective-permute-start | bytes 1142792 | tf_op jit(solution)/shard_map/ppermute | solution.py:101
  38.5 23.3 %collective-permute-start.7 = (f32[1280,128]{1,0:T(8,128)S(1)}, f32[1280,128]{1,0:T(8,128)S(1)}, u32[]{:S(2)}, u32[]{:S(2)}) collective-permute-start(f32[1280,128]{1,0:T(8,128)S(1)} %get-tuple-element.40.own), channel_id=1, source_target_pairs={{1,0},{9,8},{17,16},{25,24},{33,32},{41,40},{49,48},{57,56},{2,1},... | collective-permute-start | bytes 1966088 | tf_op jit(solution)/shard_map/ppermute | solution.py:85
  43.3 18.4 %collective-permute-start.8 = (f32[1280,128]{1,0:T(8,128)}, f32[1280,128]{1,0:T(8,128)S(1)}, u32[]{:S(2)}, u32[]{:S(2)}) collective-permute-start(f32[1280,128]{1,0:T(8,128)} %get-tuple-element.41), channel_id=1, source_target_pairs={{71,127},{79,119},{87,111},{95,103},{103,95},{111,87},{119,79},{12... | collective-permute-start | bytes 1966088 | tf_op jit(solution)/shard_map/ppermute | solution.py:91
  47.0 16.4 %collective-permute-start.4 = (f32[1024,128]{1,0:T(8,128)S(1)}, f32[1024,128]{1,0:T(8,128)S(1)}, u32[]{:S(2)}, u32[]{:S(2)}) collective-permute-start(f32[1024,128]{1,0:T(8,128)S(1)} %get-tuple-element.38), channel_id=1, source_target_pairs={{0,8},{8,16},{16,24},{24,32},{32,40},{40,48},{48,56},{56,0},{1,9},... | collective-permute-start | bytes 1572872 | tf_op jit(solution)/shard_map/ppermute | solution.py:96
  47.0 17.0 %collective-permute-start.5 = (f32[1024,128]{1,0:T(8,128)S(1)}, f32[1024,128]{1,0:T(8,128)S(1)}, u32[]{:S(2)}, u32[]{:S(2)}) collective-permute-start(f32[1024,128]{1,0:T(8,128)S(1)} %get-tuple-element.39), channel_id=1, source_target_pairs={{0,56},{8,0},{16,8},{24,16},{32,24},{40,32},{48,40},{56,48},{1,57}... | collective-permute-start | bytes 1572872 | tf_op jit(solution)/shard_map/ppermute | solution.py:101
  59.3 25.2 %collective-permute-start.11 = (f32[936,128]{1,0:T(8,128)S(1)}, f32[936,128]{1,0:T(8,128)S(1)}, u32[]{:S(2)}, u32[]{:S(2)}) collective-permute-start(f32[936,128]{1,0:T(8,128)S(1)} %get-tuple-element.48), channel_id=1, source_target_pairs={{0,1},{8,9},{16,17},{24,25},{32,33},{40,41},{48,49},{56,57},{1,2},... | collective-permute-start | bytes 1437704 | tf_op jit(solution)/shard_map/ppermute | solution.py:79
  62.8 7.0 %collective-permute-start.10 = (f32[512,128]{1,0:T(8,128)S(1)}, f32[512,128]{1,0:T(8,128)S(1)}, u32[]{:S(2)}, u32[]{:S(2)}) collective-permute-start(f32[512,128]{1,0:T(8,128)S(1)} %get-tuple-element.44), channel_id=1, source_target_pairs={{0,56},{8,0},{16,8},{24,16},{32,24},{40,32},{48,40},{56,48},{1,57}... | collective-permute-start | bytes 786440 | tf_op jit(solution)/shard_map/ppermute | solution.py:101
  62.9 7.0 %collective-permute-start.9 = (f32[512,128]{1,0:T(8,128)S(1)}, f32[512,128]{1,0:T(8,128)S(1)}, u32[]{:S(2)}, u32[]{:S(2)}) collective-permute-start(f32[512,128]{1,0:T(8,128)S(1)} %get-tuple-element.43), channel_id=1, source_target_pairs={{0,8},{8,16},{16,24},{24,32},{32,40},{40,48},{48,56},{56,0},{1,9},... | collective-permute-start | bytes 786440 | tf_op jit(solution)/shard_map/ppermute | solution.py:96
  63.4 21.8 %collective-permute-start.13 = (f32[936,128]{1,0:T(8,128)S(1)}, f32[936,128]{1,0:T(8,128)S(1)}, u32[]{:S(2)}, u32[]{:S(2)}) collective-permute-start(f32[936,128]{1,0:T(8,128)S(1)} %get-tuple-element.48), channel_id=1, source_target_pairs={{71,127},{79,119},{87,111},{95,103},{103,95},{111,87},{119,79},{12... | collective-permute-start | bytes 1437704 | tf_op jit(solution)/shard_map/ppermute | solution.py:91
  64.1 31.5 %collective-permute-start.12 = (f32[936,128]{1,0:T(8,128)S(1)}, f32[936,128]{1,0:T(8,128)S(1)}, u32[]{:S(2)}, u32[]{:S(2)}) collective-permute-start(f32[936,128]{1,0:T(8,128)S(1)} %get-tuple-element.49), channel_id=1, source_target_pairs={{1,0},{9,8},{17,16},{25,24},{33,32},{41,40},{49,48},{57,56},{2,1},... | collective-permute-start | bytes 1437704 | tf_op jit(solution)/shard_map/ppermute | solution.py:85
  76.2 27.4 %collective-permute-start.16 = (f32[1024,128]{1,0:T(8,128)S(1)}, f32[1024,128]{1,0:T(8,128)S(1)}, u32[]{:S(2)}, u32[]{:S(2)}) collective-permute-start(f32[1024,128]{1,0:T(8,128)S(1)} %get-tuple-element.54), channel_id=1, source_target_pairs={{0,1},{8,9},{16,17},{24,25},{32,33},{40,41},{48,49},{56,57},{1,2},... | collective-permute-start | bytes 1572872 | tf_op jit(solution)/shard_map/ppermute | solution.py:79
  82.0 24.7 %collective-permute-start.17 = (f32[1024,128]{1,0:T(8,128)S(1)}, f32[1024,128]{1,0:T(8,128)S(1)}, u32[]{:S(2)}, u32[]{:S(2)}) collective-permute-start(f32[1024,128]{1,0:T(8,128)S(1)} %get-tuple-element.55), channel_id=1, source_target_pairs={{1,0},{9,8},{17,16},{25,24},{33,32},{41,40},{49,48},{57,56},{2,1},... | collective-permute-start | bytes 1572872 | tf_op jit(solution)/shard_map/ppermute | solution.py:85
  84.5 22.3 %collective-permute-start.18 = (f32[1024,128]{1,0:T(8,128)S(1)}, f32[1024,128]{1,0:T(8,128)S(1)}, u32[]{:S(2)}, u32[]{:S(2)}) collective-permute-start(f32[1024,128]{1,0:T(8,128)S(1)} %get-tuple-element.54), channel_id=1, source_target_pairs={{71,127},{79,119},{87,111},{95,103},{103,95},{111,87},{119,79},{12... | collective-permute-start | bytes 1572872 | tf_op jit(solution)/shard_map/ppermute | solution.py:91
  95.6 15.0 %copy-start.8 = (f32[296,128]{1,0:T(8,128)S(1)}, f32[296,128]{1,0:T(8,128)}, u32[]{:S(2)}) copy-start(f32[296,128]{1,0:T(8,128)} %get-tuple-element.33.mine) | copy-start | bytes 454660
  95.6 15.0 %copy-start.9 = (f32[2,3,3,1024]{3,0,2,1:T(2,128)S(1)}, f32[2,3,3,1024]{3,0,2,1:T(2,128)}, u32[]{:S(2)}) copy-start(f32[2,3,3,1024]{3,0,2,1:T(2,128)} %param.17) | copy-start | bytes 221188
  95.6 15.0 %copy-start.12 = (s32[3,3,1024]{2,1,0:T(4,128)S(1)}, s32[3,3,1024]{2,1,0:T(4,128)}, u32[]{:S(2)}) copy-start(s32[3,3,1024]{2,1,0:T(4,128)} %sea_cells.3) | copy-start | bytes 110596
  95.6 15.0 %copy-start.13 = (s32[3,3,1024]{2,1,0:T(4,128)S(1)}, s32[3,3,1024]{2,1,0:T(4,128)}, u32[]{:S(2)}) copy-start(s32[3,3,1024]{2,1,0:T(4,128)} %air_cells.3) | copy-start | bytes 110596
  96.7 21.8 %copy-start.4 = (f32[4,32,32,128]{3,2,1,0:T(8,128)S(1)}, f32[4,32,32,128]{3,2,1,0:T(8,128)}, u32[]{:S(2)}) copy-start(f32[4,32,32,128]{3,2,1,0:T(8,128)} %state.3) | copy-start | bytes 6291460
  96.7 21.8 %copy-start.14 = (f32[32,128]{1,0:T(8,128)S(1)}, f32[32,128]{1,0:T(8,128)}, u32[]{:S(2)}) copy-start(f32[32,128]{1,0:T(8,128)} %kappa.2) | copy-start | bytes 49156
  96.7 24.4 %collective-permute-start.14 = (f32[664,128]{1,0:T(8,128)S(1)}, f32[664,128]{1,0:T(8,128)S(1)}, u32[]{:S(2)}, u32[]{:S(2)}) collective-permute-start(f32[664,128]{1,0:T(8,128)S(1)} %get-tuple-element.51), channel_id=1, source_target_pairs={{0,8},{8,16},{16,24},{24,32},{32,40},{40,48},{48,56},{56,0},{1,9},... | collective-permute-start | bytes 1019912 | tf_op jit(solution)/shard_map/ppermute | solution.py:96
  96.7 24.4 %collective-permute-start.15 = (f32[664,128]{1,0:T(8,128)S(1)}, f32[664,128]{1,0:T(8,128)S(1)}, u32[]{:S(2)}, u32[]{:S(2)}) collective-permute-start(f32[664,128]{1,0:T(8,128)S(1)} %get-tuple-element.52), channel_id=1, source_target_pairs={{0,56},{8,0},{16,8},{24,16},{32,24},{40,32},{48,40},{56,48},{1,57}... | collective-permute-start | bytes 1019912 | tf_op jit(solution)/shard_map/ppermute | solution.py:101
  107.6 17.8 %collective-permute-start.19 = (f32[512,128]{1,0:T(8,128)S(1)}, f32[512,128]{1,0:T(8,128)S(1)}, u32[]{:S(2)}, u32[]{:S(2)}) collective-permute-start(f32[512,128]{1,0:T(8,128)S(1)} %get-tuple-element.57), channel_id=1, source_target_pairs={{0,8},{8,16},{16,24},{24,32},{32,40},{40,48},{48,56},{56,0},{1,9},... | collective-permute-start | bytes 786440 | tf_op jit(solution)/shard_map/ppermute | solution.py:96
  107.6 17.8 %collective-permute-start.20 = (f32[512,128]{1,0:T(8,128)S(1)}, f32[512,128]{1,0:T(8,128)S(1)}, u32[]{:S(2)}, u32[]{:S(2)}) collective-permute-start(f32[512,128]{1,0:T(8,128)S(1)} %get-tuple-element.58), channel_id=1, source_target_pairs={{0,56},{8,0},{16,8},{24,16},{32,24},{40,32},{48,40},{56,48},{1,57}... | collective-permute-start | bytes 786440 | tf_op jit(solution)/shard_map/ppermute | solution.py:101

commit v8 on v7

--- a/solution.py
+++ b/solution.py
@@ -198,11 +198,11 @@
     halo = SIDE if final else NEAR
     xo, wo, eo, xn, wn, en = refs[:6]
     if final:
-        xf, wf, ef, xts, w2, e2, surface, out = refs[6:14]
-        scratch = refs[14:]
+        xf, wf, ef, xts, w1, e1, w2, e2, surface, out = refs[6:16]
+        scratch = refs[16:]
     else:
-        state, top, bottom = refs[6:9]
-        scratch = refs[9:]
+        state, top, bottom, mw, me = refs[6:11]
+        scratch = refs[11:]
     s0, s1, cc, cw, ce, cd, cu = scratch
     pairs = RW // 2 + halo
     block = (CL + 2 * halo) // 8
@@ -237,10 +237,11 @@
                 coefficients(to, west_cols, *west)
                 coefficients(to, east_cols, *east)
                 if final:
-                    rows = pl.ds(pl.multiple_of(to * SIDE, SIDE), SIDE)
+                    line, side = (i, (w1, e1)) if start == halo else (to, (w2, e2))
+                    rows = pl.ds(pl.multiple_of(line * SIDE, SIDE), SIDE)
                     s0[to, mid] = xts[to]
-                    s0[to, west_cols] = w2[rows, :][SIDE - halo :]
-                    s0[to, east_cols] = e2[rows, :][:halo]
+                    s0[to, west_cols] = side[0][rows, :]
+                    s0[to, east_cols] = side[1][rows, :]
                 else:
                     s0[to, mid] = x[0, i]
                     s0[to, west_cols] = w[lines[0], :][SIDE - halo :]
@@ -281,8 +282,9 @@
             rows(src, dst, 2 * p + 1, 2)
             return carry
 
-        lax.fori_loop(s, pairs // 2 - 1, body, 0)
+        lax.fori_loop(s, pairs // 2 - 2, body, 0)
         rows(src, dst, pairs - 1, 1)
+        rows(src, dst, pairs - 3, 2)
 
     def two(n, carry):
         step(s0, s1, n)
@@ -310,6 +312,8 @@
         low = lax.broadcasted_iota(jnp.int32, (CL, CL), 1) < CL // 2
         for i in range(RW // 2):
             state[i] = s0[i + halo, mid]
+            mw[i * SIDE : (i + 1) * SIDE] = s0[i + halo, EDGE : EDGE + SIDE]
+            me[i * SIDE : (i + 1) * SIDE] = s0[i + halo, EDGE + CL - SIDE : EDGE + CL]
         half = SIDE // 2
         for k in range(half):
             near, far = s0[halo + k, mid], s0[halo + k + half, mid]
@@ -343,8 +347,9 @@
             rows[SIDE - 1 - kk] = jnp.where(low, down, up)
     count = RW // 2 + SIDE
     for i in range(count):
+        xts[i] = rows[i]
+    for i in range(SIDE):
         where = pl.ds(i * SIDE, SIDE)
-        xts[i] = rows[i]
         mw[where, :] = rows[i][:SIDE]
         me[where, :] = rows[i][CL - SIDE :]
 
@@ -754,15 +759,16 @@
         return [pltpu.VMEM((RW // 2 + halo, WIDTH, CL), F32)] * 7
 
     pair = shape(SIDE // 2 * CL, CL)
-    state, top, bottom = call(
+    state, top, bottom, mw, me = call(
         functools.partial(deep_kernel, False),
-        (shape(RW // 2, CL, CL), pair, pair),
+        (shape(RW // 2, CL, CL), pair, pair) + (shape(RW // 2 * SIDE, CL),) * 2,
         (xo, wo, eo, xn, wn, en),
         scratch=buffers(NEAR),
         flops=40_000_000,
         mib=FIRST_MIB,
     )
     south, north = to_north(top), to_south(bottom)
+    w1, e1 = to_east(me), to_west(mw)
     fold = across_fold(top)
 
     side = shape(SURF + 3 * NEAR * SIDE, CL)
@@ -782,7 +788,7 @@
         flops=10_000_000,
     )
 
-    side = shape((RW // 2 + SIDE) * SIDE, CL)
+    side = shape(SIDE * SIDE, CL)
     xts, mw, me = call(
         join_kernel,
         (shape(RW // 2 + SIDE, CL, CL), side, side),
@@ -791,7 +797,9 @@
     ocean_next = call(
         functools.partial(deep_kernel, True),
         shape(2 * LV * RW, CL),
-        (xo, wo, eo, xn, wn, en, xf, w3, e3, xts, to_east(me), to_west(mw), surface),
+        (
+            xo, wo, eo, xn, wn, en, xf, w3, e3, xts, w1, e1, to_east(me), to_west(mw), surface,
+        ),
         scratch=buffers(SIDE),
         flops=60_000_000,
         mib=FINAL_MIB,

time: 144 us -> 143 us (level)
  waiting for transfers between devices: 28.9 us -> 34.7 us
  local copies, waits for them, and re-layouts: 5.17 us -> 0.97 us
  Pallas kernels: 58.3 us -> 56.3 us
    ppermute x4, waiting for transfers between devices: 14.4 us -> 4.03 us  [to_south(): return lax.ppermute(value, AXES, pairs)]
    ppermute x4, waiting for transfers between devices: 14.5 us -> 24.1 us  [to_north(): return lax.ppermute(value, AXES, pairs)]
    ppermute x4, starting transfers between devices: 19.1 us -> 12.8 us  [to_south(): return lax.ppermute(value, AXES, pairs)]
    unnamed x30 -> x22, local copies, waits for them, and re-layouts: 5.17 us -> 0.97 us
    ppermute x4, starting transfers between devices: 16.2 us -> 20.2 us  [to_north(): return lax.ppermute(value, AXES, pairs)]
    ppermute x5 -> x6, waiting for transfers between devices: 0.01 us -> 3.4 us  [to_west(): return lax.ppermute(value, 'gx', [(x, (x - 1) % nx) for x in range(nx)])]
    ppermute x5 -> x6, waiting for transfers between devices: 0.04 us -> 3.16 us  [to_east(): return lax.ppermute(value, 'gx', [(x, (x + 1) % nx) for x in range(nx)])]
    pallas_call x13, Pallas kernels: 55.6 us -> 53.6 us  [call(): pl.pallas_call(kernel, grid=(1,) if blocks else (), out_shape=outs, in_sp...]
  transfers between devices with their start and end apart: 21 -> 23, of which waited for: 5 -> 7; matrix products, arithmetic and copies ran while one was open for 0% -> 0% of each run, Pallas kernels for 27% -> 26%
where the time goes in v8:
time: 143 us; the launch traced here: 142 us
  Pallas kernels  56.3 us (39%)
  starting transfers between devices  48.7 us (34%)
  waiting for transfers between devices  34.7 us (24%)
    pallas_call x13, Pallas kernels, call(): pl.pallas_call(kernel, grid=(1,) if blocks else (), out_shape=outs, in_sp...  53.6 us
    ppermute x4, waiting for transfers between devices, to_north(): return lax.ppermute(value, AXES, pairs)  24.1 us
    ppermute x4, starting transfers between devices, to_north(): return lax.ppermute(value, AXES, pairs)  20.2 us
    ppermute x6, starting transfers between devices, to_west(): return lax.ppermute(value, 'gx', [(x, (x - 1) % nx) for x in range(nx)])  13.1 us
    ppermute x4, starting transfers between devices, to_south(): return lax.ppermute(value, AXES, pairs)  12.8 us
    ppermute x4, waiting for transfers between devices, to_south(): return lax.ppermute(value, AXES, pairs)  4.03 us
    ppermute x6, waiting for transfers between devices, to_west(): return lax.ppermute(value, 'gx', [(x, (x - 1) % nx) for x in range(nx)])  3.4 us
    ppermute x6, waiting for transfers between devices, to_east(): return lax.ppermute(value, 'gx', [(x, (x + 1) % nx) for x in range(nx)])  3.16 us
  transfers between devices with their start and end apart: 23, of which 7 were waited for; matrix products, arithmetic and copies ran while one was open for 0% of the time, Pallas kernels for 26%

profile of v8, /device:TPU:4, one launch (start us, length us, event | category | flops | bytes accessed | tf_op | source)
XLA Modules:
  0.0 141.7 jit_solution(14614652696982109444)
XLA Ops:
  0.7 2.0 %shard_map.112 = (f32[296,128]{1,0:T(8,128)}, f32[296,128]{1,0:T(8,128)}, f32[296,128]{1,0:T(8,128)}) custom-call(f32[2,32,32,128]{3,2,1,0:T(8,128)} %tracers.3, f32[2,32,32,128]{3,2,1,0:T(8,128)} %flow.3, f32[4,32,32,128]{3,2,1,0:T(8,128)} %state.3, s32[3,3,1024]{2,1,0:T(4,128)} %sea_cells.3, s32[3,3,1024]{2,1,0:T(4,128)} %air_cells.3, ...), custom_call_target="tpu_custom_call" | custom-call | flops 1000000 | bytes 1000000 | tf_op jit(solution)/shard_map/pallas_call | solution.py:46
  2.7 5.8 %collective-permute-start = (f32[296,128]{1,0:T(8,128)}, f32[296,128]{1,0:T(8,128)S(1)}, u32[]{:S(2)}, u32[]{:S(2)}) collective-permute-start(f32[296,128]{1,0:T(8,128)} %get-tuple-element.34), channel_id=1, source_target_pairs={{0,1},{8,9},{16,17},{24,25},{32,33},{40,41},{48,49},{56,57},{1,2},... | collective-permute-start | bytes 454664 | tf_op jit(solution)/shard_map/ppermute | solution.py:79
  8.4 2.5 %collective-permute-start.1 = (f32[296,128]{1,0:T(8,128)}, f32[296,128]{1,0:T(8,128)S(1)}, u32[]{:S(2)}, u32[]{:S(2)}) collective-permute-start(f32[296,128]{1,0:T(8,128)} %get-tuple-element.36), channel_id=1, source_target_pairs={{1,0},{9,8},{17,16},{25,24},{33,32},{41,40},{49,48},{57,56},{2,1},... | collective-permute-start | bytes 454664 | tf_op jit(solution)/shard_map/ppermute | solution.py:85
  10.9 4.3 %collective-permute-done.up = f32[296,128]{1,0:T(8,128)S(1)} collective-permute-done((f32[296,128]{1,0:T(8,128)}, f32[296,128]{1,0:T(8,128)S(1)}, u32[]{:S(2)}, u32[]{:S(2)}) %collective-permute-start) | collective-permute-done | bytes 151584 | tf_op jit(solution)/shard_map/ppermute | solution.py:79
  15.2 2.2 %collective-permute-done.1.down = f32[296,128]{1,0:T(8,128)S(1)} collective-permute-done((f32[296,128]{1,0:T(8,128)}, f32[296,128]{1,0:T(8,128)S(1)}, u32[]{:S(2)}, u32[]{:S(2)}) %collective-permute-start.1) | collective-permute-done | bytes 151584 | tf_op jit(solution)/shard_map/ppermute | solution.py:85
  17.4 0.9 copy-done.4
  18.4 0.1 shard_map.113
  18.4 0.0 collective-permute-start.2
  18.4 2.9 %collective-permute-start.3 = (f32[744,128]{1,0:T(8,128)S(1)}, f32[744,128]{1,0:T(8,128)S(1)}, u32[]{:S(2)}, u32[]{:S(2)}) collective-permute-start(f32[744,128]{1,0:T(8,128)S(1)} %get-tuple-element.38), channel_id=1, source_target_pairs={{0,56},{8,0},{16,8},{24,16},{32,24},{40,32},{48,40},{56,48},{1,57}... | collective-permute-start | bytes 1142792 | tf_op jit(solution)/shard_map/ppermute | solution.py:101
  21.4 1.4 shard_map.117
  22.8 3.5 %collective-permute-start.6 = (f32[1280,128]{1,0:T(8,128)S(1)}, f32[1280,128]{1,0:T(8,128)S(1)}, u32[]{:S(2)}, u32[]{:S(2)}) collective-permute-start(f32[1280,128]{1,0:T(8,128)S(1)} %get-tuple-element.43), channel_id=1, source_target_pairs={{0,1},{8,9},{16,17},{24,25},{32,33},{40,41},{48,49},{56,57},{1,2},... | collective-permute-start | bytes 1966088 | tf_op jit(solution)/shard_map/ppermute | solution.py:79
  26.3 4.7 %collective-permute-start.7 = (f32[1280,128]{1,0:T(8,128)S(1)}, f32[1280,128]{1,0:T(8,128)S(1)}, u32[]{:S(2)}, u32[]{:S(2)}) collective-permute-start(f32[1280,128]{1,0:T(8,128)S(1)} %get-tuple-element.42.own), channel_id=1, source_target_pairs={{1,0},{9,8},{17,16},{25,24},{33,32},{41,40},{49,48},{57,56},{2,1},... | collective-permute-start | bytes 1966088 | tf_op jit(solution)/shard_map/ppermute | solution.py:85
  31.1 0.7 collective-permute-start.8
  31.8 2.9 %shard_map.116 = (f32[4,16,128,128]{3,2,1,0:T(8,128)S(1)}, f32[1024,128]{1,0:T(8,128)S(1)}, f32[1024,128]{1,0:T(8,128)S(1)}) custom-call(f32[2048,128]{1,0:T(8,128)S(1)} %bitcast.6, f32[2048,128]{1,0:T(8,128)S(1)} %bitcast.9, f32[1024,128]{1,0:T(8,128)S(1)} %bitcast.12, s32[32,128]{1,0:T(8,128)S(1)} %copy-done.7), custom_call_target="tpu_custom_call" | custom-call | flops 10000000 | bytes 1000000 | tf_op jit(solution)/shard_map/pallas_call | solution.py:46
  34.7 0.0 collective-permute-done.2.west
  34.7 0.0 collective-permute-start.4
  34.7 0.0 collective-permute-done.3.east
  34.7 2.9 %collective-permute-start.5 = (f32[1024,128]{1,0:T(8,128)S(1)}, f32[1024,128]{1,0:T(8,128)S(1)}, u32[]{:S(2)}, u32[]{:S(2)}) collective-permute-start(f32[1024,128]{1,0:T(8,128)S(1)} %get-tuple-element.41), channel_id=1, source_target_pairs={{0,56},{8,0},{16,8},{24,16},{32,24},{40,32},{48,40},{56,48},{1,57}... | collective-permute-start | bytes 1572872 | tf_op jit(solution)/shard_map/ppermute | solution.py:101
  37.7 0.7 shard_map.119
  38.4 8.6 %shard_map.120 = (f32[2,32,128]{2,1,0:T(8,128)}, f32[7,32,128]{2,1,0:T(8,128)S(1)}, f32[936,128]{1,0:T(8,128)S(1)}, f32[936,128]{1,0:T(8,128)S(1)}) custom-call(f32[296,128]{1,0:T(8,128)S(1)} %collective-permute-done.up, f32[296,128]{1,0:T(8,128)S(1)} %copy-done.4, f32[296,128]{1,0:T(8,128)S(1)} %collective-permute-done.1.down, ...), custom_call_target="tpu_custom_call" | custom-call | flops 20000000 | bytes 1000000 | tf_op jit(solution)/shard_map/pallas_call | solution.py:46
  47.0 6.3 %collective-permute-done.6.south = f32[1280,128]{1,0:T(8,128)S(1)} collective-permute-done((f32[1280,128]{1,0:T(8,128)S(1)}, f32[1280,128]{1,0:T(8,128)S(1)}, u32[]{:S(2)}, u32[]{:S(2)}) %collective-permute-start.6) | collective-permute-done | bytes 655392 | tf_op jit(solution)/shard_map/ppermute | solution.py:79
  53.3 5.9 %collective-permute-start.11 = (f32[936,128]{1,0:T(8,128)S(1)}, f32[936,128]{1,0:T(8,128)S(1)}, u32[]{:S(2)}, u32[]{:S(2)}) collective-permute-start(f32[936,128]{1,0:T(8,128)S(1)} %get-tuple-element.50), channel_id=1, source_target_pairs={{0,1},{8,9},{16,17},{24,25},{32,33},{40,41},{48,49},{56,57},{1,2},... | collective-permute-start | bytes 1437704 | tf_op jit(solution)/shard_map/ppermute | solution.py:79
  59.2 0.0 collective-permute-done.7.north
  59.2 0.7 collective-permute-start.13
  59.9 0.0 collective-permute-done.8.fold
  59.9 2.4 %collective-permute-start.12 = (f32[936,128]{1,0:T(8,128)S(1)}, f32[936,128]{1,0:T(8,128)S(1)}, u32[]{:S(2)}, u32[]{:S(2)}) collective-permute-start(f32[936,128]{1,0:T(8,128)S(1)} %get-tuple-element.51), channel_id=1, source_target_pairs={{1,0},{9,8},{17,16},{25,24},{33,32},{41,40},{49,48},{57,56},{2,1},... | collective-permute-start | bytes 1437704 | tf_op jit(solution)/shard_map/ppermute | solution.py:85
  62.2 1.1 shard_map.118
  63.3 0.0 collective-permute-done.4.refs_1_
  63.3 0.0 collective-permute-start.10
  63.4 0.5 collective-permute-start.9
  63.9 3.4 %collective-permute-done.10.refs_5_ = f32[512,128]{1,0:T(8,128)S(1)} collective-permute-done((f32[512,128]{1,0:T(8,128)S(1)}, f32[512,128]{1,0:T(8,128)S(1)}, u32[]{:S(2)}, u32[]{:S(2)}) %collective-permute-start.10) | collective-permute-done | bytes 262176 | tf_op jit(solution)/shard_map/ppermute | solution.py:101
  67.2 3.1 %collective-permute-done.9.refs_4_ = f32[512,128]{1,0:T(8,128)S(1)} collective-permute-done((f32[512,128]{1,0:T(8,128)S(1)}, f32[512,128]{1,0:T(8,128)S(1)}, u32[]{:S(2)}, u32[]{:S(2)}) %collective-permute-start.9) | collective-permute-done | bytes 262176 | tf_op jit(solution)/shard_map/ppermute | solution.py:96
  70.4 5.9 %shard_map.122 = (f32[16,128,128]{2,1,0:T(8,128)S(1)}, f32[1024,128]{1,0:T(8,128)S(1)}, f32[1024,128]{1,0:T(8,128)S(1)}, f32[256,128]{1,0:T(8,128)S(1)}, f32[256,128]{1,0:T(8,128)S(1)}) custom-call(f32[4,16,128,128]{3,2,1,0:T(8,128)S(1)} %get-tuple-element.39.refs_0_, f32[1024,128]{1,0:T(8,128)S(1)} %collective-permute-done.4.refs_1_, ...), custom_call_target="tpu_custom_call" | custom-call | flops 40000000 | bytes 1000000 | tf_op jit(solution)/shard_map/pallas_call | solution.py:46
  76.3 5.0 %collective-permute-start.16 = (f32[1024,128]{1,0:T(8,128)S(1)}, f32[1024,128]{1,0:T(8,128)S(1)}, u32[]{:S(2)}, u32[]{:S(2)}) collective-permute-start(f32[1024,128]{1,0:T(8,128)S(1)} %get-tuple-element.56), channel_id=1, source_target_pairs={{0,1},{8,9},{16,17},{24,25},{32,33},{40,41},{48,49},{56,57},{1,2},... | collective-permute-start | bytes 1572872 | tf_op jit(solution)/shard_map/ppermute | solution.py:79
  81.3 3.3 %collective-permute-start.17 = (f32[1024,128]{1,0:T(8,128)S(1)}, f32[1024,128]{1,0:T(8,128)S(1)}, u32[]{:S(2)}, u32[]{:S(2)}) collective-permute-start(f32[1024,128]{1,0:T(8,128)S(1)} %get-tuple-element.57), channel_id=1, source_target_pairs={{1,0},{9,8},{17,16},{25,24},{33,32},{41,40},{49,48},{57,56},{2,1},... | collective-permute-start | bytes 1572872 | tf_op jit(solution)/shard_map/ppermute | solution.py:85
  84.5 0.0 collective-permute-done.11.south
  84.6 0.7 collective-permute-start.18
  85.3 0.0 collective-permute-done.12.north
  85.3 0.0 copy-start.5
  85.3 0.0 copy-start.6
  85.3 0.0 copy-start.8
  85.3 0.0 copy-start.9
  85.3 1.1 shard_map.121
  86.4 0.0 copy-start.2
  86.4 0.0 copy-start.10
  86.4 0.0 collective-permute-start.14
  86.5 2.9 %collective-permute-start.15 = (f32[664,128]{1,0:T(8,128)S(1)}, f32[664,128]{1,0:T(8,128)S(1)}, u32[]{:S(2)}, u32[]{:S(2)}) collective-permute-start(f32[664,128]{1,0:T(8,128)S(1)} %get-tuple-element.54), channel_id=1, source_target_pairs={{0,56},{8,0},{16,8},{24,16},{32,24},{40,32},{48,40},{56,48},{1,57}... | collective-permute-start | bytes 1019912 | tf_op jit(solution)/shard_map/ppermute | solution.py:101
  89.4 13.4 %collective-permute-done.16.south = f32[1024,128]{1,0:T(8,128)S(1)} collective-permute-done((f32[1024,128]{1,0:T(8,128)S(1)}, f32[1024,128]{1,0:T(8,128)S(1)}, u32[]{:S(2)}, u32[]{:S(2)}) %collective-permute-start.16) | collective-permute-done | bytes 524320 | tf_op jit(solution)/shard_map/ppermute | solution.py:79
  102.9 0.0 collective-permute-start.19
  102.9 1.8 %collective-permute-done.17.north = f32[1024,128]{1,0:T(8,128)S(1)} collective-permute-done((f32[1024,128]{1,0:T(8,128)S(1)}, f32[1024,128]{1,0:T(8,128)S(1)}, u32[]{:S(2)}, u32[]{:S(2)}) %collective-permute-start.17) | collective-permute-done | bytes 524320 | tf_op jit(solution)/shard_map/ppermute | solution.py:85
  104.7 1.3 collective-permute-start.20
  105.9 0.0 collective-permute-done.18.fold
  105.9 0.8 shard_map.123
  106.7 0.0 collective-permute-start.21
  106.8 0.0 collective-permute-done.14.w2.refs_7_
  106.8 2.9 %collective-permute-start.22 = (f32[256,128]{1,0:T(8,128)S(1)}, f32[256,128]{1,0:T(8,128)S(1)}, u32[]{:S(2)}, u32[]{:S(2)}) collective-permute-start(f32[256,128]{1,0:T(8,128)S(1)} %get-tuple-element.62), channel_id=1, source_target_pairs={{0,56},{8,0},{16,8},{24,16},{32,24},{40,32},{48,40},{56,48},{1,57}... | collective-permute-start | bytes 393224 | tf_op jit(solution)/shard_map/ppermute | solution.py:101
  109.7 7.9 %shard_map.114.flux = f32[4,32,128]{2,1,0:T(8,128)S(1)} custom-call(f32[296,128]{1,0:T(8,128)S(1)} %collective-permute-done.up, f32[296,128]{1,0:T(8,128)S(1)} %copy-done.5, f32[296,128]{1,0:T(8,128)S(1)} %collective-permute-done.1.down, f32[744,128]{1,0:T(8,128)S(1)} %collective-permute-done.2.west, f32[744,128]{1,0:T(8,128)S(1)} %collective-permute-done.3.east, ...), custom_call_target="tpu_custom_call" | custom-call | flops 20000000 | bytes 1000000 | tf_op jit(solution)/shard_map/pallas_call | solution.py:46
  117.6 2.7 %shard_map.115 = f32[4,32,32,128]{3,2,1,0:T(8,128)} custom-call(f32[4,32,32,128]{3,2,1,0:T(8,128)S(1)} %copy-done.2, f32[32,128]{1,0:T(8,128)S(1)} %copy-done.10, f32[4,32,128]{2,1,0:T(8,128)S(1)} %shard_map.114.flux), custom_call_target="tpu_custom_call" | custom-call | flops 5000000 | bytes 4200000 | tf_op jit(solution)/shard_map/pallas_call | solution.py:646
  120.3 0.0 collective-permute-done.15.e2.refs_8_
  120.3 4.2 %shard_map.124.refs_14_ = f32[2,32,128]{2,1,0:T(8,128)S(1)} custom-call(f32[7,80,128]{2,1,0:T(8,128)S(1)} %get-tuple-element.63.mine, f32[664,128]{1,0:T(8,128)S(1)} %collective-permute-done.14.w2.refs_7_, f32[664,128]{1,0:T(8,128)S(1)} %collective-permute-done.15.e2.refs_8_), custom_call_target="tpu_custom_call" | custom-call | flops 10000000 | bytes 1000000 | tf_op jit(solution)/shard_map/pallas_call | solution.py:46
  124.6 0.0 collective-permute-done.19.refs_10_
  124.6 0.0 collective-permute-done.20.refs_11_
  124.6 0.0 collective-permute-done.22.refs_13_
  124.6 17.1 %shard_map.125 = f32[2048,128]{1,0:T(8,128)} custom-call(f32[4,16,128,128]{3,2,1,0:T(8,128)S(1)} %get-tuple-element.39.refs_0_, f32[1024,128]{1,0:T(8,128)S(1)} %collective-permute-done.4.refs_1_, f32[1024,128]{1,0:T(8,128)S(1)} %collective-permute-done.5.refs_2_, f32[4,8,128,128]{3,2,1,0:T(8,128)S(1)} %get-tuple-element.44.refs_3_, ...), custom_call_target="tpu_custom_call" | custom-call | flops 60000000 | bytes 1000000 | tf_op jit(solution)/shard_map/pallas_call | solution.py:46
  (18 shorter events, 0.0 us)
Async XLA Ops:
  0.6 20.8 %copy-start = (f32[2,32,32,128]{3,2,1,0:T(8,128)S(1)}, f32[2,32,32,128]{3,2,1,0:T(8,128)}, u32[]{:S(2)}) copy-start(f32[2,32,32,128]{3,2,1,0:T(8,128)} %tracers.3) | copy-start | bytes 3145732
  0.6 20.7 %copy-start.1 = (f32[2,32,32,128]{3,2,1,0:T(8,128)S(1)}, f32[2,32,32,128]{3,2,1,0:T(8,128)}, u32[]{:S(2)}) copy-start(f32[2,32,32,128]{3,2,1,0:T(8,128)} %flow.3) | copy-start | bytes 3145732
  0.7 20.7 %copy-start.3 = (f32[32,32,128]{2,1,0:T(8,128)S(1)}, f32[32,32,128]{2,1,0:T(8,128)}, u32[]{:S(2)}) copy-start(f32[32,32,128]{2,1,0:T(8,128)} %kappa.3) | copy-start | bytes 1572868
  0.7 20.7 %copy-start.7 = (s32[32,128]{1,0:T(8,128)S(1)}, s32[32,128]{1,0:T(8,128)}, u32[]{:S(2)}) copy-start(s32[32,128]{1,0:T(8,128)} %mask.7) | copy-start | bytes 49156
  2.7 12.5 %collective-permute-start = (f32[296,128]{1,0:T(8,128)}, f32[296,128]{1,0:T(8,128)S(1)}, u32[]{:S(2)}, u32[]{:S(2)}) collective-permute-start(f32[296,128]{1,0:T(8,128)} %get-tuple-element.34), channel_id=1, source_target_pairs={{0,1},{8,9},{16,17},{24,25},{32,33},{40,41},{48,49},{56,57},{1,2},... | collective-permute-start | bytes 454664 | tf_op jit(solution)/shard_map/ppermute | solution.py:79
  8.4 9.0 %collective-permute-start.1 = (f32[296,128]{1,0:T(8,128)}, f32[296,128]{1,0:T(8,128)S(1)}, u32[]{:S(2)}, u32[]{:S(2)}) collective-permute-start(f32[296,128]{1,0:T(8,128)} %get-tuple-element.36), channel_id=1, source_target_pairs={{1,0},{9,8},{17,16},{25,24},{33,32},{41,40},{49,48},{57,56},{2,1},... | collective-permute-start | bytes 454664 | tf_op jit(solution)/shard_map/ppermute | solution.py:85
  17.4 0.9 copy-start.4
  18.4 16.3 %collective-permute-start.2 = (f32[744,128]{1,0:T(8,128)S(1)}, f32[744,128]{1,0:T(8,128)S(1)}, u32[]{:S(2)}, u32[]{:S(2)}) collective-permute-start(f32[744,128]{1,0:T(8,128)S(1)} %get-tuple-element.37), channel_id=1, source_target_pairs={{0,8},{8,16},{16,24},{24,32},{32,40},{40,48},{48,56},{56,0},{1,9},... | collective-permute-start | bytes 1142792 | tf_op jit(solution)/shard_map/ppermute | solution.py:96
  18.4 16.3 %collective-permute-start.3 = (f32[744,128]{1,0:T(8,128)S(1)}, f32[744,128]{1,0:T(8,128)S(1)}, u32[]{:S(2)}, u32[]{:S(2)}) collective-permute-start(f32[744,128]{1,0:T(8,128)S(1)} %get-tuple-element.38), channel_id=1, source_target_pairs={{0,56},{8,0},{16,8},{24,16},{32,24},{40,32},{48,40},{56,48},{1,57}... | collective-permute-start | bytes 1142792 | tf_op jit(solution)/shard_map/ppermute | solution.py:101
  22.8 30.5 %collective-permute-start.6 = (f32[1280,128]{1,0:T(8,128)S(1)}, f32[1280,128]{1,0:T(8,128)S(1)}, u32[]{:S(2)}, u32[]{:S(2)}) collective-permute-start(f32[1280,128]{1,0:T(8,128)S(1)} %get-tuple-element.43), channel_id=1, source_target_pairs={{0,1},{8,9},{16,17},{24,25},{32,33},{40,41},{48,49},{56,57},{1,2},... | collective-permute-start | bytes 1966088 | tf_op jit(solution)/shard_map/ppermute | solution.py:79
  26.3 32.8 %collective-permute-start.7 = (f32[1280,128]{1,0:T(8,128)S(1)}, f32[1280,128]{1,0:T(8,128)S(1)}, u32[]{:S(2)}, u32[]{:S(2)}) collective-permute-start(f32[1280,128]{1,0:T(8,128)S(1)} %get-tuple-element.42.own), channel_id=1, source_target_pairs={{1,0},{9,8},{17,16},{25,24},{33,32},{41,40},{49,48},{57,56},{2,1},... | collective-permute-start | bytes 1966088 | tf_op jit(solution)/shard_map/ppermute | solution.py:85
  31.1 28.8 %collective-permute-start.8 = (f32[1280,128]{1,0:T(8,128)S(1)}, f32[1280,128]{1,0:T(8,128)S(1)}, u32[]{:S(2)}, u32[]{:S(2)}) collective-permute-start(f32[1280,128]{1,0:T(8,128)S(1)} %get-tuple-element.43), channel_id=1, source_target_pairs={{71,127},{79,119},{87,111},{95,103},{103,95},{111,87},{119,79},{12... | collective-permute-start | bytes 1966088 | tf_op jit(solution)/shard_map/ppermute | solution.py:91
  34.7 28.6 %collective-permute-start.4 = (f32[1024,128]{1,0:T(8,128)S(1)}, f32[1024,128]{1,0:T(8,128)S(1)}, u32[]{:S(2)}, u32[]{:S(2)}) collective-permute-start(f32[1024,128]{1,0:T(8,128)S(1)} %get-tuple-element.40), channel_id=1, source_target_pairs={{0,8},{8,16},{16,24},{24,32},{32,40},{40,48},{48,56},{56,0},{1,9},... | collective-permute-start | bytes 1572872 | tf_op jit(solution)/shard_map/ppermute | solution.py:96
  34.7 28.6 %collective-permute-start.5 = (f32[1024,128]{1,0:T(8,128)S(1)}, f32[1024,128]{1,0:T(8,128)S(1)}, u32[]{:S(2)}, u32[]{:S(2)}) collective-permute-start(f32[1024,128]{1,0:T(8,128)S(1)} %get-tuple-element.41), channel_id=1, source_target_pairs={{0,56},{8,0},{16,8},{24,16},{32,24},{40,32},{48,40},{56,48},{1,57}... | collective-permute-start | bytes 1572872 | tf_op jit(solution)/shard_map/ppermute | solution.py:101
  53.3 31.3 %collective-permute-start.11 = (f32[936,128]{1,0:T(8,128)S(1)}, f32[936,128]{1,0:T(8,128)S(1)}, u32[]{:S(2)}, u32[]{:S(2)}) collective-permute-start(f32[936,128]{1,0:T(8,128)S(1)} %get-tuple-element.50), channel_id=1, source_target_pairs={{0,1},{8,9},{16,17},{24,25},{32,33},{40,41},{48,49},{56,57},{1,2},... | collective-permute-start | bytes 1437704 | tf_op jit(solution)/shard_map/ppermute | solution.py:79
  59.2 26.1 %collective-permute-start.13 = (f32[936,128]{1,0:T(8,128)S(1)}, f32[936,128]{1,0:T(8,128)S(1)}, u32[]{:S(2)}, u32[]{:S(2)}) collective-permute-start(f32[936,128]{1,0:T(8,128)S(1)} %get-tuple-element.50), channel_id=1, source_target_pairs={{71,127},{79,119},{87,111},{95,103},{103,95},{111,87},{119,79},{12... | collective-permute-start | bytes 1437704 | tf_op jit(solution)/shard_map/ppermute | solution.py:91
  59.9 25.4 %collective-permute-start.12 = (f32[936,128]{1,0:T(8,128)S(1)}, f32[936,128]{1,0:T(8,128)S(1)}, u32[]{:S(2)}, u32[]{:S(2)}) collective-permute-start(f32[936,128]{1,0:T(8,128)S(1)} %get-tuple-element.51), channel_id=1, source_target_pairs={{1,0},{9,8},{17,16},{25,24},{33,32},{41,40},{49,48},{57,56},{2,1},... | collective-permute-start | bytes 1437704 | tf_op jit(solution)/shard_map/ppermute | solution.py:85
  63.3 3.9 %collective-permute-start.10 = (f32[512,128]{1,0:T(8,128)S(1)}, f32[512,128]{1,0:T(8,128)S(1)}, u32[]{:S(2)}, u32[]{:S(2)}) collective-permute-start(f32[512,128]{1,0:T(8,128)S(1)} %get-tuple-element.46), channel_id=1, source_target_pairs={{0,56},{8,0},{16,8},{24,16},{32,24},{40,32},{48,40},{56,48},{1,57}... | collective-permute-start | bytes 786440 | tf_op jit(solution)/shard_map/ppermute | solution.py:101
  63.4 7.0 %collective-permute-start.9 = (f32[512,128]{1,0:T(8,128)S(1)}, f32[512,128]{1,0:T(8,128)S(1)}, u32[]{:S(2)}, u32[]{:S(2)}) collective-permute-start(f32[512,128]{1,0:T(8,128)S(1)} %get-tuple-element.45), channel_id=1, source_target_pairs={{0,8},{8,16},{16,24},{24,32},{32,40},{40,48},{48,56},{56,0},{1,9},... | collective-permute-start | bytes 786440 | tf_op jit(solution)/shard_map/ppermute | solution.py:96
  76.3 26.6 %collective-permute-start.16 = (f32[1024,128]{1,0:T(8,128)S(1)}, f32[1024,128]{1,0:T(8,128)S(1)}, u32[]{:S(2)}, u32[]{:S(2)}) collective-permute-start(f32[1024,128]{1,0:T(8,128)S(1)} %get-tuple-element.56), channel_id=1, source_target_pairs={{0,1},{8,9},{16,17},{24,25},{32,33},{40,41},{48,49},{56,57},{1,2},... | collective-permute-start | bytes 1572872 | tf_op jit(solution)/shard_map/ppermute | solution.py:79
  81.3 23.4 %collective-permute-start.17 = (f32[1024,128]{1,0:T(8,128)S(1)}, f32[1024,128]{1,0:T(8,128)S(1)}, u32[]{:S(2)}, u32[]{:S(2)}) collective-permute-start(f32[1024,128]{1,0:T(8,128)S(1)} %get-tuple-element.57), channel_id=1, source_target_pairs={{1,0},{9,8},{17,16},{25,24},{33,32},{41,40},{49,48},{57,56},{2,1},... | collective-permute-start | bytes 1572872 | tf_op jit(solution)/shard_map/ppermute | solution.py:85
  84.6 21.4 %collective-permute-start.18 = (f32[1024,128]{1,0:T(8,128)S(1)}, f32[1024,128]{1,0:T(8,128)S(1)}, u32[]{:S(2)}, u32[]{:S(2)}) collective-permute-start(f32[1024,128]{1,0:T(8,128)S(1)} %get-tuple-element.56), channel_id=1, source_target_pairs={{71,127},{79,119},{87,111},{95,103},{103,95},{111,87},{119,79},{12... | collective-permute-start | bytes 1572872 | tf_op jit(solution)/shard_map/ppermute | solution.py:91
  85.3 24.4 %copy-start.5 = (f32[296,128]{1,0:T(8,128)S(1)}, f32[296,128]{1,0:T(8,128)}, u32[]{:S(2)}) copy-start(f32[296,128]{1,0:T(8,128)} %get-tuple-element.35.mine) | copy-start | bytes 454660
  85.3 24.4 %copy-start.6 = (f32[2,3,3,1024]{3,0,2,1:T(2,128)S(1)}, f32[2,3,3,1024]{3,0,2,1:T(2,128)}, u32[]{:S(2)}) copy-start(f32[2,3,3,1024]{3,0,2,1:T(2,128)} %param.17) | copy-start | bytes 221188
  85.3 24.4 %copy-start.8 = (s32[3,3,1024]{2,1,0:T(4,128)S(1)}, s32[3,3,1024]{2,1,0:T(4,128)}, u32[]{:S(2)}) copy-start(s32[3,3,1024]{2,1,0:T(4,128)} %sea_cells.3) | copy-start | bytes 110596
  85.3 24.4 %copy-start.9 = (s32[3,3,1024]{2,1,0:T(4,128)S(1)}, s32[3,3,1024]{2,1,0:T(4,128)}, u32[]{:S(2)}) copy-start(s32[3,3,1024]{2,1,0:T(4,128)} %air_cells.3) | copy-start | bytes 110596
  86.4 31.2 %copy-start.2 = (f32[4,32,32,128]{3,2,1,0:T(8,128)S(1)}, f32[4,32,32,128]{3,2,1,0:T(8,128)}, u32[]{:S(2)}) copy-start(f32[4,32,32,128]{3,2,1,0:T(8,128)} %state.3) | copy-start | bytes 6291460
  86.4 31.2 %copy-start.10 = (f32[32,128]{1,0:T(8,128)S(1)}, f32[32,128]{1,0:T(8,128)}, u32[]{:S(2)}) copy-start(f32[32,128]{1,0:T(8,128)} %kappa.2) | copy-start | bytes 49156
  86.4 20.3 %collective-permute-start.14 = (f32[664,128]{1,0:T(8,128)S(1)}, f32[664,128]{1,0:T(8,128)S(1)}, u32[]{:S(2)}, u32[]{:S(2)}) collective-permute-start(f32[664,128]{1,0:T(8,128)S(1)} %get-tuple-element.53), channel_id=1, source_target_pairs={{0,8},{8,16},{16,24},{24,32},{32,40},{40,48},{48,56},{56,0},{1,9},... | collective-permute-start | bytes 1019912 | tf_op jit(solution)/shard_map/ppermute | solution.py:96
  86.5 33.8 %collective-permute-start.15 = (f32[664,128]{1,0:T(8,128)S(1)}, f32[664,128]{1,0:T(8,128)S(1)}, u32[]{:S(2)}, u32[]{:S(2)}) collective-permute-start(f32[664,128]{1,0:T(8,128)S(1)} %get-tuple-element.54), channel_id=1, source_target_pairs={{0,56},{8,0},{16,8},{24,16},{32,24},{40,32},{48,40},{56,48},{1,57}... | collective-permute-start | bytes 1019912 | tf_op jit(solution)/shard_map/ppermute | solution.py:101
  102.9 21.7 %collective-permute-start.19 = (f32[256,128]{1,0:T(8,128)S(1)}, f32[256,128]{1,0:T(8,128)S(1)}, u32[]{:S(2)}, u32[]{:S(2)}) collective-permute-start(f32[256,128]{1,0:T(8,128)S(1)} %get-tuple-element.59), channel_id=1, source_target_pairs={{0,8},{8,16},{16,24},{24,32},{32,40},{40,48},{48,56},{56,0},{1,9},... | collective-permute-start | bytes 393224 | tf_op jit(solution)/shard_map/ppermute | solution.py:96
  104.7 19.9 %collective-permute-start.20 = (f32[256,128]{1,0:T(8,128)S(1)}, f32[256,128]{1,0:T(8,128)S(1)}, u32[]{:S(2)}, u32[]{:S(2)}) collective-permute-start(f32[256,128]{1,0:T(8,128)S(1)} %get-tuple-element.60), channel_id=1, source_target_pairs={{0,56},{8,0},{16,8},{24,16},{32,24},{40,32},{48,40},{56,48},{1,57}... | collective-permute-start | bytes 393224 | tf_op jit(solution)/shard_map/ppermute | solution.py:101
  106.7 17.8 %collective-permute-start.21 = (f32[256,128]{1,0:T(8,128)S(1)}, f32[256,128]{1,0:T(8,128)S(1)}, u32[]{:S(2)}, u32[]{:S(2)}) collective-permute-start(f32[256,128]{1,0:T(8,128)S(1)} %get-tuple-element.61), channel_id=1, source_target_pairs={{0,8},{8,16},{16,24},{24,32},{32,40},{40,48},{48,56},{56,0},{1,9},... | collective-permute-start | bytes 393224 | tf_op jit(solution)/shard_map/ppermute | solution.py:96
  106.8 17.8 %collective-permute-start.22 = (f32[256,128]{1,0:T(8,128)S(1)}, f32[256,128]{1,0:T(8,128)S(1)}, u32[]{:S(2)}, u32[]{:S(2)}) collective-permute-start(f32[256,128]{1,0:T(8,128)S(1)} %get-tuple-element.62), channel_id=1, source_target_pairs={{0,56},{8,0},{16,8},{24,16},{32,24},{40,32},{48,40},{56,48},{1,57}... | collective-permute-start | bytes 393224 | tf_op jit(solution)/shard_map/ppermute | solution.py:101
